TPU v7x, 128 devices: a whole 4x4x4 slice. The times are simulated.
128 devices in a mesh: local: 16 (over z, y), data: 8 (over x, core).
Axes of the slice: x: 4, y: 4, z: 4, core: 2. Of those that a mesh axis runs over, the one named last changes fastest.
Arguments:
- tokens: bfloat16 [16384, 2048], P(('local', 'data'))
- grad_out: bfloat16 [16384, 2048], P(('local', 'data'))
- w_up: bfloat16 [2, 2048, 8192], P(None, ('local', 'data'))
- w_down: bfloat16 [2, 8192, 2048], P(None, ('local', 'data'))
Outputs:
- output 1: bfloat16 [16384, 2048], P(('local', 'data'))
- output 2: bfloat16 [16384, 2048], P(('local', 'data'))
- output 3: float32 [2, 2048, 8192], P(None, ('local', 'data'))
- output 4: float32 [2, 8192, 2048], P(None, ('local', 'data'))
All inputs are finite; a program needn't handle non-finite values.
Results may differ from a plain program's by a relative error of at most 0.0142873.
Values are sent between devices in bfloat16 or wider.
A program may use at most 1 GiB of HBM per device.

v0:
```python
import jax
import jax.numpy as jnp
from jax import lax
from jax.sharding import PartitionSpec as P

NORM_EPS = 1e-6
BOTH_AXES = ('local', 'data')
CONTRACT_ROWS = (((0,), (0,)), ((), ()))
CONTRACT_COLS = (((1,), (1,)), ((), ()))


def rms_norm(x_f32):
    return x_f32 * lax.rsqrt(jnp.mean(x_f32 * x_f32, axis=-1, keepdims=True) + NORM_EPS)


def gelu_tanh(values):
    return jax.nn.gelu(values, approximate=True)


def solution(mesh):
    n_local = mesh.shape['local']
    tok_spec = P(BOTH_AXES, None)
    w_spec = P(None, BOTH_AXES, None)

    def device_fn(tokens, grad_out, w_up, w_down):
        num_layers = w_up.shape[0]
        loc_index = lax.axis_index('local')
        saved_acts = []
        hidden_state = tokens
        for layer_idx in range(num_layers):
            up_full = lax.all_gather(w_up[layer_idx], BOTH_AXES, axis=0, tiled=True)
            down_full = lax.all_gather(w_down[layer_idx], BOTH_AXES, axis=0, tiled=True)
            up_rows = up_full.shape[0] // n_local
            down_rows = down_full.shape[0] // n_local
            up_second = lax.dynamic_slice_in_dim(up_full, loc_index * up_rows, up_rows, axis=0)
            down_second = lax.dynamic_slice_in_dim(down_full, loc_index * down_rows, down_rows, axis=0)
            x_f32 = hidden_state.astype(jnp.float32)
            normed = rms_norm(x_f32).astype(jnp.bfloat16)
            pre_act = jnp.dot(normed, up_full, preferred_element_type=jnp.float32).astype(jnp.bfloat16)
            hidden = gelu_tanh(pre_act.astype(jnp.float32)).astype(jnp.bfloat16)
            saved_acts.append((hidden_state, normed, pre_act, hidden, up_second, down_second))
            hidden_state = (x_f32 + jnp.dot(hidden, down_full, preferred_element_type=jnp.float32)).astype(jnp.bfloat16)
        cotangent = grad_out
        grads_up = [None] * num_layers
        grads_down = [None] * num_layers
        for layer_idx in reversed(range(num_layers)):
            layer_in, normed, pre_act, hidden, up_second, down_second = saved_acts[layer_idx]
            up_full = lax.all_gather(up_second, 'local', axis=0, tiled=True)
            down_full = lax.all_gather(down_second, 'local', axis=0, tiled=True)
            down_part = lax.dot_general(hidden, cotangent, CONTRACT_ROWS, preferred_element_type=jnp.float32)
            d_hidden = lax.dot_general(cotangent, down_full, CONTRACT_COLS, preferred_element_type=jnp.float32).astype(jnp.bfloat16)
            _, gelu_back = jax.vjp(gelu_tanh, pre_act.astype(jnp.float32))
            d_pre = gelu_back(d_hidden.astype(jnp.float32))[0].astype(jnp.bfloat16)
            up_part = lax.dot_general(normed, d_pre, CONTRACT_ROWS, preferred_element_type=jnp.float32)
            d_normed = lax.dot_general(d_pre, up_full, CONTRACT_COLS, preferred_element_type=jnp.float32)
            _, norm_back = jax.vjp(rms_norm, layer_in.astype(jnp.float32))
            cotangent = (cotangent.astype(jnp.float32) + norm_back(d_normed)[0]).astype(jnp.bfloat16)
            grads_up[layer_idx] = lax.psum_scatter(up_part, BOTH_AXES, scatter_dimension=0, tiled=True)
            grads_down[layer_idx] = lax.psum_scatter(down_part, BOTH_AXES, scatter_dimension=0, tiled=True)
        return hidden_state, cotangent, jnp.stack(grads_up), jnp.stack(grads_down)

    return jax.shard_map(device_fn, mesh=mesh, in_specs=(tok_spec, tok_spec, w_spec, w_spec), out_specs=(tok_spec, tok_spec, w_spec, w_spec), check_vma=False)
```

profile of v0, /device:TPU:1, one launch (start us, length us, event | category | flops | bytes accessed | tf_op | source)
XLA Modules:
  0.0 4249.0 jit_solution(13906489191920257494)
XLA Ops:
  7.2 1.9 fusion.92
  9.2 1.9 fusion.91
  12.4 109.1 %all-gather.23.cloned.1.call-done = bf16[1,8192,2048]{2,1,0:T(8,128)(2,1)} async-done(((bf16[1,64,2048]{2,1,0:T(8,128)(2,1)}), bf16[1,8192,2048]{2,1,0:T(8,128)(2,1)}) %all-gather.23.cloned.1.call-update) | async-done | bytes 33554448 | tf_op jit(solution)/shard_map/all_gather | solution.py:32
  121.5 3.2 constant_dynamic-slice_fusion.3
  124.7 106.0 %all-gather.21.cloned.1.call-done = bf16[1,2048,8192]{2,1,0:T(8,128)(2,1)} async-done(((bf16[1,16,8192]{2,1,0:T(8,128)(2,1)}), bf16[1,2048,8192]{2,1,0:T(8,128)(2,1)}) %all-gather.21.cloned.1.call-update) | async-done | bytes 33554448 | tf_op jit(solution)/shard_map/all_gather | solution.py:31
  230.7 3.1 constant_dynamic-slice_fusion.2
  233.9 106.1 %all-gather.19.cloned.1.call-done = bf16[1,8192,2048]{2,1,0:T(8,128)(2,1)} async-done(((bf16[1,64,2048]{2,1,0:T(8,128)(2,1)}), bf16[1,8192,2048]{2,1,0:T(8,128)(2,1)}) %all-gather.19.cloned.1.call-update) | async-done | bytes 33554448 | tf_op jit(solution)/shard_map/all_gather | solution.py:32
  340.0 3.2 constant_dynamic-slice_fusion.1
  343.2 105.8 %all-gather.17.cloned.1.call-done = bf16[1,2048,8192]{2,1,0:T(8,128)(2,1)} async-done(((bf16[1,16,8192]{2,1,0:T(8,128)(2,1)}), bf16[1,2048,8192]{2,1,0:T(8,128)(2,1)}) %all-gather.17.cloned.1.call-update) | async-done | bytes 33554448 | tf_op jit(solution)/shard_map/all_gather | solution.py:31
  449.1 3.1 constant_dynamic-slice_fusion
  452.4 13.0 fusion.19
  465.5 15.2 multiply_reduce_fusion.1
  480.7 17.2 fusion.25
  497.9 149.0 %all-gather.25.cloned.1.call-done = bf16[1,8192,2048]{2,1,0:T(8,128)(2,1)} async-done(((bf16[1,512,2048]{2,1,0:T(8,128)(2,1)}), bf16[1,8192,2048]{2,1,0:T(8,128)(2,1)}) %all-gather.25.cloned.1.call-update) | async-done | bytes 33554448 | tf_op jit(solution)/shard_map/all_gather | solution.py:49
  646.9 19.2 fusion.56
  667.4 23.1 fusion.88
  690.6 154.9 %all-gather.27.cloned.1.call-done = bf16[1,2048,8192]{2,1,0:T(8,128)(2,1)} async-done(((bf16[1,128,8192]{2,1,0:T(8,128)(2,1)}), bf16[1,2048,8192]{2,1,0:T(8,128)(2,1)}) %all-gather.27.cloned.1.call-update) | async-done | bytes 33554448 | tf_op jit(solution)/shard_map/all_gather | solution.py:48
  845.6 16.7 multiply_reduce_fusion
  862.6 181.9 %all-gather.29.cloned.1.call-done = bf16[1,8192,2048]{2,1,0:T(8,128)(2,1)} async-done(((bf16[1,512,2048]{2,1,0:T(8,128)(2,1)}), bf16[1,8192,2048]{2,1,0:T(8,128)(2,1)}) %all-gather.29.cloned.1.call-update) | async-done | bytes 33554448 | tf_op jit(solution)/shard_map/all_gather | solution.py:49
  1044.5 18.8 fusion.49
  1063.3 24.8 fusion.83
  1088.2 25.4 fusion.90
  1113.6 25.6 fusion.89
  1139.3 17.7 fusion.67
  1157.0 86.3 %all-gather.31.cloned.1.call-done = bf16[1,2048,8192]{2,1,0:T(8,128)(2,1)} async-done(((bf16[1,128,8192]{2,1,0:T(8,128)(2,1)}), bf16[1,2048,8192]{2,1,0:T(8,128)(2,1)}) %all-gather.31.cloned.1.call-update) | async-done | bytes 33554448 | tf_op jit(solution)/shard_map/all_gather | solution.py:48
  1243.3 16.5 fusion.82
  1261.0 730.6 %reduce-scatter.7.cloned.1.call-done = f32[16,8192]{1,0:T(8,128)} async-done(((f32[2048,8192]{1,0:T(8,128)}), f32[16,8192]{1,0:T(8,128)}) %reduce-scatter.7.cloned.1.call-update) | async-done | bytes 524304 | tf_op jit(solution)/shard_map/reduce_scatter | solution.py:58
  1991.6 749.2 %reduce-scatter.5.cloned.1.call-done = f32[16,8192]{1,0:T(8,128)} async-done(((f32[2048,8192]{1,0:T(8,128)}), f32[16,8192]{1,0:T(8,128)}) %reduce-scatter.5.cloned.1.call-update) | async-done | bytes 524304 | tf_op jit(solution)/shard_map/reduce_scatter | solution.py:58
  2740.8 2.2 pad_maximum_fusion
  2743.1 747.2 %reduce-scatter.11.cloned.1.call-done = f32[64,2048]{1,0:T(8,128)} async-done(((f32[8192,2048]{1,0:T(8,128)}), f32[64,2048]{1,0:T(8,128)}) %reduce-scatter.11.cloned.1.call-update) | async-done | bytes 524304 | tf_op jit(solution)/shard_map/reduce_scatter | solution.py:59
  3490.2 749.2 %reduce-scatter.9.cloned.1.call-done = f32[64,2048]{1,0:T(8,128)} async-done(((f32[8192,2048]{1,0:T(8,128)}), f32[64,2048]{1,0:T(8,128)}) %reduce-scatter.9.cloned.1.call-update) | async-done | bytes 524304 | tf_op jit(solution)/shard_map/reduce_scatter | solution.py:59
  4239.5 2.3 pad_maximum_fusion.1
  (43 shorter events, 4.9 us)
Async XLA Ops:
  7.2 114.3 %all-gather.23.cloned.1.call-start = ((), (), s32[]{:S(2)}) async-start(), calls=%async_computation.11 | async-start | bytes 33816576 | tf_op jit(solution)/shard_map/all_gather | solution.py:32
  9.1 221.6 %all-gather.21.cloned.1.call-start = ((), (), s32[]{:S(2)}) async-start(), calls=%async_computation.10 | async-start | bytes 33816576 | tf_op jit(solution)/shard_map/all_gather | solution.py:31
  11.0 328.9 %all-gather.19.cloned.1.call-start = ((), (), s32[]{:S(2)}) async-start(), calls=%async_computation.9 | async-start | bytes 33816576 | tf_op jit(solution)/shard_map/all_gather | solution.py:32
  11.8 437.3 %all-gather.17.cloned.1.call-start = ((), (), s32[]{:S(2)}) async-start(), calls=%async_computation.8 | async-start | bytes 33816576 | tf_op jit(solution)/shard_map/all_gather | solution.py:31
  12.3 634.5 %all-gather.25.cloned.1.call-start = ((), (), s32[]{:S(2)}) async-start(), calls=%async_computation.12 | async-start | bytes 35651584 | tf_op jit(solution)/shard_map/all_gather | solution.py:49
  124.7 720.9 %all-gather.27.cloned.1.call-start = ((), (), s32[]{:S(2)}) async-start(), calls=%async_computation.13 | async-start | bytes 35651584 | tf_op jit(solution)/shard_map/all_gather | solution.py:48
  233.8 810.6 %all-gather.29.cloned.1.call-start = ((), (), s32[]{:S(2)}) async-start(), calls=%async_computation.14 | async-start | bytes 35651584 | tf_op jit(solution)/shard_map/all_gather | solution.py:49
  343.1 109.1 %copy-start.1 = (bf16[128,2048]{1,0:T(8,128)(2,1)S(1)}, bf16[128,2048]{1,0:T(8,128)(2,1)}, u32[]{:S(2)}) copy-start(bf16[128,2048]{1,0:T(8,128)(2,1)} %param.4) | copy-start | bytes 1572868
  343.2 900.2 %all-gather.31.cloned.1.call-start = ((), (), s32[]{:S(2)}) async-start(), calls=%async_computation.15 | async-start | bytes 35651584 | tf_op jit(solution)/shard_map/all_gather | solution.py:48
  452.2 1539.4 %reduce-scatter.7.cloned.1.call-start = ((), (), s32[]{:S(2)}) async-start(), calls=%async_computation.5 | async-start | bytes 67633152 | tf_op jit(solution)/shard_map/reduce_scatter | solution.py:58
  452.4 13.0 copy-start.4
  465.5 15.2 copy-start
  480.7 166.2 %copy-start.3 = (bf16[128,2048]{1,0:T(8,128)(2,1)S(1)}, bf16[128,2048]{1,0:T(8,128)(2,1)}, u32[]{:S(2)}) copy-start(bf16[128,2048]{1,0:T(8,128)(2,1)} %param.5) | copy-start | bytes 1572868
  666.1 1.3 copy-start.2
  690.6 2050.3 %reduce-scatter.5.cloned.1.call-start = ((), (), s32[]{:S(2)}) async-start(), calls=%async_computation.4 | async-start | bytes 67633152 | tf_op jit(solution)/shard_map/reduce_scatter | solution.py:58
  1088.1 2402.1 %reduce-scatter.11.cloned.1.call-start = ((), (), s32[]{:S(2)}) async-start(), calls=%async_computation.7 | async-start | bytes 67633152 | tf_op jit(solution)/shard_map/reduce_scatter | solution.py:59
  1113.6 3125.9 %reduce-scatter.9.cloned.1.call-start = ((), (), s32[]{:S(2)}) async-start(), calls=%async_computation.6 | async-start | bytes 67633152 | tf_op jit(solution)/shard_map/reduce_scatter | solution.py:59
  1157.0 102.8 %copy-start.5 = (f32[128]{0:T(128)S(1)}, f32[128]{0:T(128)}, u32[]{:S(2)}) copy-start(f32[128]{0:T(128)} %copy-done.4) | copy-start | bytes 1540
Sparse Core Ops, SparseCore 0:
  11.5 109.9 all-gather.22
  125.0 105.6 all-gather.20
  234.3 105.6 all-gather.18
  343.4 105.6 all-gather.16
  451.0 195.7 all-gather.24
  648.9 196.6 all-gather.26
  847.7 196.7 all-gather.28
  1046.6 196.6 all-gather.30
  1245.8 745.7 reduce-scatter.6
  1993.8 746.9 reduce-scatter.4
  2743.2 746.9 reduce-scatter.10
  3492.5 746.9 reduce-scatter.8
where the time goes:
time: 4260 us; the launch traced here: 4250 us
  waiting for transfers between devices  3980 us (93%)
  matrix products  233 us (5%)
    reduce_scatter x2, waiting for transfers between devices, device_fn(): lax.psum_scatter(down_part, BOTH_AXES, scatter_dimension=0, tiled=True)  1500 us
    reduce_scatter x2, waiting for transfers between devices, device_fn(): lax.psum_scatter(up_part, BOTH_AXES, scatter_dimension=0, tiled=True)  1480 us
    all_gather x2, waiting for transfers between devices, device_fn(): down_full = lax.all_gather(down_second, 'local', axis=0, tiled=True)  331 us
    all_gather x2, waiting for transfers between devices, device_fn(): up_full = lax.all_gather(up_second, 'local', axis=0, tiled=True)  241 us
    all_gather x2, waiting for transfers between devices, device_fn(): down_full = lax.all_gather(w_down[layer_idx], BOTH_AXES, axis=0, tiled=True)  215 us
    all_gather x2, waiting for transfers between devices, device_fn(): up_full = lax.all_gather(w_up[layer_idx], BOTH_AXES, axis=0, tiled=True)  212 us
  transfers between devices with their start and end apart: 12, of which 12 were waited for; matrix products, arithmetic and copies ran while one was open for 6% of the time, Pallas kernels for 0%

commit v1 on v0

v1 whole, which is shorter than its diff:
```python
import jax
import jax.numpy as jnp
from jax import lax
from jax.sharding import PartitionSpec as P

NORM_EPS = 1e-6
BOTH_AXES = ('local', 'data')
CONTRACT_ROWS = (((0,), (0,)), ((), ()))
CONTRACT_COLS = (((1,), (1,)), ((), ()))


def rms_norm(x_f32):
    return x_f32 * lax.rsqrt(jnp.mean(x_f32 * x_f32, axis=-1, keepdims=True) + NORM_EPS)


def gelu_tanh(values):
    return jax.nn.gelu(values, approximate=True)


def solution(mesh):
    nl, nd = mesh.shape['local'], mesh.shape['data']
    tok_spec = P(BOTH_AXES, None)
    w_spec = P(None, BOTH_AXES, None)

    def device_fn(tokens, grad_out, w_up, w_down):
        num_layers, up_rows, ffn = w_up.shape
        down_rows = w_down.shape[1]

        def gather_up(w):
            cols = w.reshape(up_rows, nl, nd, down_rows).transpose(2, 0, 1, 3).reshape(nd, up_rows, nl * down_rows)
            rows = lax.all_to_all(cols, 'data', 0, 0, tiled=True)
            return lax.all_gather(rows.reshape(nd * up_rows, nl * down_rows), 'local', axis=0, tiled=True)

        def gather_down(w):
            return lax.all_gather(w, 'local', axis=0, tiled=True)

        def scatter_up(part):
            mine = lax.psum_scatter(part, 'local', scatter_dimension=0, tiled=True)
            cols = lax.all_to_all(mine.reshape(nd, up_rows, nl * down_rows), 'data', 0, 0, tiled=True)
            return cols.reshape(nd, up_rows, nl, down_rows).transpose(1, 2, 0, 3).reshape(up_rows, ffn)

        def scatter_down(part):
            return lax.psum_scatter(part, 'local', scatter_dimension=0, tiled=True)

        g_full = lax.all_gather(grad_out, 'data', axis=0, tiled=True)
        x = tokens
        saved = []
        for l in range(num_layers):
            up, down = gather_up(w_up[l]), gather_down(w_down[l])
            x_f32 = x.astype(jnp.float32)
            u = rms_norm(x_f32).astype(jnp.bfloat16)
            u_full = lax.all_gather(u, 'data', axis=0, tiled=True)
            a = jnp.dot(u_full, up, preferred_element_type=jnp.float32).astype(jnp.bfloat16)
            s = gelu_tanh(a.astype(jnp.float32)).astype(jnp.bfloat16)
            saved.append((x, u_full, a, s))
            part = jnp.dot(s, down, preferred_element_type=jnp.float32)
            x = (x_f32 + lax.psum_scatter(part, 'data', scatter_dimension=0, tiled=True)).astype(jnp.bfloat16)
        dy, dy_full = grad_out, g_full
        grads_up, grads_down = [None] * num_layers, [None] * num_layers
        for l in reversed(range(num_layers)):
            if l < num_layers - 1:
                w_up, w_down, dy_full = lax.optimization_barrier((w_up, w_down, lax.all_gather(dy, 'data', axis=0, tiled=True)))
                up, down = gather_up(w_up[l]), gather_down(w_down[l])
            x_in, u_full, a, s = saved[l]
            ds = lax.dot_general(dy_full, down, CONTRACT_COLS, preferred_element_type=jnp.float32).astype(jnp.bfloat16)
            _, gelu_back = jax.vjp(gelu_tanh, a.astype(jnp.float32))
            da = gelu_back(ds.astype(jnp.float32))[0].astype(jnp.bfloat16)
            du_part = lax.dot_general(da, up, CONTRACT_COLS, preferred_element_type=jnp.float32)
            down_part = lax.dot_general(s, dy_full, CONTRACT_ROWS, preferred_element_type=jnp.float32)
            up_part = lax.dot_general(u_full, da, CONTRACT_ROWS, preferred_element_type=jnp.float32)
            du = lax.psum_scatter(du_part, 'data', scatter_dimension=0, tiled=True)
            _, norm_back = jax.vjp(rms_norm, x_in.astype(jnp.float32))
            dy = (dy.astype(jnp.float32) + norm_back(du)[0]).astype(jnp.bfloat16)
            grads_up[l] = scatter_up(up_part)
            grads_down[l] = scatter_down(down_part)
        return x, dy, jnp.stack(grads_up), jnp.stack(grads_down)

    return jax.shard_map(device_fn, mesh=mesh, in_specs=(tok_spec, tok_spec, w_spec, w_spec), out_specs=(tok_spec, tok_spec, w_spec, w_spec), check_vma=False)
```

time: 4260 us -> 1080 us (0.25)
  waiting for transfers between devices: 3980 us -> 858 us
  matrix products: 233 us -> 114 us
  blocking collectives: 0 us -> 49.6 us
    reduce_scatter x4 -> x8, waiting for transfers between devices: 2980 us -> 504 us  [the longest x2 164 us: scatter_up(): mine = lax.psum_scatter(part, 'local', scatter_dimension=0, tiled=True)]
    all_gather x8 -> x10, waiting for transfers between devices: 999 us -> 353 us  [the longest x3 135 us: gather_up(): lax.all_gather(rows.reshape(nd * up_rows, nl * down_rows), 'local', axis=...]
    dot_general x12, matrix products: 233 us -> 114 us  [the longest x2 22 us: device_fn(): part = jnp.dot(s, down, preferred_element_type=jnp.float32)]
    all_to_all x0 -> x4, blocking collectives: none -> 49.6 us  [the longest x3 34 us: gather_up(): rows = lax.all_to_all(cols, 'data', 0, 0, tiled=True)]
  transfers between devices with their start and end apart: 12 -> 19, of which waited for: 12 -> 18; matrix products, arithmetic and copies ran while one was open for 6% -> 9% of each run, Pallas kernels for 0% -> 0%
where the time goes in v1:
time: 1080 us
  waiting for transfers between devices  858 us (79%)
  matrix products  114 us (11%)
  blocking collectives  49.6 us (5%)
  other arithmetic  17.1 us (2%)
  between operations  14.7 us (1%)
  local copies, waits for them, and re-layouts  14.4 us (1%)
    reduce_scatter x2, waiting for transfers between devices, scatter_up(): mine = lax.psum_scatter(part, 'local', scatter_dimension=0, tiled=True)  164 us
    reduce_scatter x2, waiting for transfers between devices, scatter_down(): return lax.psum_scatter(part, 'local', scatter_dimension=0, tiled=True)  158 us
    all_gather x3, waiting for transfers between devices, gather_up(): lax.all_gather(rows.reshape(nd * up_rows, nl * down_rows), 'local', axis=...  135 us
    all_gather x3, waiting for transfers between devices, gather_down(): return lax.all_gather(w, 'local', axis=0, tiled=True)  106 us
    reduce_scatter x2, waiting for transfers between devices, device_fn(): lax.psum_scatter(part, 'data', scatter_dimension=0, tiled=True)  92.4 us
    reduce_scatter x2, waiting for transfers between devices, device_fn(): du = lax.psum_scatter(du_part, 'data', scatter_dimension=0, tiled=True)  89.5 us
    all_gather x2, waiting for transfers between devices, device_fn(): u_full = lax.all_gather(u, 'data', axis=0, tiled=True)  54.5 us
    all_to_all x3, blocking collectives, gather_up(): rows = lax.all_to_all(cols, 'data', 0, 0, tiled=True)  34 us
  transfers between devices with their start and end apart: 19, of which 18 were waited for; matrix products, arithmetic and copies ran while one was open for 9% of the time, Pallas kernels for 0%

profile of v1, /device:TPU:1, one launch (start us, length us, event | category | flops | bytes accessed | tf_op | source)
XLA Modules:
  0.0 1076.5 jit_solution(11874744012150509232)
XLA Ops:
  12.6 12.1 %all_to_all.25 = bf16[8,16,1024]{2,1,0:T(8,128)(2,1)} all-to-all(bf16[8,16,1024]{2,1,0:T(8,128)(2,1)S(1)} %reshape.70), channel_id=1, replica_groups=mesh['local'=16,'data'=8] {'data'}, dimensions={0} | all-to-all | bytes 524288 | tf_op jit(solution)/shard_map/all_to_all | solution.py:31
  25.7 20.4 %all-gather.14.cloned.1.call-done = bf16[1024,2048]{1,0:T(8,128)(2,1)} async-done(((bf16[128,2048]{1,0:T(8,128)(2,1)}), bf16[1024,2048]{1,0:T(8,128)(2,1)}) %all-gather.14.cloned.1.call-update) | async-done | bytes 4194320 | tf_op jit(solution)/shard_map/all_gather | solution.py:52
  46.1 52.7 %all-gather.16.cloned.1.call-done = bf16[2048,1024]{1,0:T(8,128)(2,1)} async-done(((bf16[128,1024]{1,0:T(8,128)(2,1)}), bf16[2048,1024]{1,0:T(8,128)(2,1)}) %all-gather.16.cloned.1.call-update) | async-done | bytes 4194320 | tf_op jit(solution)/shard_map/all_gather | solution.py:32
  98.7 9.2 convolution_convert_fusion.1
  108.0 44.3 %all-gather.28.cloned.1.call-done = bf16[1,1024,2048]{2,1,0:T(8,128)(2,1)} async-done(((bf16[1,64,2048]{2,1,0:T(8,128)(2,1)}), bf16[1,1024,2048]{2,1,0:T(8,128)(2,1)}) %all-gather.28.cloned.1.call-update) | async-done | bytes 4194320 | tf_op jit(solution)/shard_map/all_gather | solution.py:35
  152.3 11.0 %fusion.28 = f32[1024,2048]{1,0:T(8,128)} fusion(bf16[1,1024,2048]{2,1,0:T(8,128)(2,1)} %all-gather.28.cloned.1.call-done, bf16[1024,1024]{1,0:T(8,128)(2,1)} %convolution_convert_fusion.1), kind=kOutput, calls=%fused_computation.40 | convolution fusion | flops 4305453056 | bytes 14680064 | tf_op jit(solution)/shard_map/dot_general | solution.py:56
  164.3 12.1 %all_to_all.26 = bf16[8,16,1024]{2,1,0:T(8,128)(2,1)} all-to-all(bf16[8,16,1024]{2,1,0:T(8,128)(2,1)S(1)} %reshape.72), channel_id=1, replica_groups=mesh['local'=16,'data'=8] {'data'}, dimensions={0} | all-to-all | bytes 524288 | tf_op jit(solution)/shard_map/all_to_all | solution.py:31
  176.5 39.3 %reduce-scatter.9.cloned.1.call-done = f32[128,2048]{1,0:T(8,128)} async-done(((f32[1024,2048]{1,0:T(8,128)}), f32[128,2048]{1,0:T(8,128)}) %reduce-scatter.9.cloned.1.call-update) | async-done | bytes 1048592 | tf_op jit(solution)/shard_map/reduce_scatter | solution.py:57
  220.1 48.4 %all-gather.20.cloned.1.call-done = bf16[2048,1024]{1,0:T(8,128)(2,1)} async-done(((bf16[128,1024]{1,0:T(8,128)(2,1)}), bf16[2048,1024]{1,0:T(8,128)(2,1)}) %all-gather.20.cloned.1.call-update) | async-done | bytes 4194320 | tf_op jit(solution)/shard_map/all_gather | solution.py:32
  268.4 34.2 %all-gather.18.cloned.1.call-done = bf16[1024,2048]{1,0:T(8,128)(2,1)} async-done(((bf16[128,2048]{1,0:T(8,128)(2,1)}), bf16[1024,2048]{1,0:T(8,128)(2,1)}) %all-gather.18.cloned.1.call-update) | async-done | bytes 4194320 | tf_op jit(solution)/shard_map/all_gather | solution.py:52
  302.6 9.3 convolution_convert_fusion
  311.9 24.2 %all-gather.22.cloned.1.call-done = bf16[1024,2048]{1,0:T(8,128)(2,1)} async-done(((bf16[128,2048]{1,0:T(8,128)(2,1)}), bf16[1024,2048]{1,0:T(8,128)(2,1)}) %all-gather.22.cloned.1.call-update) | async-done | bytes 4194320 | tf_op jit(solution)/shard_map/all_gather | solution.py:45
  336.1 53.3 %all-gather.30.cloned.1.call-done = bf16[1,1024,2048]{2,1,0:T(8,128)(2,1)} async-done(((bf16[1,64,2048]{2,1,0:T(8,128)(2,1)}), bf16[1,1024,2048]{2,1,0:T(8,128)(2,1)}) %all-gather.30.cloned.1.call-update) | async-done | bytes 4194320 | tf_op jit(solution)/shard_map/all_gather | solution.py:35
  389.4 11.0 %fusion.4 = bf16[1024,1024]{1,0:T(8,128)(2,1)S(1)} fusion(bf16[1024,1024]{1,0:T(8,128)(2,1)} %convolution_convert_fusion, bf16[1024,2048]{1,0:T(8,128)(2,1)} %all-gather.22.cloned.1.call-done, bf16[1,1024,2048]{2,1,0:T(8,128)(2,1)} %all-gather.30.cloned.1.call-done), kind=kOutput, calls=%fused_computation.16 | convolution fusion | flops 4319084544 | bytes 12582912 | tf_op jit(solution)/shard_map/dot_general | solution.py:65
  409.1 11.0 %fusion.26 = f32[1024,2048]{1,0:T(8,128)} fusion(bf16[1,1024,2048]{2,1,0:T(8,128)(2,1)} %all-gather.30.cloned.1.call-done, bf16[1024,1024]{1,0:T(8,128)(2,1)} %convolution_convert_fusion), kind=kOutput, calls=%fused_computation.38 | convolution fusion | flops 4305453056 | bytes 14680064 | tf_op jit(solution)/shard_map/dot_general | solution.py:56
  420.2 40.4 %reduce-scatter.13.cloned.1.call-done = f32[128,2048]{1,0:T(8,128)} async-done(((f32[1024,2048]{1,0:T(8,128)}), f32[128,2048]{1,0:T(8,128)}) %reduce-scatter.13.cloned.1.call-update) | async-done | bytes 1048592 | tf_op jit(solution)/shard_map/reduce_scatter | solution.py:71
  462.0 53.0 %reduce-scatter.11.cloned.1.call-done = f32[128,2048]{1,0:T(8,128)} async-done(((f32[1024,2048]{1,0:T(8,128)}), f32[128,2048]{1,0:T(8,128)}) %reduce-scatter.11.cloned.1.call-update) | async-done | bytes 1048592 | tf_op jit(solution)/shard_map/reduce_scatter | solution.py:57
  518.0 32.4 %all-gather.24.cloned.1.call-done = bf16[1024,2048]{1,0:T(8,128)(2,1)} async-done(((bf16[128,2048]{1,0:T(8,128)(2,1)}), bf16[1024,2048]{1,0:T(8,128)(2,1)}) %all-gather.24.cloned.1.call-update) | async-done | bytes 4194320 | tf_op jit(solution)/shard_map/all_gather | solution.py:62
  552.2 9.7 all_to_all.27
  562.0 10.7 fusion.60
  574.3 9.3 fusion.48
  585.2 9.4 fusion.51
  594.8 8.7 all-gather.32.cloned.1.call-done
  603.5 10.4 fusion.7
  622.1 34.4 %all-gather.26.cloned.1.call-done = bf16[2048,1024]{1,0:T(8,128)(2,1)} async-done(((bf16[128,1024]{1,0:T(8,128)(2,1)}), bf16[2048,1024]{1,0:T(8,128)(2,1)}) %all-gather.26.cloned.1.call-update) | async-done | bytes 4194320 | tf_op jit(solution)/shard_map/all_gather | solution.py:32
  656.5 8.9 fusion.58
  665.4 78.0 %reduce-scatter.19.cloned.1.call-done = f32[128,1024]{1,0:T(8,128)} async-done(((f32[2048,1024]{1,0:T(8,128)}), f32[128,1024]{1,0:T(8,128)}) %reduce-scatter.19.cloned.1.call-update) | async-done | bytes 524304 | tf_op jit(solution)/shard_map/reduce_scatter | solution.py:38
  743.5 15.7 %all_to_all.28 = f32[8,16,1024]{2,1,0:T(8,128)S(1)} all-to-all(f32[8,16,1024]{2,1,0:T(8,128)} %bitcast.71), channel_id=1, replica_groups=mesh['local'=16,'data'=8] {'data'}, dimensions={0} | all-to-all | bytes 1048576 | tf_op jit(solution)/shard_map/all_to_all | solution.py:39
  761.2 70.3 %reduce-scatter.23.cloned.1.call-done = f32[64,2048]{1,0:T(8,128)} async-done(((f32[1024,2048]{1,0:T(8,128)}), f32[64,2048]{1,0:T(8,128)}) %reduce-scatter.23.cloned.1.call-update) | async-done | bytes 524304 | tf_op jit(solution)/shard_map/reduce_scatter | solution.py:43
  831.5 87.9 %reduce-scatter.21.cloned.1.call-done = f32[64,2048]{1,0:T(8,128)} async-done(((f32[1024,2048]{1,0:T(8,128)}), f32[64,2048]{1,0:T(8,128)}) %reduce-scatter.21.cloned.1.call-update) | async-done | bytes 524304 | tf_op jit(solution)/shard_map/reduce_scatter | solution.py:43
  921.7 85.9 %reduce-scatter.17.cloned.1.call-done = f32[128,1024]{1,0:T(8,128)} async-done(((f32[2048,1024]{1,0:T(8,128)}), f32[128,1024]{1,0:T(8,128)}) %reduce-scatter.17.cloned.1.call-update) | async-done | bytes 524304 | tf_op jit(solution)/shard_map/reduce_scatter | solution.py:38
  1014.2 49.1 %reduce-scatter.15.cloned.1.call-done = f32[128,2048]{1,0:T(8,128)} async-done(((f32[1024,2048]{1,0:T(8,128)}), f32[128,2048]{1,0:T(8,128)}) %reduce-scatter.15.cloned.1.call-update) | async-done | bytes 1048592 | tf_op jit(solution)/shard_map/reduce_scatter | solution.py:71
  (98 shorter events, 55.1 us)
Async XLA Ops:
  7.2 17.6 %copy-start.4 = (bf16[2,64,2048]{2,1,0:T(8,128)(2,1)S(1)}, bf16[2,64,2048]{2,1,0:T(8,128)(2,1)}, u32[]{:S(2)}) copy-start(bf16[2,64,2048]{2,1,0:T(8,128)(2,1)} %param.7) | copy-start | bytes 1572868
  7.2 38.9 %all-gather.14.cloned.1.call-start = ((), (), s32[]{:S(2)}) async-start(), calls=%async_computation.13 | async-start | bytes 4718592 | tf_op jit(solution)/shard_map/all_gather | solution.py:52
  10.5 88.2 %all-gather.16.cloned.1.call-start = ((), (), s32[]{:S(2)}) async-start(), calls=%async_computation.14 | async-start | bytes 4456448 | tf_op jit(solution)/shard_map/all_gather | solution.py:32
  24.7 127.5 %all-gather.28.cloned.1.call-start = ((), (), s32[]{:S(2)}) async-start(), calls=%async_computation.28 | async-start | bytes 4456448 | tf_op jit(solution)/shard_map/all_gather | solution.py:35
  25.6 190.2 %reduce-scatter.9.cloned.1.call-start = ((), (), s32[]{:S(2)}) async-start(), calls=%async_computation.15 | async-start | bytes 9437184 | tf_op jit(solution)/shard_map/reduce_scatter | solution.py:57
  163.3 52.6 %copy-start = (bf16[128,2048]{1,0:T(8,128)(2,1)S(1)}, bf16[128,2048]{1,0:T(8,128)(2,1)}, u32[]{:S(2)}) copy-start(bf16[128,2048]{1,0:T(8,128)(2,1)} %param.4) | copy-start | bytes 1572868
  163.3 105.1 %all-gather.20.cloned.1.call-start = ((), (), s32[]{:S(2)}) async-start(), calls=%async_computation.17 | async-start | bytes 4456448 | tf_op jit(solution)/shard_map/all_gather | solution.py:32
  176.5 126.1 %all-gather.18.cloned.1.call-start = ((), (), s32[]{:S(2)}) async-start(), calls=%async_computation.16 | async-start | bytes 4718592 | tf_op jit(solution)/shard_map/all_gather | solution.py:52
  218.3 117.8 %all-gather.22.cloned.1.call-start = ((), (), s32[]{:S(2)}) async-start(), calls=%async_computation.19 | async-start | bytes 4718592 | tf_op jit(solution)/shard_map/all_gather | solution.py:45
  219.1 170.3 %all-gather.30.cloned.1.call-start = ((), (), s32[]{:S(2)}) async-start(), calls=%async_computation.29 | async-start | bytes 4456448 | tf_op jit(solution)/shard_map/all_gather | solution.py:35
  219.8 240.8 %reduce-scatter.13.cloned.1.call-start = ((), (), s32[]{:S(2)}) async-start(), calls=%async_computation.20 | async-start | bytes 9437184 | tf_op jit(solution)/shard_map/reduce_scatter | solution.py:71
  389.3 12.3 %copy-start.6 = (bf16[2048,1024]{1,0:T(8,128)(2,1)S(1)}, bf16[2048,1024]{1,0:T(8,128)(2,1)}, u32[]{:S(2)}) copy-start(bf16[2048,1024]{1,0:T(8,128)(2,1)} %all-gather.20.cloned.1.call-done) | copy-start | bytes 12582916
  400.3 1.4 copy-start.9
  408.6 106.4 %reduce-scatter.11.cloned.1.call-start = ((), (), s32[]{:S(2)}) async-start(), calls=%async_computation.18 | async-start | bytes 9437184 | tf_op jit(solution)/shard_map/reduce_scatter | solution.py:57
  420.1 94.9 %copy-start.2 = (bf16[128,2048]{1,0:T(8,128)(2,1)S(1)}, bf16[128,2048]{1,0:T(8,128)(2,1)}, u32[]{:S(2)}) copy-start(bf16[128,2048]{1,0:T(8,128)(2,1)} %param.5) | copy-start | bytes 1572868
  420.1 131.1 %slice-start = ((bf16[2,16,8192]{2,1,0:T(8,128)(2,1)}), bf16[1,16,8192]{2,1,0:T(8,128)(2,1)S(1)}, s32[]{:S(2)}) async-start(bf16[2,16,8192]{2,1,0:T(8,128)(2,1)} %param.6), calls=%async_computation.31 | async-start | bytes 524288 | tf_op jit(solution)/shard_map/slice | solution.py:63
  420.1 130.3 %all-gather.24.cloned.1.call-start = ((), (), s32[]{:S(2)}) async-start(), calls=%async_computation.21 | async-start | bytes 4718592 | tf_op jit(solution)/shard_map/all_gather | solution.py:62
  517.9 85.6 %all-gather.32.cloned.1.call-start = ((), (), s32[]{:S(2)}) async-start(), calls=%async_computation.30 | async-start | bytes 4456448 | tf_op jit(solution)/shard_map/all_gather | solution.py:35
  551.1 105.3 %all-gather.26.cloned.1.call-start = ((), (), s32[]{:S(2)}) async-start(), calls=%async_computation.22 | async-start | bytes 4456448 | tf_op jit(solution)/shard_map/all_gather | solution.py:32
  561.9 181.5 %reduce-scatter.19.cloned.1.call-start = ((), (), s32[]{:S(2)}) async-start(), calls=%async_computation.25 | async-start | bytes 8912896 | tf_op jit(solution)/shard_map/reduce_scatter | solution.py:38
  572.7 1.6 copy-start.8
  572.7 258.8 %reduce-scatter.23.cloned.1.call-start = ((), (), s32[]{:S(2)}) async-start(), calls=%async_computation.27 | async-start | bytes 8912896 | tf_op jit(solution)/shard_map/reduce_scatter | solution.py:43
  583.6 1.6 copy-start.7
  583.6 335.8 %reduce-scatter.21.cloned.1.call-start = ((), (), s32[]{:S(2)}) async-start(), calls=%async_computation.26 | async-start | bytes 8912896 | tf_op jit(solution)/shard_map/reduce_scatter | solution.py:43
  594.6 413.0 %reduce-scatter.17.cloned.1.call-start = ((), (), s32[]{:S(2)}) async-start(), calls=%async_computation.24 | async-start | bytes 8912896 | tf_op jit(solution)/shard_map/reduce_scatter | solution.py:38
  603.5 11.7 %copy-start.5 = (bf16[1024,2048]{1,0:T(8,128)(2,1)S(1)}, bf16[1024,2048]{1,0:T(8,128)(2,1)}, u32[]{:S(2)}) copy-start(bf16[1024,2048]{1,0:T(8,128)(2,1)} %all-gather.14.cloned.1.call-done) | copy-start | bytes 12582916
  613.9 1.3 copy-start.10
  622.0 34.5 %copy-start.11 = (bf16[1024,1024]{1,0:T(8,128)(2,1)S(1)}, bf16[1024,1024]{1,0:T(8,128)(2,1)}, u32[]{:S(2)}) copy-start(bf16[1024,1024]{1,0:T(8,128)(2,1)} %copy-done.10) | copy-start | bytes 6291460
  622.0 441.2 %reduce-scatter.15.cloned.1.call-start = ((), (), s32[]{:S(2)}) async-start(), calls=%async_computation.23 | async-start | bytes 9437184 | tf_op jit(solution)/shard_map/reduce_scatter | solution.py:71
  759.4 305.3 %copy-start.1 = (bf16[128,2048]{1,0:T(8,128)(2,1)S(1)}, bf16[128,2048]{1,0:T(8,128)(2,1)}, u32[]{:S(2)}) copy-start(bf16[128,2048]{1,0:T(8,128)(2,1)} %get-tuple-element.12) | copy-start | bytes 1572868
  1007.6 59.5 %all-to-all-start.3 = ((f32[8,16,1024]{2,1,0:T(8,128)}), f32[8,16,1024]{2,1,0:T(8,128)S(1)}, u32[]{:S(2)}, u32[]{:S(2)}) async-start(f32[8,16,1024]{2,1,0:T(8,128)} %bitcast.72), calls=%async_computation.8 | async-start | bytes 1048576 | tf_op jit(solution)/shard_map/all_to_all | solution.py:39
  1064.7 3.7 copy-start.3
Sparse Core Ops, SparseCore 0:
  10.6 35.3 all-gather.13
  48.2 50.4 all-gather.15
  101.5 50.7 all-gather.27
  163.4 52.3 reduce-scatter.8
  217.8 50.5 all-gather.19
  270.6 31.9 all-gather.17
  304.3 31.7 all-gather.21
  338.8 50.4 all-gather.29
  408.7 51.8 reduce-scatter.12
  462.8 52.1 reduce-scatter.10
  518.0 32.3 all-gather.23
  553.0 50.5 all-gather.31
  605.7 50.7 all-gather.25
  659.7 83.6 reduce-scatter.18
  746.7 84.7 reduce-scatter.22
  834.8 84.5 reduce-scatter.20
  922.6 84.8 reduce-scatter.16
  1009.8 53.3 reduce-scatter.14

commit v2 on v0

v2 whole, which is shorter than its diff:
```python
import functools

import jax
import jax.numpy as jnp
from jax import lax
from jax.experimental import pallas as pl
from jax.experimental.pallas import tpu as pltpu
from jax.sharding import PartitionSpec as P

NORM_EPS = 1e-6
BOTH_AXES = ('local', 'data')
CONTRACT_ROWS = (((0,), (0,)), ((), ()))
CONTRACT_COLS = (((1,), (1,)), ((), ()))
MESH = pl.DeviceIdType.MESH
RING = 4
F32, BF16 = jnp.float32, jnp.bfloat16

LINK_RATE = 46.6e3
PAIR_RATE = 600e3
LOCAL_RATE = 3000e3
HOP = 2.2


def gelu_tanh(values):
    return jax.nn.gelu(values, approximate=True)


class Event:
    def __init__(self):
        self.time = None


class Copy:
    def __init__(self, desc, time, remote):
        self.desc, self.time, self.remote = desc, time, remote

    def wait(self):
        if self.remote:
            self.desc.wait_recv()
        else:
            self.desc.wait()


class Net:
    def __init__(self, send_sems, recv_sems, local_sems):
        self.send_sems, self.recv_sems, self.local_sems = send_sems, recv_sems, local_sems
        self.n_remote = self.n_local = 0
        self.now = 0.0
        self.free = {}
        self.sent = []
        self.flows = []
        here = lax.axis_index('local')
        there = lax.axis_index('data')
        self.data = there
        self.pos = {'z': here // RING, 'y': here % RING, 'x': there // 2}
        self.core = there % 2

    def at(self, axis, step):
        return (self.pos[axis] + (step + RING)) % RING

    def device(self, axis, step):
        if axis == 'p':
            return {'data': self.pos['x'] * 2 + (1 - self.core)}
        if axis == 'd':
            return {'data': (self.data + step) % (2 * RING)}
        to = self.at(axis, step)
        if axis == 'x':
            return {'data': to * 2 + self.core}
        if axis == 'y':
            return {'local': self.pos['z'] * RING + to}
        return {'local': to * RING + self.pos['y']}

    def barrier(self, axes):
        peers = [(axis, step) for axis in axes for step in ((1, -1) if axis in 'xyz' else (1,) if axis == 'p' else range(1, 2 * RING))]
        semaphore = pltpu.get_barrier_semaphore()
        for axis, step in peers:
            pl.semaphore_signal(semaphore, inc=1, device_id=self.device(axis, step), device_id_type=MESH)
        pl.semaphore_wait(semaphore, len(peers))

    def send(self, src, dst, axis, step=1):
        k = self.n_remote
        self.n_remote += 1
        desc = pltpu.make_async_remote_copy(
            src_ref=src, dst_ref=dst, send_sem=self.send_sems.at[k], recv_sem=self.recv_sems.at[k],
            device_id=self.device(axis, step), device_id_type=MESH)
        desc.start()
        size = 1
        for n in dst.shape:
            size *= n
        size *= dst.dtype.itemsize
        rate = PAIR_RATE if axis == 'p' else LINK_RATE
        key = (axis, step)
        done = max(self.free.get(key, 0.0), self.now) + size / rate
        self.free[key] = done
        copy = Copy(desc, done + HOP, True)
        self.sent.append(copy)
        return copy

    def load(self, src, dst):
        k = self.n_local
        self.n_local += 1
        desc = pltpu.make_async_copy(src, dst, self.local_sems.at[k])
        desc.start()
        size = 1
        for n in dst.shape:
            size *= n
        return Copy(desc, self.now + 1.0 + size * dst.dtype.itemsize / LOCAL_RATE, False)

    def spend(self, microseconds):
        self.now += microseconds

    def spawn(self, flow):
        self.step(flow)

    def step(self, flow):
        try:
            self.flows.append((flow, next(flow)))
        except StopIteration:
            pass

    def run(self):
        while self.flows:
            best, best_time = None, None
            for k, (_, items) in enumerate(self.flows):
                if any(item.time is None for item in items):
                    continue
                time = max([item.time for item in items] + [0.0])
                if best is None or time < best_time:
                    best, best_time = k, time
            flow, items = self.flows.pop(best)
            for item in items:
                if isinstance(item, Copy):
                    item.wait()
            self.now = max(self.now, best_time)
            self.step(flow)

    def finish(self):
        for copy in self.sent:
            copy.desc.wait_send()


def rows_loop(rows, chunk, body):
    chunk = min(chunk, rows)

    def step(k, carry):
        body(pl.ds(pl.multiple_of(k * chunk, chunk), chunk))
        return carry

    lax.fori_loop(0, rows // chunk, step, 0)


def add_into(net, dst, *others):
    rows, cols = dst.shape

    def body(at):
        total = dst[at, :]
        for other in others:
            total = total + other[at, :]
        dst[at, :] = total

    rows_loop(rows, 16, body)
    net.spend(rows * cols * 4 * (1 + len(others)) / 4e6)


def fire(net, event):
    event.time = net.now


def exchange_back(net, src, dst, done):
    rows = dst.shape[1]

    def block(k):
        return src.at[pl.ds(pl.multiple_of(k * rows, rows), rows)]

    own = net.load(block(net.data), dst.at[net.data])
    copies = [net.send(block((net.data + k) % (2 * RING)), dst.at[net.data], 'd', k) for k in range(1, 2 * RING)]
    yield [own] + copies
    fire(net, done)


def exchange(net, src, dst, done):
    own = net.load(src.at[:, net.data], dst.at[:, net.data])
    copies = [net.send(src.at[:, (net.data + k) % (2 * RING)], dst.at[:, net.data], 'd', k) for k in range(1, 2 * RING)]
    yield [own] + copies
    fire(net, done)


def gather_x(net, full, done):
    half = full.shape[1] // 2
    lo, hi = pl.ds(0, half), pl.ds(half, half)

    def block(step):
        return full.at[net.at('x', step) * 2 + net.core]

    def part(step, rows):
        return full.at[net.at('x', step) * 2 + net.core, rows]

    forth = net.send(block(0), block(0), 'x', 1)
    back = net.send(block(0), block(0), 'x', -1)
    pair = [net.send(block(0), block(0), 'p')]
    yield [forth]
    forth = net.send(part(-1, lo), part(-1, lo), 'x', 1)
    pair.append(net.send(block(-1), block(-1), 'p'))
    yield [back]
    back = net.send(part(1, hi), part(1, hi), 'x', -1)
    pair.append(net.send(block(1), block(1), 'p'))
    yield [forth, back]
    pair.append(net.send(block(2), block(2), 'p'))
    yield pair
    fire(net, done)


def gather_yz(net, own, full, first, done):
    second = 'y' if first == 'z' else 'z'
    half = own.shape[0] // 2
    lo, hi = pl.ds(0, half), pl.ds(half, half)

    def index(one, two):
        at_one, at_two = net.at(first, one), net.at(second, two)
        return (at_one, at_two) if first == 'z' else (at_two, at_one)

    def block(one, two):
        return full.at[index(one, two)]

    def part(one, two, rows):
        return full.at[index(one, two) + (rows,)]

    ends = []

    def relay(one, forth, back, end):
        yield [forth]
        forth = net.send(part(one, -1, lo), part(one, -1, lo), second, 1)
        yield [back]
        back = net.send(part(one, 1, hi), part(one, 1, hi), second, -1)
        yield [forth, back]
        fire(net, end)

    def spread(src, one):
        forth = net.send(src, block(one, 0), second, 1)
        back = net.send(src, block(one, 0), second, -1)
        end = Event()
        ends.append(end)
        net.spawn(relay(one, forth, back, end))

    mine = net.load(own, block(0, 0))
    forth = net.send(own, block(0, 0), first, 1)
    back = net.send(own, block(0, 0), first, -1)
    spread(own, 0)
    yield [forth]
    forth = net.send(part(-1, 0, lo), part(-1, 0, lo), first, 1)
    spread(block(-1, 0), -1)
    yield [back]
    back = net.send(part(1, 0, hi), part(1, 0, hi), first, -1)
    spread(block(1, 0), 1)
    yield [forth, back]
    spread(block(2, 0), 2)
    yield [mine] + ends
    fire(net, done)


def reduce_ring(net, axis, far, ahead, behind, mine, relay_f, relay_b, last_f, last_b, done):
    half = mine.shape[0] // 2
    lo, hi = pl.ds(0, half), pl.ds(half, half)
    first_f = net.send(far.at[lo], relay_f, axis, 1)
    first_b = net.send(far.at[hi], relay_b, axis, -1)
    direct_f = net.send(ahead.at[hi], last_f.at[hi], axis, 1)
    direct_b = net.send(behind.at[lo], last_b.at[lo], axis, -1)
    yield [first_f]
    add_into(net, ahead.at[lo], relay_f)
    summed_f = net.send(ahead.at[lo], last_f.at[lo], axis, 1)
    yield [first_b]
    add_into(net, behind.at[hi], relay_b)
    summed_b = net.send(behind.at[hi], last_b.at[hi], axis, -1)
    yield [direct_f, direct_b, summed_f, summed_b]
    add_into(net, mine, last_f, last_b)
    fire(net, done)


STEPS = (2, 1, -1, 0)


def reduce_x(net, part, acc, other, relay_f, relay_b, last_f, last_b, done):
    half = acc.shape[1] // 2
    lo, hi = pl.ds(0, half), pl.ds(half, half)
    pairs, mine = [], []
    for k, step in enumerate(STEPS):
        pairs.append(net.send(part.at[net.at('x', step) * 2 + (1 - net.core)], other.at[k], 'p'))
        mine.append(net.load(part.at[net.at('x', step) * 2 + net.core], acc.at[k]))
    yield [pairs[0], mine[0]]
    add_into(net, acc.at[0], other.at[0])
    first_f = net.send(acc.at[0, lo], relay_f, 'x', 1)
    first_b = net.send(acc.at[0, hi], relay_b, 'x', -1)
    yield [pairs[1], mine[1]]
    add_into(net, acc.at[1], other.at[1])
    direct_f = net.send(acc.at[1, hi], last_f.at[hi], 'x', 1)
    yield [pairs[2], mine[2]]
    add_into(net, acc.at[2], other.at[2])
    direct_b = net.send(acc.at[2, lo], last_b.at[lo], 'x', -1)
    yield [pairs[3], mine[3]]
    add_into(net, acc.at[3], other.at[3])
    yield [first_f]
    add_into(net, acc.at[1, lo], relay_f)
    summed_f = net.send(acc.at[1, lo], last_f.at[lo], 'x', 1)
    yield [first_b]
    add_into(net, acc.at[2, hi], relay_b)
    summed_b = net.send(acc.at[2, hi], last_b.at[hi], 'x', -1)
    yield [direct_f, direct_b, summed_f, summed_b]
    add_into(net, acc.at[3], last_f, last_b)
    fire(net, done)


def reduce_yz(net, part, first, sums, ahead, behind, relay1, last1, relay2, last2, start, done):
    second = 'y' if first == 'z' else 'z'
    half = sums.shape[1] // 2
    lo, hi = pl.ds(0, half), pl.ds(half, half)

    def index(one, two):
        at_one, at_two = net.at(first, one), net.at(second, two)
        return (at_one, at_two) if first == 'z' else (at_two, at_one)

    def ring(k, end):
        two = STEPS[k]
        loads = [net.load(part.at[index(1, two) + (lo,)], ahead.at[k]),
                 net.load(part.at[index(-1, two) + (hi,)], behind.at[k]),
                 net.load(part.at[index(0, two)], sums.at[k])]
        first_f = net.send(part.at[index(2, two) + (lo,)], relay1.at[0, k], first, 1)
        first_b = net.send(part.at[index(2, two) + (hi,)], relay1.at[1, k], first, -1)
        direct_f = net.send(part.at[index(1, two) + (hi,)], last1.at[0, k, hi], first, 1)
        direct_b = net.send(part.at[index(-1, two) + (lo,)], last1.at[1, k, lo], first, -1)
        yield [first_f, loads[0]]
        add_into(net, ahead.at[k], relay1.at[0, k])
        summed_f = net.send(ahead.at[k], last1.at[0, k, lo], first, 1)
        yield [first_b, loads[1]]
        add_into(net, behind.at[k], relay1.at[1, k])
        summed_b = net.send(behind.at[k], last1.at[1, k, hi], first, -1)
        yield [direct_f, direct_b, summed_f, summed_b, loads[2]]
        add_into(net, sums.at[k], last1.at[0, k], last1.at[1, k])
        fire(net, end)

    if start is not None:
        yield [start]
    ends = [Event() for _ in STEPS]
    for k in range(RING):
        net.spawn(ring(k, ends[k]))
    yield [ends[0]]
    first_f = net.send(sums.at[0, lo], relay2.at[0], second, 1)
    first_b = net.send(sums.at[0, hi], relay2.at[1], second, -1)
    yield [ends[1]]
    direct_f = net.send(sums.at[1, hi], last2.at[0, hi], second, 1)
    yield [ends[2]]
    direct_b = net.send(sums.at[2, lo], last2.at[1, lo], second, -1)
    yield [first_f]
    add_into(net, sums.at[1, lo], relay2.at[0])
    summed_f = net.send(sums.at[1, lo], last2.at[0, lo], second, 1)
    yield [first_b]
    add_into(net, sums.at[2, hi], relay2.at[1])
    summed_b = net.send(sums.at[2, hi], last2.at[1, hi], second, -1)
    yield [ends[3], direct_f, direct_b, summed_f, summed_b]
    add_into(net, sums.at[3], last2.at[0], last2.at[1])
    fire(net, done)


def reduce_yz_scratch(rows, cols):
    return [pltpu.VMEM((RING, rows, cols), F32), pltpu.VMEM((RING, rows // 2, cols), F32), pltpu.VMEM((RING, rows // 2, cols), F32),
            pltpu.VMEM((2, RING, rows // 2, cols), F32), pltpu.VMEM((2, RING, rows, cols), F32),
            pltpu.VMEM((2, rows // 2, cols), F32), pltpu.VMEM((2, rows, cols), F32)]


def reduce_x_scratch(rows, cols):
    return [pltpu.VMEM((RING, rows, cols), F32), pltpu.VMEM((RING, rows, cols), F32), pltpu.VMEM((rows // 2, cols), F32),
            pltpu.VMEM((rows // 2, cols), F32), pltpu.VMEM((rows, cols), F32), pltpu.VMEM((rows, cols), F32)]


def norm_rows(x_ref, u_ref):
    def body(at):
        x = x_ref[at, :].astype(F32)
        u_ref[at, :] = (x * lax.rsqrt(jnp.mean(x * x, axis=-1, keepdims=True) + NORM_EPS)).astype(BF16)

    rows_loop(x_ref.shape[0], 16, body)


def norm_back_rows(x_ref, dy_ref, du_ref, dx_ref):
    def body(at):
        x = x_ref[at, :].astype(F32)
        du = du_ref[at, :]
        r = lax.rsqrt(jnp.mean(x * x, axis=-1, keepdims=True) + NORM_EPS)
        dot = jnp.mean(x * du, axis=-1, keepdims=True)
        dx_ref[at, :] = (dy_ref[at, :].astype(F32) + (r * du - x * (r * r * r * dot))).astype(BF16)

    rows_loop(x_ref.shape[0], 16, body)


def add_rows(x_ref, y_ref, out_ref):
    def body(at):
        out_ref[at, :] = (x_ref[at, :].astype(F32) + y_ref[at, :]).astype(BF16)

    rows_loop(x_ref.shape[0], 16, body)


def call(body, out_shape, out_spaces, in_spaces, scratch, remote, local, collective_id, *args):
    spaces = {'v': pl.BlockSpec(memory_space=pltpu.VMEM), 'h': pl.BlockSpec(memory_space=pl.ANY)}

    def kernel(*refs):
        sems = refs[-3:]
        net = Net(*sems)
        body(net, *refs[:-3])
        net.finish()
        assert net.n_remote <= remote and net.n_local <= local, (net.n_remote, net.n_local)
        if PRINT:
            print(body.__name__, net.n_remote, net.n_local, round(net.now, 1))

    return pl.pallas_call(
        kernel, out_shape=out_shape, in_specs=[spaces[s] for s in in_spaces], out_specs=[spaces[s] for s in out_spaces],
        scratch_shapes=list(scratch) + [pltpu.SemaphoreType.DMA((remote,)), pltpu.SemaphoreType.DMA((remote,)), pltpu.SemaphoreType.DMA((local,))],
        compiler_params=pltpu.CompilerParams(collective_id=collective_id, has_side_effects=True, vmem_limit_bytes=67000000),
        cost_estimate=pl.CostEstimate(flops=10**8, bytes_accessed=10**7, transcendentals=0),
        name=body.__name__)(*args)


PRINT = False


def solution(mesh):
    nl, nd = mesh.shape['local'], mesh.shape['data']
    tok_spec = P(BOTH_AXES, None)
    w_spec = P(None, BOTH_AXES, None)

    def device_fn(tokens, grad_out, w_up, w_down):
        num_layers, ur, ffn = w_up.shape
        dr = w_down.shape[1]
        rows, width = tokens.shape
        hidden = nl * dr
        shape = jax.ShapeDtypeStruct
        cols = w_up.reshape(num_layers, ur, nl, nd, dr).transpose(0, 3, 1, 2, 4).reshape(num_layers, nd, ur, hidden)
        up_full = shape((RING, RING, nd, ur, hidden), BF16)
        down_full = shape((RING, RING, dr, width), BF16)
        act_full = shape((nd, rows, width), BF16)
        own = shape((rows, width), BF16)
        rx = reduce_x_scratch(rows, width)
        ryz_up = reduce_yz_scratch(nd * ur, hidden)
        ryz_down = reduce_yz_scratch(dr, width)

        def prologue(net, x_ref, w_up_ref, w_down_ref, up_ref, down_ref, u_ref, block_ref):
            net.barrier('dyz')
            blocks = Event()
            net.spawn(exchange(net, w_up_ref, block_ref, blocks))
            norm_rows(x_ref, u_ref.at[net.data])
            net.spawn(gather_x(net, u_ref, Event()))
            net.spawn(gather_yz(net, w_down_ref.at[0], down_ref, 'z', Event()))

            def up():
                yield [blocks]
                net.spawn(gather_yz(net, block_ref.at[0], up_ref, 'y', Event()))

            net.spawn(up())
            net.run()

        def forward(net, part_ref, x_ref, g_in_ref, block_ref, w_down_ref, up_ref, down_ref, u_ref, g_ref, next_ref, *scratch):
            net.barrier('pxyz')
            reduced, gathered = Event(), Event()
            net.spawn(reduce_x(net, part_ref, *scratch, reduced))
            net.spawn(gather_yz(net, block_ref.at[1], up_ref, 'y', Event()))
            net.spawn(gather_yz(net, w_down_ref.at[1], down_ref, 'z', Event()))

            def act():
                yield [reduced]
                add_rows(x_ref, scratch[0].at[3], next_ref)
                norm_rows(next_ref, u_ref.at[net.data])
                net.spend(0.5)
                net.spawn(gather_x(net, u_ref, gathered))
                yield [net.load(g_in_ref, g_ref.at[net.data])]
                net.spawn(gather_x(net, g_ref, Event()))

            net.spawn(act())
            net.run()

        def turn(net, du_ref, part_ref, dup_ref, ddown_ref, x_ref, g_ref, block_ref, w_down_ref,
                 out_ref, dy_ref, dy_full_ref, up_ref, down_ref, dw_up_ref, dw_down_ref, *scratch):
            net.barrier('dyz')
            r1, r2, s1, s2 = scratch[:6], scratch[6:12], scratch[12:19], scratch[19:26]
            reduced, gathered, out, summed1, summed2 = (Event() for _ in range(5))
            net.spawn(reduce_x(net, du_ref, *r1, reduced))
            net.spawn(gather_yz(net, block_ref.at[0], up_ref, 'y', Event()))
            net.spawn(gather_yz(net, w_down_ref.at[0], down_ref, 'z', Event()))
            net.spawn(reduce_yz(net, dup_ref, 'y', *s1, None, summed1))
            net.spawn(reduce_yz(net, ddown_ref, 'z', *s2, None, summed2))

            def act():
                yield [reduced]
                norm_back_rows(x_ref, g_ref, r1[0].at[3], dy_ref)
                net.spend(0.7)
                yield [net.load(dy_ref, dy_full_ref.at[net.data])]
                net.spawn(gather_x(net, dy_full_ref, gathered))
                net.spawn(reduce_x(net, part_ref, *r2, out))
                yield [out]
                add_rows(x_ref, r2[0].at[3], out_ref)

            def grads():
                yield [summed1]
                net.spawn(exchange_back(net, s1[0].at[3], dw_up_ref, Event()))
                yield [summed2]
                yield [net.load(s2[0].at[3], dw_down_ref)]

            net.spawn(act())
            net.spawn(grads())
            net.run()

        def last(net, du_ref, dup_ref, ddown_ref, x_ref, g_ref, dx_ref, dw_up_ref, dw_down_ref, *scratch):
            net.barrier('dyz')
            r1, s1, s2 = scratch[:6], scratch[6:13], scratch[13:20]
            reduced, summed1, summed2 = (Event() for _ in range(3))
            net.spawn(reduce_x(net, du_ref, *r1, reduced))
            net.spawn(reduce_yz(net, dup_ref, 'y', *s1, None, summed1))
            net.spawn(reduce_yz(net, ddown_ref, 'z', *s2, None, summed2))

            def act():
                yield [reduced]
                norm_back_rows(x_ref, g_ref, r1[0].at[3], dx_ref)
                net.spend(0.7)

            def grads():
                yield [summed1]
                net.spawn(exchange_back(net, s1[0].at[3], dw_up_ref, Event()))
                yield [summed2]
                yield [net.load(s2[0].at[3], dw_down_ref)]

            net.spawn(act())
            net.spawn(grads())
            net.run()

        def flat_act(full):
            return full.reshape(nd * rows, width)

        def flat_up(full):
            return full.reshape(nl * nd * ur, hidden)

        def flat_down(full):
            return full.reshape(hidden, width)

        def dot(a, b):
            return jnp.dot(a, b, preferred_element_type=F32)

        def hidden_of(u_full, up):
            a = dot(u_full, up).astype(BF16)
            return a, gelu_tanh(a.astype(F32)).astype(BF16)

        def hidden_back(a, dy_full, down):
            ds = lax.dot_general(dy_full, down, CONTRACT_COLS, preferred_element_type=F32).astype(BF16)
            _, back = jax.vjp(gelu_tanh, a.astype(F32))
            return back(ds.astype(F32))[0].astype(BF16)

        def split_part(part):
            return part.reshape(nd, rows, width)

        def grads_of(u_full, s, da, dy_full):
            d_up = lax.dot_general(u_full, da, CONTRACT_ROWS, preferred_element_type=F32)
            d_down = lax.dot_general(s, dy_full, CONTRACT_ROWS, preferred_element_type=F32)
            return d_up.reshape(RING, RING, nd * ur, hidden), d_down.reshape(RING, RING, dr, width)

        def own_up(d_up):
            return d_up.reshape(nd, ur, nl, dr).transpose(1, 2, 0, 3).reshape(ur, ffn)

        d_up_own, d_down_own = shape((nd, ur, hidden), F32), shape((dr, width), F32)

        up0, down0, u0, blocks = call(
            prologue, [up_full, down_full, act_full, shape((num_layers, nd, ur, hidden), BF16)], 'vvvh', 'vhh', [], 64, 8, 0,
            tokens, cols, w_down)
        u0 = flat_act(u0)
        a0, s0 = hidden_of(u0, flat_up(up0))
        part0 = split_part(dot(s0, flat_down(down0)))
        up1, down1, u1, g_full, x1 = call(
            forward, [up_full, down_full, act_full, act_full, own], 'vvvvv', 'hvhhh', rx, 72, 12, 1,
            part0, tokens, grad_out, blocks, w_down)
        u1, g_full, up1, down1 = flat_act(u1), flat_act(g_full), flat_up(up1), flat_down(down1)
        a1, s1 = hidden_of(u1, up1)
        da1 = hidden_back(a1, g_full, down1)
        du1 = split_part(lax.dot_general(da1, up1, CONTRACT_COLS, preferred_element_type=F32))
        part1 = split_part(dot(s1, down1))
        d_up1, d_down1 = grads_of(u1, s1, da1, g_full)
        x_out, dy0, dy_full, up0, down0, dw_up1, dw_down1 = call(
            turn, [own, own, act_full, up_full, down_full, d_up_own, d_down_own], 'vvvvvhh', 'hhhhvvhh', rx + rx + ryz_up + ryz_down, 144, 48, 2,
            du1, part1, d_up1, d_down1, x1, grad_out, blocks, w_down)
        dy_full, up0, down0 = flat_act(dy_full), flat_up(up0), flat_down(down0)
        da0 = hidden_back(a0, dy_full, down0)
        du0 = split_part(lax.dot_general(da0, up0, CONTRACT_COLS, preferred_element_type=F32))
        d_up0, d_down0 = grads_of(u0, s0, da0, dy_full)
        dx, dw_up0, dw_down0 = call(
            last, [own, d_up_own, d_down_own], 'vhh', 'hhhvv', rx + ryz_up + ryz_down, 96, 48, 3,
            du0, d_up0, d_down0, tokens, dy0)
        return x_out, dx, jnp.stack([own_up(dw_up0), own_up(dw_up1)]), jnp.stack([dw_down0, dw_down1])

    return jax.shard_map(device_fn, mesh=mesh, in_specs=(tok_spec, tok_spec, w_spec, w_spec), out_specs=(tok_spec, tok_spec, w_spec, w_spec), check_vma=False)
```

time: 4260 us -> 580 us (0.14)
  waiting for transfers between devices: 3980 us -> 0 us
  Pallas kernels: 0 us -> 400 us
  matrix products: 233 us -> 109 us
    reduce_scatter x4 -> x0, waiting for transfers between devices: 2980 us -> none  [the longest x2 1500 us: device_fn(): lax.psum_scatter(down_part, BOTH_AXES, scatter_dimension=0, tiled=True)]
    all_gather x8 -> x0, waiting for transfers between devices: 999 us -> none  [the longest x2 331 us: device_fn(): down_full = lax.all_gather(down_second, 'local', axis=0, tiled=True)]
    pallas_call x0 -> x4, Pallas kernels: none -> 400 us  [call(): pl.pallas_call(kernel, out_shape=out_shape, in_specs=[spaces[s] for s in...]
    dot_general x12, matrix products: 233 us -> 109 us  [the longest x4 38.8 us: dot(): return jnp.dot(a, b, preferred_element_type=F32)]
  transfers between devices with their start and end apart: 12 -> 0, of which waited for: 12 -> 0; matrix products, arithmetic and copies ran while one was open for 6% -> 0% of each run, Pallas kernels for 0% -> 0%
where the time goes in v2:
time: 580 us; the launch traced here: 572 us
  Pallas kernels  400 us (69%)
  matrix products  109 us (19%)
  local copies, waits for them, and re-layouts  49.9 us (9%)
  other arithmetic  12.2 us (2%)
    pallas_call x4, Pallas kernels, call(): pl.pallas_call(kernel, out_shape=out_shape, in_specs=[spaces[s] for s in...  400 us
    dot_general x4, matrix products, dot(): return jnp.dot(a, b, preferred_element_type=F32)  38.8 us
    dot_general x2, matrix products, hidden_back(): lax.dot_general(dy_full, down, CONTRACT_COLS, preferred_element_type=F32)  22.9 us
    dot_general x2, matrix products, grads_of(): lax.dot_general(s, dy_full, CONTRACT_ROWS, preferred_element_type=F32)  17.4 us
    dot_general x2, matrix products, grads_of(): lax.dot_general(u_full, da, CONTRACT_ROWS, preferred_element_type=F32)  13.8 us
    dot_general x2, local copies, waits for them, and re-layouts, grads_of(): lax.dot_general(u_full, da, CONTRACT_ROWS, preferred_element_type=F32)  12.8 us

profile of v2, /device:TPU:1, one launch (start us, length us, event | category | flops | bytes accessed | tf_op | source)
XLA Modules:
  0.0 571.9 jit_solution(8970795744441932685)
XLA Ops:
  0.6 2.1 reshape.66
  2.9 1.5 reshape.67.refs_1_
  4.4 61.8 %prologue.1 = (bf16[4,4,8,16,1024]{4,3,2,1,0:T(8,128)(2,1)}, bf16[4,4,64,2048]{3,2,1,0:T(8,128)(2,1)}, bf16[8,128,2048]{2,1,0:T(8,128)(2,1)}, bf16[2,8,16,1024]{3,2,1,0:T(8,128)(2,1)}) custom-call(bf16[128,2048]{1,0:T(8,128)(2,1)} %refs_3_.1, bf16[2,8,16,1024]{3,2,1,0:T(8,128)(2,1)} %reshape.67.refs_1_, bf16[2,64,2048]{2,1,0:T(8,128)(2,1)} %refs_7_.1), custom_call_target="tpu_custom_call" | custom-call | flops 100000000 | bytes 10000000 | tf_op jit(solution)/shard_map/prologue/pallas_call | solution.py:412
  66.2 6.4 %copy.51 = bf16[2048,1024]{1,0:T(8,128)(2,1)} copy(bf16[2048,1024]{0,1:T(8,128)(2,1)} %bitcast.113) | data formatting | bytes 8388608 | tf_op jit(solution)/shard_map/dot_general | solution.py:556
  72.6 11.4 %multiply_multiply_fusion.1 = (f32[1024,1024]{1,0:T(8,128)}, f32[1024,1024]{1,0:T(8,128)}, bf16[1024,1024]{1,0:T(8,128)(2,1)S(1)}) fusion(bf16[1024,2048]{1,0:T(8,128)(2,1)} %bitcast.114, bf16[2048,1024]{1,0:T(8,128)(2,1)} %bitcast.137), kind=kOutput, calls=%fused_computation.12 | convolution fusion | flops 4300210176 | bytes 18874368 | tf_op jit(solution)/shard_map/dot_general | solution.py:541
  84.0 5.4 copy.49
  89.5 2.8 fusion.21
  92.2 3.9 copy.53
  96.2 3.0 copy.35
  99.2 5.4 copy.33
  104.5 4.6 multiply_convert_fusion
  109.2 3.0 copy.61
  112.2 10.6 %fusion.38.refs_0_ = f32[8,128,2048]{2,1,0:T(8,128)} fusion(bf16[8,128,1024]{2,1,0:T(8,128)(2,1)} %bitcast.121, bf16[1024,2048,1]{1,0,2:T(8,128)(2,1)} %bitcast.128), kind=kOutput, calls=%fused_computation.57 | convolution fusion | flops 4294967296 | bytes 14680064 | tf_op jit(solution)/shard_map/dot_general | solution.py:541
  122.7 89.6 %forward.1 = (bf16[4,4,8,16,1024]{4,3,2,1,0:T(8,128)(2,1)}, bf16[4,4,64,2048]{3,2,1,0:T(8,128)(2,1)}, bf16[8,128,2048]{2,1,0:T(8,128)(2,1)}, bf16[8,128,2048]{2,1,0:T(8,128)(2,1)}, bf16[128,2048]{1,0:T(8,128)(2,1)}) custom-call(f32[8,128,2048]{2,1,0:T(8,128)} %fusion.38.refs_0_, bf16[128,2048]{1,0:T(8,128)(2,1)} %refs_3_.1, bf16[128,2048]{1,0:T(8,128)(2,1)} %refs_5_.1, ...), custom_call_target="tpu_custom_call" | custom-call | flops 100000000 | bytes 10000000 | tf_op jit(solution)/shard_map/forward/pallas_call | solution.py:412
  212.4 6.4 %copy.44 = bf16[2048,1024]{1,0:T(8,128)(2,1)} copy(bf16[2048,1024]{0,1:T(8,128)(2,1)} %bitcast.115) | data formatting | bytes 8388608 | tf_op jit(solution)/shard_map/dot_general | solution.py:556
  218.8 10.1 %fusion.33 = (bf16[1024,1024]{1,0:T(8,128)(2,1)}, bf16[1024,1024]{1,0:T(8,128)(2,1)S(1)}) fusion(bf16[1024,2048]{1,0:T(8,128)(2,1)} %bitcast.116, bf16[2048,1024]{1,0:T(8,128)(2,1)} %bitcast.132), kind=kOutput, calls=%fused_computation.45 | convolution fusion | flops 4306501632 | bytes 12582912 | tf_op jit(solution)/shard_map/dot_general | solution.py:541
  228.9 8.2 %fusion.7 = bf16[1024,1024]{1,0:T(8,128)(2,1)} fusion(bf16[1024,1024]{1,0:T(8,128)(2,1)S(1)} %get-tuple-element.46, bf16[1024,2048]{1,0:T(8,128)(2,1)S(1)} %bitcast.135, bf16[1024,2048]{1,0:T(8,128)(2,1)S(1)} %bitcast.130), kind=kOutput, calls=%fused_computation.19 | convolution fusion | flops 4319084544 | bytes 12582912 | tf_op jit(solution)/shard_map/dot_general | solution.py:548
  237.2 1.4 fusion.27
  238.6 2.6 copy.45
  241.2 10.7 %fusion.41.refs_3_ = f32[4,4,64,2048]{3,2,1,0:T(8,128)} fusion(bf16[4,4,64,1024]{3,2,1,0:T(8,128)(2,1)} %bitcast.122, bf16[1024,2048,1,1]{1,0,3,2:T(8,128)(2,1)} %bitcast.134), kind=kOutput, calls=%fused_computation.60 | convolution fusion | flops 4294967296 | bytes 14680064 | tf_op jit(solution)/shard_map/dot_general | solution.py:557
  251.9 6.7 %fusion.39.refs_0_ = f32[8,128,2048]{2,1,0:T(8,128)} fusion(bf16[8,128,1024]{2,1,0:T(8,128)(2,1)S(1)} %bitcast.139, bf16[2048,1024,1]{1,0,2:T(8,128)(2,1)S(1)} %bitcast.133), kind=kOutput, calls=%fused_computation.58 | convolution fusion | flops 4294967296 | bytes 14680064 | tf_op jit(solution)/shard_map/dot_general | solution.py:577
  258.7 6.7 %fusion.34.refs_2_ = f32[4,4,128,1024]{3,2,1,0:T(8,128)} fusion(bf16[4,4,128,1024]{3,2,1,0:T(8,128)(2,1)S(1)} %bitcast.112, bf16[1024,1024]{1,0:T(8,128)(2,1)S(1)} %copy-done.13), kind=kOutput, calls=%fused_computation.48 | convolution fusion | flops 4294967296 | bytes 14680064 | tf_op jit(solution)/shard_map/dot_general | solution.py:556
  265.3 6.7 %fusion.40.refs_1_ = f32[8,128,2048]{2,1,0:T(8,128)} fusion(bf16[8,128,1024]{2,1,0:T(8,128)(2,1)S(1)} %bitcast.138, bf16[1024,2048,1]{1,0,2:T(8,128)(2,1)S(1)} %bitcast.131), kind=kOutput, calls=%fused_computation.59 | convolution fusion | flops 4294967296 | bytes 14680064 | tf_op jit(solution)/shard_map/dot_general | solution.py:541
  272.0 148.0 %turn.1 = (bf16[128,2048]{1,0:T(8,128)(2,1)}, bf16[128,2048]{1,0:T(8,128)(2,1)}, bf16[8,128,2048]{2,1,0:T(8,128)(2,1)}, bf16[4,4,8,16,1024]{4,3,2,1,0:T(8,128)(2...) custom-call(f32[8,128,2048]{2,1,0:T(8,128)} %fusion.39.refs_0_, ...), custom_call_target="tpu_custom_call" | custom-call | flops 100000000 | bytes 10000000 | tf_op jit(solution)/shard_map/turn/pallas_call | solution.py:412
  420.0 14.7 %fusion.10 = bf16[1024,1024]{0,1:T(8,128)(2,1)} fusion(f32[1024,1024]{0,1:T(8,128)} %copy.49, f32[1024,1024]{0,1:T(8,128)} %copy.35, f32[1024,1024]{0,1:T(8,128)} %copy.33, bf16[1024,2048]{1,0:T(8,128)(2,1)} %bitcast.126, bf16[1024,2048]{1,0:T(8,128)(2,1)} %bitcast.136), kind=kOutput, calls=%fused_computation.22 | convolution fusion | flops 4314890240 | bytes 23068672 | tf_op jit(solution)/shard_map/dot_general | solution.py:548
  436.8 2.9 copy.62
  439.6 9.1 %fusion.42.refs_0_ = f32[8,128,2048]{2,1,0:T(8,128)} fusion(bf16[8,128,1024]{2,1,0:T(8,128)(2,1)S(1)} %bitcast.123, bf16[2048,1024,1]{1,0,2:T(8,128)(2,1)} %bitcast.129), kind=kOutput, calls=%fused_computation.61 | convolution fusion | flops 4294967296 | bytes 14680064 | tf_op jit(solution)/shard_map/dot_general | solution.py:585
  448.7 7.1 %fusion.36.refs_1_ = f32[4,4,128,1024]{3,2,1,0:T(8,128)} fusion(bf16[4,4,128,1024]{3,2,1,0:T(8,128)(2,1)S(1)} %bitcast.111, bf16[1024,1024]{0,1:T(8,128)(2,1)S(1)} %copy-done.3), kind=kOutput, calls=%fused_computation.50 | convolution fusion | flops 4294967296 | bytes 14680064 | tf_op jit(solution)/shard_map/dot_general | solution.py:556
  455.8 6.7 %fusion.43.refs_2_ = f32[4,4,64,2048]{3,2,1,0:T(8,128)} fusion(bf16[4,4,64,1024]{3,2,1,0:T(8,128)(2,1)S(1)} %bitcast.120, bf16[1024,2048,1,1]{1,0,3,2:T(8,128)(2,1)S(1)} %bitcast.127), kind=kOutput, calls=%fused_computation.62 | convolution fusion | flops 4294967296 | bytes 14680064 | tf_op jit(solution)/shard_map/dot_general | solution.py:557
  462.6 100.5 %last.1 = (bf16[128,2048]{1,0:T(8,128)(2,1)}, f32[8,16,1024]{2,1,0:T(8,128)}, f32[64,2048]{1,0:T(8,128)}) custom-call(f32[8,128,2048]{2,1,0:T(8,128)} %fusion.42.refs_0_, f32[4,4,128,1024]{3,2,1,0:T(8,128)} %fusion.36.refs_1_, f32[4,4,64,2048]{3,2,1,0:T(8,128)} %fusion.43.refs_2_, bf16[128,2048]{1,0:T(8,128)(2,1)} %refs_3_.1, ...), custom_call_target="tpu_custom_call" | custom-call | flops 100000000 | bytes 10000000 | tf_op jit(solution)/shard_map/last/pallas_call | solution.py:412
  563.1 2.3 pad_maximum_fusion.1
  569.6 1.9 copy.69
  (37 shorter events, 6.4 us)
Async XLA Ops:
  218.8 10.2 %copy-start.8 = (bf16[4,4,64,2048]{3,2,1,0:T(8,128)(2,1)S(1)}, bf16[4,4,64,2048]{3,2,1,0:T(8,128)(2,1)}, u32[]{:S(2)}) copy-start(bf16[4,4,64,2048]{3,2,1,0:T(8,128)(2,1)} %get-tuple-element.28) | copy-start | bytes 12582916
  218.8 10.2 %copy-start.11 = (bf16[8,128,2048]{2,1,0:T(8,128)(2,1)S(1)}, bf16[8,128,2048]{2,1,0:T(8,128)(2,1)}, u32[]{:S(2)}) copy-start(bf16[8,128,2048]{2,1,0:T(8,128)(2,1)} %get-tuple-element.27) | copy-start | bytes 12582916
  241.2 10.7 %copy-start.10 = (bf16[4,4,8,16,1024]{4,3,2,1,0:T(8,128)(2,1)S(1)}, bf16[4,4,8,16,1024]{4,3,2,1,0:T(8,128)(2,1)}, u32[]{:S(2)}) copy-start(bf16[4,4,8,16,1024]{4,3,2,1,0:T(8,128)(2,1)} %get-tuple-element.30) | copy-start | bytes 12582916
  241.2 10.7 %copy-start.13 = (bf16[1024,1024]{1,0:T(8,128)(2,1)S(1)}, bf16[1024,1024]{1,0:T(8,128)(2,1)}, u32[]{:S(2)}) copy-start(bf16[1024,1024]{1,0:T(8,128)(2,1)} %fusion.7) | copy-start | bytes 6291460
  251.9 6.8 %copy-start.1 = (bf16[2048,1024]{1,0:T(8,128)(2,1)S(1)}, bf16[2048,1024]{1,0:T(8,128)(2,1)}, u32[]{:S(2)}) copy-start(bf16[2048,1024]{1,0:T(8,128)(2,1)} %copy.44) | copy-start | bytes 12582916
  258.7 6.7 %copy-start.9 = (bf16[4,4,64,2048]{3,2,1,0:T(8,128)(2,1)S(1)}, bf16[4,4,64,2048]{3,2,1,0:T(8,128)(2,1)}, u32[]{:S(2)}) copy-start(bf16[4,4,64,2048]{3,2,1,0:T(8,128)(2,1)} %get-tuple-element.28) | copy-start | bytes 12582916
  258.7 6.7 %copy-start.12 = (bf16[1024,1024]{1,0:T(8,128)(2,1)S(1)}, bf16[1024,1024]{1,0:T(8,128)(2,1)}, u32[]{:S(2)}) copy-start(bf16[1024,1024]{1,0:T(8,128)(2,1)} %get-tuple-element.45) | copy-start | bytes 6291460
  420.0 14.8 %copy-start.5 = (f32[8,16,1024]{2,1,0:T(8,128)S(1)}, f32[8,16,1024]{2,1,0:T(8,128)}, u32[]{:S(2)}) copy-start(f32[8,16,1024]{2,1,0:T(8,128)} %get-tuple-element.39) | copy-start | bytes 1572868
  439.6 9.1 %copy-start = (bf16[2048,1024]{1,0:T(8,128)(2,1)S(1)}, bf16[2048,1024]{1,0:T(8,128)(2,1)}, u32[]{:S(2)}) copy-start(bf16[2048,1024]{1,0:T(8,128)(2,1)} %copy.51) | copy-start | bytes 12582916
  439.6 9.1 %copy-start.3 = (bf16[1024,1024]{0,1:T(8,128)(2,1)S(1)}, bf16[1024,1024]{0,1:T(8,128)(2,1)}, u32[]{:S(2)}) copy-start(bf16[1024,1024]{0,1:T(8,128)(2,1)} %fusion.10) | copy-start | bytes 6291460
  448.7 7.1 %copy-start.2 = (bf16[1024,1024]{1,0:T(8,128)(2,1)S(1)}, bf16[1024,1024]{1,0:T(8,128)(2,1)}, u32[]{:S(2)}) copy-start(bf16[1024,1024]{1,0:T(8,128)(2,1)} %copy.53) | copy-start | bytes 6291460
  448.7 7.1 %copy-start.7 = (bf16[8,128,2048]{2,1,0:T(8,128)(2,1)S(1)}, bf16[8,128,2048]{2,1,0:T(8,128)(2,1)}, u32[]{:S(2)}) copy-start(bf16[8,128,2048]{2,1,0:T(8,128)(2,1)} %get-tuple-element.33) | copy-start | bytes 12582916
  563.1 4.7 copy-start.4
  565.4 3.4 copy-start.6

commit v3 on v2

--- a/solution.py
+++ b/solution.py
@@ -19,6 +19,8 @@
 PAIR_RATE = 600e3
 LOCAL_RATE = 3000e3
 HOP = 2.2
+SLACK = 1.0
+GELU_C = 0.7978845608028654
 
 
 def gelu_tanh(values):
@@ -26,13 +28,13 @@
 
 
 class Event:
-    def __init__(self):
-        self.time = None
+    def __init__(self, time=None, rank=0, name=''):
+        self.time, self.rank, self.name = time, rank, name
 
 
 class Copy:
     def __init__(self, desc, time, remote):
-        self.desc, self.time, self.remote = desc, time, remote
+        self.desc, self.time, self.remote, self.rank = desc, time, remote, 0
 
     def wait(self):
         if self.remote:
@@ -120,18 +122,21 @@
 
     def run(self):
         while self.flows:
-            best, best_time = None, None
+            best = None
             for k, (_, items) in enumerate(self.flows):
                 if any(item.time is None for item in items):
                     continue
                 time = max([item.time for item in items] + [0.0])
-                if best is None or time < best_time:
-                    best, best_time = k, time
-            flow, items = self.flows.pop(best)
+                late = max(item.rank for item in items)
+                rank = (max(time, self.now) + (SLACK if late else 0.0), late, time)
+                if best is None or rank < best[0]:
+                    best = (rank, k, time)
+            _, k, time = best
+            flow, items = self.flows.pop(k)
             for item in items:
                 if isinstance(item, Copy):
                     item.wait()
-            self.now = max(self.now, best_time)
+            self.now = max(self.now, time)
             self.step(flow)
 
     def finish(self):
@@ -164,6 +169,20 @@
 
 def fire(net, event):
     event.time = net.now
+    if PRINT and event.name:
+        print('   %7.1f %s' % (net.now, event.name))
+
+
+def exchange(net, src, dst, done):
+    rows = src.shape[2]
+
+    def mine():
+        return dst.at[:, pl.ds(pl.multiple_of(net.data * rows, rows), rows)]
+
+    own = net.load(src.at[:, net.data], mine())
+    copies = [net.send(src.at[:, (net.data + k) % (2 * RING)], mine(), 'd', k) for k in range(1, 2 * RING)]
+    yield [own] + copies
+    fire(net, done)
 
 
 def exchange_back(net, src, dst, done):
@@ -178,14 +197,7 @@
     fire(net, done)
 
 
-def exchange(net, src, dst, done):
-    own = net.load(src.at[:, net.data], dst.at[:, net.data])
-    copies = [net.send(src.at[:, (net.data + k) % (2 * RING)], dst.at[:, net.data], 'd', k) for k in range(1, 2 * RING)]
-    yield [own] + copies
-    fire(net, done)
-
-
-def gather_x(net, full, done):
+def gather_x(net, full, done, issued=None):
     half = full.shape[1] // 2
     lo, hi = pl.ds(0, half), pl.ds(half, half)
 
@@ -204,109 +216,114 @@
     yield [back]
     back = net.send(part(1, hi), part(1, hi), 'x', -1)
     pair.append(net.send(block(1), block(1), 'p'))
+    if issued is not None:
+        fire(net, issued)
     yield [forth, back]
     pair.append(net.send(block(2), block(2), 'p'))
     yield pair
     fire(net, done)
 
 
-def gather_yz(net, own, full, first, done):
+def gather_yz(net, own, full, first, done, issued=None):
     second = 'y' if first == 'z' else 'z'
-    half = own.shape[0] // 2
-    lo, hi = pl.ds(0, half), pl.ds(half, half)
-
-    def index(one, two):
+    size = own.shape[0]
+    half = size // 2
+    all_rows, lo, hi = pl.ds(0, size), pl.ds(0, half), pl.ds(half, half)
+
+    def part(one, two, rows):
         at_one, at_two = net.at(first, one), net.at(second, two)
-        return (at_one, at_two) if first == 'z' else (at_two, at_one)
-
-    def block(one, two):
-        return full.at[index(one, two)]
-
-    def part(one, two, rows):
-        return full.at[index(one, two) + (rows,)]
+        return full.at[(at_one * RING + at_two if first == 'z' else at_two * RING + at_one), rows]
 
     ends = []
+    left = [RING]
 
     def relay(one, forth, back, end):
         yield [forth]
         forth = net.send(part(one, -1, lo), part(one, -1, lo), second, 1)
         yield [back]
         back = net.send(part(one, 1, hi), part(one, 1, hi), second, -1)
+        left[0] -= 1
+        if left[0] == 0 and issued is not None:
+            fire(net, issued)
         yield [forth, back]
         fire(net, end)
 
     def spread(src, one):
-        forth = net.send(src, block(one, 0), second, 1)
-        back = net.send(src, block(one, 0), second, -1)
+        forth = net.send(src, part(one, 0, all_rows), second, 1)
+        back = net.send(src, part(one, 0, all_rows), second, -1)
         end = Event()
         ends.append(end)
         net.spawn(relay(one, forth, back, end))
 
-    mine = net.load(own, block(0, 0))
-    forth = net.send(own, block(0, 0), first, 1)
-    back = net.send(own, block(0, 0), first, -1)
+    mine = net.load(own, part(0, 0, all_rows))
+    forth = net.send(own, part(0, 0, all_rows), first, 1)
+    back = net.send(own, part(0, 0, all_rows), first, -1)
     spread(own, 0)
     yield [forth]
     forth = net.send(part(-1, 0, lo), part(-1, 0, lo), first, 1)
-    spread(block(-1, 0), -1)
+    spread(part(-1, 0, all_rows), -1)
     yield [back]
     back = net.send(part(1, 0, hi), part(1, 0, hi), first, -1)
-    spread(block(1, 0), 1)
+    spread(part(1, 0, all_rows), 1)
     yield [forth, back]
-    spread(block(2, 0), 2)
+    spread(part(2, 0, all_rows), 2)
     yield [mine] + ends
     fire(net, done)
 
 
-def reduce_ring(net, axis, far, ahead, behind, mine, relay_f, relay_b, last_f, last_b, done):
-    half = mine.shape[0] // 2
+STEPS = (2, 1, -1, 0)
+
+
+def reduce_x(net, part, made, scratch, done):
+    other, relay_f, relay_b, last_f, last_b = scratch
+    half = part.shape[2] // 2
     lo, hi = pl.ds(0, half), pl.ds(half, half)
-    first_f = net.send(far.at[lo], relay_f, axis, 1)
-    first_b = net.send(far.at[hi], relay_b, axis, -1)
-    direct_f = net.send(ahead.at[hi], last_f.at[hi], axis, 1)
-    direct_b = net.send(behind.at[lo], last_b.at[lo], axis, -1)
+
+    def acc(k, rows=None):
+        return part.at[k, net.core] if rows is None else part.at[k, net.core, rows]
+
+    pairs = [None] * RING
+    ready = [Event() for _ in STEPS]
+
+    def pair(k):
+        yield [made[k]]
+        pairs[k] = net.send(part.at[k, 1 - net.core], other.at[k], 'p')
+        yield [pairs[k]]
+        add_into(net, acc(k), other.at[k])
+        fire(net, ready[k])
+
+    for k in range(RING):
+        net.spawn(pair(k))
+    yield [ready[0]]
+    first_f = net.send(acc(0, lo), relay_f, 'x', 1)
+    first_b = net.send(acc(0, hi), relay_b, 'x', -1)
+    yield [ready[1]]
+    direct_f = net.send(acc(1, hi), last_f.at[hi], 'x', 1)
+    yield [ready[2]]
+    direct_b = net.send(acc(2, lo), last_b.at[lo], 'x', -1)
     yield [first_f]
-    add_into(net, ahead.at[lo], relay_f)
-    summed_f = net.send(ahead.at[lo], last_f.at[lo], axis, 1)
+    add_into(net, acc(1, lo), relay_f)
+    summed_f = net.send(acc(1, lo), last_f.at[lo], 'x', 1)
     yield [first_b]
-    add_into(net, behind.at[hi], relay_b)
-    summed_b = net.send(behind.at[hi], last_b.at[hi], axis, -1)
-    yield [direct_f, direct_b, summed_f, summed_b]
-    add_into(net, mine, last_f, last_b)
+    add_into(net, acc(2, hi), relay_b)
+    summed_b = net.send(acc(2, hi), last_b.at[hi], 'x', -1)
+    yield [ready[3], direct_f, direct_b, summed_f, summed_b]
+    add_into(net, acc(3), last_f, last_b)
     fire(net, done)
 
 
-STEPS = (2, 1, -1, 0)
-
-
-def reduce_x(net, part, acc, other, relay_f, relay_b, last_f, last_b, done):
-    half = acc.shape[1] // 2
-    lo, hi = pl.ds(0, half), pl.ds(half, half)
-    pairs, mine = [], []
+def reduce_x_scratch(rows, cols):
+    return [pltpu.VMEM((RING, rows, cols), F32), pltpu.VMEM((rows // 2, cols), F32), pltpu.VMEM((rows // 2, cols), F32),
+            pltpu.VMEM((rows, cols), F32), pltpu.VMEM((rows, cols), F32)]
+
+
+def load_parts(net, src, part, made):
     for k, step in enumerate(STEPS):
-        pairs.append(net.send(part.at[net.at('x', step) * 2 + (1 - net.core)], other.at[k], 'p'))
-        mine.append(net.load(part.at[net.at('x', step) * 2 + net.core], acc.at[k]))
-    yield [pairs[0], mine[0]]
-    add_into(net, acc.at[0], other.at[0])
-    first_f = net.send(acc.at[0, lo], relay_f, 'x', 1)
-    first_b = net.send(acc.at[0, hi], relay_b, 'x', -1)
-    yield [pairs[1], mine[1]]
-    add_into(net, acc.at[1], other.at[1])
-    direct_f = net.send(acc.at[1, hi], last_f.at[hi], 'x', 1)
-    yield [pairs[2], mine[2]]
-    add_into(net, acc.at[2], other.at[2])
-    direct_b = net.send(acc.at[2, lo], last_b.at[lo], 'x', -1)
-    yield [pairs[3], mine[3]]
-    add_into(net, acc.at[3], other.at[3])
-    yield [first_f]
-    add_into(net, acc.at[1, lo], relay_f)
-    summed_f = net.send(acc.at[1, lo], last_f.at[lo], 'x', 1)
-    yield [first_b]
-    add_into(net, acc.at[2, hi], relay_b)
-    summed_b = net.send(acc.at[2, hi], last_b.at[hi], 'x', -1)
-    yield [direct_f, direct_b, summed_f, summed_b]
-    add_into(net, acc.at[3], last_f, last_b)
-    fire(net, done)
+        def bring(k=k, step=step):
+            yield [net.load(src.at[pl.ds(net.at('x', step) * 2, 2)], part.at[k])]
+            fire(net, made[k])
+
+        net.spawn(bring())
 
 
 def reduce_yz(net, part, first, sums, ahead, behind, relay1, last1, relay2, last2, start, done):
@@ -366,11 +383,6 @@
             pltpu.VMEM((2, rows // 2, cols), F32), pltpu.VMEM((2, rows, cols), F32)]
 
 
-def reduce_x_scratch(rows, cols):
-    return [pltpu.VMEM((RING, rows, cols), F32), pltpu.VMEM((RING, rows, cols), F32), pltpu.VMEM((rows // 2, cols), F32),
-            pltpu.VMEM((rows // 2, cols), F32), pltpu.VMEM((rows, cols), F32), pltpu.VMEM((rows, cols), F32)]
-
-
 def norm_rows(x_ref, u_ref):
     def body(at):
         x = x_ref[at, :].astype(F32)
@@ -420,6 +432,69 @@
 PRINT = False
 
 
+WIDE = 512
+
+
+def wide_loop(total, body):
+    wide = min(WIDE, total)
+
+    def step(k, carry):
+        body(k, wide, pl.ds(pl.multiple_of(k * wide, wide), wide))
+        return carry
+
+    lax.fori_loop(0, total // wide, step, 0)
+
+
+def flat(value):
+    return value.reshape(value.shape[0] * value.shape[1], value.shape[2])
+
+
+def dot_rows(a, b):
+    return jnp.dot(flat(a), flat(b), preferred_element_type=F32)
+
+
+def dot_cols(a, b):
+    return lax.dot_general(flat(a), flat(b), CONTRACT_COLS, preferred_element_type=F32)
+
+
+def gelu(a):
+    return 0.5 * a * (1.0 + jnp.tanh(GELU_C * (a + 0.044715 * a * a * a)))
+
+
+def hidden_rows(net, chip, u, up, a, s):
+    at = pl.ds(chip * 2, 2)
+
+    def body(_, wide, cols):
+        pre = dot_rows(u[at], up[:, :, cols]).astype(BF16)
+        a[at, :, cols] = pre.reshape(2, -1, wide)
+        s[at, :, cols] = gelu(pre.astype(F32)).astype(BF16).reshape(2, -1, wide)
+
+    wide_loop(up.shape[2], body)
+    net.spend(2.4)
+
+
+def down_rows(net, chip, s, down, part):
+    at = pl.ds(chip * 2, 2)
+
+    def body(_, wide, cols):
+        part[:, :, cols] = dot_rows(s[at], down[:, :, cols]).reshape(2, -1, wide)
+
+    wide_loop(down.shape[2], body)
+    net.spend(1.8)
+
+
+def hidden_back_rows(net, chip, dy, down, ds):
+    at = pl.ds(chip * 2, 2)
+    rows = down.shape[1]
+
+    def body(k, wide, cols):
+        blocks = pl.ds(k * (wide // rows), wide // rows)
+        ds[at, :, cols] = dot_cols(dy[at], down[blocks]).astype(BF16).reshape(2, -1, wide)
+
+    wide_loop(down.shape[0] * rows, body)
+    net.spend(2.4)
+
+
 def solution(mesh):
     nl, nd = mesh.shape['local'], mesh.shape['data']
     tok_spec = P(BOTH_AXES, None)
@@ -432,54 +507,97 @@
         hidden = nl * dr
         shape = jax.ShapeDtypeStruct
         cols = w_up.reshape(num_layers, ur, nl, nd, dr).transpose(0, 3, 1, 2, 4).reshape(num_layers, nd, ur, hidden)
-        up_full = shape((RING, RING, nd, ur, hidden), BF16)
-        down_full = shape((RING, RING, dr, width), BF16)
+        up_full = shape((nl, nd * ur, hidden), BF16)
+        down_full = shape((nl, dr, width), BF16)
         act_full = shape((nd, rows, width), BF16)
+        hid_full = shape((nd, rows, hidden), BF16)
         own = shape((rows, width), BF16)
-        rx = reduce_x_scratch(rows, width)
+        part_vmem = pltpu.VMEM((RING, 2, rows, width), F32)
+        rx = [part_vmem] + reduce_x_scratch(rows, width)
         ryz_up = reduce_yz_scratch(nd * ur, hidden)
         ryz_down = reduce_yz_scratch(dr, width)
 
-        def prologue(net, x_ref, w_up_ref, w_down_ref, up_ref, down_ref, u_ref, block_ref):
+        def vmem(like):
+            return pltpu.VMEM(like.shape, like.dtype)
+
+        def forward(net, x_ref, g_in, cols_in, down_in, block_out, u_out, a_out, s_out, up_out, down_out, next_out, g_out, ds_out, x_out,
+                    u, g, u1, up0, down0, up1, down1, a, s, ds, part, *rx_scratch):
             net.barrier('dyz')
-            blocks = Event()
-            net.spawn(exchange(net, w_up_ref, block_ref, blocks))
-            norm_rows(x_ref, u_ref.at[net.data])
-            net.spawn(gather_x(net, u_ref, Event()))
-            net.spawn(gather_yz(net, w_down_ref.at[0], down_ref, 'z', Event()))
-
-            def up():
+            blocks, got_u, got_g, got_u1, got_up0, got_down0, got_up1, got_down1, reduced = (Event() for _ in range(9))
+            made = [Event() for _ in STEPS]
+            hidden_made = [Event() for _ in STEPS]
+            got_up0.rank = 2
+            names = dict(blocks=blocks, got_u=got_u, got_g=got_g, got_u1=got_u1, got_up0=got_up0, got_down0=got_down0, got_up1=got_up1,
+                         got_down1=got_down1, reduced=reduced)
+            for name, event in names.items():
+                event.name = name
+            for k in range(RING):
+                made[k].name, hidden_made[k].name = 'made%d' % k, 'hidden%d' % k
+            net.spawn(exchange(net, cols_in, block_out, blocks))
+            norm_rows(x_ref, u.at[net.data])
+            net.spend(0.5)
+            sent_u, sent_up0, sent_down0 = Event(name='sent_u'), Event(name='sent_up0'), Event(name='sent_down0')
+            net.spawn(gather_x(net, u, got_u, sent_u))
+            net.spawn(gather_yz(net, down_in.at[0], down0, 'z', got_down0, sent_down0))
+
+            def up_first():
                 yield [blocks]
-                net.spawn(gather_yz(net, block_ref.at[0], up_ref, 'y', Event()))
-
-            net.spawn(up())
-            net.run()
-
-        def forward(net, part_ref, x_ref, g_in_ref, block_ref, w_down_ref, up_ref, down_ref, u_ref, g_ref, next_ref, *scratch):
-            net.barrier('pxyz')
-            reduced, gathered = Event(), Event()
-            net.spawn(reduce_x(net, part_ref, *scratch, reduced))
-            net.spawn(gather_yz(net, block_ref.at[1], up_ref, 'y', Event()))
-            net.spawn(gather_yz(net, w_down_ref.at[1], down_ref, 'z', Event()))
+                net.spawn(gather_yz(net, block_out.at[0], up0, 'y', got_up0, sent_up0))
+
+            def second():
+                yield [sent_up0, sent_down0]
+                net.spawn(gather_yz(net, block_out.at[1], up1, 'y', got_up1))
+                net.spawn(gather_yz(net, down_in.at[1], down1, 'z', got_down1))
+
+            def grad():
+                yield [net.load(g_in, g.at[net.data]), sent_u]
+                net.spawn(gather_x(net, g, got_g))
+
+            def save(event, *pairs):
+                yield [event]
+                yield [net.load(src, dst) for src, dst in pairs]
+
+            def hidden_flow():
+                yield [got_u, got_up0]
+                for k, step in enumerate(STEPS):
+                    hidden_rows(net, net.at('x', step), u, up0, a, s)
+                    fire(net, hidden_made[k])
+                    yield [Event(net.now, 2)]
+                yield [net.load(a, a_out), net.load(s, s_out), net.load(u, u_out)]
+
+            def down_flow():
+                for k, step in enumerate(STEPS):
+                    yield [hidden_made[k], got_down0, Event(0.0, 1)]
+                    down_rows(net, net.at('x', step), s, down0, part.at[k])
+                    fire(net, made[k])
 
             def act():
                 yield [reduced]
-                add_rows(x_ref, scratch[0].at[3], next_ref)
-                norm_rows(next_ref, u_ref.at[net.data])
-                net.spend(0.5)
-                net.spawn(gather_x(net, u_ref, gathered))
-                yield [net.load(g_in_ref, g_ref.at[net.data])]
-                net.spawn(gather_x(net, g_ref, Event()))
-
-            net.spawn(act())
+                add_rows(x_ref, part.at[3, net.core], x_out)
+                norm_rows(x_out, u1.at[net.data])
+                net.spend(1.0)
+                net.spawn(gather_x(net, u1, got_u1))
+
+            def back_flow():
+                for k, step in enumerate(STEPS):
+                    yield [got_g, got_down1, Event(0.0, 3)]
+                    hidden_back_rows(net, net.at('x', step), g, down1, ds)
+                yield [net.load(ds, ds_out)]
+
+            for flow in (up_first(), second(), grad(), hidden_flow(), down_flow(), act(), back_flow(),
+                         reduce_x(net, part, made, rx_scratch, reduced),
+                         save(got_up1, (up1, up_out)), save(got_down1, (down1, down_out)), save(got_u1, (u1, next_out)), save(got_g, (g, g_out))):
+                net.spawn(flow)
             net.run()
 
-        def turn(net, du_ref, part_ref, dup_ref, ddown_ref, x_ref, g_ref, block_ref, w_down_ref,
-                 out_ref, dy_ref, dy_full_ref, up_ref, down_ref, dw_up_ref, dw_down_ref, *scratch):
+        def turn(net, du_ref, dup_ref, ddown_ref, x_ref, g_ref, block_ref, w_down_ref,
+                 dy_ref, dy_full_ref, up_ref, down_ref, dw_up_ref, dw_down_ref, *scratch):
             net.barrier('dyz')
-            r1, r2, s1, s2 = scratch[:6], scratch[6:12], scratch[12:19], scratch[19:26]
-            reduced, gathered, out, summed1, summed2 = (Event() for _ in range(5))
-            net.spawn(reduce_x(net, du_ref, *r1, reduced))
+            r1, s1, s2 = scratch[:6], scratch[6:13], scratch[13:20]
+            reduced, gathered, summed1, summed2 = (Event() for _ in range(4))
+            made = [Event() for _ in STEPS]
+            load_parts(net, du_ref, r1[0], made)
+            net.spawn(reduce_x(net, r1[0], made, r1[1:], reduced))
             net.spawn(gather_yz(net, block_ref.at[0], up_ref, 'y', Event()))
             net.spawn(gather_yz(net, w_down_ref.at[0], down_ref, 'z', Event()))
             net.spawn(reduce_yz(net, dup_ref, 'y', *s1, None, summed1))
@@ -487,13 +605,10 @@
 
             def act():
                 yield [reduced]
-                norm_back_rows(x_ref, g_ref, r1[0].at[3], dy_ref)
+                norm_back_rows(x_ref, g_ref, r1[0].at[3, net.core], dy_ref)
                 net.spend(0.7)
                 yield [net.load(dy_ref, dy_full_ref.at[net.data])]
                 net.spawn(gather_x(net, dy_full_ref, gathered))
-                net.spawn(reduce_x(net, part_ref, *r2, out))
-                yield [out]
-                add_rows(x_ref, r2[0].at[3], out_ref)
 
             def grads():
                 yield [summed1]
@@ -505,18 +620,27 @@
             net.spawn(grads())
             net.run()
 
-        def last(net, du_ref, dup_ref, ddown_ref, x_ref, g_ref, dx_ref, dw_up_ref, dw_down_ref, *scratch):
+        def last(net, du_ref, part_ref, dup_ref, ddown_ref, x_ref, dy_ref, x1_ref, dx_ref, out_ref, dw_up_ref, dw_down_ref, *scratch):
             net.barrier('dyz')
-            r1, s1, s2 = scratch[:6], scratch[6:13], scratch[13:20]
-            reduced, summed1, summed2 = (Event() for _ in range(3))
-            net.spawn(reduce_x(net, du_ref, *r1, reduced))
+            r1, r2, s1, s2 = scratch[:6], scratch[6:12], scratch[12:19], scratch[19:26]
+            reduced, out, summed1, summed2 = (Event() for _ in range(4))
+            made1, made2 = [Event() for _ in STEPS], [Event() for _ in STEPS]
+            load_parts(net, du_ref, r1[0], made1)
+            net.spawn(reduce_x(net, r1[0], made1, r1[1:], reduced))
             net.spawn(reduce_yz(net, dup_ref, 'y', *s1, None, summed1))
             net.spawn(reduce_yz(net, ddown_ref, 'z', *s2, None, summed2))
 
             def act():
                 yield [reduced]
-                norm_back_rows(x_ref, g_ref, r1[0].at[3], dx_ref)
+                norm_back_rows(x_ref, dy_ref, r1[0].at[3, net.core], dx_ref)
                 net.spend(0.7)
+
+            def forward_out():
+                yield [Event(20.0)]
+                load_parts(net, part_ref, r2[0], made2)
+                net.spawn(reduce_x(net, r2[0], made2, r2[1:], out))
+                yield [out]
+                add_rows(x1_ref, r2[0].at[3, net.core], out_ref)
 
             def grads():
                 yield [summed1]
@@ -525,6 +649,7 @@
                 yield [net.load(s2[0].at[3], dw_down_ref)]
 
             net.spawn(act())
+            net.spawn(forward_out())
             net.spawn(grads())
             net.run()
 
@@ -544,8 +669,7 @@
             a = dot(u_full, up).astype(BF16)
             return a, gelu_tanh(a.astype(F32)).astype(BF16)
 
-        def hidden_back(a, dy_full, down):
-            ds = lax.dot_general(dy_full, down, CONTRACT_COLS, preferred_element_type=F32).astype(BF16)
+        def pre_back(a, ds):
             _, back = jax.vjp(gelu_tanh, a.astype(F32))
             return back(ds.astype(F32))[0].astype(BF16)
 
@@ -562,31 +686,29 @@
 
         d_up_own, d_down_own = shape((nd, ur, hidden), F32), shape((dr, width), F32)
 
-        up0, down0, u0, blocks = call(
-            prologue, [up_full, down_full, act_full, shape((num_layers, nd, ur, hidden), BF16)], 'vvvh', 'vhh', [], 64, 8, 0,
-            tokens, cols, w_down)
-        u0 = flat_act(u0)
-        a0, s0 = hidden_of(u0, flat_up(up0))
-        part0 = split_part(dot(s0, flat_down(down0)))
-        up1, down1, u1, g_full, x1 = call(
-            forward, [up_full, down_full, act_full, act_full, own], 'vvvvv', 'hvhhh', rx, 72, 12, 1,
-            part0, tokens, grad_out, blocks, w_down)
-        u1, g_full, up1, down1 = flat_act(u1), flat_act(g_full), flat_up(up1), flat_down(down1)
+        blocks, u0, a0, s0, up1, down1, u1, g_full, ds1, x1 = call(
+            forward, [shape((num_layers, nd * ur, hidden), BF16), act_full, hid_full, hid_full, up_full, down_full, act_full, act_full, hid_full, own],
+            'hhhhhhhhhv', 'vhhh',
+            [vmem(act_full)] * 3 + [vmem(up_full), vmem(down_full)] * 2 + [vmem(hid_full)] * 3 + rx, 128, 32, 0,
+            tokens, grad_out, cols, w_down)
+        u0, u1, g_full = flat_act(u0), flat_act(u1), flat_act(g_full)
+        a0, s0, ds1 = (t.reshape(nd * rows, hidden) for t in (a0, s0, ds1))
+        up1, down1 = flat_up(up1), flat_down(down1)
         a1, s1 = hidden_of(u1, up1)
-        da1 = hidden_back(a1, g_full, down1)
+        da1 = pre_back(a1, ds1)
         du1 = split_part(lax.dot_general(da1, up1, CONTRACT_COLS, preferred_element_type=F32))
         part1 = split_part(dot(s1, down1))
         d_up1, d_down1 = grads_of(u1, s1, da1, g_full)
-        x_out, dy0, dy_full, up0, down0, dw_up1, dw_down1 = call(
-            turn, [own, own, act_full, up_full, down_full, d_up_own, d_down_own], 'vvvvvhh', 'hhhhvvhh', rx + rx + ryz_up + ryz_down, 144, 48, 2,
-            du1, part1, d_up1, d_down1, x1, grad_out, blocks, w_down)
+        dy0, dy_full, up0, down0, dw_up1, dw_down1 = call(
+            turn, [own, act_full, up_full, down_full, d_up_own, d_down_own], 'vvvvhh', 'hhhvvhh', rx + ryz_up + ryz_down, 144, 48, 1,
+            du1, d_up1, d_down1, x1, grad_out, blocks, w_down)
         dy_full, up0, down0 = flat_act(dy_full), flat_up(up0), flat_down(down0)
-        da0 = hidden_back(a0, dy_full, down0)
+        da0 = pre_back(a0, lax.dot_general(dy_full, down0, CONTRACT_COLS, preferred_element_type=F32).astype(BF16))
         du0 = split_part(lax.dot_general(da0, up0, CONTRACT_COLS, preferred_element_type=F32))
         d_up0, d_down0 = grads_of(u0, s0, da0, dy_full)
-        dx, dw_up0, dw_down0 = call(
-            last, [own, d_up_own, d_down_own], 'vhh', 'hhhvv', rx + ryz_up + ryz_down, 96, 48, 3,
-            du0, d_up0, d_down0, tokens, dy0)
+        dx, x_out, dw_up0, dw_down0 = call(
+            last, [own, own, d_up_own, d_down_own], 'vvhh', 'hhhhvvv', rx + rx + ryz_up + ryz_down, 96, 56, 2,
+            du0, part1, d_up0, d_down0, tokens, dy0, x1)
         return x_out, dx, jnp.stack([own_up(dw_up0), own_up(dw_up1)]), jnp.stack([dw_down0, dw_down1])
 
     return jax.shard_map(device_fn, mesh=mesh, in_specs=(tok_spec, tok_spec, w_spec, w_spec), out_specs=(tok_spec, tok_spec, w_spec, w_spec), check_vma=False)

time: 580 us -> 558 us (0.962)
  matrix products: 109 us -> 93.6 us
  Pallas kernels: 400 us -> 387 us
    dot_general x4 -> x2, matrix products: 38.8 us -> 21.7 us  [dot(): return jnp.dot(a, b, preferred_element_type=F32)]
    convert_element_type x0 -> x3, local copies, waits for them, and re-layouts: none -> 16.4 us  [the longest x2 11 us: pre_back(): _, back = jax.vjp(gelu_tanh, a.astype(F32))]
    pallas_call x4 -> x3, Pallas kernels: 400 us -> 387 us  [call(): pl.pallas_call(kernel, out_shape=out_shape, in_specs=[spaces[s] for s in...]
    dot_general x2 -> x1, matrix products: 22.9 us -> 11.3 us  [device_fn(): lax.dot_general(dy_full, down0, CONTRACT_COLS, preferred_element_type=F32)]
    convert_element_type x3 -> x1, local copies, waits for them, and re-layouts: 9.53 us -> 2.85 us  [hidden_of(): return (a, gelu_tanh(a.astype(F32)).astype(BF16))]
    convert_element_type x0 -> x1, other arithmetic: none -> 6.47 us  [pre_back(): _, back = jax.vjp(gelu_tanh, a.astype(F32))]
    dot_general x2, matrix products: 13.8 us -> 19.8 us  [grads_of(): lax.dot_general(u_full, da, CONTRACT_ROWS, preferred_element_type=F32)]
where the time goes in v3:
time: 558 us; the launch traced here: 550 us
  Pallas kernels  387 us (69%)
  matrix products  93.6 us (17%)
  local copies, waits for them, and re-layouts  52.6 us (9%)
  other arithmetic  16 us (3%)
    pallas_call x3, Pallas kernels, call(): pl.pallas_call(kernel, out_shape=out_shape, in_specs=[spaces[s] for s in...  387 us
    dot_general x2, matrix products, dot(): return jnp.dot(a, b, preferred_element_type=F32)  21.7 us
    dot_general x2, matrix products, grads_of(): lax.dot_general(u_full, da, CONTRACT_ROWS, preferred_element_type=F32)  19.8 us
    dot_general x2, matrix products, grads_of(): lax.dot_general(s, dy_full, CONTRACT_ROWS, preferred_element_type=F32)  19.4 us
    dot_general x2, local copies, waits for them, and re-layouts, grads_of(): lax.dot_general(u_full, da, CONTRACT_ROWS, preferred_element_type=F32)  12.8 us
    dot_general x1, matrix products, device_fn(): lax.dot_general(dy_full, down0, CONTRACT_COLS, preferred_element_type=F32)  11.3 us

profile of v3, /device:TPU:1, one launch (start us, length us, event | category | flops | bytes accessed | tf_op | source)
XLA Modules:
  0.0 550.1 jit_solution(13636599349060801370)
XLA Ops:
  0.6 2.1 reshape.67
  2.9 1.5 reshape.68.refs_2_
  4.4 129.0 %forward.1 = (bf16[2,128,1024]{2,1,0:T(8,128)(2,1)}, bf16[8,128,2048]{2,1,0:T(8,128)(2,1)}, bf16[8,128,1024]{2,1,0:T(8,128)(2,1)}, bf16[8,128,1024]{2,1,0:T(8,12...) custom-call(bf16[128,2048]{1,0:T(8,128)(2,1)} %refs_4_.3, ...), custom_call_target="tpu_custom_call" | custom-call | flops 100000000 | bytes 10000000 | tf_op jit(solution)/shard_map/forward/pallas_call | solution.py:424
  133.4 6.5 %bitcast_convert_fusion = (f32[1024,1024]{1,0:T(8,128)}, f32[1024,1024]{1,0:T(8,128)}) fusion(bf16[8,128,1024]{2,1,0:T(8,128)(2,1)} %get-tuple-element.32, bf16[8,128,1024]{2,1,0:T(8,128)(2,1)} %get-tuple-element.24), kind=kLoop, calls=%fused_computation.35 | loop fusion | flops 2097152 | bytes 12582912 | tf_op jit(solution)/shard_map/convert_element_type | solution.py:673
  139.8 5.6 %copy.50 = f32[1024,1024]{0,1:T(8,128)} copy(f32[1024,1024]{1,0:T(8,128)} %get-tuple-element.48) | data formatting | bytes 8388608 | tf_op jit(solution)/shard_map/convert_element_type | solution.py:673
  145.5 11.2 %fusion.24 = (bf16[1024,1024]{0,1:T(8,128)(2,1)}, f32[1024,1024]{1,0:T(8,128)}) fusion(bf16[1024,2048]{1,0:T(8,128)(2,1)} %bitcast.80, bf16[2048,1024]{1,0:T(8,128)(2,1)} %bitcast.97), kind=kOutput, calls=%fused_computation.31 | convolution fusion | flops 4306501632 | bytes 14680064 | tf_op jit(solution)/shard_map/dot_general | solution.py:666
  156.7 5.4 copy.38
  162.1 5.4 copy.39
  167.4 6.3 %multiply_convert_fusion = (bf16[1024,1024]{0,1:T(8,128)(2,1)}, bf16[1024,1024]{0,1:T(8,128)(2,1)S(1)}) fusion(f32[1024,1024]{0,1:T(8,128)} %copy.38, f32[1024,1024]{0,1:T(8,128)} %copy.39), kind=kLoop, calls=%fused_computation.32 | loop fusion | flops 23068672 | bytes 12582912 | tf_op jit(solution)/shard_map/convert_element_type | solution.py:670
  173.7 2.6 copy.65
  176.3 10.6 %fusion.29.refs_0_ = f32[8,128,2048]{2,1,0:T(8,128)} fusion(bf16[8,128,1024]{2,1,0:T(8,128)(2,1)} %bitcast.91, bf16[2048,1024,1]{1,0,2:T(8,128)(2,1)} %bitcast.98), kind=kOutput, calls=%fused_computation.43 | convolution fusion | flops 4294967296 | bytes 14680064 | tf_op jit(solution)/shard_map/dot_general | solution.py:699
  186.9 6.4 %copy.43 = bf16[2048,1024]{1,0:T(8,128)(2,1)} copy(bf16[2048,1024]{0,1:T(8,128)(2,1)} %bitcast.81) | data formatting | bytes 8388608 | tf_op jit(solution)/shard_map/dot_general | solution.py:680
  193.3 9.0 %fusion.27.refs_1_ = f32[4,4,128,1024]{3,2,1,0:T(8,128)} fusion(bf16[4,4,128,1024]{3,2,1,0:T(8,128)(2,1)} %bitcast.82, bf16[1024,1024]{0,1:T(8,128)(2,1)S(1)} %get-tuple-element.45), kind=kOutput, calls=%fused_computation.36 | convolution fusion | flops 4294967296 | bytes 14680064 | tf_op jit(solution)/shard_map/dot_general | solution.py:680
  202.3 2.9 copy.45
  205.1 8.9 %fusion.30.refs_2_ = f32[4,4,64,2048]{3,2,1,0:T(8,128)} fusion(bf16[4,4,64,1024]{3,2,1,0:T(8,128)(2,1)S(1)} %bitcast.88, bf16[1024,2048,1,1]{1,0,3,2:T(8,128)(2,1)} %bitcast.96), kind=kOutput, calls=%fused_computation.44 | convolution fusion | flops 4294967296 | bytes 14680064 | tf_op jit(solution)/shard_map/dot_general | solution.py:681
  214.0 156.4 %turn.1 = (bf16[128,2048]{1,0:T(8,128)(2,1)}, bf16[8,128,2048]{2,1,0:T(8,128)(2,1)}, bf16[16,128,1024]{2,1,0:T(8,128)(2,1)}, bf16[16,64,2048]{2,1,0:T(8,128)(2,1...) custom-call(f32[8,128,2048]{2,1,0:T(8,128)} %fusion.29.refs_0_, f32[4,4,128,1024]{3,2,1,0:T(8,128)} %fusion.27.refs_1_, ...), custom_call_target="tpu_custom_call" | custom-call | flops 100000000 | bytes 10000000 | tf_op jit(solution)/shard_map/turn/pallas_call | solution.py:424
  370.5 11.3 %fusion.2 = bf16[1024,1024]{0,1:T(8,128)(2,1)S(1)} fusion(f32[1024,1024]{0,1:T(8,128)} %copy.50, bf16[1024,2048]{1,0:T(8,128)(2,1)} %bitcast.99, bf16[1024,2048]{1,0:T(8,128)(2,1)} %bitcast.102), kind=kOutput, calls=%fused_computation.9 | convolution fusion | flops 4318035968 | bytes 14680064 | tf_op jit(solution)/shard_map/dot_general | solution.py:706
  381.8 2.6 copy.67
  384.4 10.7 %fusion.31.refs_0_ = f32[8,128,2048]{2,1,0:T(8,128)} fusion(bf16[8,128,1024]{2,1,0:T(8,128)(2,1)} %bitcast.92, bf16[2048,1024,1]{1,0,2:T(8,128)(2,1)} %bitcast.101), kind=kOutput, calls=%fused_computation.45 | convolution fusion | flops 4294967296 | bytes 14680064 | tf_op jit(solution)/shard_map/dot_general | solution.py:707
  395.2 2.7 copy.68
  397.9 10.6 %fusion.32.refs_1_ = f32[8,128,2048]{2,1,0:T(8,128)} fusion(bf16[8,128,1024]{2,1,0:T(8,128)(2,1)} %bitcast.89, bf16[1024,2048,1]{1,0,2:T(8,128)(2,1)} %bitcast.95), kind=kOutput, calls=%fused_computation.46 | convolution fusion | flops 4294967296 | bytes 14680064 | tf_op jit(solution)/shard_map/dot_general | solution.py:666
  408.5 6.4 %copy.55 = bf16[2048,1024]{1,0:T(8,128)(2,1)} copy(bf16[2048,1024]{0,1:T(8,128)(2,1)} %bitcast.79) | data formatting | bytes 8388608 | tf_op jit(solution)/shard_map/dot_general | solution.py:680
  414.9 10.8 %fusion.25.refs_2_ = f32[4,4,128,1024]{3,2,1,0:T(8,128)} fusion(bf16[4,4,128,1024]{3,2,1,0:T(8,128)(2,1)} %bitcast.83, bf16[1024,1024]{0,1:T(8,128)(2,1)} %copy-done.2), kind=kOutput, calls=%fused_computation.33 | convolution fusion | flops 4294967296 | bytes 14680064 | tf_op jit(solution)/shard_map/dot_general | solution.py:680
  425.7 2.5 copy.57
  428.2 10.5 %fusion.33.refs_3_ = f32[4,4,64,2048]{3,2,1,0:T(8,128)} fusion(bf16[4,4,64,1024]{3,2,1,0:T(8,128)(2,1)} %bitcast.90, bf16[1024,2048,1,1]{1,0,3,2:T(8,128)(2,1)} %bitcast.100), kind=kOutput, calls=%fused_computation.47 | convolution fusion | flops 4294967296 | bytes 14680064 | tf_op jit(solution)/shard_map/dot_general | solution.py:681
  438.7 101.3 %last.1 = (bf16[128,2048]{1,0:T(8,128)(2,1)}, bf16[128,2048]{1,0:T(8,128)(2,1)}, f32[8,16,1024]{2,1,0:T(8,128)}, f32[64,2048]{1,0:T(8,128)}) custom-call(f32[8,128,2048]{2,1,0:T(8,128)} %fusion.31.refs_0_, f32[8,128,2048]{2,1,0:T(8,128)} %fusion.32.refs_1_, f32[4,4,128,1024]{3,2,1,0:T(8,128)} %fusion.25.refs_2_, f32[4,4,64,2048]{3,2,1,0:T(8,128)} %fusion.33.refs_3_, ...), custom_call_target="tpu_custom_call" | custom-call | flops 100000000 | bytes 10000000 | tf_op jit(solution)/shard_map/last/pallas_call | solution.py:424
  540.0 1.4 reshape.79
  541.4 0.6 copy.59
  543.6 1.0 pad_maximum_fusion
  544.7 2.3 pad_maximum_fusion.1
  546.9 1.9 copy.74
  548.8 0.8 copy.75
  (15 shorter events, 1.8 us)
Async XLA Ops:
  381.8 2.6 copy-start.2
  384.4 10.7 %copy-start = (bf16[1024,1024]{0,1:T(8,128)(2,1)S(1)}, bf16[1024,1024]{0,1:T(8,128)(2,1)}, u32[]{:S(2)}) copy-start(bf16[1024,1024]{0,1:T(8,128)(2,1)} %get-tuple-element.44) | copy-start | bytes 6291460
  414.9 10.8 %copy-start.1 = (bf16[8,128,1024]{2,1,0:T(8,128)(2,1)S(1)}, bf16[8,128,1024]{2,1,0:T(8,128)(2,1)}, u32[]{:S(2)}) copy-start(bf16[8,128,1024]{2,1,0:T(8,128)(2,1)} %get-tuple-element.36) | copy-start | bytes 6291460
  540.0 2.4 copy-start.3
  542.6 6.2 %copy-start.4 = (bf16[128,2048]{1,0:T(8,128)(2,1)S(1)}, bf16[128,2048]{1,0:T(8,128)(2,1)}, u32[]{:S(2)}) copy-start(bf16[128,2048]{1,0:T(8,128)(2,1)} %get-tuple-element.55) | copy-start | bytes 1572868

commit v4 on v3

--- a/solution.py
+++ b/solution.py
@@ -23,10 +23,6 @@
 GELU_C = 0.7978845608028654
 
 
-def gelu_tanh(values):
-    return jax.nn.gelu(values, approximate=True)
-
-
 class Event:
     def __init__(self, time=None, rank=0, name=''):
         self.time, self.rank, self.name = time, rank, name
@@ -43,9 +39,17 @@
             self.desc.wait()
 
 
+class Credit:
+    def __init__(self, semaphore, count, time):
+        self.semaphore, self.count, self.time, self.rank = semaphore, count, time, 0
+
+    def wait(self):
+        pl.semaphore_wait(self.semaphore, self.count)
+
+
 class Net:
-    def __init__(self, send_sems, recv_sems, local_sems):
-        self.send_sems, self.recv_sems, self.local_sems = send_sems, recv_sems, local_sems
+    def __init__(self, send_sems, recv_sems, local_sems, credit_sems):
+        self.send_sems, self.recv_sems, self.local_sems, self.credit_sems = send_sems, recv_sems, local_sems, credit_sems
         self.n_remote = self.n_local = 0
         self.now = 0.0
         self.free = {}
@@ -72,12 +76,26 @@
             return {'local': self.pos['z'] * RING + to}
         return {'local': to * RING + self.pos['y']}
 
+    def peers(self, axes):
+        return [(axis, step) for axis in axes for step in ((1, -1) if axis in 'xyz' else (1,) if axis == 'p' else range(1, 2 * RING))]
+
+    def signal(self, semaphore, axes):
+        for axis, step in self.peers(axes):
+            pl.semaphore_signal(semaphore, inc=1, device_id=self.device(axis, step), device_id_type=MESH)
+
     def barrier(self, axes):
-        peers = [(axis, step) for axis in axes for step in ((1, -1) if axis in 'xyz' else (1,) if axis == 'p' else range(1, 2 * RING))]
         semaphore = pltpu.get_barrier_semaphore()
-        for axis, step in peers:
-            pl.semaphore_signal(semaphore, inc=1, device_id=self.device(axis, step), device_id_type=MESH)
-        pl.semaphore_wait(semaphore, len(peers))
+        self.signal(semaphore, axes)
+        pl.semaphore_wait(semaphore, len(self.peers(axes)))
+
+    def grant(self, k, axes):
+        self.signal(self.credit_sems.at[k], axes)
+        return Credit(self.credit_sems.at[k], len(self.peers(axes)), self.now + HOP)
+
+    def drain(self, copies):
+        for copy in copies:
+            copy.desc.wait_send()
+            self.sent.remove(copy)
 
     def send(self, src, dst, axis, step=1):
         k = self.n_remote
@@ -134,7 +152,7 @@
             _, k, time = best
             flow, items = self.flows.pop(k)
             for item in items:
-                if isinstance(item, Copy):
+                if not isinstance(item, Event):
                     item.wait()
             self.now = max(self.now, time)
             self.step(flow)
@@ -309,6 +327,7 @@
     summed_b = net.send(acc(2, hi), last_b.at[hi], 'x', -1)
     yield [ready[3], direct_f, direct_b, summed_f, summed_b]
     add_into(net, acc(3), last_f, last_b)
+    done.copies = pairs + [first_f, first_b, direct_f, direct_b, summed_f, summed_b]
     fire(net, done)
 
 
@@ -326,59 +345,77 @@
         net.spawn(bring())
 
 
-def reduce_yz(net, part, first, sums, ahead, behind, relay1, last1, relay2, last2, start, done):
+def reduce_yz(net, part, first, scratch, start, done):
+    ahead, behind, mine, relay1, last1, relay2, last2 = scratch
     second = 'y' if first == 'z' else 'z'
-    half = sums.shape[1] // 2
-    lo, hi = pl.ds(0, half), pl.ds(half, half)
-
-    def index(one, two):
+    half = mine.shape[0] // 2
+    lo, hi, all_rows = pl.ds(0, half), pl.ds(half, half), pl.ds(0, 2 * half)
+
+    def term(one, two, rows=all_rows):
         at_one, at_two = net.at(first, one), net.at(second, two)
-        return (at_one, at_two) if first == 'z' else (at_two, at_one)
-
-    def ring(k, end):
+        return part.at[(at_one * RING + at_two if first == 'z' else at_two * RING + at_one), rows]
+
+    def bring(gate, src, dst, got):
+        yield [gate]
+        yield [net.load(src, dst)]
+        fire(net, got)
+
+    free = [[Event() for _ in range(RING + 1)] for _ in range(3)]
+    got = [[Event() for _ in range(RING)] for _ in range(3)]
+    ends = [Event() for _ in STEPS]
+
+    def ring(k):
         two = STEPS[k]
-        loads = [net.load(part.at[index(1, two) + (lo,)], ahead.at[k]),
-                 net.load(part.at[index(-1, two) + (hi,)], behind.at[k]),
-                 net.load(part.at[index(0, two)], sums.at[k])]
-        first_f = net.send(part.at[index(2, two) + (lo,)], relay1.at[0, k], first, 1)
-        first_b = net.send(part.at[index(2, two) + (hi,)], relay1.at[1, k], first, -1)
-        direct_f = net.send(part.at[index(1, two) + (hi,)], last1.at[0, k, hi], first, 1)
-        direct_b = net.send(part.at[index(-1, two) + (lo,)], last1.at[1, k, lo], first, -1)
-        yield [first_f, loads[0]]
-        add_into(net, ahead.at[k], relay1.at[0, k])
-        summed_f = net.send(ahead.at[k], last1.at[0, k, lo], first, 1)
-        yield [first_b, loads[1]]
-        add_into(net, behind.at[k], relay1.at[1, k])
-        summed_b = net.send(behind.at[k], last1.at[1, k, hi], first, -1)
-        yield [direct_f, direct_b, summed_f, summed_b, loads[2]]
-        add_into(net, sums.at[k], last1.at[0, k], last1.at[1, k])
-        fire(net, end)
+        net.spawn(bring(free[0][k], term(1, two, lo), ahead, got[0][k]))
+        net.spawn(bring(free[1][k], term(-1, two, hi), behind, got[1][k]))
+        net.spawn(bring(free[2][k], term(0, two), mine, got[2][k]))
+        first_f = net.send(term(2, two, lo), relay1.at[0, k], first, 1)
+        first_b = net.send(term(2, two, hi), relay1.at[1, k], first, -1)
+        direct_f = net.send(term(1, two, hi), last1.at[0, k, hi], first, 1)
+        direct_b = net.send(term(-1, two, lo), last1.at[1, k, lo], first, -1)
+        yield [first_f, got[0][k]]
+        add_into(net, relay1.at[0, k], ahead)
+        fire(net, free[0][k + 1])
+        summed_f = net.send(relay1.at[0, k], last1.at[0, k, lo], first, 1)
+        yield [first_b, got[1][k]]
+        add_into(net, relay1.at[1, k], behind)
+        fire(net, free[1][k + 1])
+        summed_b = net.send(relay1.at[1, k], last1.at[1, k, hi], first, -1)
+        yield [direct_f, direct_b, summed_f, summed_b, got[2][k]]
+        add_into(net, last1.at[0, k], last1.at[1, k], mine)
+        fire(net, free[2][k + 1])
+        fire(net, ends[k])
+
+    def sums(k, rows=all_rows):
+        return last1.at[0, k, rows]
 
     if start is not None:
         yield [start]
-    ends = [Event() for _ in STEPS]
+    for events in free:
+        fire(net, events[0])
     for k in range(RING):
-        net.spawn(ring(k, ends[k]))
+        net.spawn(ring(k))
     yield [ends[0]]
-    first_f = net.send(sums.at[0, lo], relay2.at[0], second, 1)
-    first_b = net.send(sums.at[0, hi], relay2.at[1], second, -1)
+    first_f = net.send(sums(0, lo), relay2.at[0], second, 1)
+    first_b = net.send(sums(0, hi), relay2.at[1], second, -1)
     yield [ends[1]]
-    direct_f = net.send(sums.at[1, hi], last2.at[0, hi], second, 1)
+    direct_f = net.send(sums(1, hi), last2.at[0, hi], second, 1)
     yield [ends[2]]
-    direct_b = net.send(sums.at[2, lo], last2.at[1, lo], second, -1)
+    direct_b = net.send(sums(2, lo), last2.at[1, lo], second, -1)
     yield [first_f]
-    add_into(net, sums.at[1, lo], relay2.at[0])
-    summed_f = net.send(sums.at[1, lo], last2.at[0, lo], second, 1)
+    add_into(net, sums(1, lo), relay2.at[0])
+    summed_f = net.send(sums(1, lo), last2.at[0, lo], second, 1)
     yield [first_b]
-    add_into(net, sums.at[2, hi], relay2.at[1])
-    summed_b = net.send(sums.at[2, hi], last2.at[1, hi], second, -1)
+    add_into(net, sums(2, hi), relay2.at[1])
+    summed_b = net.send(sums(2, hi), last2.at[1, hi], second, -1)
     yield [ends[3], direct_f, direct_b, summed_f, summed_b]
-    add_into(net, sums.at[3], last2.at[0], last2.at[1])
+    add_into(net, sums(3), last2.at[0], last2.at[1])
+    done.total = sums(3)
     fire(net, done)
 
 
 def reduce_yz_scratch(rows, cols):
-    return [pltpu.VMEM((RING, rows, cols), F32), pltpu.VMEM((RING, rows // 2, cols), F32), pltpu.VMEM((RING, rows // 2, cols), F32),
+    return [pltpu.VMEM((rows // 2, cols), F32), pltpu.VMEM((rows // 2, cols), F32), pltpu.VMEM((rows, cols), F32),
             pltpu.VMEM((2, RING, rows // 2, cols), F32), pltpu.VMEM((2, RING, rows, cols), F32),
             pltpu.VMEM((2, rows // 2, cols), F32), pltpu.VMEM((2, rows, cols), F32)]
 
@@ -396,8 +433,8 @@
         x = x_ref[at, :].astype(F32)
         du = du_ref[at, :]
         r = lax.rsqrt(jnp.mean(x * x, axis=-1, keepdims=True) + NORM_EPS)
-        dot = jnp.mean(x * du, axis=-1, keepdims=True)
-        dx_ref[at, :] = (dy_ref[at, :].astype(F32) + (r * du - x * (r * r * r * dot))).astype(BF16)
+        xr = x * r
+        dx_ref[at, :] = (dy_ref[at, :].astype(F32) + r * (du - xr * jnp.mean(xr * du, axis=-1, keepdims=True))).astype(BF16)
 
     rows_loop(x_ref.shape[0], 16, body)
 
@@ -413,9 +450,9 @@
     spaces = {'v': pl.BlockSpec(memory_space=pltpu.VMEM), 'h': pl.BlockSpec(memory_space=pl.ANY)}
 
     def kernel(*refs):
-        sems = refs[-3:]
-        net = Net(*sems)
-        body(net, *refs[:-3])
+        net = Net(*refs[-5:-1])
+        net.tile_sems = refs[-1]
+        body(net, *refs[:-5])
         net.finish()
         assert net.n_remote <= remote and net.n_local <= local, (net.n_remote, net.n_local)
         if PRINT:
@@ -423,7 +460,8 @@
 
     return pl.pallas_call(
         kernel, out_shape=out_shape, in_specs=[spaces[s] for s in in_spaces], out_specs=[spaces[s] for s in out_spaces],
-        scratch_shapes=list(scratch) + [pltpu.SemaphoreType.DMA((remote,)), pltpu.SemaphoreType.DMA((remote,)), pltpu.SemaphoreType.DMA((local,))],
+        scratch_shapes=list(scratch) + [pltpu.SemaphoreType.DMA((remote,)), pltpu.SemaphoreType.DMA((remote,)), pltpu.SemaphoreType.DMA((local,)),
+                                               pltpu.SemaphoreType.REGULAR((2,)), pltpu.SemaphoreType.DMA((2,))],
         compiler_params=pltpu.CompilerParams(collective_id=collective_id, has_side_effects=True, vmem_limit_bytes=67000000),
         cost_estimate=pl.CostEstimate(flops=10**8, bytes_accessed=10**7, transcendentals=0),
         name=body.__name__)(*args)
@@ -493,6 +531,82 @@
 
     wide_loop(down.shape[0] * rows, body)
     net.spend(2.4)
+
+
+def gelu_both(a):
+    t = jnp.tanh(GELU_C * (a + 0.044715 * a * a * a))
+    return 0.5 * a * (1.0 + t), 0.5 * (1.0 + t) + 0.5 * a * (1.0 - t * t) * (GELU_C * (1.0 + 3 * 0.044715 * a * a))
+
+
+def hidden_turn_rows(net, chip, u, up, s, ds):
+    at = pl.ds(chip * 2, 2)
+
+    def body(_, wide, cols):
+        pre = dot_rows(u[at], up[:, :, cols]).astype(BF16).astype(F32)
+        value, slope = gelu_both(pre)
+        s[at, :, cols] = value.astype(BF16).reshape(2, -1, wide)
+        ds[at, :, cols] = (ds[at, :, cols].astype(F32) * slope.reshape(2, -1, wide)).astype(BF16)
+
+    wide_loop(up.shape[2], body)
+    net.spend(2.8)
+
+
+def pre_back_rows(net, chip, dy, down, a, da):
+    at = pl.ds(chip * 2, 2)
+    rows = down.shape[1]
+
+    def body(k, wide, cols):
+        blocks = pl.ds(k * (wide // rows), wide // rows)
+        ds = dot_cols(dy[at], down[blocks]).astype(BF16).astype(F32).reshape(2, -1, wide)
+        da[at, :, cols] = (ds * gelu_both(a[at, :, cols].astype(F32))[1]).astype(BF16)
+
+    wide_loop(down.shape[0] * rows, body)
+    net.spend(2.8)
+
+
+def input_back_rows(net, chip, da, up, part):
+    at = pl.ds(chip * 2, 2)
+    rows = up.shape[1]
+
+    def body(k, wide, cols):
+        blocks = pl.ds(k * (wide // rows), wide // rows)
+        part[:, :, cols] = dot_cols(da[at], up[blocks]).reshape(2, -1, wide)
+
+    wide_loop(up.shape[0] * rows, body)
+    net.spend(2.2)
+
+
+def stored_tiles(net, count, compute, stage, out):
+    def store(t):
+        return pltpu.make_async_copy(stage.at[t % 2], out(t), net.tile_sems.at[t % 2])
+
+    def step(t, carry):
+        @pl.when(t >= 2)
+        def _():
+            store(t - 2).wait()
+
+        compute(t, stage.at[t % 2])
+        store(t).start()
+        return carry
+
+    lax.fori_loop(0, count, step, 0)
+    for t in range(max(count - 2, 0), count):
+        store(t).wait()
+
+
+def dot_tokens(a, b):
+    return lax.dot_general(flat(a), flat(b), CONTRACT_ROWS, preferred_element_type=F32)
+
+
+def grad_tiles(net, lhs, rhs, stage, out):
+    _, blocks, rows, cols = stage.shape
+    wide = blocks * rows
+
+    def compute(t, slot):
+        slot[...] = dot_tokens(lhs[:, :, pl.ds(pl.multiple_of(t * wide, wide), wide)], rhs[...]).reshape(blocks, rows, cols)
+
+    stored_tiles(net, lhs.shape[2] // wide, compute, stage, lambda t: out.at[pl.ds(t * blocks, blocks)])
+    net.spend(3.6 * lhs.shape[2] / 1024)
 
 
 def solution(mesh):
@@ -586,38 +700,107 @@
 
             for flow in (up_first(), second(), grad(), hidden_flow(), down_flow(), act(), back_flow(),
                          reduce_x(net, part, made, rx_scratch, reduced),
-                         save(got_up1, (up1, up_out)), save(got_down1, (down1, down_out)), save(got_u1, (u1, next_out)), save(got_g, (g, g_out))):
+                         save(got_up1, (up1, up_out)), save(got_down1, *[(down1.at[:, :, pl.ds(h * down_out.shape[3], down_out.shape[3])], down_out.at[h]) for h in range(2)]), save(got_u1, (u1, next_out)), save(got_g, (g, g_out))):
                 net.spawn(flow)
             net.run()
 
-        def turn(net, du_ref, dup_ref, ddown_ref, x_ref, g_ref, block_ref, w_down_ref,
-                 dy_ref, dy_full_ref, up_ref, down_ref, dw_up_ref, dw_down_ref, *scratch):
+        def turn(net, u_in, up_in, down_in, ds_in, g_in, u0_in, a0_in, s0_in, x_ref, g_own, block_in, w_down_in,
+                 dy_ref, y_out, du_out, d_up0, d_down0, d_up1, d_down1, dw_up, dw_down,
+                 u, up1, up0, down0, half_in, ds, s, stage_up, stage_down, part, *scratch):
             net.barrier('dyz')
-            r1, s1, s2 = scratch[:6], scratch[6:13], scratch[13:20]
-            reduced, gathered, summed1, summed2 = (Event() for _ in range(4))
-            made = [Event() for _ in STEPS]
-            load_parts(net, du_ref, r1[0], made)
-            net.spawn(reduce_x(net, r1[0], made, r1[1:], reduced))
-            net.spawn(gather_yz(net, block_ref.at[0], up_ref, 'y', Event()))
-            net.spawn(gather_yz(net, w_down_ref.at[0], down_ref, 'z', Event()))
-            net.spawn(reduce_yz(net, dup_ref, 'y', *s1, None, summed1))
-            net.spawn(reduce_yz(net, ddown_ref, 'z', *s2, None, summed2))
+            rx_scratch, s_up, s_down = scratch[:5], scratch[5:12], scratch[12:19]
+            names = ('inputs', 'hidden', 'du_sent', 'reduced', 'got_dy', 'got_up0', 'got_down0', 'd_down1', 'd_up1', 'y_made', 'acts', 'd_down0', 'da0', 'd_up0', 'summed_up', 'summed_down', 'all_du')
+            ev = {name: Event(name=name) for name in names}
+            made = [Event(name='made%d' % k) for k in range(RING)]
+            wide = half_in.shape[2]
+
+            def columns(h):
+                return pl.ds(h * wide, wide)
+
+            net.spawn(gather_yz(net, w_down_in.at[0], down0, 'z', ev['got_down0']))
+            net.spawn(gather_yz(net, block_in.at[0], up0, 'y', ev['got_up0']))
+            net.spawn(reduce_x(net, part, made, rx_scratch, ev['reduced']))
+            net.spawn(reduce_yz(net, d_up1, 'y', s_up, ev['d_up1'], ev['summed_up']))
+            net.spawn(reduce_yz(net, d_down1, 'z', s_down, ev['d_down1'], ev['summed_down']))
+
+            def layer1():
+                yield [net.load(ds_in, ds), net.load(up_in, up1), net.load(u_in, u)]
+                for k, step in enumerate(STEPS):
+                    hidden_turn_rows(net, net.at('x', step), u, up1, s, ds)
+                    if k == RING - 1:
+                        fire(net, ev['hidden'])
+                    yield [Event(net.now, 1)]
+                    input_back_rows(net, net.at('x', step), ds, up1, part.at[k])
+                    fire(net, made[k])
+                    yield [Event(net.now, 1)]
+                fire(net, ev['all_du'])
+
+            def grads1():
+                for h in range(2):
+                    yield [net.load(g_in.at[:, :, columns(h)], half_in), Event(0.0, 2), ev['hidden']]
+                    grad_tiles(net, s, half_in, stage_down, d_down1.at[:, :, columns(h)])
+                fire(net, ev['d_down1'])
+                yield [Event(net.now, 2)]
+                for h in range(2):
+                    grad_tiles(net, u.at[:, :, columns(h)], ds, stage_up, d_up1.at[pl.ds(h * (nl // 2), nl // 2)])
+                    yield [Event(net.now, 2)]
+                fire(net, ev['d_up1'])
+
+            def layer1_out():
+                yield [ev['all_du'], ev['d_up1']]
+                yield [net.load(down_in.at[h], up1.at[:, pl.ds(h * dr, dr)]) for h in range(2)]
+                for h in range(2):
+                    def compute(chip, slot, h=h):
+                        slot[...] = dot_rows(s[pl.ds(chip * 2, 2)], up1[:, pl.ds(h * dr, dr)]).reshape(2, rows, wide)
+
+                    stored_tiles(net, RING, compute, stage_up, lambda chip, h=h: y_out.at[pl.ds(chip * 2, 2), :, columns(h)])
+                    net.spend(3.6)
+                    yield [Event(net.now, 3)]
+                fire(net, ev['y_made'])
+                yield [net.load(a0_in, up1.at[pl.ds(0, nd)]), net.load(s0_in, up1.at[pl.ds(nd, nd)])]
+                fire(net, ev['acts'])
 
             def act():
-                yield [reduced]
-                norm_back_rows(x_ref, g_ref, r1[0].at[3, net.core], dy_ref)
+                yield [ev['d_up1']]
+                credit = net.grant(0, 'xp')
+                yield [ev['reduced'], credit]
+                norm_back_rows(x_ref, g_own, part.at[3, net.core], dy_ref)
                 net.spend(0.7)
-                yield [net.load(dy_ref, dy_full_ref.at[net.data])]
-                net.spawn(gather_x(net, dy_full_ref, gathered))
-
-            def grads():
-                yield [summed1]
-                net.spawn(exchange_back(net, s1[0].at[3], dw_up_ref, Event()))
-                yield [summed2]
-                yield [net.load(s2[0].at[3], dw_down_ref)]
-
-            net.spawn(act())
-            net.spawn(grads())
+                yield [net.load(dy_ref, u.at[net.data])]
+                net.spawn(gather_x(net, u, ev['got_dy']))
+
+            def layer0():
+                a0, s0 = up1.at[pl.ds(0, nd)], up1.at[pl.ds(nd, nd)]
+                yield [ev['got_dy'], ev['acts'], Event(0.0, 2)]
+                for h in range(2):
+                    grad_tiles(net, s0, u.at[:, :, columns(h)], stage_down, d_down0.at[:, :, columns(h)])
+                    yield [Event(net.now, 2)]
+                yield [ev['got_down0'], Event(0.0, 2)]
+                for step in STEPS:
+                    pre_back_rows(net, net.at('x', step), u, down0, a0, ds)
+                    yield [Event(net.now, 2)]
+                fire(net, ev['da0'])
+                for h in range(2):
+                    yield [net.load(u0_in.at[:, :, columns(h)], half_in), Event(0.0, 2)]
+                    grad_tiles(net, half_in, ds, stage_up, d_up0.at[pl.ds(h * (nl // 2), nl // 2)])
+                net.drain(ev['reduced'].copies)
+                copies = []
+                for k, step in enumerate(STEPS):
+                    yield [ev['got_up0'], Event(0.0, 2)]
+                    input_back_rows(net, net.at('x', step), ds, up0, part.at[k])
+                    copies.append(net.load(part.at[k], du_out.at[pl.ds(net.at('x', step) * 2, 2)]))
+                yield copies
+
+            def sums():
+                yield [ev['summed_down']]
+                yield [net.load(ev['summed_down'].total, dw_down)]
+
+            def sums_up():
+                yield [ev['summed_up']]
+                net.spawn(exchange_back(net, ev['summed_up'].total, dw_up, Event()))
+
+            for flow in (layer1(), grads1(), layer1_out(), act(), layer0(), sums(), sums_up()):
+                net.spawn(flow)
             net.run()
 
         def last(net, du_ref, part_ref, dup_ref, ddown_ref, x_ref, dy_ref, x1_ref, dx_ref, out_ref, dw_up_ref, dw_down_ref, *scratch):
@@ -627,8 +810,8 @@
             made1, made2 = [Event() for _ in STEPS], [Event() for _ in STEPS]
             load_parts(net, du_ref, r1[0], made1)
             net.spawn(reduce_x(net, r1[0], made1, r1[1:], reduced))
-            net.spawn(reduce_yz(net, dup_ref, 'y', *s1, None, summed1))
-            net.spawn(reduce_yz(net, ddown_ref, 'z', *s2, None, summed2))
+            net.spawn(reduce_yz(net, dup_ref, 'y', s1, None, summed1))
+            net.spawn(reduce_yz(net, ddown_ref, 'z', s2, None, summed2))
 
             def act():
                 yield [reduced]
@@ -644,68 +827,33 @@
 
             def grads():
                 yield [summed1]
-                net.spawn(exchange_back(net, s1[0].at[3], dw_up_ref, Event()))
+                net.spawn(exchange_back(net, summed1.total, dw_up_ref, Event()))
                 yield [summed2]
-                yield [net.load(s2[0].at[3], dw_down_ref)]
+                yield [net.load(summed2.total, dw_down_ref)]
 
             net.spawn(act())
             net.spawn(forward_out())
             net.spawn(grads())
             net.run()
 
-        def flat_act(full):
-            return full.reshape(nd * rows, width)
-
-        def flat_up(full):
-            return full.reshape(nl * nd * ur, hidden)
-
-        def flat_down(full):
-            return full.reshape(hidden, width)
-
-        def dot(a, b):
-            return jnp.dot(a, b, preferred_element_type=F32)
-
-        def hidden_of(u_full, up):
-            a = dot(u_full, up).astype(BF16)
-            return a, gelu_tanh(a.astype(F32)).astype(BF16)
-
-        def pre_back(a, ds):
-            _, back = jax.vjp(gelu_tanh, a.astype(F32))
-            return back(ds.astype(F32))[0].astype(BF16)
-
-        def split_part(part):
-            return part.reshape(nd, rows, width)
-
-        def grads_of(u_full, s, da, dy_full):
-            d_up = lax.dot_general(u_full, da, CONTRACT_ROWS, preferred_element_type=F32)
-            d_down = lax.dot_general(s, dy_full, CONTRACT_ROWS, preferred_element_type=F32)
-            return d_up.reshape(RING, RING, nd * ur, hidden), d_down.reshape(RING, RING, dr, width)
-
         def own_up(d_up):
             return d_up.reshape(nd, ur, nl, dr).transpose(1, 2, 0, 3).reshape(ur, ffn)
 
         d_up_own, d_down_own = shape((nd, ur, hidden), F32), shape((dr, width), F32)
 
         blocks, u0, a0, s0, up1, down1, u1, g_full, ds1, x1 = call(
-            forward, [shape((num_layers, nd * ur, hidden), BF16), act_full, hid_full, hid_full, up_full, down_full, act_full, act_full, hid_full, own],
+            forward, [shape((num_layers, nd * ur, hidden), BF16), act_full, hid_full, hid_full, up_full, shape((2, nl, dr, width // 2), BF16),
+                      act_full, act_full, hid_full, own],
             'hhhhhhhhhv', 'vhhh',
             [vmem(act_full)] * 3 + [vmem(up_full), vmem(down_full)] * 2 + [vmem(hid_full)] * 3 + rx, 128, 32, 0,
             tokens, grad_out, cols, w_down)
-        u0, u1, g_full = flat_act(u0), flat_act(u1), flat_act(g_full)
-        a0, s0, ds1 = (t.reshape(nd * rows, hidden) for t in (a0, s0, ds1))
-        up1, down1 = flat_up(up1), flat_down(down1)
-        a1, s1 = hidden_of(u1, up1)
-        da1 = pre_back(a1, ds1)
-        du1 = split_part(lax.dot_general(da1, up1, CONTRACT_COLS, preferred_element_type=F32))
-        part1 = split_part(dot(s1, down1))
-        d_up1, d_down1 = grads_of(u1, s1, da1, g_full)
-        dy0, dy_full, up0, down0, dw_up1, dw_down1 = call(
-            turn, [own, act_full, up_full, down_full, d_up_own, d_down_own], 'vvvvhh', 'hhhvvhh', rx + ryz_up + ryz_down, 144, 48, 1,
-            du1, d_up1, d_down1, x1, grad_out, blocks, w_down)
-        dy_full, up0, down0 = flat_act(dy_full), flat_up(up0), flat_down(down0)
-        da0 = pre_back(a0, lax.dot_general(dy_full, down0, CONTRACT_COLS, preferred_element_type=F32).astype(BF16))
-        du0 = split_part(lax.dot_general(da0, up0, CONTRACT_COLS, preferred_element_type=F32))
-        d_up0, d_down0 = grads_of(u0, s0, da0, dy_full)
+        part_full = shape((nd, rows, width), F32)
+        d_up_full, d_down_full = shape((nl, nd * ur, hidden), F32), shape((nl, dr, width), F32)
+        dy0, part1, du0, d_up0, d_down0, _, _, dw_up1, dw_down1 = call(
+            turn, [own, part_full, part_full, d_up_full, d_down_full, d_up_full, d_down_full, d_up_own, d_down_own], 'vhhhhhhhh', 'hhhhhhhhvvhh',
+            [vmem(act_full), vmem(up_full), vmem(up_full), vmem(down_full), pltpu.VMEM((nd, rows, width // 2), BF16), vmem(hid_full), vmem(hid_full),
+             pltpu.VMEM((2, 2, nd * ur, hidden), F32), pltpu.VMEM((2, nl // RING, dr, width // 2), F32)] + rx + ryz_up + ryz_down, 144, 64, 1,
+            u1, up1, down1, ds1, g_full, u0, a0, s0, x1, grad_out, blocks, w_down)
         dx, x_out, dw_up0, dw_down0 = call(
             last, [own, own, d_up_own, d_down_own], 'vvhh', 'hhhhvvv', rx + rx + ryz_up + ryz_down, 96, 56, 2,
             du0, part1, d_up0, d_down0, tokens, dy0, x1)

time: 558 us -> 391 us (0.70); the launches traced: 550 us -> 391 us
  matrix products: 93.6 us -> 0 us
  local copies, waits for them, and re-layouts: 52.6 us -> 11 us
  other arithmetic: 16 us -> 3.37 us
  Pallas kernels: 387 us -> 376 us
    dot_general x9 -> x0, matrix products: 93.6 us -> none  [the longest x2 21.7 us: dot(): return jnp.dot(a, b, preferred_element_type=F32)]
    dot_general x6 -> x0, local copies, waits for them, and re-layouts: 23.3 us -> none  [the longest x2 12.8 us: grads_of(): lax.dot_general(u_full, da, CONTRACT_ROWS, preferred_element_type=F32)]
    convert_element_type x4 -> x0, local copies, waits for them, and re-layouts: 19.2 us -> none  [the longest x2 11 us: pre_back(): _, back = jax.vjp(gelu_tanh, a.astype(F32))]
    convert_element_type x2 -> x0, other arithmetic: 12.7 us -> none  [the longest x1 6.47 us: pre_back(): _, back = jax.vjp(gelu_tanh, a.astype(F32))]
    pallas_call x3, Pallas kernels: 387 us -> 376 us  [call(): pl.pallas_call(kernel, out_shape=out_shape, in_specs=[spaces[s] for s in...]
where the time goes in v4:
time: 391 us
  Pallas kernels  376 us (96%)
  local copies, waits for them, and re-layouts  11 us (3%)
    pallas_call x3, Pallas kernels, call(): pl.pallas_call(kernel, out_shape=out_shape, in_specs=[spaces[s] for s in...  376 us

profile of v4, /device:TPU:1, one launch (start us, length us, event | category | flops | bytes accessed | tf_op | source)
XLA Modules:
  0.0 390.8 jit_solution(16977844682894441507)
XLA Ops:
  0.6 2.1 reshape.20
  2.7 0.2 copy.12
  2.9 1.5 reshape.21.refs_2_
  4.4 129.1 %forward.1 = (bf16[2,128,1024]{2,1,0:T(8,128)(2,1)}, bf16[8,128,2048]{2,1,0:T(8,128)(2,1)}, bf16[8,128,1024]{2,1,0:T(8,128)(2,1)}, bf16[8,128,1024]{2,1,0:T(8,12...) custom-call(bf16[128,2048]{1,0:T(8,128)(2,1)} %refs_4_.1, ...), custom_call_target="tpu_custom_call" | custom-call | flops 100000000 | bytes 10000000 | tf_op jit(solution)/shard_map/forward/pallas_call | solution.py:461
  133.5 144.6 %turn.1 = (bf16[128,2048]{1,0:T(8,128)(2,1)}, f32[8,128,2048]{2,1,0:T(8,128)}, f32[8,128,2048]{2,1,0:T(8,128)}, f32[16,128,1024]{2,1,0:T(8,128)}, f32[16,64,2048...) custom-call(bf16[8,128,2048]{2,1,0:T(8,128)(2,1)} %get-tuple-element, ...), custom_call_target="tpu_custom_call" | custom-call | flops 100000000 | bytes 10000000 | tf_op jit(solution)/shard_map/turn/pallas_call | solution.py:461
  278.0 102.1 %last.1 = (bf16[128,2048]{1,0:T(8,128)(2,1)}, bf16[128,2048]{1,0:T(8,128)(2,1)}, f32[8,16,1024]{2,1,0:T(8,128)}, f32[64,2048]{1,0:T(8,128)}) custom-call(f32[8,128,2048]{2,1,0:T(8,128)} %get-tuple-element.35.refs_0_, f32[8,128,2048]{2,1,0:T(8,128)} %get-tuple-element.36.refs_1_, f32[16,128,1024]{2,1,0:T(8,128)} %get-tuple-element.37.refs_2_, ...), custom_call_target="tpu_custom_call" | custom-call | flops 100000000 | bytes 10000000 | tf_op jit(solution)/shard_map/last/pallas_call | solution.py:461
  380.1 0.0 copy-start
  380.1 2.3 pad_maximum_fusion.1
  382.5 1.3 reshape.22
  383.8 0.6 copy.9
  384.4 0.4 stack_reshape.6
  384.8 0.0 copy-done
  384.8 0.3 reshape.23
  385.1 0.6 copy.10
  385.7 0.4 stack_reshape.7
  386.0 1.0 pad_maximum_fusion
  387.1 1.9 copy.15
  389.0 1.9 copy.16
Async XLA Ops:
  380.1 4.6 %copy-start = (f32[8,16,1024]{2,1,0:T(8,128)S(1)}, f32[8,16,1024]{2,1,0:T(8,128)}, u32[]{:S(2)}) copy-start(f32[8,16,1024]{2,1,0:T(8,128)} %get-tuple-element.43) | copy-start | bytes 1572868

commit v5 on v4

--- a/solution.py
+++ b/solution.py
@@ -15,10 +15,10 @@
 RING = 4
 F32, BF16 = jnp.float32, jnp.bfloat16
 
-LINK_RATE = 46.6e3
+LINK_RATE = 43.0e3
 PAIR_RATE = 600e3
 LOCAL_RATE = 3000e3
-HOP = 2.2
+HOP = 2.5
 SLACK = 1.0
 GELU_C = 0.7978845608028654
 
@@ -210,8 +210,8 @@
         return src.at[pl.ds(pl.multiple_of(k * rows, rows), rows)]
 
     own = net.load(block(net.data), dst.at[net.data])
-    copies = [net.send(block((net.data + k) % (2 * RING)), dst.at[net.data], 'd', k) for k in range(1, 2 * RING)]
-    yield [own] + copies
+    done.copies = [net.send(block((net.data + k) % (2 * RING)), dst.at[net.data], 'd', k) for k in range(1, 2 * RING)]
+    yield [own] + done.copies
     fire(net, done)
 
 
@@ -242,24 +242,24 @@
     fire(net, done)
 
 
-def gather_yz(net, own, full, first, done, issued=None):
+def gather_yz(net, own, full, first, done, issued=None, offset=0, near=False):
     second = 'y' if first == 'z' else 'z'
     size = own.shape[0]
     half = size // 2
-    all_rows, lo, hi = pl.ds(0, size), pl.ds(0, half), pl.ds(half, half)
+    all_rows, lo, hi = pl.ds(offset, size), pl.ds(offset, half), pl.ds(offset + half, half)
 
     def part(one, two, rows):
-        at_one, at_two = net.at(first, one), net.at(second, two)
-        return full.at[(at_one * RING + at_two if first == 'z' else at_two * RING + at_one), rows]
+        return full.at[yz_index(net, first, one, two), rows]
 
     ends = []
-    left = [RING]
+    left = [3 if near else RING]
 
     def relay(one, forth, back, end):
-        yield [forth]
-        forth = net.send(part(one, -1, lo), part(one, -1, lo), second, 1)
-        yield [back]
-        back = net.send(part(one, 1, hi), part(one, 1, hi), second, -1)
+        if not near:
+            yield [forth]
+            forth = net.send(part(one, -1, lo), part(one, -1, lo), second, 1)
+            yield [back]
+            back = net.send(part(one, 1, hi), part(one, 1, hi), second, -1)
         left[0] -= 1
         if left[0] == 0 and issued is not None:
             fire(net, issued)
@@ -278,15 +278,26 @@
     back = net.send(own, part(0, 0, all_rows), first, -1)
     spread(own, 0)
     yield [forth]
-    forth = net.send(part(-1, 0, lo), part(-1, 0, lo), first, 1)
+    if not near:
+        forth = net.send(part(-1, 0, lo), part(-1, 0, lo), first, 1)
     spread(part(-1, 0, all_rows), -1)
     yield [back]
-    back = net.send(part(1, 0, hi), part(1, 0, hi), first, -1)
+    if not near:
+        back = net.send(part(1, 0, hi), part(1, 0, hi), first, -1)
     spread(part(1, 0, all_rows), 1)
-    yield [forth, back]
-    spread(part(2, 0, all_rows), 2)
+    if not near:
+        yield [forth, back]
+        spread(part(2, 0, all_rows), 2)
     yield [mine] + ends
     fire(net, done)
+
+
+def yz_index(net, first, one, two):
+    at_one, at_two = net.at(first, one), net.at('y' if first == 'z' else 'z', two)
+    return at_one * RING + at_two if first == 'z' else at_two * RING + at_one
+
+
+FAR = [(2, 0), (2, 1), (2, -1), (2, 2), (0, 2), (1, 2), (-1, 2)]
 
 
 STEPS = (2, 1, -1, 0)
@@ -345,73 +356,105 @@
         net.spawn(bring())
 
 
-def reduce_yz(net, part, first, scratch, start, done):
-    ahead, behind, mine, relay1, last1, relay2, last2 = scratch
-    second = 'y' if first == 'z' else 'z'
-    half = mine.shape[0] // 2
-    lo, hi, all_rows = pl.ds(0, half), pl.ds(half, half), pl.ds(0, 2 * half)
-
-    def term(one, two, rows=all_rows):
-        at_one, at_two = net.at(first, one), net.at(second, two)
-        return part.at[(at_one * RING + at_two if first == 'z' else at_two * RING + at_one), rows]
-
-    def bring(gate, src, dst, got):
-        yield [gate]
-        yield [net.load(src, dst)]
-        fire(net, got)
-
-    free = [[Event() for _ in range(RING + 1)] for _ in range(3)]
-    got = [[Event() for _ in range(RING)] for _ in range(3)]
-    ends = [Event() for _ in STEPS]
-
-    def ring(k):
-        two = STEPS[k]
-        net.spawn(bring(free[0][k], term(1, two, lo), ahead, got[0][k]))
-        net.spawn(bring(free[1][k], term(-1, two, hi), behind, got[1][k]))
-        net.spawn(bring(free[2][k], term(0, two), mine, got[2][k]))
-        first_f = net.send(term(2, two, lo), relay1.at[0, k], first, 1)
-        first_b = net.send(term(2, two, hi), relay1.at[1, k], first, -1)
-        direct_f = net.send(term(1, two, hi), last1.at[0, k, hi], first, 1)
-        direct_b = net.send(term(-1, two, lo), last1.at[1, k, lo], first, -1)
-        yield [first_f, got[0][k]]
-        add_into(net, relay1.at[0, k], ahead)
-        fire(net, free[0][k + 1])
-        summed_f = net.send(relay1.at[0, k], last1.at[0, k, lo], first, 1)
-        yield [first_b, got[1][k]]
-        add_into(net, relay1.at[1, k], behind)
-        fire(net, free[1][k + 1])
-        summed_b = net.send(relay1.at[1, k], last1.at[1, k, hi], first, -1)
-        yield [direct_f, direct_b, summed_f, summed_b, got[2][k]]
-        add_into(net, last1.at[0, k], last1.at[1, k], mine)
-        fire(net, free[2][k + 1])
-        fire(net, ends[k])
-
-    def sums(k, rows=all_rows):
-        return last1.at[0, k, rows]
-
-    if start is not None:
-        yield [start]
-    for events in free:
-        fire(net, events[0])
-    for k in range(RING):
-        net.spawn(ring(k))
-    yield [ends[0]]
-    first_f = net.send(sums(0, lo), relay2.at[0], second, 1)
-    first_b = net.send(sums(0, hi), relay2.at[1], second, -1)
-    yield [ends[1]]
-    direct_f = net.send(sums(1, hi), last2.at[0, hi], second, 1)
-    yield [ends[2]]
-    direct_b = net.send(sums(2, lo), last2.at[1, lo], second, -1)
-    yield [first_f]
-    add_into(net, sums(1, lo), relay2.at[0])
-    summed_f = net.send(sums(1, lo), last2.at[0, lo], second, 1)
-    yield [first_b]
-    add_into(net, sums(2, hi), relay2.at[1])
-    summed_b = net.send(sums(2, hi), last2.at[1, hi], second, -1)
-    yield [ends[3], direct_f, direct_b, summed_f, summed_b]
-    add_into(net, sums(3), last2.at[0], last2.at[1])
-    done.total = sums(3)
-    fire(net, done)
+class Sums:
+    def __init__(self, net, first, scratch):
+        self.net, self.first, self.scratch = net, first, scratch
+        self.second = 'y' if first == 'z' else 'z'
+        self.free = [Event(0.0) for _ in range(3)]
+        self.relays_free, self.all_free = Event(0.0), Event(0.0)
+        self.phase1 = []
+        self.phase2 = []
+
+    def release(self, credit, axes, copies, event):
+        self.net.drain(copies)
+        yield [self.net.grant(credit, axes)]
+        fire(self.net, event)
+
+    def run(self, part, start, done, credit=None):
+        net, first, second = self.net, self.first, self.second
+        ahead, behind, mine, relay1, last1, relay2, last2 = self.scratch
+        relays_free, all_free = self.relays_free, self.all_free
+        half = mine.shape[0] // 2
+        lo, hi, all_rows = pl.ds(0, half), pl.ds(half, half), pl.ds(0, 2 * half)
+
+        def term(one, two, rows=all_rows):
+            return part.at[yz_index(net, first, one, two), rows]
+
+        def bring(gate, src, dst, got):
+            yield [gate, start]
+            yield [net.load(src, dst)]
+            fire(net, got)
+
+        free = [[gate] + [Event() for _ in range(RING)] for gate in self.free]
+        self.free = [events[RING] for events in free]
+        got = [[Event() for _ in range(RING)] for _ in range(3)]
+        ends = [Event() for _ in STEPS]
+        relay_copies = []
+
+        def ring(k):
+            two = STEPS[k]
+            net.spawn(bring(free[0][k], term(1, two, lo), ahead, got[0][k]))
+            net.spawn(bring(free[1][k], term(-1, two, hi), behind, got[1][k]))
+            net.spawn(bring(free[2][k], term(0, two), mine, got[2][k]))
+            first_f = net.send(term(2, two, lo), relay1.at[0, k], first, 1)
+            first_b = net.send(term(2, two, hi), relay1.at[1, k], first, -1)
+            direct, sent = [], Event()
+
+            def directs():
+                yield [all_free]
+                direct.append(net.send(term(1, two, hi), last1.at[0, k, hi], first, 1))
+                direct.append(net.send(term(-1, two, lo), last1.at[1, k, lo], first, -1))
+                fire(net, sent)
+
+            net.spawn(directs())
+            yield [first_f, got[0][k]]
+            add_into(net, relay1.at[0, k], ahead)
+            fire(net, free[0][k + 1])
+            yield [all_free]
+            summed_f = net.send(relay1.at[0, k], last1.at[0, k, lo], first, 1)
+            yield [first_b, got[1][k]]
+            add_into(net, relay1.at[1, k], behind)
+            fire(net, free[1][k + 1])
+            summed_b = net.send(relay1.at[1, k], last1.at[1, k, hi], first, -1)
+            relay_copies.extend([summed_f, summed_b])
+            yield [sent]
+            yield direct + [summed_f, summed_b, got[2][k]]
+            add_into(net, last1.at[0, k], last1.at[1, k], mine)
+            fire(net, free[2][k + 1])
+            fire(net, ends[k])
+
+        def sums(k, rows=all_rows):
+            return last1.at[0, k, rows]
+
+        yield [start, relays_free]
+        for k in range(RING):
+            net.spawn(ring(k))
+        if credit is not None:
+            self.relays_free = Event()
+
+            def relays():
+                yield ends
+                yield from self.release(credit, first, relay_copies, self.relays_free)
+
+            net.spawn(relays())
+        yield [ends[0]]
+        first_f = net.send(sums(0, lo), relay2.at[0], second, 1)
+        first_b = net.send(sums(0, hi), relay2.at[1], second, -1)
+        yield [ends[1]]
+        direct_f = net.send(sums(1, hi), last2.at[0, hi], second, 1)
+        yield [ends[2]]
+        direct_b = net.send(sums(2, lo), last2.at[1, lo], second, -1)
+        yield [first_f]
+        add_into(net, sums(1, lo), relay2.at[0])
+        summed_f = net.send(sums(1, lo), last2.at[0, lo], second, 1)
+        yield [first_b]
+        add_into(net, sums(2, hi), relay2.at[1])
+        summed_b = net.send(sums(2, hi), last2.at[1, hi], second, -1)
+        yield [ends[3], direct_f, direct_b, summed_f, summed_b]
+        add_into(net, sums(3), last2.at[0], last2.at[1])
+        done.total = sums(3)
+        done.copies = [first_f, first_b, direct_f, direct_b, summed_f, summed_b]
+        fire(net, done)
 
 
 def reduce_yz_scratch(rows, cols):
@@ -444,6 +487,32 @@
         out_ref[at, :] = (x_ref[at, :].astype(F32) + y_ref[at, :]).astype(BF16)
 
     rows_loop(x_ref.shape[0], 16, body)
+
+
+def swap_halves(even, odd):
+    low = lax.broadcasted_iota(jnp.int32, even.shape, len(even.shape) - 1) < even.shape[-1] // 2
+    shift = even.shape[-1] // 2
+    axis = len(even.shape) - 1
+    return jnp.where(low, even, pltpu.roll(odd, shift, axis)), jnp.where(low, pltpu.roll(even, shift, axis), odd)
+
+
+def split_columns(w_ref, cols_ref):
+    tile = w_ref.shape[2] // (4 * RING * RING)
+    for l in range(w_ref.shape[0]):
+        for x in range(RING):
+            for p in range(cols_ref.shape[3] // tile):
+                pair = [w_ref[l, :, pl.ds((i * RING + x) * tile, tile)].astype(F32) for i in (2 * p, 2 * p + 1)]
+                for c, value in enumerate(swap_halves(*pair)):
+                    cols_ref[l, 2 * x + c, :, pl.ds(p * tile, tile)] = value.astype(cols_ref.dtype)
+
+
+def join_columns(cols_ref, w_ref):
+    tile = w_ref.shape[1] // (4 * RING * RING)
+    for x in range(RING):
+        for p in range(cols_ref.shape[2] // tile):
+            pair = [cols_ref[2 * x + c, :, pl.ds(p * tile, tile)] for c in range(2)]
+            for i, value in zip((2 * p, 2 * p + 1), swap_halves(*pair)):
+                w_ref[:, pl.ds((i * RING + x) * tile, tile)] = value
 
 
 def call(body, out_shape, out_spaces, in_spaces, scratch, remote, local, collective_id, *args):
@@ -461,7 +530,7 @@
     return pl.pallas_call(
         kernel, out_shape=out_shape, in_specs=[spaces[s] for s in in_spaces], out_specs=[spaces[s] for s in out_spaces],
         scratch_shapes=list(scratch) + [pltpu.SemaphoreType.DMA((remote,)), pltpu.SemaphoreType.DMA((remote,)), pltpu.SemaphoreType.DMA((local,)),
-                                               pltpu.SemaphoreType.REGULAR((2,)), pltpu.SemaphoreType.DMA((2,))],
+                                               pltpu.SemaphoreType.REGULAR((8,)), pltpu.SemaphoreType.DMA((2,))],
         compiler_params=pltpu.CompilerParams(collective_id=collective_id, has_side_effects=True, vmem_limit_bytes=67000000),
         cost_estimate=pl.CostEstimate(flops=10**8, bytes_accessed=10**7, transcendentals=0),
         name=body.__name__)(*args)
@@ -508,7 +577,7 @@
         s[at, :, cols] = gelu(pre.astype(F32)).astype(BF16).reshape(2, -1, wide)
 
     wide_loop(up.shape[2], body)
-    net.spend(2.4)
+    net.spend(1.4)
 
 
 def down_rows(net, chip, s, down, part):
@@ -518,7 +587,7 @@
         part[:, :, cols] = dot_rows(s[at], down[:, :, cols]).reshape(2, -1, wide)
 
     wide_loop(down.shape[2], body)
-    net.spend(1.8)
+    net.spend(1.5)
 
 
 def hidden_back_rows(net, chip, dy, down, ds):
@@ -530,7 +599,7 @@
         ds[at, :, cols] = dot_cols(dy[at], down[blocks]).astype(BF16).reshape(2, -1, wide)
 
     wide_loop(down.shape[0] * rows, body)
-    net.spend(2.4)
+    net.spend(1.4)
 
 
 def gelu_both(a):
@@ -548,7 +617,7 @@
         ds[at, :, cols] = (ds[at, :, cols].astype(F32) * slope.reshape(2, -1, wide)).astype(BF16)
 
     wide_loop(up.shape[2], body)
-    net.spend(2.8)
+    net.spend(1.8)
 
 
 def pre_back_rows(net, chip, dy, down, a, da):
@@ -561,7 +630,7 @@
         da[at, :, cols] = (ds * gelu_both(a[at, :, cols].astype(F32))[1]).astype(BF16)
 
     wide_loop(down.shape[0] * rows, body)
-    net.spend(2.8)
+    net.spend(1.9)
 
 
 def input_back_rows(net, chip, da, up, part):
@@ -573,7 +642,7 @@
         part[:, :, cols] = dot_cols(da[at], up[blocks]).reshape(2, -1, wide)
 
     wide_loop(up.shape[0] * rows, body)
-    net.spend(2.2)
+    net.spend(1.6)
 
 
 def stored_tiles(net, count, compute, stage, out):
@@ -606,7 +675,7 @@
         slot[...] = dot_tokens(lhs[:, :, pl.ds(pl.multiple_of(t * wide, wide), wide)], rhs[...]).reshape(blocks, rows, cols)
 
     stored_tiles(net, lhs.shape[2] // wide, compute, stage, lambda t: out.at[pl.ds(t * blocks, blocks)])
-    net.spend(3.6 * lhs.shape[2] / 1024)
+    net.spend(3.2 * lhs.shape[2] / 1024)
 
 
 def solution(mesh):
@@ -620,7 +689,6 @@
         rows, width = tokens.shape
         hidden = nl * dr
         shape = jax.ShapeDtypeStruct
-        cols = w_up.reshape(num_layers, ur, nl, nd, dr).transpose(0, 3, 1, 2, 4).reshape(num_layers, nd, ur, hidden)
         up_full = shape((nl, nd * ur, hidden), BF16)
         down_full = shape((nl, dr, width), BF16)
         act_full = shape((nd, rows, width), BF16)
@@ -634,8 +702,8 @@
         def vmem(like):
             return pltpu.VMEM(like.shape, like.dtype)
 
-        def forward(net, x_ref, g_in, cols_in, down_in, block_out, u_out, a_out, s_out, up_out, down_out, next_out, g_out, ds_out, x_out,
-                    u, g, u1, up0, down0, up1, down1, a, s, ds, part, *rx_scratch):
+        def forward(net, x_ref, g_in, w_up_ref, down_in, block_out, u_out, a_out, s_out, up_out, down_out, next_out, g_out, ds_out, keep_out, x_out,
+                    cols, u, g, u1, up0, down0, up1, down1, a, s, ds, part, *rx_scratch):
             net.barrier('dyz')
             blocks, got_u, got_g, got_u1, got_up0, got_down0, got_up1, got_down1, reduced = (Event() for _ in range(9))
             made = [Event() for _ in STEPS]
@@ -647,7 +715,8 @@
                 event.name = name
             for k in range(RING):
                 made[k].name, hidden_made[k].name = 'made%d' % k, 'hidden%d' % k
-            net.spawn(exchange(net, cols_in, block_out, blocks))
+            split_columns(w_up_ref, cols)
+            net.spawn(exchange(net, cols, block_out, blocks))
             norm_rows(x_ref, u.at[net.data])
             net.spend(0.5)
             sent_u, sent_up0, sent_down0 = Event(name='sent_u'), Event(name='sent_up0'), Event(name='sent_down0')
@@ -684,6 +753,7 @@
                     yield [hidden_made[k], got_down0, Event(0.0, 1)]
                     down_rows(net, net.at('x', step), s, down0, part.at[k])
                     fire(net, made[k])
+                yield [net.load(down0.at[yz_index(net, 'z', *far)], keep_out.at[k]) for k, far in enumerate(FAR)]
 
             def act():
                 yield [reduced]
@@ -704,24 +774,28 @@
                 net.spawn(flow)
             net.run()
 
-        def turn(net, u_in, up_in, down_in, ds_in, g_in, u0_in, a0_in, s0_in, x_ref, g_own, block_in, w_down_in,
-                 dy_ref, y_out, du_out, d_up0, d_down0, d_up1, d_down1, dw_up, dw_down,
-                 u, up1, up0, down0, half_in, ds, s, stage_up, stage_down, part, *scratch):
+        def turn(net, u_in, up_in, down_in, ds_in, g_in, u0_in, a0_in, s0_in, keep_in, x_ref, x0_ref, g_own, block_in, w_down_in,
+                 x_out, dx_out, d_up0, d_down0, d_up1, d_down1, dw_up1, dw_down1, dw_up0, dw_down0,
+                 dy, u, up1, up0, down0, half_in, ds, s, stage_up, stage_down, part, *scratch):
             net.barrier('dyz')
-            rx_scratch, s_up, s_down = scratch[:5], scratch[5:12], scratch[12:19]
-            names = ('inputs', 'hidden', 'du_sent', 'reduced', 'got_dy', 'got_up0', 'got_down0', 'd_down1', 'd_up1', 'y_made', 'acts', 'd_down0', 'da0', 'd_up0', 'summed_up', 'summed_down', 'all_du')
+            rx_scratch = scratch[:5]
+            sums_up, sums_down = Sums(net, 'y', scratch[5:12]), Sums(net, 'z', scratch[12:19])
+            names = ('hidden', 'all_du', 'reduced', 'sent_dy', 'got_dy', 'got_up0', 'got_up0_rest', 'got_down0', 'd_down1', 'd_up1', 'y_reduced', 'acts',
+                     'd_down0', 'd_up0', 'du_reduced', 'sum_up1', 'sum_down1', 'sum_up0', 'sum_down0', 'out_up1', 'out_up0')
             ev = {name: Event(name=name) for name in names}
-            made = [Event(name='made%d' % k) for k in range(RING)]
+            made, y_made, du_made = ([Event(name='%s%d' % (name, k)) for k in range(RING)] for name in ('made', 'y_made', 'du_made'))
             wide = half_in.shape[2]
+            top = nd * ur * 3 // 4
 
             def columns(h):
                 return pl.ds(h * wide, wide)
 
-            net.spawn(gather_yz(net, w_down_in.at[0], down0, 'z', ev['got_down0']))
-            net.spawn(gather_yz(net, block_in.at[0], up0, 'y', ev['got_up0']))
+            net.spawn(gather_yz(net, w_down_in.at[0], down0, 'z', ev['got_down0'], near=True))
+            net.spawn(gather_yz(net, block_in.at[0, pl.ds(0, top)], up0, 'y', ev['got_up0']))
+            net.spawn(gather_yz(net, block_in.at[0, pl.ds(top, nd * ur - top)], up0, 'z', ev['got_up0_rest'], offset=top))
             net.spawn(reduce_x(net, part, made, rx_scratch, ev['reduced']))
-            net.spawn(reduce_yz(net, d_up1, 'y', s_up, ev['d_up1'], ev['summed_up']))
-            net.spawn(reduce_yz(net, d_down1, 'z', s_down, ev['d_down1'], ev['summed_down']))
+            net.spawn(sums_up.run(d_up1, ev['d_up1'], ev['sum_up1'], 3))
+            net.spawn(sums_down.run(d_down1, ev['d_down1'], ev['sum_down1'], 4))
 
             def layer1():
                 yield [net.load(ds_in, ds), net.load(up_in, up1), net.load(u_in, u)]
@@ -746,28 +820,33 @@
                     yield [Event(net.now, 2)]
                 fire(net, ev['d_up1'])
 
-            def layer1_out():
-                yield [ev['all_du'], ev['d_up1']]
-                yield [net.load(down_in.at[h], up1.at[:, pl.ds(h * dr, dr)]) for h in range(2)]
-                for h in range(2):
-                    def compute(chip, slot, h=h):
-                        slot[...] = dot_rows(s[pl.ds(chip * 2, 2)], up1[:, pl.ds(h * dr, dr)]).reshape(2, rows, wide)
-
-                    stored_tiles(net, RING, compute, stage_up, lambda chip, h=h: y_out.at[pl.ds(chip * 2, 2), :, columns(h)])
-                    net.spend(3.6)
-                    yield [Event(net.now, 3)]
-                fire(net, ev['y_made'])
-                yield [net.load(a0_in, up1.at[pl.ds(0, nd)]), net.load(s0_in, up1.at[pl.ds(nd, nd)])]
-                fire(net, ev['acts'])
-
             def act():
                 yield [ev['d_up1']]
                 credit = net.grant(0, 'xp')
                 yield [ev['reduced'], credit]
-                norm_back_rows(x_ref, g_own, part.at[3, net.core], dy_ref)
+                norm_back_rows(x_ref, g_own, part.at[3, net.core], dy)
                 net.spend(0.7)
-                yield [net.load(dy_ref, u.at[net.data])]
-                net.spawn(gather_x(net, u, ev['got_dy']))
+                yield [net.load(dy, u.at[net.data])]
+                net.spawn(gather_x(net, u, ev['got_dy'], ev['sent_dy']))
+
+            def layer1_out():
+                yield [ev['all_du'], ev['d_up1']]
+                yield [net.load(down_in.at[h], up1.at[:, pl.ds(h * dr, dr)]) for h in range(2)]
+                yield [ev['reduced'], ev['sent_dy']]
+                net.drain(ev['reduced'].copies)
+                yield [net.grant(1, 'xp')]
+                net.spawn(reduce_x(net, part, y_made, rx_scratch, ev['y_reduced']))
+                for k, step in enumerate(STEPS):
+                    chip = net.at('x', step)
+                    for h in range(2):
+                        net.spend(-0.7)
+                        down_rows(net, chip, s, up1.at[:, pl.ds(h * dr, dr)], part.at[k, :, :, columns(h)])
+                    fire(net, y_made[k])
+                    yield [Event(net.now, 2)]
+                yield [net.load(a0_in, up1.at[pl.ds(0, nd)]), net.load(s0_in, up1.at[pl.ds(nd, nd)])]
+                fire(net, ev['acts'])
+                yield [ev['y_reduced']]
+                add_rows(x_ref, part.at[3, net.core], x_out)
 
             def layer0():
                 a0, s0 = up1.at[pl.ds(0, nd)], up1.at[pl.ds(nd, nd)]
@@ -775,88 +854,78 @@
                 for h in range(2):
                     grad_tiles(net, s0, u.at[:, :, columns(h)], stage_down, d_down0.at[:, :, columns(h)])
                     yield [Event(net.now, 2)]
-                yield [ev['got_down0'], Event(0.0, 2)]
+                fire(net, ev['d_down0'])
+                yield [ev['got_down0'], Event(0.0, 2)] + [net.load(keep_in.at[k], down0.at[yz_index(net, 'z', *far)]) for k, far in enumerate(FAR)]
                 for step in STEPS:
                     pre_back_rows(net, net.at('x', step), u, down0, a0, ds)
                     yield [Event(net.now, 2)]
-                fire(net, ev['da0'])
                 for h in range(2):
                     yield [net.load(u0_in.at[:, :, columns(h)], half_in), Event(0.0, 2)]
                     grad_tiles(net, half_in, ds, stage_up, d_up0.at[pl.ds(h * (nl // 2), nl // 2)])
-                net.drain(ev['reduced'].copies)
-                copies = []
+                fire(net, ev['d_up0'])
+                yield [ev['y_reduced'], ev['got_up0'], ev['got_up0_rest'], Event(0.0, 2)]
+                net.drain(ev['y_reduced'].copies)
+                yield [net.grant(2, 'xp')]
+                net.spawn(reduce_x(net, part, du_made, rx_scratch, ev['du_reduced']))
                 for k, step in enumerate(STEPS):
-                    yield [ev['got_up0'], Event(0.0, 2)]
                     input_back_rows(net, net.at('x', step), ds, up0, part.at[k])
-                    copies.append(net.load(part.at[k], du_out.at[pl.ds(net.at('x', step) * 2, 2)]))
-                yield copies
-
-            def sums():
-                yield [ev['summed_down']]
-                yield [net.load(ev['summed_down'].total, dw_down)]
-
-            def sums_up():
-                yield [ev['summed_up']]
-                net.spawn(exchange_back(net, ev['summed_up'].total, dw_up, Event()))
-
-            for flow in (layer1(), grads1(), layer1_out(), act(), layer0(), sums(), sums_up()):
+                    fire(net, du_made[k])
+                    yield [Event(net.now, 2)]
+                yield [ev['du_reduced']]
+                norm_back_rows(x0_ref, dy, part.at[3, net.core], dx_out)
+
+            def out_down1():
+                yield [ev['sum_down1']]
+                yield [net.load(ev['sum_down1'].total, dw_down1)]
+                sums_down.all_free = free = Event()
+                net.spawn(sums_down.run(d_down0, ev['d_down0'], ev['sum_down0']))
+                yield from sums_down.release(6, 'yz', ev['sum_down1'].copies, free)
+
+            def out_up1():
+                yield [ev['sum_up1']]
+                net.spawn(exchange_back(net, ev['sum_up1'].total, dw_up1, ev['out_up1']))
+                yield [ev['out_up1']]
+                sums_up.all_free = free = Event()
+                net.spawn(sums_up.run(d_up0, ev['d_up0'], ev['sum_up0']))
+                yield from sums_up.release(5, 'yz', ev['sum_up1'].copies + ev['out_up1'].copies, free)
+
+            def out_down0():
+                yield [ev['sum_down0']]
+                yield [net.load(ev['sum_down0'].total, dw_down0)]
+
+            def out_up0():
+                yield [ev['sum_up0']]
+                net.spawn(exchange_back(net, ev['sum_up0'].total, dw_up0, ev['out_up0']))
+
+            for flow in (layer1(), grads1(), act(), layer1_out(), layer0(), out_down1(), out_up1(), out_down0(), out_up0()):
                 net.spawn(flow)
             net.run()
 
-        def last(net, du_ref, part_ref, dup_ref, ddown_ref, x_ref, dy_ref, x1_ref, dx_ref, out_ref, dw_up_ref, dw_down_ref, *scratch):
-            net.barrier('dyz')
-            r1, r2, s1, s2 = scratch[:6], scratch[6:12], scratch[12:19], scratch[19:26]
-            reduced, out, summed1, summed2 = (Event() for _ in range(4))
-            made1, made2 = [Event() for _ in STEPS], [Event() for _ in STEPS]
-            load_parts(net, du_ref, r1[0], made1)
-            net.spawn(reduce_x(net, r1[0], made1, r1[1:], reduced))
-            net.spawn(reduce_yz(net, dup_ref, 'y', s1, None, summed1))
-            net.spawn(reduce_yz(net, ddown_ref, 'z', s2, None, summed2))
-
-            def act():
-                yield [reduced]
-                norm_back_rows(x_ref, dy_ref, r1[0].at[3, net.core], dx_ref)
-                net.spend(0.7)
-
-            def forward_out():
-                yield [Event(20.0)]
-                load_parts(net, part_ref, r2[0], made2)
-                net.spawn(reduce_x(net, r2[0], made2, r2[1:], out))
-                yield [out]
-                add_rows(x1_ref, r2[0].at[3, net.core], out_ref)
-
-            def grads():
-                yield [summed1]
-                net.spawn(exchange_back(net, summed1.total, dw_up_ref, Event()))
-                yield [summed2]
-                yield [net.load(summed2.total, dw_down_ref)]
-
-            net.spawn(act())
-            net.spawn(forward_out())
-            net.spawn(grads())
-            net.run()
-
-        def own_up(d_up):
-            return d_up.reshape(nd, ur, nl, dr).transpose(1, 2, 0, 3).reshape(ur, ffn)
+        def finish(up1_ref, up0_ref, down1_ref, down0_ref, x_ref, dx_ref, x_out, dx_out, up_out, down_out):
+            for l, (up_ref, down_ref) in enumerate(((up0_ref, down0_ref), (up1_ref, down1_ref))):
+                join_columns(up_ref, up_out.at[l])
+                rows_loop(dr, 16, lambda at: down_out.at[l].__setitem__((at, slice(None)), down_ref[at, :]))
+            rows_loop(rows, 16, lambda at: x_out.__setitem__((at, slice(None)), x_ref[at, :]))
+            rows_loop(rows, 16, lambda at: dx_out.__setitem__((at, slice(None)), dx_ref[at, :]))
 
         d_up_own, d_down_own = shape((nd, ur, hidden), F32), shape((dr, width), F32)
 
-        blocks, u0, a0, s0, up1, down1, u1, g_full, ds1, x1 = call(
+        blocks, u0, a0, s0, up1, down1, u1, g_full, ds1, keep, x1 = call(
             forward, [shape((num_layers, nd * ur, hidden), BF16), act_full, hid_full, hid_full, up_full, shape((2, nl, dr, width // 2), BF16),
-                      act_full, act_full, hid_full, own],
-            'hhhhhhhhhv', 'vhhh',
-            [vmem(act_full)] * 3 + [vmem(up_full), vmem(down_full)] * 2 + [vmem(hid_full)] * 3 + rx, 128, 32, 0,
-            tokens, grad_out, cols, w_down)
-        part_full = shape((nd, rows, width), F32)
+                      act_full, act_full, hid_full, shape((len(FAR), dr, width), BF16), own],
+            'hhhhhhhhhhv', 'vhvh',
+            [pltpu.VMEM((num_layers, nd, ur, hidden), BF16)] + [vmem(act_full)] * 3 + [vmem(up_full), vmem(down_full)] * 2 + [vmem(hid_full)] * 3 + rx,
+            128, 40, 0, tokens, grad_out, w_up, w_down)
         d_up_full, d_down_full = shape((nl, nd * ur, hidden), F32), shape((nl, dr, width), F32)
-        dy0, part1, du0, d_up0, d_down0, _, _, dw_up1, dw_down1 = call(
-            turn, [own, part_full, part_full, d_up_full, d_down_full, d_up_full, d_down_full, d_up_own, d_down_own], 'vhhhhhhhh', 'hhhhhhhhvvhh',
-            [vmem(act_full), vmem(up_full), vmem(up_full), vmem(down_full), pltpu.VMEM((nd, rows, width // 2), BF16), vmem(hid_full), vmem(hid_full),
-             pltpu.VMEM((2, 2, nd * ur, hidden), F32), pltpu.VMEM((2, nl // RING, dr, width // 2), F32)] + rx + ryz_up + ryz_down, 144, 64, 1,
-            u1, up1, down1, ds1, g_full, u0, a0, s0, x1, grad_out, blocks, w_down)
-        dx, x_out, dw_up0, dw_down0 = call(
-            last, [own, own, d_up_own, d_down_own], 'vvhh', 'hhhhvvv', rx + rx + ryz_up + ryz_down, 96, 56, 2,
-            du0, part1, d_up0, d_down0, tokens, dy0, x1)
-        return x_out, dx, jnp.stack([own_up(dw_up0), own_up(dw_up1)]), jnp.stack([dw_down0, dw_down1])
+        x_out, dx, _, _, _, _, *grads = call(
+            turn, [own, own] + [d_up_full, d_down_full] * 2 + [d_up_own, d_down_own] * 2, 'vv' + 'h' * 8, 'hhhhhhhhhvvvhh',
+            [vmem(own), vmem(act_full), vmem(up_full), vmem(up_full), vmem(down_full), pltpu.VMEM((nd, rows, width // 2), BF16), vmem(hid_full), vmem(hid_full),
+             pltpu.VMEM((2, 2, nd * ur, hidden), F32), pltpu.VMEM((2, nl // RING, dr, width // 2), F32)] + rx + ryz_up + ryz_down, 240, 96, 1,
+            u1, up1, down1, ds1, g_full, u0, a0, s0, keep, x1, tokens, grad_out, blocks, w_down)
+        up1_own, down1_own, up0_own, down0_own = grads
+        return pl.pallas_call(
+            finish, out_shape=[own, own, shape(w_up.shape, F32), shape(w_down.shape, F32)], name='finish',
+            in_specs=[pl.BlockSpec(memory_space=pltpu.VMEM)] * 6, out_specs=[pl.BlockSpec(memory_space=pltpu.VMEM)] * 4,
+        )(up1_own, up0_own, down1_own, down0_own, x_out, dx)
 
     return jax.shard_map(device_fn, mesh=mesh, in_specs=(tok_spec, tok_spec, w_spec, w_spec), out_specs=(tok_spec, tok_spec, w_spec, w_spec), check_vma=False)

time: 391 us -> 385 us (0.985)
  local copies, waits for them, and re-layouts: 11 us -> 0 us
  Pallas kernels: 376 us -> 384 us
    reshape x5 -> x0, local copies, waits for them, and re-layouts: 5.34 us -> none  [the longest x3 3.76 us: device_fn(): w_up.reshape(num_layers, ur, nl, nd, dr).transpose(0, 3, 1, 2, 4)]
    pallas_call x0 -> x1, Pallas kernels: none -> 4.1 us  [device_fn(): pl.pallas_call(finish, out_shape=[own, own, shape(w_up.shape, F32), shape...]
    pallas_call x3 -> x2, Pallas kernels: 376 us -> 380 us  [call(): pl.pallas_call(kernel, out_shape=out_shape, in_specs=[spaces[s] for s in...]
where the time goes in v5:
time: 385 us; the launch traced here: 384 us
  Pallas kernels  384 us (100%)
    pallas_call x2, Pallas kernels, call(): pl.pallas_call(kernel, out_shape=out_shape, in_specs=[spaces[s] for s in...  380 us

profile of v5, /device:TPU:1, one launch (start us, length us, event | category | flops | bytes accessed | tf_op | source)
XLA Modules:
  0.0 384.3 jit_solution(7757412252457690239)
XLA Ops:
  0.6 131.1 %forward.1 = (bf16[2,128,1024]{2,1,0:T(8,128)(2,1)}, bf16[8,128,2048]{2,1,0:T(8,128)(2,1)}, bf16[8,128,1024]{2,1,0:T(8,128)(2,1)}, bf16[8,128,1024]{2,1,0:T(8,12...) custom-call(bf16[128,2048]{1,0:T(8,128)(2,1)} %refs_10_.1, ...), custom_call_target="tpu_custom_call" | custom-call | flops 100000000 | bytes 10000000 | tf_op jit(solution)/shard_map/forward/pallas_call | solution.py:530
  131.7 248.4 %turn.1 = (bf16[128,2048]{1,0:T(8,128)(2,1)}, bf16[128,2048]{1,0:T(8,128)(2,1)}, f32[16,128,1024]{2,1,0:T(8,128)}, f32[16,64,2048]{2,1,0:T(8,128)}, f32[16,128,1...) custom-call(bf16[8,128,2048]{2,1,0:T(8,128)(2,1)} %get-tuple-element, ...), custom_call_target="tpu_custom_call" | custom-call | flops 100000000 | bytes 10000000 | tf_op jit(solution)/shard_map/turn/pallas_call | solution.py:530
  380.2 4.1 %finish.1 = (bf16[128,2048]{1,0:T(8,128)(2,1)}, bf16[128,2048]{1,0:T(8,128)(2,1)}, f32[2,16,8192]{2,1,0:T(8,128)}, f32[2,64,2048]{2,1,0:T(8,128)}) custom-call(f32[8,16,1024]{2,1,0:T(8,128)} %get-tuple-element.32.up1_ref, f32[8,16,1024]{2,1,0:T(8,128)} %get-tuple-element.33.up0_ref, f32[64,2048]{1,0:T(8,128)} %get-tuple-element.34.down1_ref, ...), custom_call_target="tpu_custom_call" | custom-call | tf_op jit(solution)/shard_map/finish/pallas_call | solution.py:926

commit v6 on v5

--- a/solution.py
+++ b/solution.py
@@ -1,4 +1,4 @@
-import functools
+import contextlib
 
 import jax
 import jax.numpy as jnp
@@ -15,12 +15,18 @@
 RING = 4
 F32, BF16 = jnp.float32, jnp.bfloat16
 
-LINK_RATE = 43.0e3
+LINK_RATE = 46.0e3
 PAIR_RATE = 600e3
 LOCAL_RATE = 3000e3
-HOP = 2.5
-SLACK = 1.0
+HOP = 2.4
+PAIR_HOP = 1.0
+ENTRY = 3.0
+SLACK = 0.1
 GELU_C = 0.7978845608028654
+
+
+def scope(label):
+    return jax.named_scope(label) if SCOPES else contextlib.nullcontext()
 
 
 class Event:
@@ -30,7 +36,7 @@
 
 class Copy:
     def __init__(self, desc, time, remote):
-        self.desc, self.time, self.remote, self.rank = desc, time, remote, 0
+        self.desc, self.time, self.remote, self.rank, self.waited = desc, time, remote, 0, False
 
     def wait(self):
         if self.remote:
@@ -41,7 +47,7 @@
 
 class Credit:
     def __init__(self, semaphore, count, time):
-        self.semaphore, self.count, self.time, self.rank = semaphore, count, time, 0
+        self.semaphore, self.count, self.time, self.rank, self.waited = semaphore, count, time, 0, False
 
     def wait(self):
         pl.semaphore_wait(self.semaphore, self.count)
@@ -55,6 +61,7 @@
         self.free = {}
         self.sent = []
         self.flows = []
+        self.labels = {}
         here = lax.axis_index('local')
         there = lax.axis_index('data')
         self.data = there
@@ -83,10 +90,13 @@
         for axis, step in self.peers(axes):
             pl.semaphore_signal(semaphore, inc=1, device_id=self.device(axis, step), device_id_type=MESH)
 
-    def barrier(self, axes):
-        semaphore = pltpu.get_barrier_semaphore()
-        self.signal(semaphore, axes)
-        pl.semaphore_wait(semaphore, len(self.peers(axes)))
+    def arrive(self, axes):
+        self.entry, self.entered = pltpu.get_barrier_semaphore(), len(self.peers(axes))
+        self.signal(self.entry, axes)
+
+    def enter(self):
+        pl.semaphore_wait(self.entry, self.entered)
+        self.now = max(self.now, ENTRY)
 
     def grant(self, k, axes):
         self.signal(self.credit_sems.at[k], axes)
@@ -109,10 +119,12 @@
             size *= n
         size *= dst.dtype.itemsize
         rate = PAIR_RATE if axis == 'p' else LINK_RATE
+        if axis == 'd':
+            axis, step, size = ('p', 1, size) if step == 1 else ('x', 1 if step < RING + 2 else -1, size)
         key = (axis, step)
         done = max(self.free.get(key, 0.0), self.now) + size / rate
         self.free[key] = done
-        copy = Copy(desc, done + HOP, True)
+        copy = Copy(desc, done + (PAIR_HOP if axis == 'p' else HOP), True)
         self.sent.append(copy)
         return copy
 
@@ -124,7 +136,14 @@
         size = 1
         for n in dst.shape:
             size *= n
-        return Copy(desc, self.now + 1.0 + size * dst.dtype.itemsize / LOCAL_RATE, False)
+        done = max(self.free.get('hbm', 0.0), self.now) + size * dst.dtype.itemsize / LOCAL_RATE
+        self.free['hbm'] = done
+        return Copy(desc, done + 0.9, False)
+
+    def save(self, src, dst):
+        copy = self.load(src, dst)
+        copy.time += 4.0
+        return copy
 
     def spend(self, microseconds):
         self.now += microseconds
@@ -134,6 +153,9 @@
 
     def step(self, flow):
         try:
+            if flow not in self.labels:
+                self.labels[flow] = [flow.__name__, len(self.labels), 0]
+            self.labels[flow][2] += 1
             self.flows.append((flow, next(flow)))
         except StopIteration:
             pass
@@ -151,11 +173,18 @@
                     best = (rank, k, time)
             _, k, time = best
             flow, items = self.flows.pop(k)
-            for item in items:
-                if not isinstance(item, Event):
-                    item.wait()
+            label = '%s_%d_%d' % tuple(self.labels[flow])
+            with scope('w_' + label):
+                for item in items:
+                    if not isinstance(item, Event) and not item.waited:
+                        item.wait()
+                        item.waited = True
+            before = self.now
             self.now = max(self.now, time)
-            self.step(flow)
+            if PRINT:
+                print('STEP', label, round(before, 2), round(self.now, 2))
+            with scope('s_' + label):
+                self.step(flow)
 
     def finish(self):
         for copy in self.sent:
@@ -192,13 +221,13 @@
 
 
 def exchange(net, src, dst, done):
-    rows = src.shape[2]
+    rows = src.shape[1]
 
     def mine():
-        return dst.at[:, pl.ds(pl.multiple_of(net.data * rows, rows), rows)]
-
-    own = net.load(src.at[:, net.data], mine())
-    copies = [net.send(src.at[:, (net.data + k) % (2 * RING)], mine(), 'd', k) for k in range(1, 2 * RING)]
+        return dst.at[pl.ds(pl.multiple_of(net.data * rows, rows), rows)]
+
+    own = net.load(src.at[net.data], mine())
+    copies = [net.send(src.at[(net.data + k) % (2 * RING)], mine(), 'd', k) for k in (4, 5, 2, 3, 6, 7, 1)]
     yield [own] + copies
     fire(net, done)
 
@@ -210,14 +239,29 @@
         return src.at[pl.ds(pl.multiple_of(k * rows, rows), rows)]
 
     own = net.load(block(net.data), dst.at[net.data])
-    done.copies = [net.send(block((net.data + k) % (2 * RING)), dst.at[net.data], 'd', k) for k in range(1, 2 * RING)]
-    yield [own] + done.copies
+    copies = [net.send(block((net.data + k) % (2 * RING)), dst.at[net.data], 'd', k) for k in (4, 5, 2, 3, 6, 7, 1)]
+    yield [own] + copies
     fire(net, done)
 
 
-def gather_x(net, full, done, issued=None):
+def copy_rows(net, src, dst):
+    def body(at):
+        dst[at, :] = src[at, :]
+
+    rows_loop(src.shape[0], 16, body)
+    net.spend(0.2)
+
+
+def gather_x(net, full, done, issued=None, chips=None):
     half = full.shape[1] // 2
     lo, hi = pl.ds(0, half), pl.ds(half, half)
+    chips = chips or {step: Event() for step in STEPS}
+    left = [2]
+    done.copies = []
+
+    def send(*args):
+        done.copies.append(net.send(*args))
+        return done.copies[-1]
 
     def block(step):
         return full.at[net.at('x', step) * 2 + net.core]
@@ -225,20 +269,35 @@
     def part(step, rows):
         return full.at[net.at('x', step) * 2 + net.core, rows]
 
-    forth = net.send(block(0), block(0), 'x', 1)
-    back = net.send(block(0), block(0), 'x', -1)
-    pair = [net.send(block(0), block(0), 'p')]
-    yield [forth]
-    forth = net.send(part(-1, lo), part(-1, lo), 'x', 1)
-    pair.append(net.send(block(-1), block(-1), 'p'))
-    yield [back]
-    back = net.send(part(1, hi), part(1, hi), 'x', -1)
-    pair.append(net.send(block(1), block(1), 'p'))
-    if issued is not None:
-        fire(net, issued)
-    yield [forth, back]
-    pair.append(net.send(block(2), block(2), 'p'))
-    yield pair
+    relays = []
+
+    def side(step, first, second, mine):
+        yield [mine[0]]
+        relays.append(send(part(step, first), part(step, first), 'x', -step))
+        left[0] -= 1
+        if left[0] == 0:
+            net.spawn(far())
+            if issued is not None:
+                fire(net, issued)
+        yield [mine[1]]
+        pair = send(block(step), block(step), 'p')
+        yield [pair]
+        fire(net, chips[step])
+
+    def far():
+        yield relays
+        pair = send(block(2), block(2), 'p')
+        yield [pair]
+        fire(net, chips[2])
+
+    forth = [send(part(0, rows), part(0, rows), 'x', 1) for rows in (lo, hi)]
+    back = [send(part(0, rows), part(0, rows), 'x', -1) for rows in (hi, lo)]
+    pair = send(block(0), block(0), 'p')
+    net.spawn(side(-1, lo, hi, forth))
+    net.spawn(side(1, hi, lo, back))
+    yield [pair]
+    fire(net, chips[0])
+    yield [chips[step] for step in STEPS]
     fire(net, done)
 
 
@@ -246,50 +305,66 @@
     second = 'y' if first == 'z' else 'z'
     size = own.shape[0]
     half = size // 2
-    all_rows, lo, hi = pl.ds(offset, size), pl.ds(offset, half), pl.ds(offset + half, half)
+    lo, hi = pl.ds(offset, half), pl.ds(offset + half, half)
+    source = {True: own.at[pl.ds(0, half)], False: own.at[pl.ds(half, half)]}
 
     def part(one, two, rows):
         return full.at[yz_index(net, first, one, two), rows]
 
-    ends = []
-    left = [3 if near else RING]
-
-    def relay(one, forth, back, end):
+    left = [3 if near else RING, 3 if near else RING]
+
+    def arrived(which):
+        left[which] -= 1
+        if left[which] == 0 and (done, issued)[which] is not None:
+            fire(net, (done, issued)[which])
+
+    def send(one, rows, axis, step):
+        src = source[rows is lo] if one == 0 else part(one, 0, rows)
+        return net.send(src, part(one, 0, rows), axis, step)
+
+    def column(one):
+        forth = [send(one, rows, second, 1) for rows in (lo, hi)]
+        back = [send(one, rows, second, -1) for rows in (hi, lo)]
+
+        def finish():
+            if near:
+                arrived(1)
+                yield forth + back
+            else:
+                yield [forth[0]]
+                relays = [net.send(part(one, -1, lo), part(one, -1, lo), second, 1)]
+                yield [back[0]]
+                relays.append(net.send(part(one, 1, hi), part(one, 1, hi), second, -1))
+                arrived(1)
+                yield [forth[1], back[1]] + relays
+            arrived(0)
+
+        net.spawn(finish())
+
+    relays = []
+
+    def side(step, first_half, mine):
+        yield [mine[0]]
         if not near:
-            yield [forth]
-            forth = net.send(part(one, -1, lo), part(one, -1, lo), second, 1)
-            yield [back]
-            back = net.send(part(one, 1, hi), part(one, 1, hi), second, -1)
-        left[0] -= 1
-        if left[0] == 0 and issued is not None:
-            fire(net, issued)
-        yield [forth, back]
-        fire(net, end)
-
-    def spread(src, one):
-        forth = net.send(src, part(one, 0, all_rows), second, 1)
-        back = net.send(src, part(one, 0, all_rows), second, -1)
-        end = Event()
-        ends.append(end)
-        net.spawn(relay(one, forth, back, end))
-
-    mine = net.load(own, part(0, 0, all_rows))
-    forth = net.send(own, part(0, 0, all_rows), first, 1)
-    back = net.send(own, part(0, 0, all_rows), first, -1)
-    spread(own, 0)
-    yield [forth]
-    if not near:
-        forth = net.send(part(-1, 0, lo), part(-1, 0, lo), first, 1)
-    spread(part(-1, 0, all_rows), -1)
-    yield [back]
-    if not near:
-        back = net.send(part(1, 0, hi), part(1, 0, hi), first, -1)
-    spread(part(1, 0, all_rows), 1)
-    if not near:
-        yield [forth, back]
-        spread(part(2, 0, all_rows), 2)
-    yield [mine] + ends
-    fire(net, done)
+            relays.append(net.send(part(step, 0, first_half), part(step, 0, first_half), first, -step))
+            if len(relays) == 2:
+                net.spawn(far())
+        yield [mine[1]]
+        column(step)
+
+    def far():
+        yield relays
+        column(2)
+
+    mine = [net.load(source[True], part(0, 0, lo)), net.load(source[False], part(0, 0, hi))]
+    forth = [send(0, rows, first, 1) for rows in (lo, hi)]
+    back = [send(0, rows, first, -1) for rows in (hi, lo)]
+    column(0)
+    net.spawn(side(-1, lo, forth))
+    net.spawn(side(1, hi, back))
+    left[0] += 1
+    yield mine
+    arrived(0)
 
 
 def yz_index(net, first, one, two):
@@ -301,6 +376,8 @@
 
 
 STEPS = (2, 1, -1, 0)
+WUP = 1
+WDOWN = 1
 
 
 def reduce_x(net, part, made, scratch, done):
@@ -323,22 +400,33 @@
 
     for k in range(RING):
         net.spawn(pair(k))
-    yield [ready[0]]
-    first_f = net.send(acc(0, lo), relay_f, 'x', 1)
-    first_b = net.send(acc(0, hi), relay_b, 'x', -1)
-    yield [ready[1]]
-    direct_f = net.send(acc(1, hi), last_f.at[hi], 'x', 1)
-    yield [ready[2]]
-    direct_b = net.send(acc(2, lo), last_b.at[lo], 'x', -1)
-    yield [first_f]
+    sent = {}
+    started = Event()
+
+    def part_flow(k):
+        yield [ready[k]]
+        if k == 0:
+            sent['first_f'] = net.send(acc(0, lo), relay_f, 'x', 1)
+            sent['first_b'] = net.send(acc(0, hi), relay_b, 'x', -1)
+        elif k == 1:
+            sent['direct_f'] = net.send(acc(1, hi), last_f.at[hi], 'x', 1)
+        else:
+            sent['direct_b'] = net.send(acc(2, lo), last_b.at[lo], 'x', -1)
+        if len(sent) == 4:
+            fire(net, started)
+
+    for k in range(3):
+        net.spawn(part_flow(k))
+    yield [started]
+    yield [sent['first_f']]
     add_into(net, acc(1, lo), relay_f)
     summed_f = net.send(acc(1, lo), last_f.at[lo], 'x', 1)
-    yield [first_b]
+    yield [sent['first_b']]
     add_into(net, acc(2, hi), relay_b)
     summed_b = net.send(acc(2, hi), last_b.at[hi], 'x', -1)
-    yield [ready[3], direct_f, direct_b, summed_f, summed_b]
+    yield [ready[3], sent['direct_f'], sent['direct_b'], summed_f, summed_b]
     add_into(net, acc(3), last_f, last_b)
-    done.copies = pairs + [first_f, first_b, direct_f, direct_b, summed_f, summed_b]
+    done.copies = pairs + list(sent.values()) + [summed_f, summed_b]
     fire(net, done)
 
 
@@ -357,7 +445,8 @@
 
 
 class Sums:
-    def __init__(self, net, first, scratch):
+    def __init__(self, net, first, scratch, window):
+        self.window = window
         self.net, self.first, self.scratch = net, first, scratch
         self.second = 'y' if first == 'z' else 'z'
         self.free = [Event(0.0) for _ in range(3)]
@@ -370,7 +459,7 @@
         yield [self.net.grant(credit, axes)]
         fire(self.net, event)
 
-    def run(self, part, start, done, credit=None):
+    def run(self, part, start, done, credit=None, mark=None, hold=None):
         net, first, second = self.net, self.first, self.second
         ahead, behind, mine, relay1, last1, relay2, last2 = self.scratch
         relays_free, all_free = self.relays_free, self.all_free
@@ -378,7 +467,8 @@
         lo, hi, all_rows = pl.ds(0, half), pl.ds(half, half), pl.ds(0, 2 * half)
 
         def term(one, two, rows=all_rows):
-            return part.at[yz_index(net, first, one, two), rows]
+            start = yz_index(net, first, one, two) * (2 * half) + rows.start
+            return part.at[pl.ds(pl.multiple_of(start, half), rows.size)]
 
         def bring(gate, src, dst, got):
             yield [gate, start]
@@ -389,10 +479,13 @@
         self.free = [events[RING] for events in free]
         got = [[Event() for _ in range(RING)] for _ in range(3)]
         ends = [Event() for _ in STEPS]
+        passed = [Event() for _ in STEPS]
         relay_copies = []
 
         def ring(k):
             two = STEPS[k]
+            if k >= self.window:
+                yield [passed[k - self.window]]
             net.spawn(bring(free[0][k], term(1, two, lo), ahead, got[0][k]))
             net.spawn(bring(free[1][k], term(-1, two, hi), behind, got[1][k]))
             net.spawn(bring(free[2][k], term(0, two), mine, got[2][k]))
@@ -417,6 +510,9 @@
             fire(net, free[1][k + 1])
             summed_b = net.send(relay1.at[1, k], last1.at[1, k, hi], first, -1)
             relay_copies.extend([summed_f, summed_b])
+            fire(net, passed[k])
+            if k == RING - 1 and mark is not None:
+                fire(net, mark)
             yield [sent]
             yield direct + [summed_f, summed_b, got[2][k]]
             add_into(net, last1.at[0, k], last1.at[1, k], mine)
@@ -437,7 +533,7 @@
                 yield from self.release(credit, first, relay_copies, self.relays_free)
 
             net.spawn(relays())
-        yield [ends[0]]
+        yield [ends[0]] + ([hold] if hold else [])
         first_f = net.send(sums(0, lo), relay2.at[0], second, 1)
         first_b = net.send(sums(0, hi), relay2.at[1], second, -1)
         yield [ends[1]]
@@ -537,9 +633,12 @@
 
 
 PRINT = False
+SCOPES = False
 
 
 WIDE = 512
+GR = 2
+DU = 3
 
 
 def wide_loop(total, body):
@@ -577,7 +676,7 @@
         s[at, :, cols] = gelu(pre.astype(F32)).astype(BF16).reshape(2, -1, wide)
 
     wide_loop(up.shape[2], body)
-    net.spend(1.4)
+    net.spend(1.7)
 
 
 def down_rows(net, chip, s, down, part):
@@ -587,7 +686,7 @@
         part[:, :, cols] = dot_rows(s[at], down[:, :, cols]).reshape(2, -1, wide)
 
     wide_loop(down.shape[2], body)
-    net.spend(1.5)
+    net.spend(1.76)
 
 
 def hidden_back_rows(net, chip, dy, down, ds):
@@ -599,7 +698,7 @@
         ds[at, :, cols] = dot_cols(dy[at], down[blocks]).astype(BF16).reshape(2, -1, wide)
 
     wide_loop(down.shape[0] * rows, body)
-    net.spend(1.4)
+    net.spend(1.5)
 
 
 def gelu_both(a):
@@ -617,7 +716,7 @@
         ds[at, :, cols] = (ds[at, :, cols].astype(F32) * slope.reshape(2, -1, wide)).astype(BF16)
 
     wide_loop(up.shape[2], body)
-    net.spend(1.8)
+    net.spend(2.1)
 
 
 def pre_back_rows(net, chip, dy, down, a, da):
@@ -630,7 +729,7 @@
         da[at, :, cols] = (ds * gelu_both(a[at, :, cols].astype(F32))[1]).astype(BF16)
 
     wide_loop(down.shape[0] * rows, body)
-    net.spend(1.9)
+    net.spend(1.95)
 
 
 def input_back_rows(net, chip, da, up, part):
@@ -642,7 +741,7 @@
         part[:, :, cols] = dot_cols(da[at], up[blocks]).reshape(2, -1, wide)
 
     wide_loop(up.shape[0] * rows, body)
-    net.spend(1.6)
+    net.spend(1.9)
 
 
 def stored_tiles(net, count, compute, stage, out):
@@ -668,13 +767,12 @@
 
 
 def grad_tiles(net, lhs, rhs, stage, out):
-    _, blocks, rows, cols = stage.shape
-    wide = blocks * rows
+    wide = stage.shape[1]
 
     def compute(t, slot):
-        slot[...] = dot_tokens(lhs[:, :, pl.ds(pl.multiple_of(t * wide, wide), wide)], rhs[...]).reshape(blocks, rows, cols)
-
-    stored_tiles(net, lhs.shape[2] // wide, compute, stage, lambda t: out.at[pl.ds(t * blocks, blocks)])
+        slot[...] = dot_tokens(lhs[:, :, pl.ds(pl.multiple_of(t * wide, wide), wide)], rhs[...])
+
+    stored_tiles(net, lhs.shape[2] // wide, compute, stage, lambda t: out.at[pl.ds(pl.multiple_of(t * wide, wide), wide)])
     net.spend(3.2 * lhs.shape[2] / 1024)
 
 
@@ -703,85 +801,85 @@
             return pltpu.VMEM(like.shape, like.dtype)
 
         def forward(net, x_ref, g_in, w_up_ref, down_in, block_out, u_out, a_out, s_out, up_out, down_out, next_out, g_out, ds_out, keep_out, x_out,
-                    cols, u, g, u1, up0, down0, up1, down1, a, s, ds, part, *rx_scratch):
-            net.barrier('dyz')
-            blocks, got_u, got_g, got_u1, got_up0, got_down0, got_up1, got_down1, reduced = (Event() for _ in range(9))
-            made = [Event() for _ in STEPS]
-            hidden_made = [Event() for _ in STEPS]
-            got_up0.rank = 2
-            names = dict(blocks=blocks, got_u=got_u, got_g=got_g, got_u1=got_u1, got_up0=got_up0, got_down0=got_down0, got_up1=got_up1,
-                         got_down1=got_down1, reduced=reduced)
-            for name, event in names.items():
-                event.name = name
-            for k in range(RING):
-                made[k].name, hidden_made[k].name = 'made%d' % k, 'hidden%d' % k
+                    cols, next_own, u, g, up0, down0, up1, down1, a, s, ds, part, *rx_scratch):
+            net.arrive('dyz')
+            names = ('blocks', 'blocks1', 'sent_u', 'got_u', 'got_g', 'sent_up0', 'sent_down0', 'got_up0', 'got_down0', 'got_up1', 'got_down1', 'reduced')
+            ev = {name: Event(name=name) for name in names}
+            ev['got_up0'].rank = 2
+            made = [Event(name='made%d' % k) for k in range(RING)]
+            hidden_made = [Event(name='hidden%d' % k) for k in range(RING)]
+            grad = net.load(g_in, g.at[net.data])
             split_columns(w_up_ref, cols)
-            net.spawn(exchange(net, cols, block_out, blocks))
             norm_rows(x_ref, u.at[net.data])
-            net.spend(0.5)
-            sent_u, sent_up0, sent_down0 = Event(name='sent_u'), Event(name='sent_up0'), Event(name='sent_down0')
-            net.spawn(gather_x(net, u, got_u, sent_u))
-            net.spawn(gather_yz(net, down_in.at[0], down0, 'z', got_down0, sent_down0))
+            net.enter()
+            net.spawn(exchange(net, cols.at[0], block_out.at[0], ev['blocks']))
+            net.spawn(gather_yz(net, down_in.at[0], down0, 'z', ev['got_down0'], ev['sent_down0']))
+            net.spawn(gather_x(net, u, ev['got_u'], ev['sent_u']))
 
             def up_first():
-                yield [blocks]
-                net.spawn(gather_yz(net, block_out.at[0], up0, 'y', got_up0, sent_up0))
+                yield [ev['blocks']]
+                net.spawn(gather_yz(net, block_out.at[0], up0, 'y', ev['got_up0'], ev['sent_up0']))
+                yield [ev['sent_u']]
+                net.spawn(exchange(net, cols.at[1], block_out.at[1], ev['blocks1']))
+                yield [grad]
+                net.spawn(gather_x(net, g, ev['got_g']))
 
             def second():
-                yield [sent_up0, sent_down0]
-                net.spawn(gather_yz(net, block_out.at[1], up1, 'y', got_up1))
-                net.spawn(gather_yz(net, down_in.at[1], down1, 'z', got_down1))
-
-            def grad():
-                yield [net.load(g_in, g.at[net.data]), sent_u]
-                net.spawn(gather_x(net, g, got_g))
+                yield [ev['sent_up0'], ev['sent_down0'], ev['blocks1']]
+                net.spawn(gather_yz(net, block_out.at[1], up1, 'y', ev['got_up1']))
+                net.spawn(gather_yz(net, down_in.at[1], down1, 'z', ev['got_down1']))
 
             def save(event, *pairs):
-                yield [event]
-                yield [net.load(src, dst) for src, dst in pairs]
+                yield [ev[event]]
+                yield [net.save(src, dst) for src, dst in pairs]
 
             def hidden_flow():
-                yield [got_u, got_up0]
+                yield [ev['got_u'], ev['got_up0']]
                 for k, step in enumerate(STEPS):
                     hidden_rows(net, net.at('x', step), u, up0, a, s)
                     fire(net, hidden_made[k])
                     yield [Event(net.now, 2)]
-                yield [net.load(a, a_out), net.load(s, s_out), net.load(u, u_out)]
+                yield [net.save(a, a_out), net.save(s, s_out), net.save(u, u_out)]
 
             def down_flow():
                 for k, step in enumerate(STEPS):
-                    yield [hidden_made[k], got_down0, Event(0.0, 1)]
+                    yield [hidden_made[k], ev['got_down0'], Event(0.0, 1)]
                     down_rows(net, net.at('x', step), s, down0, part.at[k])
                     fire(net, made[k])
-                yield [net.load(down0.at[yz_index(net, 'z', *far)], keep_out.at[k]) for k, far in enumerate(FAR)]
+                yield [net.save(down0.at[yz_index(net, 'z', *far)], keep_out.at[k]) for k, far in enumerate(FAR)]
 
             def act():
-                yield [reduced]
+                yield [ev['reduced']]
                 add_rows(x_ref, part.at[3, net.core], x_out)
-                norm_rows(x_out, u1.at[net.data])
+                norm_rows(x_out, next_own)
                 net.spend(1.0)
-                net.spawn(gather_x(net, u1, got_u1))
+                yield [net.load(next_own, next_out)]
 
             def back_flow():
                 for k, step in enumerate(STEPS):
-                    yield [got_g, got_down1, Event(0.0, 3)]
+                    yield [ev['got_g'], ev['got_down1'], Event(0.0, 3)]
                     hidden_back_rows(net, net.at('x', step), g, down1, ds)
                 yield [net.load(ds, ds_out)]
 
-            for flow in (up_first(), second(), grad(), hidden_flow(), down_flow(), act(), back_flow(),
-                         reduce_x(net, part, made, rx_scratch, reduced),
-                         save(got_up1, (up1, up_out)), save(got_down1, *[(down1.at[:, :, pl.ds(h * down_out.shape[3], down_out.shape[3])], down_out.at[h]) for h in range(2)]), save(got_u1, (u1, next_out)), save(got_g, (g, g_out))):
+            half = down_out.shape[3]
+            for flow in (up_first(), second(), hidden_flow(), down_flow(), act(), back_flow(), reduce_x(net, part, made, rx_scratch, ev['reduced']),
+                         save('got_up1', (up1, up_out)), save('got_down1', *[(down1.at[:, :, pl.ds(h * half, half)], down_out.at[h]) for h in range(2)]),
+                         save('got_g', (g, g_out))):
                 net.spawn(flow)
             net.run()
 
         def turn(net, u_in, up_in, down_in, ds_in, g_in, u0_in, a0_in, s0_in, keep_in, x_ref, x0_ref, g_own, block_in, w_down_in,
                  x_out, dx_out, d_up0, d_down0, d_up1, d_down1, dw_up1, dw_down1, dw_up0, dw_down0,
-                 dy, u, up1, up0, down0, half_in, ds, s, stage_up, stage_down, part, *scratch):
-            net.barrier('dyz')
+                 own_up, u, up1, up0, down0, half_in, ds, s, stage, part, *scratch):
+            net.arrive('dyz')
+            inputs = [net.load(u_in, u.at[net.data]), net.load(up_in, up1), net.load(ds_in, ds)]
+            inputs[0].wait()
+            inputs[0].waited = True
+            net.enter()
             rx_scratch = scratch[:5]
-            sums_up, sums_down = Sums(net, 'y', scratch[5:12]), Sums(net, 'z', scratch[12:19])
-            names = ('hidden', 'all_du', 'reduced', 'sent_dy', 'got_dy', 'got_up0', 'got_up0_rest', 'got_down0', 'd_down1', 'd_up1', 'y_reduced', 'acts',
-                     'd_down0', 'd_up0', 'du_reduced', 'sum_up1', 'sum_down1', 'sum_up0', 'sum_down0', 'out_up1', 'out_up0')
+            sums_up, sums_down = Sums(net, 'y', scratch[5:12], WUP), Sums(net, 'z', scratch[12:19], WDOWN)
+            names = ('got_u', 'hidden', 'all_du', 'reduced', 'sent_dy', 'got_dy', 'got_up0', 'got_up0_rest', 'got_down0', 'd_down1', 'd_up1', 'y_reduced', 'acts',
+                     'd_down0', 'da0', 'd_up0', 'du_reduced', 'sum_up1', 'sum_down1', 'sum_up0', 'sum_down0', 'up0_passed', 'out_up1', 'out_up0')
             ev = {name: Event(name=name) for name in names}
             made, y_made, du_made = ([Event(name='%s%d' % (name, k)) for k in range(RING)] for name in ('made', 'y_made', 'du_made'))
             wide = half_in.shape[2]
@@ -790,6 +888,9 @@
             def columns(h):
                 return pl.ds(h * wide, wide)
 
+            here = {step: Event(name='u%d' % step) for step in STEPS}
+            dy_here = {step: Event() for step in STEPS}
+            net.spawn(gather_x(net, u, ev['got_u'], chips=here))
             net.spawn(gather_yz(net, w_down_in.at[0], down0, 'z', ev['got_down0'], near=True))
             net.spawn(gather_yz(net, block_in.at[0, pl.ds(0, top)], up0, 'y', ev['got_up0']))
             net.spawn(gather_yz(net, block_in.at[0, pl.ds(top, nd * ur - top)], up0, 'z', ev['got_up0_rest'], offset=top))
@@ -797,71 +898,83 @@
             net.spawn(sums_up.run(d_up1, ev['d_up1'], ev['sum_up1'], 3))
             net.spawn(sums_down.run(d_down1, ev['d_down1'], ev['sum_down1'], 4))
 
-            def layer1():
-                yield [net.load(ds_in, ds), net.load(up_in, up1), net.load(u_in, u)]
-                for k, step in enumerate(STEPS):
-                    hidden_turn_rows(net, net.at('x', step), u, up1, s, ds)
-                    if k == RING - 1:
-                        fire(net, ev['hidden'])
-                    yield [Event(net.now, 1)]
-                    input_back_rows(net, net.at('x', step), ds, up1, part.at[k])
-                    fire(net, made[k])
-                    yield [Event(net.now, 1)]
-                fire(net, ev['all_du'])
+            left = [RING, RING]
+
+            def layer1(k, step):
+                yield [here[step], Event(0.0, 1)] + inputs[1:]
+                hidden_turn_rows(net, net.at('x', step), u, up1, s, ds)
+                left[0] -= 1
+                if left[0] == 0:
+                    fire(net, ev['hidden'])
+                yield [Event(net.now, DU)]
+                input_back_rows(net, net.at('x', step), ds, up1, part.at[k])
+                fire(net, made[k])
+                left[1] -= 1
+                if left[1] == 0:
+                    fire(net, ev['all_du'])
 
             def grads1():
                 for h in range(2):
-                    yield [net.load(g_in.at[:, :, columns(h)], half_in), Event(0.0, 2), ev['hidden']]
-                    grad_tiles(net, s, half_in, stage_down, d_down1.at[:, :, columns(h)])
+                    yield [net.load(g_in.at[:, :, columns(h)], half_in), Event(0.0, GR), ev['hidden']]
+                    grad_tiles(net, s, half_in, stage, d_down1.at[:, columns(h)])
                 fire(net, ev['d_down1'])
-                yield [Event(net.now, 2)]
                 for h in range(2):
-                    grad_tiles(net, u.at[:, :, columns(h)], ds, stage_up, d_up1.at[pl.ds(h * (nl // 2), nl // 2)])
-                    yield [Event(net.now, 2)]
+                    yield [Event(net.now, GR)]
+                    grad_tiles(net, u.at[:, :, columns(h)], ds, stage, d_up1.at[columns(h)])
                 fire(net, ev['d_up1'])
 
             def act():
-                yield [ev['d_up1']]
+                yield [ev['d_up1'], ev['got_u']]
+                net.drain(ev['got_u'].copies)
                 credit = net.grant(0, 'xp')
                 yield [ev['reduced'], credit]
-                norm_back_rows(x_ref, g_own, part.at[3, net.core], dy)
+                norm_back_rows(x_ref, g_own, part.at[3, net.core], u.at[net.data])
                 net.spend(0.7)
-                yield [net.load(dy, u.at[net.data])]
-                net.spawn(gather_x(net, u, ev['got_dy'], ev['sent_dy']))
+                net.spawn(gather_x(net, u, ev['got_dy'], ev['sent_dy'], dy_here))
 
             def layer1_out():
                 yield [ev['all_du'], ev['d_up1']]
                 yield [net.load(down_in.at[h], up1.at[:, pl.ds(h * dr, dr)]) for h in range(2)]
-                yield [ev['reduced'], ev['sent_dy']]
+                yield [ev['reduced'], Event(0.0, 2)]
                 net.drain(ev['reduced'].copies)
-                yield [net.grant(1, 'xp')]
+                credit = net.grant(1, 'xp')
+                for k, step in enumerate(STEPS):
+                    for h in range(2):
+                        net.spend(-0.88)
+                        down_rows(net, net.at('x', step), s, up1.at[:, pl.ds(h * dr, dr)], part.at[k, :, :, columns(h)])
+                    yield [Event(net.now, 2)]
+                loads = [net.load(a0_in, up1.at[pl.ds(0, nd)]), net.load(s0_in, up1.at[pl.ds(nd, nd)])]
+                loads += [net.load(keep_in.at[k], down0.at[yz_index(net, 'z', *far)]) for k, far in enumerate(FAR)]
+                yield loads
+                fire(net, ev['acts'])
+                yield [ev['sent_dy'], credit]
                 net.spawn(reduce_x(net, part, y_made, rx_scratch, ev['y_reduced']))
-                for k, step in enumerate(STEPS):
-                    chip = net.at('x', step)
-                    for h in range(2):
-                        net.spend(-0.7)
-                        down_rows(net, chip, s, up1.at[:, pl.ds(h * dr, dr)], part.at[k, :, :, columns(h)])
+                for k in range(RING):
                     fire(net, y_made[k])
-                    yield [Event(net.now, 2)]
-                yield [net.load(a0_in, up1.at[pl.ds(0, nd)]), net.load(s0_in, up1.at[pl.ds(nd, nd)])]
-                fire(net, ev['acts'])
                 yield [ev['y_reduced']]
                 add_rows(x_ref, part.at[3, net.core], x_out)
 
+            a0, s0 = up1.at[pl.ds(0, nd)], up1.at[pl.ds(nd, nd)]
+            backs = [RING]
+
+            def layer0_hidden(step):
+                yield [dy_here[step], ev['acts'], ev['got_down0'], Event(0.0, 2)]
+                pre_back_rows(net, net.at('x', step), u, down0, a0, ds)
+                backs[0] -= 1
+                if backs[0] == 0:
+                    fire(net, ev['da0'])
+
             def layer0():
-                a0, s0 = up1.at[pl.ds(0, nd)], up1.at[pl.ds(nd, nd)]
-                yield [ev['got_dy'], ev['acts'], Event(0.0, 2)]
+                yield [ev['d_down1']]
+                first = net.load(u0_in.at[:, :, columns(0)], half_in)
                 for h in range(2):
-                    grad_tiles(net, s0, u.at[:, :, columns(h)], stage_down, d_down0.at[:, :, columns(h)])
-                    yield [Event(net.now, 2)]
+                    yield [ev['got_dy'], ev['acts'], Event(0.0, 3)]
+                    grad_tiles(net, s0, u.at[:, :, columns(h)], stage, d_down0.at[:, columns(h)])
                 fire(net, ev['d_down0'])
-                yield [ev['got_down0'], Event(0.0, 2)] + [net.load(keep_in.at[k], down0.at[yz_index(net, 'z', *far)]) for k, far in enumerate(FAR)]
-                for step in STEPS:
-                    pre_back_rows(net, net.at('x', step), u, down0, a0, ds)
-                    yield [Event(net.now, 2)]
                 for h in range(2):
-                    yield [net.load(u0_in.at[:, :, columns(h)], half_in), Event(0.0, 2)]
-                    grad_tiles(net, half_in, ds, stage_up, d_up0.at[pl.ds(h * (nl // 2), nl // 2)])
+                    yield [net.load(u0_in.at[:, :, columns(h)], half_in) if h else first]
+                    yield [ev['da0'], Event(0.0, 3)]
+                    grad_tiles(net, half_in, ds, stage, d_up0.at[columns(h)])
                 fire(net, ev['d_up0'])
                 yield [ev['y_reduced'], ev['got_up0'], ev['got_up0_rest'], Event(0.0, 2)]
                 net.drain(ev['y_reduced'].copies)
@@ -872,22 +985,22 @@
                     fire(net, du_made[k])
                     yield [Event(net.now, 2)]
                 yield [ev['du_reduced']]
-                norm_back_rows(x0_ref, dy, part.at[3, net.core], dx_out)
+                norm_back_rows(x0_ref, u.at[net.data], part.at[3, net.core], dx_out)
 
             def out_down1():
                 yield [ev['sum_down1']]
                 yield [net.load(ev['sum_down1'].total, dw_down1)]
                 sums_down.all_free = free = Event()
-                net.spawn(sums_down.run(d_down0, ev['d_down0'], ev['sum_down0']))
+                net.spawn(sums_down.run(d_down0, ev['d_up0'], ev['sum_down0'], hold=ev['up0_passed']))
                 yield from sums_down.release(6, 'yz', ev['sum_down1'].copies, free)
 
             def out_up1():
                 yield [ev['sum_up1']]
-                net.spawn(exchange_back(net, ev['sum_up1'].total, dw_up1, ev['out_up1']))
-                yield [ev['out_up1']]
+                copy_rows(net, ev['sum_up1'].total, own_up)
                 sums_up.all_free = free = Event()
-                net.spawn(sums_up.run(d_up0, ev['d_up0'], ev['sum_up0']))
-                yield from sums_up.release(5, 'yz', ev['sum_up1'].copies + ev['out_up1'].copies, free)
+                net.spawn(sums_up.run(d_up0, ev['d_up0'], ev['sum_up0'], mark=ev['up0_passed']))
+                yield from sums_up.release(5, 'yz', ev['sum_up1'].copies, free)
+                net.spawn(exchange_back(net, own_up, dw_up1, Event(name='out_up1')))
 
             def out_down0():
                 yield [ev['sum_down0']]
@@ -897,7 +1010,11 @@
                 yield [ev['sum_up0']]
                 net.spawn(exchange_back(net, ev['sum_up0'].total, dw_up0, ev['out_up0']))
 
-            for flow in (layer1(), grads1(), act(), layer1_out(), layer0(), out_down1(), out_up1(), out_down0(), out_up0()):
+            for k in (3, 2, 1, 0):
+                net.spawn(layer1(k, STEPS[k]))
+            for step in (0, -1, 1, 2):
+                net.spawn(layer0_hidden(step))
+            for flow in (grads1(), act(), layer1_out(), layer0(), out_down1(), out_up1(), out_down0(), out_up0()):
                 net.spawn(flow)
             net.run()
 
@@ -912,15 +1029,15 @@
 
         blocks, u0, a0, s0, up1, down1, u1, g_full, ds1, keep, x1 = call(
             forward, [shape((num_layers, nd * ur, hidden), BF16), act_full, hid_full, hid_full, up_full, shape((2, nl, dr, width // 2), BF16),
-                      act_full, act_full, hid_full, shape((len(FAR), dr, width), BF16), own],
+                      own, act_full, hid_full, shape((len(FAR), dr, width), BF16), own],
             'hhhhhhhhhhv', 'vhvh',
-            [pltpu.VMEM((num_layers, nd, ur, hidden), BF16)] + [vmem(act_full)] * 3 + [vmem(up_full), vmem(down_full)] * 2 + [vmem(hid_full)] * 3 + rx,
-            128, 40, 0, tokens, grad_out, w_up, w_down)
-        d_up_full, d_down_full = shape((nl, nd * ur, hidden), F32), shape((nl, dr, width), F32)
+            [pltpu.VMEM((num_layers, nd, ur, hidden), BF16), vmem(own)] + [vmem(act_full)] * 2 + [vmem(up_full), vmem(down_full)] * 2 + [vmem(hid_full)] * 3 + rx,
+            176, 48, 0, tokens, grad_out, w_up, w_down)
+        d_up_full, d_down_full = shape((width, hidden), F32), shape((hidden, width), F32)
         x_out, dx, _, _, _, _, *grads = call(
             turn, [own, own] + [d_up_full, d_down_full] * 2 + [d_up_own, d_down_own] * 2, 'vv' + 'h' * 8, 'hhhhhhhhhvvvhh',
-            [vmem(own), vmem(act_full), vmem(up_full), vmem(up_full), vmem(down_full), pltpu.VMEM((nd, rows, width // 2), BF16), vmem(hid_full), vmem(hid_full),
-             pltpu.VMEM((2, 2, nd * ur, hidden), F32), pltpu.VMEM((2, nl // RING, dr, width // 2), F32)] + rx + ryz_up + ryz_down, 240, 96, 1,
+            [pltpu.VMEM((nd * ur, hidden), F32), vmem(act_full), vmem(up_full), vmem(up_full), vmem(down_full), pltpu.VMEM((nd, rows, width // 2), BF16), vmem(hid_full), vmem(hid_full),
+             pltpu.VMEM((2, hidden // 2, width // 2), F32)] + rx + ryz_up + ryz_down, 288, 104, 1,
             u1, up1, down1, ds1, g_full, u0, a0, s0, keep, x1, tokens, grad_out, blocks, w_down)
         up1_own, down1_own, up0_own, down0_own = grads
         return pl.pallas_call(

time: 385 us -> 344 us (0.89)
  Pallas kernels: 384 us -> 343 us
    pallas_call x2, Pallas kernels: 380 us -> 339 us  [call(): pl.pallas_call(kernel, out_shape=out_shape, in_specs=[spaces[s] for s in...]
where the time goes in v6:
time: 344 us
  Pallas kernels  343 us (100%)
    pallas_call x2, Pallas kernels, call(): pl.pallas_call(kernel, out_shape=out_shape, in_specs=[spaces[s] for s in...  339 us

profile of v6, /device:TPU:1, one launch (start us, length us, event | category | flops | bytes accessed | tf_op | source)
XLA Modules:
  0.0 343.5 jit_solution(2798210260148761997)
XLA Ops:
  0.6 109.6 %forward.1 = (bf16[2,128,1024]{2,1,0:T(8,128)(2,1)}, bf16[8,128,2048]{2,1,0:T(8,128)(2,1)}, bf16[8,128,1024]{2,1,0:T(8,128)(2,1)}, bf16[8,128,1024]{2,1,0:T(8,12...) custom-call(bf16[128,2048]{1,0:T(8,128)(2,1)} %refs_10_.1, ...), custom_call_target="tpu_custom_call" | custom-call | flops 100000000 | bytes 10000000 | tf_op jit(solution)/shard_map/forward/pallas_call | solution.py:626
  110.2 229.2 %turn.1 = (bf16[128,2048]{1,0:T(8,128)(2,1)}, bf16[128,2048]{1,0:T(8,128)(2,1)}, f32[2048,1024]{1,0:T(8,128)}, f32[1024,2048]{1,0:T(8,128)}, f32[2048,1024]{1,0:...) custom-call(bf16[128,2048]{1,0:T(8,128)(2,1)} %get-tuple-element.21., ...), custom_call_target="tpu_custom_call" | custom-call | flops 100000000 | bytes 10000000 | tf_op jit(solution)/shard_map/turn/pallas_call | solution.py:626
  339.4 4.1 %finish.1 = (bf16[128,2048]{1,0:T(8,128)(2,1)}, bf16[128,2048]{1,0:T(8,128)(2,1)}, f32[2,16,8192]{2,1,0:T(8,128)}, f32[2,64,2048]{2,1,0:T(8,128)}) custom-call(f32[8,16,1024]{2,1,0:T(8,128)} %get-tuple-element.32.up1_ref, f32[8,16,1024]{2,1,0:T(8,128)} %get-tuple-element.33.up0_ref, f32[64,2048]{1,0:T(8,128)} %get-tuple-element.34.down1_ref, ...), custom_call_target="tpu_custom_call" | custom-call | tf_op jit(solution)/shard_map/finish/pallas_call | solution.py:1043

commit v7 on v6

--- a/solution.py
+++ b/solution.py
@@ -104,8 +104,13 @@
 
     def drain(self, copies):
         for copy in copies:
-            copy.desc.wait_send()
-            self.sent.remove(copy)
+            if copy in self.sent:
+                copy.desc.wait_send()
+                self.sent.remove(copy)
+
+    def idle(self, gap):
+        over = [copy for copy in self.sent if copy.time + 4.0 < self.now]
+        self.drain(over[:int(gap / 0.05)])
 
     def send(self, src, dst, axis, step=1):
         k = self.n_remote
@@ -167,12 +172,13 @@
                 if any(item.time is None for item in items):
                     continue
                 time = max([item.time for item in items] + [0.0])
-                late = max(item.rank for item in items)
+                late = max([item.rank for item in items] + [0])
                 rank = (max(time, self.now) + (SLACK if late else 0.0), late, time)
                 if best is None or rank < best[0]:
                     best = (rank, k, time)
             _, k, time = best
             flow, items = self.flows.pop(k)
+            self.idle(time - self.now)
             label = '%s_%d_%d' % tuple(self.labels[flow])
             with scope('w_' + label):
                 for item in items:
@@ -241,6 +247,7 @@
     own = net.load(block(net.data), dst.at[net.data])
     copies = [net.send(block((net.data + k) % (2 * RING)), dst.at[net.data], 'd', k) for k in (4, 5, 2, 3, 6, 7, 1)]
     yield [own] + copies
+    net.drain(copies)
     fire(net, done)
 
 
@@ -301,12 +308,12 @@
     fire(net, done)
 
 
-def gather_yz(net, own, full, first, done, issued=None, offset=0, near=False):
+def gather_yz(net, own, full, first, done, issued=None, offset=0, near=False, split=True):
     second = 'y' if first == 'z' else 'z'
     size = own.shape[0]
     half = size // 2
-    lo, hi = pl.ds(offset, half), pl.ds(offset + half, half)
-    source = {True: own.at[pl.ds(0, half)], False: own.at[pl.ds(half, half)]}
+    lo, hi, both = pl.ds(offset, half), pl.ds(offset + half, half), pl.ds(offset, size)
+    forward, backward = ((lo, hi), (hi, lo)) if split and not near else ((both,), (both,))
 
     def part(one, two, rows):
         return full.at[yz_index(net, first, one, two), rows]
@@ -319,12 +326,12 @@
             fire(net, (done, issued)[which])
 
     def send(one, rows, axis, step):
-        src = source[rows is lo] if one == 0 else part(one, 0, rows)
+        src = own.at[pl.ds(rows.start - offset, rows.size)] if one == 0 else part(one, 0, rows)
         return net.send(src, part(one, 0, rows), axis, step)
 
     def column(one):
-        forth = [send(one, rows, second, 1) for rows in (lo, hi)]
-        back = [send(one, rows, second, -1) for rows in (hi, lo)]
+        forth = [send(one, rows, second, 1) for rows in forward]
+        back = [send(one, rows, second, -1) for rows in backward]
 
         def finish():
             if near:
@@ -336,7 +343,7 @@
                 yield [back[0]]
                 relays.append(net.send(part(one, 1, hi), part(one, 1, hi), second, -1))
                 arrived(1)
-                yield [forth[1], back[1]] + relays
+                yield forth[1:] + back[1:] + relays
             arrived(0)
 
         net.spawn(finish())
@@ -349,16 +356,16 @@
             relays.append(net.send(part(step, 0, first_half), part(step, 0, first_half), first, -step))
             if len(relays) == 2:
                 net.spawn(far())
-        yield [mine[1]]
+        yield mine[1:]
         column(step)
 
     def far():
         yield relays
         column(2)
 
-    mine = [net.load(source[True], part(0, 0, lo)), net.load(source[False], part(0, 0, hi))]
-    forth = [send(0, rows, first, 1) for rows in (lo, hi)]
-    back = [send(0, rows, first, -1) for rows in (hi, lo)]
+    mine = [net.load(own, part(0, 0, both))]
+    forth = [send(0, rows, first, 1) for rows in forward]
+    back = [send(0, rows, first, -1) for rows in backward]
     column(0)
     net.spawn(side(-1, lo, forth))
     net.spawn(side(1, hi, back))
@@ -376,8 +383,7 @@
 
 
 STEPS = (2, 1, -1, 0)
-WUP = 1
-WDOWN = 1
+WINDOW = 2
 
 
 def reduce_x(net, part, made, scratch, done):
@@ -445,118 +451,93 @@
 
 
 class Sums:
-    def __init__(self, net, first, scratch, window):
-        self.window = window
-        self.net, self.first, self.scratch = net, first, scratch
+    def __init__(self, net, first, scratch, stage):
+        self.net, self.first, self.scratch, self.stage = net, first, scratch, stage
         self.second = 'y' if first == 'z' else 'z'
-        self.free = [Event(0.0) for _ in range(3)]
-        self.relays_free, self.all_free = Event(0.0), Event(0.0)
-        self.phase1 = []
-        self.phase2 = []
-
-    def release(self, credit, axes, copies, event):
-        self.net.drain(copies)
-        yield [self.net.grant(credit, axes)]
-        fire(self.net, event)
-
-    def run(self, part, start, done, credit=None, mark=None, hold=None):
+
+    def run(self, place, start, done, free, passed_all):
         net, first, second = self.net, self.first, self.second
-        ahead, behind, mine, relay1, last1, relay2, last2 = self.scratch
-        relays_free, all_free = self.relays_free, self.all_free
+        relay1, last1, relay2, last2 = self.scratch
+        ahead, behind, mine = self.stage
         half = mine.shape[0] // 2
         lo, hi, all_rows = pl.ds(0, half), pl.ds(half, half), pl.ds(0, 2 * half)
+        done.copies = []
+
+        def send(*args):
+            done.copies.append(net.send(*args))
+            return done.copies[-1]
 
         def term(one, two, rows=all_rows):
-            start = yz_index(net, first, one, two) * (2 * half) + rows.start
-            return part.at[pl.ds(pl.multiple_of(start, half), rows.size)]
+            return place(yz_index(net, first, one, two), rows)
 
         def bring(gate, src, dst, got):
             yield [gate, start]
             yield [net.load(src, dst)]
             fire(net, got)
 
-        free = [[gate] + [Event() for _ in range(RING)] for gate in self.free]
-        self.free = [events[RING] for events in free]
+        chain = [[gate] + [Event() for _ in range(RING)] for gate in free]
+        free[:] = [events[RING] for events in chain]
         got = [[Event() for _ in range(RING)] for _ in range(3)]
         ends = [Event() for _ in STEPS]
-        passed = [Event() for _ in STEPS]
-        relay_copies = []
+        passed = [Event() for _ in range(RING - 1)] + [passed_all]
 
         def ring(k):
             two = STEPS[k]
-            if k >= self.window:
-                yield [passed[k - self.window]]
-            net.spawn(bring(free[0][k], term(1, two, lo), ahead, got[0][k]))
-            net.spawn(bring(free[1][k], term(-1, two, hi), behind, got[1][k]))
-            net.spawn(bring(free[2][k], term(0, two), mine, got[2][k]))
-            first_f = net.send(term(2, two, lo), relay1.at[0, k], first, 1)
-            first_b = net.send(term(2, two, hi), relay1.at[1, k], first, -1)
-            direct, sent = [], Event()
-
-            def directs():
-                yield [all_free]
-                direct.append(net.send(term(1, two, hi), last1.at[0, k, hi], first, 1))
-                direct.append(net.send(term(-1, two, lo), last1.at[1, k, lo], first, -1))
-                fire(net, sent)
-
-            net.spawn(directs())
+            if k >= WINDOW:
+                yield [passed[k - WINDOW]]
+            net.spawn(bring(chain[0][k], term(1, two, lo), ahead, got[0][k]))
+            net.spawn(bring(chain[1][k], term(-1, two, hi), behind, got[1][k]))
+            net.spawn(bring(chain[2][k], term(0, two), mine, got[2][k]))
+            first_f = send(term(2, two, lo), relay1.at[0, k], first, 1)
+            first_b = send(term(2, two, hi), relay1.at[1, k], first, -1)
+            direct_f = send(term(1, two, hi), last1.at[0, k, hi], first, 1)
+            direct_b = send(term(-1, two, lo), last1.at[1, k, lo], first, -1)
             yield [first_f, got[0][k]]
             add_into(net, relay1.at[0, k], ahead)
-            fire(net, free[0][k + 1])
-            yield [all_free]
-            summed_f = net.send(relay1.at[0, k], last1.at[0, k, lo], first, 1)
+            fire(net, chain[0][k + 1])
+            summed_f = send(relay1.at[0, k], last1.at[0, k, lo], first, 1)
             yield [first_b, got[1][k]]
             add_into(net, relay1.at[1, k], behind)
-            fire(net, free[1][k + 1])
-            summed_b = net.send(relay1.at[1, k], last1.at[1, k, hi], first, -1)
-            relay_copies.extend([summed_f, summed_b])
+            fire(net, chain[1][k + 1])
+            summed_b = send(relay1.at[1, k], last1.at[1, k, hi], first, -1)
             fire(net, passed[k])
-            if k == RING - 1 and mark is not None:
-                fire(net, mark)
-            yield [sent]
-            yield direct + [summed_f, summed_b, got[2][k]]
+            yield [direct_f, direct_b, summed_f, summed_b, got[2][k]]
             add_into(net, last1.at[0, k], last1.at[1, k], mine)
-            fire(net, free[2][k + 1])
+            fire(net, chain[2][k + 1])
             fire(net, ends[k])
 
         def sums(k, rows=all_rows):
             return last1.at[0, k, rows]
 
-        yield [start, relays_free]
+        yield [start]
         for k in range(RING):
             net.spawn(ring(k))
-        if credit is not None:
-            self.relays_free = Event()
-
-            def relays():
-                yield ends
-                yield from self.release(credit, first, relay_copies, self.relays_free)
-
-            net.spawn(relays())
-        yield [ends[0]] + ([hold] if hold else [])
-        first_f = net.send(sums(0, lo), relay2.at[0], second, 1)
-        first_b = net.send(sums(0, hi), relay2.at[1], second, -1)
+        yield [ends[0]]
+        first_f = send(sums(0, lo), relay2.at[0], second, 1)
+        first_b = send(sums(0, hi), relay2.at[1], second, -1)
         yield [ends[1]]
-        direct_f = net.send(sums(1, hi), last2.at[0, hi], second, 1)
+        direct_f = send(sums(1, hi), last2.at[0, hi], second, 1)
         yield [ends[2]]
-        direct_b = net.send(sums(2, lo), last2.at[1, lo], second, -1)
+        direct_b = send(sums(2, lo), last2.at[1, lo], second, -1)
         yield [first_f]
         add_into(net, sums(1, lo), relay2.at[0])
-        summed_f = net.send(sums(1, lo), last2.at[0, lo], second, 1)
+        summed_f = send(sums(1, lo), last2.at[0, lo], second, 1)
         yield [first_b]
         add_into(net, sums(2, hi), relay2.at[1])
-        summed_b = net.send(sums(2, hi), last2.at[1, hi], second, -1)
+        summed_b = send(sums(2, hi), last2.at[1, hi], second, -1)
         yield [ends[3], direct_f, direct_b, summed_f, summed_b]
         add_into(net, sums(3), last2.at[0], last2.at[1])
         done.total = sums(3)
-        done.copies = [first_f, first_b, direct_f, direct_b, summed_f, summed_b]
         fire(net, done)
 
 
-def reduce_yz_scratch(rows, cols):
-    return [pltpu.VMEM((rows // 2, cols), F32), pltpu.VMEM((rows // 2, cols), F32), pltpu.VMEM((rows, cols), F32),
-            pltpu.VMEM((2, RING, rows // 2, cols), F32), pltpu.VMEM((2, RING, rows, cols), F32),
+def sums_scratch(rows, cols):
+    return [pltpu.VMEM((2, RING, rows // 2, cols), F32), pltpu.VMEM((2, RING, rows, cols), F32),
             pltpu.VMEM((2, rows // 2, cols), F32), pltpu.VMEM((2, rows, cols), F32)]
+
+
+def sums_stage(rows, cols):
+    return [pltpu.VMEM((rows // 2, cols), F32), pltpu.VMEM((rows // 2, cols), F32), pltpu.VMEM((rows, cols), F32)]
 
 
 def norm_rows(x_ref, u_ref):
@@ -773,7 +754,7 @@
         slot[...] = dot_tokens(lhs[:, :, pl.ds(pl.multiple_of(t * wide, wide), wide)], rhs[...])
 
     stored_tiles(net, lhs.shape[2] // wide, compute, stage, lambda t: out.at[pl.ds(pl.multiple_of(t * wide, wide), wide)])
-    net.spend(3.2 * lhs.shape[2] / 1024)
+    net.spend(3.9 * lhs.shape[2] / 1024)
 
 
 def solution(mesh):
@@ -794,8 +775,7 @@
         own = shape((rows, width), BF16)
         part_vmem = pltpu.VMEM((RING, 2, rows, width), F32)
         rx = [part_vmem] + reduce_x_scratch(rows, width)
-        ryz_up = reduce_yz_scratch(nd * ur, hidden)
-        ryz_down = reduce_yz_scratch(dr, width)
+        sums = sums_scratch(dr, hidden) * 4 + sums_stage(dr, hidden) * 2
 
         def vmem(like):
             return pltpu.VMEM(like.shape, like.dtype)
@@ -803,22 +783,37 @@
         def forward(net, x_ref, g_in, w_up_ref, down_in, block_out, u_out, a_out, s_out, up_out, down_out, next_out, g_out, ds_out, keep_out, x_out,
                     cols, next_own, u, g, up0, down0, up1, down1, a, s, ds, part, *rx_scratch):
             net.arrive('dyz')
-            names = ('blocks', 'blocks1', 'sent_u', 'got_u', 'got_g', 'sent_up0', 'sent_down0', 'got_up0', 'got_down0', 'got_up1', 'got_down1', 'reduced')
+            names = ('blocks', 'blocks1', 'sent_u', 'got_u', 'got_g', 'sent_up0', 'sent_down0', 'sent_up1', 'sent_down1', 'got_up0', 'got_down0', 'got_up1', 'got_down1', 'reduced')
             ev = {name: Event(name=name) for name in names}
             ev['got_up0'].rank = 2
             made = [Event(name='made%d' % k) for k in range(RING)]
             hidden_made = [Event(name='hidden%d' % k) for k in range(RING)]
+            def gather(name, own, full, split):
+                size = own.shape[0] // 2
+
+                def join(kind, events):
+                    yield events
+                    fire(net, ev[kind + name])
+
+                got, sent = [Event(), Event()], [Event(), Event()]
+                for k, first in enumerate('yz'):
+                    net.spawn(gather_yz(net, own.at[pl.ds(k * size, size)], full, first, got[k], sent[k], k * size, split=split))
+                net.spawn(join('got_', got))
+                net.spawn(join('sent_', sent))
+
+            net.enter()
+            gather('down0', down_in.at[0], down0, False)
+            split_columns(w_up_ref, cols)
+            net.spend(0.5)
+            net.spawn(exchange(net, cols.at[0], block_out.at[0], ev['blocks']))
+            norm_rows(x_ref, u.at[net.data])
+            net.spend(0.7)
+            net.spawn(gather_x(net, u, ev['got_u'], ev['sent_u']))
             grad = net.load(g_in, g.at[net.data])
-            split_columns(w_up_ref, cols)
-            norm_rows(x_ref, u.at[net.data])
-            net.enter()
-            net.spawn(exchange(net, cols.at[0], block_out.at[0], ev['blocks']))
-            net.spawn(gather_yz(net, down_in.at[0], down0, 'z', ev['got_down0'], ev['sent_down0']))
-            net.spawn(gather_x(net, u, ev['got_u'], ev['sent_u']))
 
             def up_first():
                 yield [ev['blocks']]
-                net.spawn(gather_yz(net, block_out.at[0], up0, 'y', ev['got_up0'], ev['sent_up0']))
+                gather('up0', block_out.at[0], up0, True)
                 yield [ev['sent_u']]
                 net.spawn(exchange(net, cols.at[1], block_out.at[1], ev['blocks1']))
                 yield [grad]
@@ -826,8 +821,9 @@
 
             def second():
                 yield [ev['sent_up0'], ev['sent_down0'], ev['blocks1']]
-                net.spawn(gather_yz(net, block_out.at[1], up1, 'y', ev['got_up1']))
-                net.spawn(gather_yz(net, down_in.at[1], down1, 'z', ev['got_down1']))
+                gather('down1', down_in.at[1], down1, False)
+                yield [ev['sent_down1']]
+                gather('up1', block_out.at[1], up1, True)
 
             def save(event, *pairs):
                 yield [ev[event]]
@@ -877,9 +873,11 @@
             inputs[0].waited = True
             net.enter()
             rx_scratch = scratch[:5]
-            sums_up, sums_down = Sums(net, 'y', scratch[5:12], WUP), Sums(net, 'z', scratch[12:19], WDOWN)
+            stages = (scratch[21:24], scratch[24:27])
+            jobs = [[Sums(net, first, scratch[5 + 8 * n + 4 * k:9 + 8 * n + 4 * k], stages[k]) for k, first in enumerate('yz')] for n in range(2)]
             names = ('got_u', 'hidden', 'all_du', 'reduced', 'sent_dy', 'got_dy', 'got_up0', 'got_up0_rest', 'got_down0', 'd_down1', 'd_up1', 'y_reduced', 'acts',
-                     'd_down0', 'da0', 'd_up0', 'du_reduced', 'sum_up1', 'sum_down1', 'sum_up0', 'sum_down0', 'up0_passed', 'out_up1', 'out_up0')
+                     'd_down0', 'da0', 'd_up0', 'du_reduced', 'out_up1', 'out_up0') + tuple(
+                'sum_%s%d%d' % (kind, layer, k) for kind in ('up', 'down') for layer in range(2) for k in range(2))
             ev = {name: Event(name=name) for name in names}
             made, y_made, du_made = ([Event(name='%s%d' % (name, k)) for k in range(RING)] for name in ('made', 'y_made', 'du_made'))
             wide = half_in.shape[2]
@@ -895,8 +893,27 @@
             net.spawn(gather_yz(net, block_in.at[0, pl.ds(0, top)], up0, 'y', ev['got_up0']))
             net.spawn(gather_yz(net, block_in.at[0, pl.ds(top, nd * ur - top)], up0, 'z', ev['got_up0_rest'], offset=top))
             net.spawn(reduce_x(net, part, made, rx_scratch, ev['reduced']))
-            net.spawn(sums_up.run(d_up1, ev['d_up1'], ev['sum_up1'], 3))
-            net.spawn(sums_down.run(d_down1, ev['d_down1'], ev['sum_down1'], 4))
+            frees = [[Event(0.0) for _ in range(3)] for _ in range(2)]
+
+            def up_place(ref, k):
+                half = nd * ur // 2
+                return lambda block, rows: ref.at[pl.ds(pl.multiple_of(block * (2 * half) + k * half + rows.start, rows.size), rows.size)]
+
+            def down_place(ref, k):
+                return lambda block, rows: ref.at[pl.ds(pl.multiple_of(block * dr + rows.start, rows.size), rows.size), columns(k)]
+
+            def sum_job(n, place, ref, ready, name, credits=()):
+                passed = [Event(), Event()]
+                for k in range(2):
+                    start = Event()
+                    ev['start_%s%d' % (name, k)] = start
+                    net.spawn(gate(start, ready + ([credits[k]] if credits else [])))
+                    net.spawn(jobs[n][k].run(place(ref, k), start, ev['sum_%s%d' % (name, k)], frees[k], passed[k]))
+                return passed
+
+            def gate(event, items):
+                yield items
+                fire(net, event)
 
             left = [RING, RING]
 
@@ -968,14 +985,14 @@
                 yield [ev['d_down1']]
                 first = net.load(u0_in.at[:, :, columns(0)], half_in)
                 for h in range(2):
-                    yield [ev['got_dy'], ev['acts'], Event(0.0, 3)]
-                    grad_tiles(net, s0, u.at[:, :, columns(h)], stage, d_down0.at[:, columns(h)])
-                fire(net, ev['d_down0'])
-                for h in range(2):
                     yield [net.load(u0_in.at[:, :, columns(h)], half_in) if h else first]
                     yield [ev['da0'], Event(0.0, 3)]
                     grad_tiles(net, half_in, ds, stage, d_up0.at[columns(h)])
                 fire(net, ev['d_up0'])
+                for h in range(2):
+                    yield [ev['got_dy'], ev['acts'], Event(0.0, 3)]
+                    grad_tiles(net, s0, u.at[:, :, columns(h)], stage, d_down0.at[:, columns(h)])
+                fire(net, ev['d_down0'])
                 yield [ev['y_reduced'], ev['got_up0'], ev['got_up0_rest'], Event(0.0, 2)]
                 net.drain(ev['y_reduced'].copies)
                 yield [net.grant(2, 'xp')]
@@ -987,34 +1004,55 @@
                 yield [ev['du_reduced']]
                 norm_back_rows(x0_ref, u.at[net.data], part.at[3, net.core], dx_out)
 
-            def out_down1():
-                yield [ev['sum_down1']]
-                yield [net.load(ev['sum_down1'].total, dw_down1)]
-                sums_down.all_free = free = Event()
-                net.spawn(sums_down.run(d_down0, ev['d_up0'], ev['sum_down0'], hold=ev['up0_passed']))
-                yield from sums_down.release(6, 'yz', ev['sum_down1'].copies, free)
-
-            def out_up1():
-                yield [ev['sum_up1']]
-                copy_rows(net, ev['sum_up1'].total, own_up)
-                sums_up.all_free = free = Event()
-                net.spawn(sums_up.run(d_up0, ev['d_up0'], ev['sum_up0'], mark=ev['up0_passed']))
-                yield from sums_up.release(5, 'yz', ev['sum_up1'].copies, free)
-                net.spawn(exchange_back(net, own_up, dw_up1, Event(name='out_up1')))
-
-            def out_down0():
-                yield [ev['sum_down0']]
-                yield [net.load(ev['sum_down0'].total, dw_down0)]
-
-            def out_up0():
-                yield [ev['sum_up0']]
-                net.spawn(exchange_back(net, ev['sum_up0'].total, dw_up0, ev['out_up0']))
+            def out_down(layer, dw_down, credit):
+                def one(k):
+                    done = ev['sum_down%d%d' % (layer, k)]
+                    yield [done]
+                    yield [net.load(done.total, dw_down.at[:, columns(k)])]
+                    if credit is not None:
+                        net.drain(done.copies)
+                        yield [net.grant(credit + k, 'yz')]
+                        fire(net, freed[credit + k])
+
+                for k in range(2):
+                    net.spawn(one(k))
+
+            def out_up(layer, dw_up, credit):
+                copied = [Event(), Event()]
+
+                def one(k):
+                    done = ev['sum_up%d%d' % (layer, k)]
+                    yield [done]
+                    copy_rows(net, done.total, own_up.at[pl.ds(k * (nd * ur // 2), nd * ur // 2)])
+                    fire(net, copied[k])
+                    if credit is not None:
+                        net.drain(done.copies)
+                        yield [net.grant(credit + k, 'yz')]
+                        fire(net, freed[credit + k])
+
+                def both():
+                    yield copied + ([ev['out_up1']] if layer == 0 else [])
+                    net.spawn(exchange_back(net, own_up, dw_up, ev['out_up%d' % layer]))
+
+                for k in range(2):
+                    net.spawn(one(k))
+                net.spawn(both())
+
+            freed = {k: Event() for k in range(3, 7)}
+            passed = sum_job(0, down_place, d_down1, [ev['d_down1']], 'down1')
+            passed = sum_job(1, up_place, d_up1, [ev['d_up1']] + passed, 'up1')
+            passed = sum_job(0, up_place, d_up0, [ev['d_up0']] + passed, 'up0', [freed[3], freed[4]])
+            sum_job(1, down_place, d_down0, [ev['d_down0']] + passed, 'down0', [freed[5], freed[6]])
+            out_down(1, dw_down1, 3)
+            out_up(1, dw_up1, 5)
+            out_up(0, dw_up0, None)
+            out_down(0, dw_down0, None)
 
             for k in (3, 2, 1, 0):
                 net.spawn(layer1(k, STEPS[k]))
             for step in (0, -1, 1, 2):
                 net.spawn(layer0_hidden(step))
-            for flow in (grads1(), act(), layer1_out(), layer0(), out_down1(), out_up1(), out_down0(), out_up0()):
+            for flow in (grads1(), act(), layer1_out(), layer0()):
                 net.spawn(flow)
             net.run()
 
@@ -1032,12 +1070,12 @@
                       own, act_full, hid_full, shape((len(FAR), dr, width), BF16), own],
             'hhhhhhhhhhv', 'vhvh',
             [pltpu.VMEM((num_layers, nd, ur, hidden), BF16), vmem(own)] + [vmem(act_full)] * 2 + [vmem(up_full), vmem(down_full)] * 2 + [vmem(hid_full)] * 3 + rx,
-            176, 48, 0, tokens, grad_out, w_up, w_down)
+            320, 64, 0, tokens, grad_out, w_up, w_down)
         d_up_full, d_down_full = shape((width, hidden), F32), shape((hidden, width), F32)
         x_out, dx, _, _, _, _, *grads = call(
             turn, [own, own] + [d_up_full, d_down_full] * 2 + [d_up_own, d_down_own] * 2, 'vv' + 'h' * 8, 'hhhhhhhhhvvvhh',
             [pltpu.VMEM((nd * ur, hidden), F32), vmem(act_full), vmem(up_full), vmem(up_full), vmem(down_full), pltpu.VMEM((nd, rows, width // 2), BF16), vmem(hid_full), vmem(hid_full),
-             pltpu.VMEM((2, hidden // 2, width // 2), F32)] + rx + ryz_up + ryz_down, 288, 104, 1,
+             pltpu.VMEM((2, hidden // 2, width // 2), F32)] + rx + sums, 400, 160, 1,
             u1, up1, down1, ds1, g_full, u0, a0, s0, keep, x1, tokens, grad_out, blocks, w_down)
         up1_own, down1_own, up0_own, down0_own = grads
         return pl.pallas_call(

time: 344 us -> 337 us (0.980)
  Pallas kernels: 343 us -> 336 us
    pallas_call x2, Pallas kernels: 339 us -> 331 us  [call(): pl.pallas_call(kernel, out_shape=out_shape, in_specs=[spaces[s] for s in...]
where the time goes in v7:
time: 337 us; the launch traced here: 336 us
  Pallas kernels  336 us (100%)
    pallas_call x2, Pallas kernels, call(): pl.pallas_call(kernel, out_shape=out_shape, in_specs=[spaces[s] for s in...  331 us

profile of v7, /device:TPU:1, one launch (start us, length us, event | category | flops | bytes accessed | tf_op | source)
XLA Modules:
  0.0 336.2 jit_solution(8102922593874664274)
XLA Ops:
  0.6 107.2 %forward.1 = (bf16[2,128,1024]{2,1,0:T(8,128)(2,1)}, bf16[8,128,2048]{2,1,0:T(8,128)(2,1)}, bf16[8,128,1024]{2,1,0:T(8,128)(2,1)}, bf16[8,128,1024]{2,1,0:T(8,12...) custom-call(bf16[128,2048]{1,0:T(8,128)(2,1)} %refs_10_.1, ...), custom_call_target="tpu_custom_call" | custom-call | flops 100000000 | bytes 10000000 | tf_op jit(solution)/shard_map/forward/pallas_call | solution.py:607
  107.9 224.2 %turn.1 = (bf16[128,2048]{1,0:T(8,128)(2,1)}, bf16[128,2048]{1,0:T(8,128)(2,1)}, f32[2048,1024]{1,0:T(8,128)}, f32[1024,2048]{1,0:T(8,128)}, f32[2048,1024]{1,0:...) custom-call(bf16[128,2048]{1,0:T(8,128)(2,1)} %get-tuple-element.21., ...), custom_call_target="tpu_custom_call" | custom-call | flops 100000000 | bytes 10000000 | tf_op jit(solution)/shard_map/turn/pallas_call | solution.py:607
  332.1 4.1 %finish.1 = (bf16[128,2048]{1,0:T(8,128)(2,1)}, bf16[128,2048]{1,0:T(8,128)(2,1)}, f32[2,16,8192]{2,1,0:T(8,128)}, f32[2,64,2048]{2,1,0:T(8,128)}) custom-call(f32[8,16,1024]{2,1,0:T(8,128)} %get-tuple-element.32.up1_ref, f32[8,16,1024]{2,1,0:T(8,128)} %get-tuple-element.33.up0_ref, f32[64,2048]{1,0:T(8,128)} %get-tuple-element.34.down1_ref, ...), custom_call_target="tpu_custom_call" | custom-call | tf_op jit(solution)/shard_map/finish/pallas_call | solution.py:1081

commit v8 on v7

--- a/solution.py
+++ b/solution.py
@@ -53,10 +53,21 @@
         pl.semaphore_wait(self.semaphore, self.count)
 
 
+class Pool:
+    def __init__(self):
+        self.slots, self.next = [], 0
+
+    def again(self):
+        self.next = 0
+        return self
+
+
 class Net:
     def __init__(self, send_sems, recv_sems, local_sems, credit_sems):
         self.send_sems, self.recv_sems, self.local_sems, self.credit_sems = send_sems, recv_sems, local_sems, credit_sems
         self.n_remote = self.n_local = 0
+        self.free_sends = list(range(send_sems.shape[0]))
+        self.free_locals = []
         self.now = 0.0
         self.free = {}
         self.sent = []
@@ -107,16 +118,29 @@
             if copy in self.sent:
                 copy.desc.wait_send()
                 self.sent.remove(copy)
+                self.free_sends.append(copy.slot)
 
     def idle(self, gap):
-        over = [copy for copy in self.sent if copy.time + 4.0 < self.now]
+        over = [copy for copy in self.sent if copy.time + 1.5 < self.now]
         self.drain(over[:int(gap / 0.05)])
 
-    def send(self, src, dst, axis, step=1):
-        k = self.n_remote
-        self.n_remote += 1
+    def send(self, src, dst, axis, step=1, pool=None):
+        if pool is not None and pool.next < len(pool.slots):
+            k = pool.slots[pool.next]
+        else:
+            k = self.n_remote
+            self.n_remote += 1
+            if pool is not None:
+                pool.slots.append(k)
+        if pool is not None:
+            pool.next += 1
+        if not self.free_sends:
+            if PRINT:
+                print('EXHAUSTED', round(self.now, 1))
+            self.drain([min(self.sent, key=lambda copy: copy.time)])
+        send_slot = self.free_sends.pop()
         desc = pltpu.make_async_remote_copy(
-            src_ref=src, dst_ref=dst, send_sem=self.send_sems.at[k], recv_sem=self.recv_sems.at[k],
+            src_ref=src, dst_ref=dst, send_sem=self.send_sems.at[send_slot], recv_sem=self.recv_sems.at[k],
             device_id=self.device(axis, step), device_id_type=MESH)
         desc.start()
         size = 1
@@ -130,12 +154,15 @@
         done = max(self.free.get(key, 0.0), self.now) + size / rate
         self.free[key] = done
         copy = Copy(desc, done + (PAIR_HOP if axis == 'p' else HOP), True)
+        copy.slot = send_slot
         self.sent.append(copy)
         return copy
 
     def load(self, src, dst):
-        k = self.n_local
-        self.n_local += 1
+        if not self.free_locals:
+            self.free_locals.append(self.n_local)
+            self.n_local += 1
+        k = self.free_locals.pop()
         desc = pltpu.make_async_copy(src, dst, self.local_sems.at[k])
         desc.start()
         size = 1
@@ -143,7 +170,9 @@
             size *= n
         done = max(self.free.get('hbm', 0.0), self.now) + size * dst.dtype.itemsize / LOCAL_RATE
         self.free['hbm'] = done
-        return Copy(desc, done + 0.9, False)
+        copy = Copy(desc, done + 0.9, False)
+        copy.slot = k
+        return copy
 
     def save(self, src, dst):
         copy = self.load(src, dst)
@@ -185,6 +214,8 @@
                     if not isinstance(item, Event) and not item.waited:
                         item.wait()
                         item.waited = True
+                        if isinstance(item, Copy) and not item.remote:
+                            self.free_locals.append(item.slot)
             before = self.now
             self.now = max(self.now, time)
             if PRINT:
@@ -259,7 +290,7 @@
     net.spend(0.2)
 
 
-def gather_x(net, full, done, issued=None, chips=None):
+def gather_x(net, full, done, issued=None, chips=None, pool=None):
     half = full.shape[1] // 2
     lo, hi = pl.ds(0, half), pl.ds(half, half)
     chips = chips or {step: Event() for step in STEPS}
@@ -267,7 +298,7 @@
     done.copies = []
 
     def send(*args):
-        done.copies.append(net.send(*args))
+        done.copies.append(net.send(*args, pool=pool))
         return done.copies[-1]
 
     def block(step):
@@ -308,7 +339,7 @@
     fire(net, done)
 
 
-def gather_yz(net, own, full, first, done, issued=None, offset=0, near=False, split=True):
+def gather_yz(net, own, full, first, done, issued=None, offset=0, near=False, split=True, pool=None):
     second = 'y' if first == 'z' else 'z'
     size = own.shape[0]
     half = size // 2
@@ -327,7 +358,7 @@
 
     def send(one, rows, axis, step):
         src = own.at[pl.ds(rows.start - offset, rows.size)] if one == 0 else part(one, 0, rows)
-        return net.send(src, part(one, 0, rows), axis, step)
+        return net.send(src, part(one, 0, rows), axis, step, pool)
 
     def column(one):
         forth = [send(one, rows, second, 1) for rows in forward]
@@ -339,9 +370,9 @@
                 yield forth + back
             else:
                 yield [forth[0]]
-                relays = [net.send(part(one, -1, lo), part(one, -1, lo), second, 1)]
+                relays = [net.send(part(one, -1, lo), part(one, -1, lo), second, 1, pool)]
                 yield [back[0]]
-                relays.append(net.send(part(one, 1, hi), part(one, 1, hi), second, -1))
+                relays.append(net.send(part(one, 1, hi), part(one, 1, hi), second, -1, pool))
                 arrived(1)
                 yield forth[1:] + back[1:] + relays
             arrived(0)
@@ -353,7 +384,7 @@
     def side(step, first_half, mine):
         yield [mine[0]]
         if not near:
-            relays.append(net.send(part(step, 0, first_half), part(step, 0, first_half), first, -step))
+            relays.append(net.send(part(step, 0, first_half), part(step, 0, first_half), first, -step, pool))
             if len(relays) == 2:
                 net.spawn(far())
         yield mine[1:]
@@ -386,7 +417,7 @@
 WINDOW = 2
 
 
-def reduce_x(net, part, made, scratch, done):
+def reduce_x(net, part, made, scratch, done, pool=None):
     other, relay_f, relay_b, last_f, last_b = scratch
     half = part.shape[2] // 2
     lo, hi = pl.ds(0, half), pl.ds(half, half)
@@ -399,7 +430,7 @@
 
     def pair(k):
         yield [made[k]]
-        pairs[k] = net.send(part.at[k, 1 - net.core], other.at[k], 'p')
+        pairs[k] = net.send(part.at[k, 1 - net.core], other.at[k], 'p', pool=pool)
         yield [pairs[k]]
         add_into(net, acc(k), other.at[k])
         fire(net, ready[k])
@@ -412,12 +443,12 @@
     def part_flow(k):
         yield [ready[k]]
         if k == 0:
-            sent['first_f'] = net.send(acc(0, lo), relay_f, 'x', 1)
-            sent['first_b'] = net.send(acc(0, hi), relay_b, 'x', -1)
+            sent['first_f'] = net.send(acc(0, lo), relay_f, 'x', 1, pool=pool)
+            sent['first_b'] = net.send(acc(0, hi), relay_b, 'x', -1, pool=pool)
         elif k == 1:
-            sent['direct_f'] = net.send(acc(1, hi), last_f.at[hi], 'x', 1)
+            sent['direct_f'] = net.send(acc(1, hi), last_f.at[hi], 'x', 1, pool=pool)
         else:
-            sent['direct_b'] = net.send(acc(2, lo), last_b.at[lo], 'x', -1)
+            sent['direct_b'] = net.send(acc(2, lo), last_b.at[lo], 'x', -1, pool=pool)
         if len(sent) == 4:
             fire(net, started)
 
@@ -426,10 +457,10 @@
     yield [started]
     yield [sent['first_f']]
     add_into(net, acc(1, lo), relay_f)
-    summed_f = net.send(acc(1, lo), last_f.at[lo], 'x', 1)
+    summed_f = net.send(acc(1, lo), last_f.at[lo], 'x', 1, pool=pool)
     yield [sent['first_b']]
     add_into(net, acc(2, hi), relay_b)
-    summed_b = net.send(acc(2, hi), last_b.at[hi], 'x', -1)
+    summed_b = net.send(acc(2, hi), last_b.at[hi], 'x', -1, pool=pool)
     yield [ready[3], sent['direct_f'], sent['direct_b'], summed_f, summed_b]
     add_into(net, acc(3), last_f, last_b)
     done.copies = pairs + list(sent.values()) + [summed_f, summed_b]
@@ -455,7 +486,7 @@
         self.net, self.first, self.scratch, self.stage = net, first, scratch, stage
         self.second = 'y' if first == 'z' else 'z'
 
-    def run(self, place, start, done, free, passed_all):
+    def run(self, place, start, done, free, passed_all, pool):
         net, first, second = self.net, self.first, self.second
         relay1, last1, relay2, last2 = self.scratch
         ahead, behind, mine = self.stage
@@ -464,7 +495,7 @@
         done.copies = []
 
         def send(*args):
-            done.copies.append(net.send(*args))
+            done.copies.append(net.send(*args, pool=pool))
             return done.copies[-1]
 
         def term(one, two, rows=all_rows):
@@ -592,7 +623,7 @@
                 w_ref[:, pl.ds((i * RING + x) * tile, tile)] = value
 
 
-def call(body, out_shape, out_spaces, in_spaces, scratch, remote, local, collective_id, *args):
+def call(body, out_shape, out_spaces, in_spaces, scratch, remote, sends, local, collective_id, *args):
     spaces = {'v': pl.BlockSpec(memory_space=pltpu.VMEM), 'h': pl.BlockSpec(memory_space=pl.ANY)}
 
     def kernel(*refs):
@@ -600,13 +631,13 @@
         net.tile_sems = refs[-1]
         body(net, *refs[:-5])
         net.finish()
-        assert net.n_remote <= remote and net.n_local <= local, (net.n_remote, net.n_local)
+        assert net.n_remote <= remote and net.n_local <= local, (body.__name__, net.n_remote, net.n_local)
         if PRINT:
             print(body.__name__, net.n_remote, net.n_local, round(net.now, 1))
 
     return pl.pallas_call(
         kernel, out_shape=out_shape, in_specs=[spaces[s] for s in in_spaces], out_specs=[spaces[s] for s in out_spaces],
-        scratch_shapes=list(scratch) + [pltpu.SemaphoreType.DMA((remote,)), pltpu.SemaphoreType.DMA((remote,)), pltpu.SemaphoreType.DMA((local,)),
+        scratch_shapes=list(scratch) + [pltpu.SemaphoreType.DMA((sends,)), pltpu.SemaphoreType.DMA((remote,)), pltpu.SemaphoreType.DMA((local,)),
                                                pltpu.SemaphoreType.REGULAR((8,)), pltpu.SemaphoreType.DMA((2,))],
         compiler_params=pltpu.CompilerParams(collective_id=collective_id, has_side_effects=True, vmem_limit_bytes=67000000),
         cost_estimate=pl.CostEstimate(flops=10**8, bytes_accessed=10**7, transcendentals=0),
@@ -618,6 +649,8 @@
 
 
 WIDE = 512
+KR, KS, KL = 134, 64, 10
+TR, TS, TL = 222, 64, 13
 GR = 2
 DU = 3
 
@@ -788,6 +821,9 @@
             ev['got_up0'].rank = 2
             made = [Event(name='made%d' % k) for k in range(RING)]
             hidden_made = [Event(name='hidden%d' % k) for k in range(RING)]
+            pools = {name: [Pool(), Pool()] for name in ('up', 'down')}
+            act_pool = Pool()
+
             def gather(name, own, full, split):
                 size = own.shape[0] // 2
 
@@ -797,7 +833,7 @@
 
                 got, sent = [Event(), Event()], [Event(), Event()]
                 for k, first in enumerate('yz'):
-                    net.spawn(gather_yz(net, own.at[pl.ds(k * size, size)], full, first, got[k], sent[k], k * size, split=split))
+                    net.spawn(gather_yz(net, own.at[pl.ds(k * size, size)], full, first, got[k], sent[k], k * size, split=split, pool=pools[name[:-1]][k].again()))
                 net.spawn(join('got_', got))
                 net.spawn(join('sent_', sent))
 
@@ -808,21 +844,26 @@
             net.spawn(exchange(net, cols.at[0], block_out.at[0], ev['blocks']))
             norm_rows(x_ref, u.at[net.data])
             net.spend(0.7)
-            net.spawn(gather_x(net, u, ev['got_u'], ev['sent_u']))
             grad = net.load(g_in, g.at[net.data])
 
             def up_first():
                 yield [ev['blocks']]
                 gather('up0', block_out.at[0], up0, True)
+                net.spawn(gather_x(net, u, ev['got_u'], ev['sent_u'], pool=act_pool))
                 yield [ev['sent_u']]
                 net.spawn(exchange(net, cols.at[1], block_out.at[1], ev['blocks1']))
-                yield [grad]
-                net.spawn(gather_x(net, g, ev['got_g']))
+                yield [ev['got_u'], grad]
+                yield [net.grant(0, 'xp')]
+                net.spawn(gather_x(net, g, ev['got_g'], pool=act_pool.again()))
 
             def second():
-                yield [ev['sent_up0'], ev['sent_down0'], ev['blocks1']]
+                yield [ev['got_down0']]
+                credit = net.grant(1, 'yz')
+                yield [ev['sent_up0'], ev['sent_down0'], ev['blocks1'], credit]
                 gather('down1', down_in.at[1], down1, False)
-                yield [ev['sent_down1']]
+                yield [ev['got_up0']]
+                credit = net.grant(2, 'yz')
+                yield [ev['sent_down1'], credit]
                 gather('up1', block_out.at[1], up1, True)
 
             def save(event, *pairs):
@@ -871,6 +912,7 @@
             inputs = [net.load(u_in, u.at[net.data]), net.load(up_in, up1), net.load(ds_in, ds)]
             inputs[0].wait()
             inputs[0].waited = True
+            net.free_locals.append(inputs[0].slot)
             net.enter()
             rx_scratch = scratch[:5]
             stages = (scratch[21:24], scratch[24:27])
@@ -888,11 +930,13 @@
 
             here = {step: Event(name='u%d' % step) for step in STEPS}
             dy_here = {step: Event() for step in STEPS}
-            net.spawn(gather_x(net, u, ev['got_u'], chips=here))
+            ag_pool, rs_pool = Pool(), Pool()
+            job_pools = [[Pool(), Pool()], [Pool(), Pool()]]
+            net.spawn(gather_x(net, u, ev['got_u'], chips=here, pool=ag_pool))
             net.spawn(gather_yz(net, w_down_in.at[0], down0, 'z', ev['got_down0'], near=True))
             net.spawn(gather_yz(net, block_in.at[0, pl.ds(0, top)], up0, 'y', ev['got_up0']))
             net.spawn(gather_yz(net, block_in.at[0, pl.ds(top, nd * ur - top)], up0, 'z', ev['got_up0_rest'], offset=top))
-            net.spawn(reduce_x(net, part, made, rx_scratch, ev['reduced']))
+            net.spawn(reduce_x(net, part, made, rx_scratch, ev['reduced'], rs_pool))
             frees = [[Event(0.0) for _ in range(3)] for _ in range(2)]
 
             def up_place(ref, k):
@@ -907,12 +951,13 @@
                 for k in range(2):
                     start = Event()
                     ev['start_%s%d' % (name, k)] = start
-                    net.spawn(gate(start, ready + ([credits[k]] if credits else [])))
-                    net.spawn(jobs[n][k].run(place(ref, k), start, ev['sum_%s%d' % (name, k)], frees[k], passed[k]))
+                    net.spawn(gate(start, ready + ([credits[k]] if credits else []), job_pools[n][k]))
+                    net.spawn(jobs[n][k].run(place(ref, k), start, ev['sum_%s%d' % (name, k)], frees[k], passed[k], job_pools[n][k]))
                 return passed
 
-            def gate(event, items):
+            def gate(event, items, pool):
                 yield items
+                pool.again()
                 fire(net, event)
 
             left = [RING, RING]
@@ -947,7 +992,7 @@
                 yield [ev['reduced'], credit]
                 norm_back_rows(x_ref, g_own, part.at[3, net.core], u.at[net.data])
                 net.spend(0.7)
-                net.spawn(gather_x(net, u, ev['got_dy'], ev['sent_dy'], dy_here))
+                net.spawn(gather_x(net, u, ev['got_dy'], ev['sent_dy'], dy_here, pool=ag_pool.again()))
 
             def layer1_out():
                 yield [ev['all_du'], ev['d_up1']]
@@ -965,7 +1010,7 @@
                 yield loads
                 fire(net, ev['acts'])
                 yield [ev['sent_dy'], credit]
-                net.spawn(reduce_x(net, part, y_made, rx_scratch, ev['y_reduced']))
+                net.spawn(reduce_x(net, part, y_made, rx_scratch, ev['y_reduced'], rs_pool.again()))
                 for k in range(RING):
                     fire(net, y_made[k])
                 yield [ev['y_reduced']]
@@ -996,7 +1041,7 @@
                 yield [ev['y_reduced'], ev['got_up0'], ev['got_up0_rest'], Event(0.0, 2)]
                 net.drain(ev['y_reduced'].copies)
                 yield [net.grant(2, 'xp')]
-                net.spawn(reduce_x(net, part, du_made, rx_scratch, ev['du_reduced']))
+                net.spawn(reduce_x(net, part, du_made, rx_scratch, ev['du_reduced'], rs_pool.again()))
                 for k, step in enumerate(STEPS):
                     input_back_rows(net, net.at('x', step), ds, up0, part.at[k])
                     fire(net, du_made[k])
@@ -1070,12 +1115,12 @@
                       own, act_full, hid_full, shape((len(FAR), dr, width), BF16), own],
             'hhhhhhhhhhv', 'vhvh',
             [pltpu.VMEM((num_layers, nd, ur, hidden), BF16), vmem(own)] + [vmem(act_full)] * 2 + [vmem(up_full), vmem(down_full)] * 2 + [vmem(hid_full)] * 3 + rx,
-            320, 64, 0, tokens, grad_out, w_up, w_down)
+            KR, KS, KL, 0, tokens, grad_out, w_up, w_down)
         d_up_full, d_down_full = shape((width, hidden), F32), shape((hidden, width), F32)
         x_out, dx, _, _, _, _, *grads = call(
             turn, [own, own] + [d_up_full, d_down_full] * 2 + [d_up_own, d_down_own] * 2, 'vv' + 'h' * 8, 'hhhhhhhhhvvvhh',
             [pltpu.VMEM((nd * ur, hidden), F32), vmem(act_full), vmem(up_full), vmem(up_full), vmem(down_full), pltpu.VMEM((nd, rows, width // 2), BF16), vmem(hid_full), vmem(hid_full),
-             pltpu.VMEM((2, hidden // 2, width // 2), F32)] + rx + sums, 400, 160, 1,
+             pltpu.VMEM((2, hidden // 2, width // 2), F32)] + rx + sums, TR, TS, TL, 1,
             u1, up1, down1, ds1, g_full, u0, a0, s0, keep, x1, tokens, grad_out, blocks, w_down)
         up1_own, down1_own, up0_own, down0_own = grads
         return pl.pallas_call(

time: 337 us -> 326 us (0.967)
  Pallas kernels: 336 us -> 324 us
    pallas_call x2, Pallas kernels: 331 us -> 320 us  [call(): pl.pallas_call(kernel, out_shape=out_shape, in_specs=[spaces[s] for s in...]
where the time goes in v8:
time: 326 us; the launch traced here: 325 us
  Pallas kernels  324 us (99%)
    pallas_call x2, Pallas kernels, call(): pl.pallas_call(kernel, out_shape=out_shape, in_specs=[spaces[s] for s in...  320 us

profile of v8, /device:TPU:1, one launch (start us, length us, event | category | flops | bytes accessed | tf_op | source)
XLA Modules:
  0.0 324.9 jit_solution(11524647485697379734)
XLA Ops:
  0.6 102.1 %forward.1 = (bf16[2,128,1024]{2,1,0:T(8,128)(2,1)}, bf16[8,128,2048]{2,1,0:T(8,128)(2,1)}, bf16[8,128,1024]{2,1,0:T(8,128)(2,1)}, bf16[8,128,1024]{2,1,0:T(8,12...) custom-call(bf16[128,2048]{1,0:T(8,128)(2,1)} %refs_10_.1, ...), custom_call_target="tpu_custom_call" | custom-call | flops 100000000 | bytes 10000000 | tf_op jit(solution)/shard_map/forward/pallas_call | solution.py:638
  102.7 218.1 %turn.1 = (bf16[128,2048]{1,0:T(8,128)(2,1)}, bf16[128,2048]{1,0:T(8,128)(2,1)}, f32[2048,1024]{1,0:T(8,128)}, f32[1024,2048]{1,0:T(8,128)}, f32[2048,1024]{1,0:...) custom-call(bf16[128,2048]{1,0:T(8,128)(2,1)} %get-tuple-element.21., ...), custom_call_target="tpu_custom_call" | custom-call | flops 100000000 | bytes 10000000 | tf_op jit(solution)/shard_map/turn/pallas_call | solution.py:638
  320.8 4.1 %finish.1 = (bf16[128,2048]{1,0:T(8,128)(2,1)}, bf16[128,2048]{1,0:T(8,128)(2,1)}, f32[2,16,8192]{2,1,0:T(8,128)}, f32[2,64,2048]{2,1,0:T(8,128)}) custom-call(f32[8,16,1024]{2,1,0:T(8,128)} %get-tuple-element.32.up1_ref, f32[8,16,1024]{2,1,0:T(8,128)} %get-tuple-element.33.up0_ref, f32[64,2048]{1,0:T(8,128)} %get-tuple-element.34.down1_ref, ...), custom_call_target="tpu_custom_call" | custom-call | tf_op jit(solution)/shard_map/finish/pallas_call | solution.py:1126

commit v9 on v8

--- a/solution.py
+++ b/solution.py
@@ -73,26 +73,32 @@
         self.sent = []
         self.flows = []
         self.labels = {}
-        here = lax.axis_index('local')
-        there = lax.axis_index('data')
-        self.data = there
-        self.pos = {'z': here // RING, 'y': here % RING, 'x': there // 2}
-        self.core = there % 2
+        here, there = lax.axis_index('local'), lax.axis_index('data')
+        pos = {'z': here // RING, 'y': lax.rem(here, RING), 'x': there // 2}
+        self.data, self.core = there, lax.rem(there, 2)
+        self.ring = {axis: [at] + [lax.rem(at + step, RING) for step in range(1, RING)] for axis, at in pos.items()}
+        self.hops = [there] + [lax.rem(there + step, 2 * RING) for step in range(1, 2 * RING)]
+        self.blocks = [at * 2 + self.core for at in self.ring['x']]
+        self.places = [[z * RING + y for y in self.ring['y']] for z in self.ring['z']]
+        self.partner = pos['x'] * 2 + (1 - self.core)
+        self.other = 1 - self.core
 
     def at(self, axis, step):
-        return (self.pos[axis] + (step + RING)) % RING
+        return self.ring[axis][step % RING]
+
+    def block(self, step):
+        return self.blocks[step % RING]
 
     def device(self, axis, step):
         if axis == 'p':
-            return {'data': self.pos['x'] * 2 + (1 - self.core)}
+            return {'data': self.partner}
         if axis == 'd':
-            return {'data': (self.data + step) % (2 * RING)}
-        to = self.at(axis, step)
+            return {'data': self.hops[step % (2 * RING)]}
         if axis == 'x':
-            return {'data': to * 2 + self.core}
+            return {'data': self.block(step)}
         if axis == 'y':
-            return {'local': self.pos['z'] * RING + to}
-        return {'local': to * RING + self.pos['y']}
+            return {'local': self.places[0][step % RING]}
+        return {'local': self.places[step % RING][0]}
 
     def peers(self, axes):
         return [(axis, step) for axis in axes for step in ((1, -1) if axis in 'xyz' else (1,) if axis == 'p' else range(1, 2 * RING))]
@@ -108,6 +114,13 @@
     def enter(self):
         pl.semaphore_wait(self.entry, self.entered)
         self.now = max(self.now, ENTRY)
+
+    def take(self, copies):
+        for copy in copies:
+            copy.wait()
+            copy.waited = True
+            self.free_locals.append(copy.slot)
+            self.now = max(self.now, copy.time)
 
     def grant(self, k, axes):
         self.signal(self.credit_sems.at[k], axes)
@@ -257,26 +270,28 @@
         print('   %7.1f %s' % (net.now, event.name))
 
 
-def exchange(net, src, dst, done):
-    rows = src.shape[1]
+def exchange(net, source, dst, done):
+    rows = dst.shape[0] // (2 * RING)
 
     def mine():
         return dst.at[pl.ds(pl.multiple_of(net.data * rows, rows), rows)]
 
-    own = net.load(src.at[net.data], mine())
-    copies = [net.send(src.at[(net.data + k) % (2 * RING)], mine(), 'd', k) for k in (4, 5, 2, 3, 6, 7, 1)]
+    own = net.load(source(net.data), mine())
+    copies = [net.send(source(net.hops[k]), mine(), 'd', k) for k in (4, 5, 2, 3, 6, 7, 1)]
     yield [own] + copies
+    net.drain(copies)
     fire(net, done)
 
 
 def exchange_back(net, src, dst, done):
     rows = dst.shape[1]
+    per = src.shape[1] // rows
 
     def block(k):
-        return src.at[pl.ds(pl.multiple_of(k * rows, rows), rows)]
+        return src.at[lax.div(k, per), pl.ds(pl.multiple_of(lax.rem(k, per) * rows, rows), rows)]
 
     own = net.load(block(net.data), dst.at[net.data])
-    copies = [net.send(block((net.data + k) % (2 * RING)), dst.at[net.data], 'd', k) for k in (4, 5, 2, 3, 6, 7, 1)]
+    copies = [net.send(block(net.hops[k]), dst.at[net.data], 'd', k) for k in (4, 5, 2, 3, 6, 7, 1)]
     yield [own] + copies
     net.drain(copies)
     fire(net, done)
@@ -302,10 +317,10 @@
         return done.copies[-1]
 
     def block(step):
-        return full.at[net.at('x', step) * 2 + net.core]
+        return full.at[net.block(step)]
 
     def part(step, rows):
-        return full.at[net.at('x', step) * 2 + net.core, rows]
+        return full.at[net.block(step), rows]
 
     relays = []
 
@@ -341,6 +356,12 @@
 
 def gather_yz(net, own, full, first, done, issued=None, offset=0, near=False, split=True, pool=None):
     second = 'y' if first == 'z' else 'z'
+    done.copies = []
+
+    def emit(*args):
+        done.copies.append(net.send(*args, pool=pool))
+        return done.copies[-1]
+
     size = own.shape[0]
     half = size // 2
     lo, hi, both = pl.ds(offset, half), pl.ds(offset + half, half), pl.ds(offset, size)
@@ -358,7 +379,7 @@
 
     def send(one, rows, axis, step):
         src = own.at[pl.ds(rows.start - offset, rows.size)] if one == 0 else part(one, 0, rows)
-        return net.send(src, part(one, 0, rows), axis, step, pool)
+        return emit(src, part(one, 0, rows), axis, step)
 
     def column(one):
         forth = [send(one, rows, second, 1) for rows in forward]
@@ -370,9 +391,9 @@
                 yield forth + back
             else:
                 yield [forth[0]]
-                relays = [net.send(part(one, -1, lo), part(one, -1, lo), second, 1, pool)]
+                relays = [emit(part(one, -1, lo), part(one, -1, lo), second, 1)]
                 yield [back[0]]
-                relays.append(net.send(part(one, 1, hi), part(one, 1, hi), second, -1, pool))
+                relays.append(emit(part(one, 1, hi), part(one, 1, hi), second, -1))
                 arrived(1)
                 yield forth[1:] + back[1:] + relays
             arrived(0)
@@ -384,7 +405,7 @@
     def side(step, first_half, mine):
         yield [mine[0]]
         if not near:
-            relays.append(net.send(part(step, 0, first_half), part(step, 0, first_half), first, -step, pool))
+            relays.append(emit(part(step, 0, first_half), part(step, 0, first_half), first, -step))
             if len(relays) == 2:
                 net.spawn(far())
         yield mine[1:]
@@ -406,8 +427,7 @@
 
 
 def yz_index(net, first, one, two):
-    at_one, at_two = net.at(first, one), net.at('y' if first == 'z' else 'z', two)
-    return at_one * RING + at_two if first == 'z' else at_two * RING + at_one
+    return net.places[one % RING][two % RING] if first == 'z' else net.places[two % RING][one % RING]
 
 
 FAR = [(2, 0), (2, 1), (2, -1), (2, 2), (0, 2), (1, 2), (-1, 2)]
@@ -430,7 +450,7 @@
 
     def pair(k):
         yield [made[k]]
-        pairs[k] = net.send(part.at[k, 1 - net.core], other.at[k], 'p', pool=pool)
+        pairs[k] = net.send(part.at[k, net.other], other.at[k], 'p', pool=pool)
         yield [pairs[k]]
         add_into(net, acc(k), other.at[k])
         fire(net, ready[k])
@@ -579,13 +599,13 @@
     rows_loop(x_ref.shape[0], 16, body)
 
 
-def norm_back_rows(x_ref, dy_ref, du_ref, dx_ref):
+def norm_back_rows(x_ref, dy_of, du_ref, dx_ref):
     def body(at):
         x = x_ref[at, :].astype(F32)
         du = du_ref[at, :]
         r = lax.rsqrt(jnp.mean(x * x, axis=-1, keepdims=True) + NORM_EPS)
         xr = x * r
-        dx_ref[at, :] = (dy_ref[at, :].astype(F32) + r * (du - xr * jnp.mean(xr * du, axis=-1, keepdims=True))).astype(BF16)
+        dx_ref[at, :] = (dy_of(at).astype(F32) + r * (du - xr * jnp.mean(xr * du, axis=-1, keepdims=True))).astype(BF16)
 
     rows_loop(x_ref.shape[0], 16, body)
 
@@ -604,14 +624,18 @@
     return jnp.where(low, even, pltpu.roll(odd, shift, axis)), jnp.where(low, pltpu.roll(even, shift, axis), odd)
 
 
-def split_columns(w_ref, cols_ref):
-    tile = w_ref.shape[2] // (4 * RING * RING)
-    for l in range(w_ref.shape[0]):
-        for x in range(RING):
-            for p in range(cols_ref.shape[3] // tile):
-                pair = [w_ref[l, :, pl.ds((i * RING + x) * tile, tile)].astype(F32) for i in (2 * p, 2 * p + 1)]
-                for c, value in enumerate(swap_halves(*pair)):
-                    cols_ref[l, 2 * x + c, :, pl.ds(p * tile, tile)] = value.astype(cols_ref.dtype)
+def split_columns(w_ref, cols_ref, layers):
+    pieces, _, wide = w_ref.shape
+    rows = layers
+    tile = pieces * wide // (4 * RING * RING)
+    for x in range(RING):
+        for p in range(wide // tile):
+            pair = []
+            for i in (2 * p, 2 * p + 1):
+                at = (i * RING + x) * tile
+                pair.append(w_ref[at // wide, pl.ds(0, rows), pl.ds(at % wide, tile)].astype(F32))
+            for c, value in enumerate(swap_halves(*pair)):
+                cols_ref[2 * x + c, pl.ds(0, rows), pl.ds(p * tile, tile)] = value.astype(cols_ref.dtype)
 
 
 def join_columns(cols_ref, w_ref):
@@ -638,7 +662,7 @@
     return pl.pallas_call(
         kernel, out_shape=out_shape, in_specs=[spaces[s] for s in in_spaces], out_specs=[spaces[s] for s in out_spaces],
         scratch_shapes=list(scratch) + [pltpu.SemaphoreType.DMA((sends,)), pltpu.SemaphoreType.DMA((remote,)), pltpu.SemaphoreType.DMA((local,)),
-                                               pltpu.SemaphoreType.REGULAR((8,)), pltpu.SemaphoreType.DMA((2,))],
+                                               pltpu.SemaphoreType.REGULAR((14,)), pltpu.SemaphoreType.DMA((2,))],
         compiler_params=pltpu.CompilerParams(collective_id=collective_id, has_side_effects=True, vmem_limit_bytes=67000000),
         cost_estimate=pl.CostEstimate(flops=10**8, bytes_accessed=10**7, transcendentals=0),
         name=body.__name__)(*args)
@@ -649,8 +673,7 @@
 
 
 WIDE = 512
-KR, KS, KL = 134, 64, 10
-TR, TS, TL = 222, 64, 13
+TR, TS, TL = 268, 64, 19
 GR = 2
 DU = 3
 
@@ -760,20 +783,20 @@
 
 def stored_tiles(net, count, compute, stage, out):
     def store(t):
-        return pltpu.make_async_copy(stage.at[t % 2], out(t), net.tile_sems.at[t % 2])
+        return pltpu.make_async_copy(stage.at[lax.rem(t, 2)], out(t), net.tile_sems.at[lax.rem(t, 2)])
 
     def step(t, carry):
         @pl.when(t >= 2)
         def _():
             store(t - 2).wait()
 
-        compute(t, stage.at[t % 2])
+        compute(t, stage.at[lax.rem(t, 2)])
         store(t).start()
         return carry
 
     lax.fori_loop(0, count, step, 0)
     for t in range(max(count - 2, 0), count):
-        store(t).wait()
+        store(jnp.int32(t)).wait()
 
 
 def dot_tokens(a, b):
@@ -813,22 +836,46 @@
         def vmem(like):
             return pltpu.VMEM(like.shape, like.dtype)
 
-        def forward(net, x_ref, g_in, w_up_ref, down_in, block_out, u_out, a_out, s_out, up_out, down_out, next_out, g_out, ds_out, keep_out, x_out,
-                    cols, next_own, u, g, up0, down0, up1, down1, a, s, ds, part, *rx_scratch):
+        def step(net, x_in, x_halves, g_in, w_up_in, w_down_in,
+                 x_out, dx_out, block_out, u_out, a_out, s_out, d_up0, d_down0, d_up1, d_down1, dw_up1, dw_down1, dw_up0, dw_down0,
+                 x, u, g, up0, up1, down0, down1, ds, s, stage, part, *scratch):
             net.arrive('dyz')
-            names = ('blocks', 'blocks1', 'sent_u', 'got_u', 'got_g', 'sent_up0', 'sent_down0', 'sent_up1', 'sent_down1', 'got_up0', 'got_down0', 'got_up1', 'got_down1', 'reduced')
+            rx_scratch = scratch[:5]
+            names = ('blocks', 'blocks1', 'sent_u', 'got_u', 'got_g', 'sent_up0', 'sent_down0', 'sent_up1', 'sent_down1', 'got_up0', 'got_down0',
+                     'got_up1', 'got_down1', 'saved', 'free0', 'reduced0', 'ds_made', 'got_u1', 'hidden', 'all_du', 'reduced1', 'sent_dy', 'got_dy',
+                     'back_up0', 'back_up0_rest', 'back_down0', 'd_down1', 'd_up1', 'y_reduced', 'acts', 'd_down0', 'da0', 'd_up0', 'du_reduced',
+                     'out_up1', 'out_up0', 'got_u0', 'y_made', 'x_saved')
             ev = {name: Event(name=name) for name in names}
+            for kind in ('up', 'down'):
+                for layer in range(2):
+                    for k in range(2):
+                        ev['sum_%s%d%d' % (kind, layer, k)] = Event(name='sum_%s%d%d' % (kind, layer, k))
             ev['got_up0'].rank = 2
-            made = [Event(name='made%d' % k) for k in range(RING)]
-            hidden_made = [Event(name='hidden%d' % k) for k in range(RING)]
+            hidden_made, made0, made1, y_made, du_made = ([Event(name='%s%d' % (name, k)) for k in range(RING)]
+                                                          for name in ('hidden_', 'made0_', 'made1_', 'y_made_', 'du_made_'))
+            wide = width // 2
+            half_up = nd * ur // 2
             pools = {name: [Pool(), Pool()] for name in ('up', 'down')}
-            act_pool = Pool()
+            act_pool, rs_pool = Pool(), Pool()
+            job_pools = [[Pool(), Pool()], [Pool(), Pool()]]
+            stages = (scratch[21:24], scratch[24:27])
+            jobs = [[Sums(net, first, scratch[5 + 8 * n + 4 * k:9 + 8 * n + 4 * k], stages[k]) for k, first in enumerate('yz')] for n in range(2)]
+            frees = [[Event(0.0) for _ in range(3)] for _ in range(2)]
+            freed = {k: Event() for k in range(10, 14)}
+
+            def columns(h):
+                return pl.ds(h * wide, wide)
+
+            inputs = [net.load(x_in, x)]
+            inputs += [net.load(w_up_in.at[l, :, pl.ds(k * hidden, hidden)], ds.at[k, pl.ds(l * ur, ur)]) for l in range(num_layers) for k in range(nd)]
 
             def gather(name, own, full, split):
                 size = own.shape[0] // 2
 
                 def join(kind, events):
                     yield events
+                    if kind == 'got_':
+                        ev[kind + name].copies = events[0].copies + events[1].copies
                     fire(net, ev[kind + name])
 
                 got, sent = [Event(), Event()], [Event(), Event()]
@@ -838,21 +885,22 @@
                 net.spawn(join('sent_', sent))
 
             net.enter()
-            gather('down0', down_in.at[0], down0, False)
-            split_columns(w_up_ref, cols)
+            gather('down0', w_down_in.at[0], down0, False)
+            net.take(inputs)
+            split_columns(ds, s, num_layers * ur)
             net.spend(0.5)
-            net.spawn(exchange(net, cols.at[0], block_out.at[0], ev['blocks']))
-            norm_rows(x_ref, u.at[net.data])
+            net.spawn(exchange(net, lambda k: s.at[k, pl.ds(0, ur)], block_out.at[0], ev['blocks']))
+            norm_rows(x, u.at[net.data])
             net.spend(0.7)
-            grad = net.load(g_in, g.at[net.data])
+            own_grads = net.load(g_in, g.at[net.data])
 
             def up_first():
                 yield [ev['blocks']]
                 gather('up0', block_out.at[0], up0, True)
                 net.spawn(gather_x(net, u, ev['got_u'], ev['sent_u'], pool=act_pool))
                 yield [ev['sent_u']]
-                net.spawn(exchange(net, cols.at[1], block_out.at[1], ev['blocks1']))
-                yield [ev['got_u'], grad]
+                net.spawn(exchange(net, lambda k: s.at[k, pl.ds(ur, ur)], block_out.at[1], ev['blocks1']))
+                yield [ev['got_u'], own_grads]
                 yield [net.grant(0, 'xp')]
                 net.spawn(gather_x(net, g, ev['got_g'], pool=act_pool.again()))
 
@@ -860,125 +908,82 @@
                 yield [ev['got_down0']]
                 credit = net.grant(1, 'yz')
                 yield [ev['sent_up0'], ev['sent_down0'], ev['blocks1'], credit]
-                gather('down1', down_in.at[1], down1, False)
+                gather('down1', w_down_in.at[1], down1, False)
                 yield [ev['got_up0']]
                 credit = net.grant(2, 'yz')
                 yield [ev['sent_down1'], credit]
                 gather('up1', block_out.at[1], up1, True)
 
-            def save(event, *pairs):
-                yield [ev[event]]
-                yield [net.save(src, dst) for src, dst in pairs]
-
             def hidden_flow():
-                yield [ev['got_u'], ev['got_up0']]
+                yield [ev['got_u'], ev['got_up0'], ev['blocks1']]
                 for k, step in enumerate(STEPS):
-                    hidden_rows(net, net.at('x', step), u, up0, a, s)
+                    hidden_rows(net, net.at('x', step), u, up0, ds, s)
                     fire(net, hidden_made[k])
                     yield [Event(net.now, 2)]
-                yield [net.save(a, a_out), net.save(s, s_out), net.save(u, u_out)]
+                yield [net.load(ds, a_out), net.load(s, s_out), net.load(u, u_out)]
+                fire(net, ev['saved'])
 
             def down_flow():
                 for k, step in enumerate(STEPS):
                     yield [hidden_made[k], ev['got_down0'], Event(0.0, 1)]
                     down_rows(net, net.at('x', step), s, down0, part.at[k])
-                    fire(net, made[k])
-                yield [net.save(down0.at[yz_index(net, 'z', *far)], keep_out.at[k]) for k, far in enumerate(FAR)]
-
-            def act():
-                yield [ev['reduced']]
-                add_rows(x_ref, part.at[3, net.core], x_out)
-                norm_rows(x_out, next_own)
+                    fire(net, made0[k])
+                fire(net, ev['free0'])
+
+            net.spawn(reduce_x(net, part, made0, rx_scratch, ev['reduced0'], rs_pool))
+            here = {step: Event(name='u%d' % step) for step in STEPS}
+            dy_here = {step: Event() for step in STEPS}
+
+            def next_layer():
+                yield [ev['saved'], ev['got_g']]
+                net.drain(ev['got_u'].copies + ev['got_g'].copies)
+                credit = net.grant(3, 'xp')
+                yield [ev['reduced0'], credit]
+                add_rows(x, part.at[3, net.core], x)
+                norm_rows(x, u.at[net.data])
                 net.spend(1.0)
-                yield [net.load(next_own, next_out)]
+                net.spawn(gather_x(net, u, ev['got_u1'], chips=here, pool=act_pool.again()))
+                net.drain(ev['reduced0'].copies)
+                yield [net.grant(4, 'xp')]
+                net.spawn(reduce_x(net, part, made1, rx_scratch, ev['reduced1'], rs_pool.again()))
 
             def back_flow():
                 for k, step in enumerate(STEPS):
-                    yield [ev['got_g'], ev['got_down1'], Event(0.0, 3)]
+                    yield [ev['got_g'], ev['got_down1'], ev['saved'], Event(0.0, 3)]
                     hidden_back_rows(net, net.at('x', step), g, down1, ds)
-                yield [net.load(ds, ds_out)]
-
-            half = down_out.shape[3]
-            for flow in (up_first(), second(), hidden_flow(), down_flow(), act(), back_flow(), reduce_x(net, part, made, rx_scratch, ev['reduced']),
-                         save('got_up1', (up1, up_out)), save('got_down1', *[(down1.at[:, :, pl.ds(h * half, half)], down_out.at[h]) for h in range(2)]),
-                         save('got_g', (g, g_out))):
-                net.spawn(flow)
-            net.run()
-
-        def turn(net, u_in, up_in, down_in, ds_in, g_in, u0_in, a0_in, s0_in, keep_in, x_ref, x0_ref, g_own, block_in, w_down_in,
-                 x_out, dx_out, d_up0, d_down0, d_up1, d_down1, dw_up1, dw_down1, dw_up0, dw_down0,
-                 own_up, u, up1, up0, down0, half_in, ds, s, stage, part, *scratch):
-            net.arrive('dyz')
-            inputs = [net.load(u_in, u.at[net.data]), net.load(up_in, up1), net.load(ds_in, ds)]
-            inputs[0].wait()
-            inputs[0].waited = True
-            net.free_locals.append(inputs[0].slot)
-            net.enter()
-            rx_scratch = scratch[:5]
-            stages = (scratch[21:24], scratch[24:27])
-            jobs = [[Sums(net, first, scratch[5 + 8 * n + 4 * k:9 + 8 * n + 4 * k], stages[k]) for k, first in enumerate('yz')] for n in range(2)]
-            names = ('got_u', 'hidden', 'all_du', 'reduced', 'sent_dy', 'got_dy', 'got_up0', 'got_up0_rest', 'got_down0', 'd_down1', 'd_up1', 'y_reduced', 'acts',
-                     'd_down0', 'da0', 'd_up0', 'du_reduced', 'out_up1', 'out_up0') + tuple(
-                'sum_%s%d%d' % (kind, layer, k) for kind in ('up', 'down') for layer in range(2) for k in range(2))
-            ev = {name: Event(name=name) for name in names}
-            made, y_made, du_made = ([Event(name='%s%d' % (name, k)) for k in range(RING)] for name in ('made', 'y_made', 'du_made'))
-            wide = half_in.shape[2]
-            top = nd * ur * 3 // 4
-
-            def columns(h):
-                return pl.ds(h * wide, wide)
-
-            here = {step: Event(name='u%d' % step) for step in STEPS}
-            dy_here = {step: Event() for step in STEPS}
-            ag_pool, rs_pool = Pool(), Pool()
-            job_pools = [[Pool(), Pool()], [Pool(), Pool()]]
-            net.spawn(gather_x(net, u, ev['got_u'], chips=here, pool=ag_pool))
-            net.spawn(gather_yz(net, w_down_in.at[0], down0, 'z', ev['got_down0'], near=True))
-            net.spawn(gather_yz(net, block_in.at[0, pl.ds(0, top)], up0, 'y', ev['got_up0']))
-            net.spawn(gather_yz(net, block_in.at[0, pl.ds(top, nd * ur - top)], up0, 'z', ev['got_up0_rest'], offset=top))
-            net.spawn(reduce_x(net, part, made, rx_scratch, ev['reduced'], rs_pool))
-            frees = [[Event(0.0) for _ in range(3)] for _ in range(2)]
-
-            def up_place(ref, k):
-                half = nd * ur // 2
-                return lambda block, rows: ref.at[pl.ds(pl.multiple_of(block * (2 * half) + k * half + rows.start, rows.size), rows.size)]
-
-            def down_place(ref, k):
-                return lambda block, rows: ref.at[pl.ds(pl.multiple_of(block * dr + rows.start, rows.size), rows.size), columns(k)]
-
-            def sum_job(n, place, ref, ready, name, credits=()):
-                passed = [Event(), Event()]
-                for k in range(2):
-                    start = Event()
-                    ev['start_%s%d' % (name, k)] = start
-                    net.spawn(gate(start, ready + ([credits[k]] if credits else []), job_pools[n][k]))
-                    net.spawn(jobs[n][k].run(place(ref, k), start, ev['sum_%s%d' % (name, k)], frees[k], passed[k], job_pools[n][k]))
-                return passed
-
-            def gate(event, items, pool):
-                yield items
-                pool.again()
-                fire(net, event)
+                fire(net, ev['ds_made'])
+
+            def again():
+                top = nd * ur * 3 // 4
+                yield [ev['free0'], ev['got_down1'], ev['ds_made']]
+                net.drain(ev['got_up0'].copies + ev['got_down0'].copies)
+                credit = net.grant(6, 'yz')
+                yield [ev['sent_up1'], credit]
+                net.spawn(gather_yz(net, w_down_in.at[0], down0, 'z', ev['back_down0'], near=True, pool=pools['down'][1].again()))
+                yield [ev['got_up1']]
+                yield [net.grant(7, 'yz')]
+                net.spawn(gather_yz(net, block_out.at[0, pl.ds(0, top)], up0, 'y', ev['back_up0'], pool=pools['up'][0].again()))
+                net.spawn(gather_yz(net, block_out.at[0, pl.ds(top, nd * ur - top)], up0, 'z', ev['back_up0_rest'], offset=top, pool=pools['up'][1].again()))
 
             left = [RING, RING]
 
             def layer1(k, step):
-                yield [here[step], Event(0.0, 1)] + inputs[1:]
+                yield [here[step], ev['ds_made'], ev['got_up1'], Event(0.0, 1)]
                 hidden_turn_rows(net, net.at('x', step), u, up1, s, ds)
                 left[0] -= 1
                 if left[0] == 0:
                     fire(net, ev['hidden'])
                 yield [Event(net.now, DU)]
                 input_back_rows(net, net.at('x', step), ds, up1, part.at[k])
-                fire(net, made[k])
+                fire(net, made1[k])
                 left[1] -= 1
                 if left[1] == 0:
                     fire(net, ev['all_du'])
 
             def grads1():
                 for h in range(2):
-                    yield [net.load(g_in.at[:, :, columns(h)], half_in), Event(0.0, GR), ev['hidden']]
-                    grad_tiles(net, s, half_in, stage, d_down1.at[:, columns(h)])
+                    yield [Event(0.0, GR), ev['hidden']]
+                    grad_tiles(net, s, g.at[:, :, columns(h)], stage, d_down1.at[:, columns(h)])
                 fire(net, ev['d_down1'])
                 for h in range(2):
                     yield [Event(net.now, GR)]
@@ -986,68 +991,96 @@
                 fire(net, ev['d_up1'])
 
             def act():
-                yield [ev['d_up1'], ev['got_u']]
-                net.drain(ev['got_u'].copies)
-                credit = net.grant(0, 'xp')
-                yield [ev['reduced'], credit]
-                norm_back_rows(x_ref, g_own, part.at[3, net.core], u.at[net.data])
+                yield [ev['d_up1'], ev['all_du'], ev['got_u1']]
+                own_g = [net.load(g_in.at[:, columns(h)], ds.at[h]) for h in range(2)]
+                net.drain(ev['got_u1'].copies)
+                credit = net.grant(5, 'xp')
+                yield [ev['reduced1'], credit] + own_g
+                norm_back_rows(x, lambda at: jnp.concatenate([ds[h, at, :] for h in range(2)], axis=-1), part.at[3, net.core], u.at[net.data])
                 net.spend(0.7)
-                net.spawn(gather_x(net, u, ev['got_dy'], ev['sent_dy'], dy_here, pool=ag_pool.again()))
+                net.spawn(gather_x(net, u, ev['got_dy'], ev['sent_dy'], dy_here, pool=act_pool.again()))
 
             def layer1_out():
-                yield [ev['all_du'], ev['d_up1']]
-                yield [net.load(down_in.at[h], up1.at[:, pl.ds(h * dr, dr)]) for h in range(2)]
-                yield [ev['reduced'], Event(0.0, 2)]
-                net.drain(ev['reduced'].copies)
-                credit = net.grant(1, 'xp')
+                yield [ev['reduced1'], Event(0.0, 2)]
+                net.drain(ev['reduced1'].copies)
+                credit = net.grant(8, 'xp')
                 for k, step in enumerate(STEPS):
-                    for h in range(2):
-                        net.spend(-0.88)
-                        down_rows(net, net.at('x', step), s, up1.at[:, pl.ds(h * dr, dr)], part.at[k, :, :, columns(h)])
+                    down_rows(net, net.at('x', step), s, down1, part.at[k])
                     yield [Event(net.now, 2)]
-                loads = [net.load(a0_in, up1.at[pl.ds(0, nd)]), net.load(s0_in, up1.at[pl.ds(nd, nd)])]
-                loads += [net.load(keep_in.at[k], down0.at[yz_index(net, 'z', *far)]) for k, far in enumerate(FAR)]
-                yield loads
-                fire(net, ev['acts'])
+                fire(net, ev['y_made'])
                 yield [ev['sent_dy'], credit]
                 net.spawn(reduce_x(net, part, y_made, rx_scratch, ev['y_reduced'], rs_pool.again()))
                 for k in range(RING):
                     fire(net, y_made[k])
                 yield [ev['y_reduced']]
-                add_rows(x_ref, part.at[3, net.core], x_out)
+                add_rows(x, part.at[3, net.core], x)
+                yield [net.load(x, x_out)]
+                fire(net, ev['x_saved'])
 
             a0, s0 = up1.at[pl.ds(0, nd)], up1.at[pl.ds(nd, nd)]
             backs = [RING]
 
+            def bring_back():
+                yield [ev['d_down1']]
+                yield [net.load(u_out, g)]
+                fire(net, ev['got_u0'])
+
+            def bring_acts():
+                yield [ev['all_du']]
+                net.drain(ev['got_up1'].copies)
+                yield [net.load(a_out, a0), net.load(s_out, s0)]
+                fire(net, ev['acts'])
+
             def layer0_hidden(step):
-                yield [dy_here[step], ev['acts'], ev['got_down0'], Event(0.0, 2)]
+                yield [dy_here[step], ev['acts'], ev['back_down0'], ev['d_up1'], Event(0.0, 2)]
                 pre_back_rows(net, net.at('x', step), u, down0, a0, ds)
                 backs[0] -= 1
                 if backs[0] == 0:
                     fire(net, ev['da0'])
 
             def layer0():
-                yield [ev['d_down1']]
-                first = net.load(u0_in.at[:, :, columns(0)], half_in)
                 for h in range(2):
-                    yield [net.load(u0_in.at[:, :, columns(h)], half_in) if h else first]
-                    yield [ev['da0'], Event(0.0, 3)]
-                    grad_tiles(net, half_in, ds, stage, d_up0.at[columns(h)])
+                    yield [ev['da0'], ev['got_u0'], Event(0.0, 3)]
+                    grad_tiles(net, g.at[:, :, columns(h)], ds, stage, d_up0.at[columns(h)])
                 fire(net, ev['d_up0'])
                 for h in range(2):
                     yield [ev['got_dy'], ev['acts'], Event(0.0, 3)]
                     grad_tiles(net, s0, u.at[:, :, columns(h)], stage, d_down0.at[:, columns(h)])
                 fire(net, ev['d_down0'])
-                yield [ev['y_reduced'], ev['got_up0'], ev['got_up0_rest'], Event(0.0, 2)]
-                net.drain(ev['y_reduced'].copies)
-                yield [net.grant(2, 'xp')]
+                yield [ev['y_reduced'], ev['back_up0'], ev['back_up0_rest'], Event(0.0, 2)]
+                net.drain(ev['y_reduced'].copies + ev['got_down1'].copies)
+                x0 = down1.at[pl.ds(0, x_halves.shape[0])]
+                yield [net.grant(9, 'xp'), net.load(x_halves, x0)]
                 net.spawn(reduce_x(net, part, du_made, rx_scratch, ev['du_reduced'], rs_pool.again()))
                 for k, step in enumerate(STEPS):
                     input_back_rows(net, net.at('x', step), ds, up0, part.at[k])
                     fire(net, du_made[k])
                     yield [Event(net.now, 2)]
-                yield [ev['du_reduced']]
-                norm_back_rows(x0_ref, u.at[net.data], part.at[3, net.core], dx_out)
+                yield [ev['du_reduced'], ev['x_saved']]
+                for q in range(x_halves.shape[0]):
+                    rows_q = pl.ds(q * dr, dr)
+                    dy_q = u.at[net.data, rows_q]
+                    norm_back_rows(x0.at[q], lambda at, dy_q=dy_q: dy_q[at, :], part.at[3, net.core, rows_q], x.at[rows_q])
+                yield [net.load(x, dx_out)]
+
+            def up_place(ref, k):
+                return lambda block, rows: ref.at[pl.ds(pl.multiple_of(block * (2 * half_up) + k * half_up + rows.start, rows.size), rows.size)]
+
+            def down_place(ref, k):
+                return lambda block, rows: ref.at[pl.ds(pl.multiple_of(block * dr + rows.start, rows.size), rows.size), columns(k)]
+
+            def gate(event, items, pool):
+                yield items
+                pool.again()
+                fire(net, event)
+
+            def sum_job(n, place, ref, ready, name, credits=()):
+                passed = [Event(), Event()]
+                for k in range(2):
+                    start = Event()
+                    net.spawn(gate(start, ready + ([credits[k]] if credits else []), job_pools[n][k]))
+                    net.spawn(jobs[n][k].run(place(ref, k), start, ev['sum_%s%d' % (name, k)], frees[k], passed[k], job_pools[n][k]))
+                return passed
 
             def out_down(layer, dw_down, credit):
                 def one(k):
@@ -1062,42 +1095,36 @@
                 for k in range(2):
                     net.spawn(one(k))
 
-            def out_up(layer, dw_up, credit):
-                copied = [Event(), Event()]
-
-                def one(k):
-                    done = ev['sum_up%d%d' % (layer, k)]
+            def out_up(n, layer, dw_up, credit):
+                totals = [ev['sum_up%d%d' % (layer, k)] for k in range(2)]
+                yield totals
+                net.drain(totals[0].copies + totals[1].copies)
+                spare = jobs[n][0].scratch[0].at[0]
+                for k, done in enumerate(totals):
+                    for q in range(2):
+                        copy_rows(net, done.total.at[pl.ds(q * spare.shape[1], spare.shape[1])], spare.at[2 * k + q])
+                done = ev['out_up%d' % layer]
+                net.spawn(exchange_back(net, spare, dw_up, done))
+                if credit is not None:
                     yield [done]
-                    copy_rows(net, done.total, own_up.at[pl.ds(k * (nd * ur // 2), nd * ur // 2)])
-                    fire(net, copied[k])
-                    if credit is not None:
-                        net.drain(done.copies)
+                    for k in range(2):
                         yield [net.grant(credit + k, 'yz')]
                         fire(net, freed[credit + k])
 
-                def both():
-                    yield copied + ([ev['out_up1']] if layer == 0 else [])
-                    net.spawn(exchange_back(net, own_up, dw_up, ev['out_up%d' % layer]))
-
-                for k in range(2):
-                    net.spawn(one(k))
-                net.spawn(both())
-
-            freed = {k: Event() for k in range(3, 7)}
             passed = sum_job(0, down_place, d_down1, [ev['d_down1']], 'down1')
             passed = sum_job(1, up_place, d_up1, [ev['d_up1']] + passed, 'up1')
-            passed = sum_job(0, up_place, d_up0, [ev['d_up0']] + passed, 'up0', [freed[3], freed[4]])
-            sum_job(1, down_place, d_down0, [ev['d_down0']] + passed, 'down0', [freed[5], freed[6]])
-            out_down(1, dw_down1, 3)
-            out_up(1, dw_up1, 5)
-            out_up(0, dw_up0, None)
+            passed = sum_job(0, up_place, d_up0, [ev['d_up0']] + passed, 'up0', [freed[10], freed[11]])
+            sum_job(1, down_place, d_down0, [ev['d_down0']] + passed, 'down0', [freed[12], freed[13]])
+            out_down(1, dw_down1, 10)
+            net.spawn(out_up(1, 1, dw_up1, 12))
+            net.spawn(out_up(0, 0, dw_up0, None))
             out_down(0, dw_down0, None)
-
             for k in (3, 2, 1, 0):
                 net.spawn(layer1(k, STEPS[k]))
             for step in (0, -1, 1, 2):
                 net.spawn(layer0_hidden(step))
-            for flow in (grads1(), act(), layer1_out(), layer0()):
+            for flow in (up_first(), second(), hidden_flow(), down_flow(), next_layer(), back_flow(), again(), grads1(), act(), layer1_out(),
+                         bring_back(), bring_acts(), layer0()):
                 net.spawn(flow)
             net.run()
 
@@ -1110,18 +1137,13 @@
 
         d_up_own, d_down_own = shape((nd, ur, hidden), F32), shape((dr, width), F32)
 
-        blocks, u0, a0, s0, up1, down1, u1, g_full, ds1, keep, x1 = call(
-            forward, [shape((num_layers, nd * ur, hidden), BF16), act_full, hid_full, hid_full, up_full, shape((2, nl, dr, width // 2), BF16),
-                      own, act_full, hid_full, shape((len(FAR), dr, width), BF16), own],
-            'hhhhhhhhhhv', 'vhvh',
-            [pltpu.VMEM((num_layers, nd, ur, hidden), BF16), vmem(own)] + [vmem(act_full)] * 2 + [vmem(up_full), vmem(down_full)] * 2 + [vmem(hid_full)] * 3 + rx,
-            KR, KS, KL, 0, tokens, grad_out, w_up, w_down)
         d_up_full, d_down_full = shape((width, hidden), F32), shape((hidden, width), F32)
-        x_out, dx, _, _, _, _, *grads = call(
-            turn, [own, own] + [d_up_full, d_down_full] * 2 + [d_up_own, d_down_own] * 2, 'vv' + 'h' * 8, 'hhhhhhhhhvvvhh',
-            [pltpu.VMEM((nd * ur, hidden), F32), vmem(act_full), vmem(up_full), vmem(up_full), vmem(down_full), pltpu.VMEM((nd, rows, width // 2), BF16), vmem(hid_full), vmem(hid_full),
-             pltpu.VMEM((2, hidden // 2, width // 2), F32)] + rx + sums, TR, TS, TL, 1,
-            u1, up1, down1, ds1, g_full, u0, a0, s0, keep, x1, tokens, grad_out, blocks, w_down)
+        x_out, dx, _, _, _, _, _, _, _, _, *grads = call(
+            step, [own, own, shape((num_layers, nd * ur, hidden), BF16), act_full, hid_full, hid_full] + [d_up_full, d_down_full] * 2
+            + [d_up_own, d_down_own] * 2, 'h' * 14, 'hhhhh',
+            [vmem(own)] + [vmem(act_full)] * 2 + [vmem(up_full)] * 2 + [vmem(down_full)] * 2 + [vmem(hid_full)] * 2
+            + [pltpu.VMEM((2, hidden // 4, width // 2), F32)] + rx + sums, TR, TS, TL, 0,
+            tokens, tokens.reshape(rows // dr, dr, width), grad_out, w_up, w_down)
         up1_own, down1_own, up0_own, down0_own = grads
         return pl.pallas_call(
             finish, out_shape=[own, own, shape(w_up.shape, F32), shape(w_down.shape, F32)], name='finish',

time: 326 us -> 318 us (0.975)
  Pallas kernels: 324 us -> 316 us
    pallas_call x2 -> x1, Pallas kernels: 320 us -> 312 us  [call(): pl.pallas_call(kernel, out_shape=out_shape, in_specs=[spaces[s] for s in...]
where the time goes in v9:
time: 318 us; the launch traced here: 317 us
  Pallas kernels  316 us (99%)
    pallas_call x1, Pallas kernels, call(): pl.pallas_call(kernel, out_shape=out_shape, in_specs=[spaces[s] for s in...  312 us

profile of v9, /device:TPU:1, one launch (start us, length us, event | category | flops | bytes accessed | tf_op | source)
XLA Modules:
  0.0 317.0 jit_solution(17157657454977696698)
XLA Ops:
  0.6 312.3 %step.1 = (bf16[128,2048]{1,0:T(8,128)(2,1)}, bf16[128,2048]{1,0:T(8,128)(2,1)}, bf16[2,128,1024]{2,1,0:T(8,128)(2,1)}, bf16[8,128,2048]{2,1,0:T(8,128)(2,1)}, b...) custom-call(bf16[128,2048]{1,0:T(8,128)(2,1)} %refs_0_.1, ...), custom_call_target="tpu_custom_call" | custom-call | flops 100000000 | bytes 10000000 | tf_op jit(solution)/shard_map/step/pallas_call | solution.py:662
  312.9 4.1 %finish.1 = (bf16[128,2048]{1,0:T(8,128)(2,1)}, bf16[128,2048]{1,0:T(8,128)(2,1)}, f32[2,16,8192]{2,1,0:T(8,128)}, f32[2,64,2048]{2,1,0:T(8,128)}) custom-call(f32[8,16,1024]{2,1,0:T(8,128)} %get-tuple-element.10.up1_ref, f32[8,16,1024]{2,1,0:T(8,128)} %get-tuple-element.11.up0_ref, f32[64,2048]{1,0:T(8,128)} %get-tuple-element.12.down1_ref, ...), custom_call_target="tpu_custom_call" | custom-call | tf_op jit(solution)/shard_map/finish/pallas_call | solution.py:1148

commit v10 on v9

--- a/solution.py
+++ b/solution.py
@@ -20,8 +20,7 @@
 LOCAL_RATE = 3000e3
 HOP = 2.4
 PAIR_HOP = 1.0
-ENTRY = 3.0
-SLACK = 0.1
+ENTRY = 4.0
 GELU_C = 0.7978845608028654
 
 
@@ -161,12 +160,13 @@
             size *= n
         size *= dst.dtype.itemsize
         rate = PAIR_RATE if axis == 'p' else LINK_RATE
+        extra = 2.0 if axis == 'd' else 0.0
         if axis == 'd':
             axis, step, size = ('p', 1, size) if step == 1 else ('x', 1 if step < RING + 2 else -1, size)
         key = (axis, step)
         done = max(self.free.get(key, 0.0), self.now) + size / rate
         self.free[key] = done
-        copy = Copy(desc, done + (PAIR_HOP if axis == 'p' else HOP), True)
+        copy = Copy(desc, done + extra + (PAIR_HOP if axis == 'p' else HOP), True)
         copy.slot = send_slot
         self.sent.append(copy)
         return copy
@@ -434,7 +434,6 @@
 
 
 STEPS = (2, 1, -1, 0)
-WINDOW = 2
 
 
 def reduce_x(net, part, made, scratch, done, pool=None):
@@ -506,7 +505,7 @@
         self.net, self.first, self.scratch, self.stage = net, first, scratch, stage
         self.second = 'y' if first == 'z' else 'z'
 
-    def run(self, place, start, done, free, passed_all, pool):
+    def run(self, place, start, done, free, passed_all, pool, window, lead):
         net, first, second = self.net, self.first, self.second
         relay1, last1, relay2, last2 = self.scratch
         ahead, behind, mine = self.stage
@@ -530,12 +529,13 @@
         free[:] = [events[RING] for events in chain]
         got = [[Event() for _ in range(RING)] for _ in range(3)]
         ends = [Event() for _ in STEPS]
-        passed = [Event() for _ in range(RING - 1)] + [passed_all]
+        passed = [Event() for _ in range(RING)]
+        passed[lead] = passed_all
 
         def ring(k):
             two = STEPS[k]
-            if k >= WINDOW:
-                yield [passed[k - WINDOW]]
+            if k >= window:
+                yield [passed[k - window]]
             net.spawn(bring(chain[0][k], term(1, two, lo), ahead, got[0][k]))
             net.spawn(bring(chain[1][k], term(-1, two, hi), behind, got[1][k]))
             net.spawn(bring(chain[2][k], term(0, two), mine, got[2][k]))
@@ -673,9 +673,15 @@
 
 
 WIDE = 512
-TR, TS, TL = 268, 64, 19
-GR = 2
-DU = 3
+EARLY = 3
+SLACK = 0.1
+R_HIDDEN, R_DOWN, R_BACK, R_TURN, R_DU, R_DDOWN, R_DDOWN2, R_DUP, R_OUT, R_PRE, R_GUP, R_GDOWN, R_DX = 2, 1, 3, 1, 3, 2, 2, 4, 2, 2, 3, 3, 2
+WINDOWS = (2, 2, 2, 2, 2, 2, 2, 2)
+AXES = ('yz', 'yz', 'yz', 'yz')
+TOP = 6
+NEAR = 'z'
+LEAD = (3, 3, 3)
+TR, TS, TL = 278, 64, 19
 
 
 def wide_loop(total, body):
@@ -810,7 +816,7 @@
         slot[...] = dot_tokens(lhs[:, :, pl.ds(pl.multiple_of(t * wide, wide), wide)], rhs[...])
 
     stored_tiles(net, lhs.shape[2] // wide, compute, stage, lambda t: out.at[pl.ds(pl.multiple_of(t * wide, wide), wide)])
-    net.spend(3.9 * lhs.shape[2] / 1024)
+    net.spend(4.35 * lhs.shape[2] / 1024)
 
 
 def solution(mesh):
@@ -844,22 +850,22 @@
             names = ('blocks', 'blocks1', 'sent_u', 'got_u', 'got_g', 'sent_up0', 'sent_down0', 'sent_up1', 'sent_down1', 'got_up0', 'got_down0',
                      'got_up1', 'got_down1', 'saved', 'free0', 'reduced0', 'ds_made', 'got_u1', 'hidden', 'all_du', 'reduced1', 'sent_dy', 'got_dy',
                      'back_up0', 'back_up0_rest', 'back_down0', 'd_down1', 'd_up1', 'y_reduced', 'acts', 'd_down0', 'da0', 'd_up0', 'du_reduced',
-                     'out_up1', 'out_up0', 'got_u0', 'y_made', 'x_saved')
+                     'out_up1', 'out_up0', 'got_u0', 'y_made', 'x_saved', 'weights_in', 'd_down1_0')
             ev = {name: Event(name=name) for name in names}
             for kind in ('up', 'down'):
                 for layer in range(2):
                     for k in range(2):
                         ev['sum_%s%d%d' % (kind, layer, k)] = Event(name='sum_%s%d%d' % (kind, layer, k))
-            ev['got_up0'].rank = 2
+            ev['got_up0'].rank = R_HIDDEN
             hidden_made, made0, made1, y_made, du_made = ([Event(name='%s%d' % (name, k)) for k in range(RING)]
                                                           for name in ('hidden_', 'made0_', 'made1_', 'y_made_', 'du_made_'))
             wide = width // 2
             half_up = nd * ur // 2
-            pools = {name: [Pool(), Pool()] for name in ('up', 'down')}
             act_pool, rs_pool = Pool(), Pool()
             job_pools = [[Pool(), Pool()], [Pool(), Pool()]]
+            pools = {'up0': [Pool(), Pool()], 'down0': [Pool(), Pool()], 'up1': job_pools[0], 'down1': job_pools[1]}
             stages = (scratch[21:24], scratch[24:27])
-            jobs = [[Sums(net, first, scratch[5 + 8 * n + 4 * k:9 + 8 * n + 4 * k], stages[k]) for k, first in enumerate('yz')] for n in range(2)]
+            job_scratch = [[scratch[5 + 8 * n + 4 * k:9 + 8 * n + 4 * k] for k in range(2)] for n in range(2)]
             frees = [[Event(0.0) for _ in range(3)] for _ in range(2)]
             freed = {k: Event() for k in range(10, 14)}
 
@@ -880,7 +886,7 @@
 
                 got, sent = [Event(), Event()], [Event(), Event()]
                 for k, first in enumerate('yz'):
-                    net.spawn(gather_yz(net, own.at[pl.ds(k * size, size)], full, first, got[k], sent[k], k * size, split=split, pool=pools[name[:-1]][k].again()))
+                    net.spawn(gather_yz(net, own.at[pl.ds(k * size, size)], full, first, got[k], sent[k], k * size, split=split, pool=pools[name][k]))
                 net.spawn(join('got_', got))
                 net.spawn(join('sent_', sent))
 
@@ -900,18 +906,13 @@
                 net.spawn(gather_x(net, u, ev['got_u'], ev['sent_u'], pool=act_pool))
                 yield [ev['sent_u']]
                 net.spawn(exchange(net, lambda k: s.at[k, pl.ds(ur, ur)], block_out.at[1], ev['blocks1']))
-                yield [ev['got_u'], own_grads]
-                yield [net.grant(0, 'xp')]
-                net.spawn(gather_x(net, g, ev['got_g'], pool=act_pool.again()))
+                yield [own_grads]
+                net.spawn(gather_x(net, g, ev['got_g']))
 
             def second():
-                yield [ev['got_down0']]
-                credit = net.grant(1, 'yz')
-                yield [ev['sent_up0'], ev['sent_down0'], ev['blocks1'], credit]
+                yield [ev['sent_up0'], ev['sent_down0'], ev['blocks1']]
                 gather('down1', w_down_in.at[1], down1, False)
-                yield [ev['got_up0']]
-                credit = net.grant(2, 'yz')
-                yield [ev['sent_down1'], credit]
+                yield [made0[EARLY]]
                 gather('up1', block_out.at[1], up1, True)
 
             def hidden_flow():
@@ -919,13 +920,13 @@
                 for k, step in enumerate(STEPS):
                     hidden_rows(net, net.at('x', step), u, up0, ds, s)
                     fire(net, hidden_made[k])
-                    yield [Event(net.now, 2)]
+                    yield [Event(net.now, R_HIDDEN)]
                 yield [net.load(ds, a_out), net.load(s, s_out), net.load(u, u_out)]
                 fire(net, ev['saved'])
 
             def down_flow():
                 for k, step in enumerate(STEPS):
-                    yield [hidden_made[k], ev['got_down0'], Event(0.0, 1)]
+                    yield [hidden_made[k], ev['got_down0'], Event(0.0, R_DOWN)]
                     down_rows(net, net.at('x', step), s, down0, part.at[k])
                     fire(net, made0[k])
                 fire(net, ev['free0'])
@@ -949,31 +950,34 @@
 
             def back_flow():
                 for k, step in enumerate(STEPS):
-                    yield [ev['got_g'], ev['got_down1'], ev['saved'], Event(0.0, 3)]
+                    yield [ev['got_g'], ev['got_down1'], ev['saved'], Event(0.0, R_BACK)]
                     hidden_back_rows(net, net.at('x', step), g, down1, ds)
                 fire(net, ev['ds_made'])
 
             def again():
-                top = nd * ur * 3 // 4
-                yield [ev['free0'], ev['got_down1'], ev['ds_made']]
+                top = nd * ur * TOP // 8
+                yield [ev['free0'], ev['ds_made']]
                 net.drain(ev['got_up0'].copies + ev['got_down0'].copies)
                 credit = net.grant(6, 'yz')
-                yield [ev['sent_up1'], credit]
-                net.spawn(gather_yz(net, w_down_in.at[0], down0, 'z', ev['back_down0'], near=True, pool=pools['down'][1].again()))
-                yield [ev['got_up1']]
+                yield [credit]
+                net.spawn(gather_yz(net, w_down_in.at[0], down0, NEAR, ev['back_down0'], near=True, pool=pools['down0'][1].again()))
+                net.spawn(gather_yz(net, block_out.at[0, pl.ds(0, top)], up0, 'y', ev['back_up0'], pool=pools['up0'][0].again()))
+                net.spawn(gather_yz(net, block_out.at[0, pl.ds(top, nd * ur - top)], up0, 'z', ev['back_up0_rest'], offset=top, pool=pools['up0'][1].again()))
+
+            def weights():
+                yield [ev['got_up1'], ev['got_down1']]
                 yield [net.grant(7, 'yz')]
-                net.spawn(gather_yz(net, block_out.at[0, pl.ds(0, top)], up0, 'y', ev['back_up0'], pool=pools['up'][0].again()))
-                net.spawn(gather_yz(net, block_out.at[0, pl.ds(top, nd * ur - top)], up0, 'z', ev['back_up0_rest'], offset=top, pool=pools['up'][1].again()))
+                fire(net, ev['weights_in'])
 
             left = [RING, RING]
 
             def layer1(k, step):
-                yield [here[step], ev['ds_made'], ev['got_up1'], Event(0.0, 1)]
+                yield [here[step], ev['ds_made'], ev['got_up1'], Event(0.0, R_TURN)]
                 hidden_turn_rows(net, net.at('x', step), u, up1, s, ds)
                 left[0] -= 1
                 if left[0] == 0:
                     fire(net, ev['hidden'])
-                yield [Event(net.now, DU)]
+                yield [Event(net.now, R_DU)]
                 input_back_rows(net, net.at('x', step), ds, up1, part.at[k])
                 fire(net, made1[k])
                 left[1] -= 1
@@ -982,11 +986,11 @@
 
             def grads1():
                 for h in range(2):
-                    yield [Event(0.0, GR), ev['hidden']]
+                    yield [Event(0.0, R_DDOWN2 if h else R_DDOWN), ev['hidden']]
                     grad_tiles(net, s, g.at[:, :, columns(h)], stage, d_down1.at[:, columns(h)])
-                fire(net, ev['d_down1'])
+                    fire(net, ev['d_down1' if h else 'd_down1_0'])
                 for h in range(2):
-                    yield [Event(net.now, GR)]
+                    yield [Event(net.now, R_DUP)]
                     grad_tiles(net, u.at[:, :, columns(h)], ds, stage, d_up1.at[columns(h)])
                 fire(net, ev['d_up1'])
 
@@ -1001,12 +1005,12 @@
                 net.spawn(gather_x(net, u, ev['got_dy'], ev['sent_dy'], dy_here, pool=act_pool.again()))
 
             def layer1_out():
-                yield [ev['reduced1'], Event(0.0, 2)]
+                yield [ev['reduced1'], Event(0.0, R_OUT)]
                 net.drain(ev['reduced1'].copies)
                 credit = net.grant(8, 'xp')
                 for k, step in enumerate(STEPS):
                     down_rows(net, net.at('x', step), s, down1, part.at[k])
-                    yield [Event(net.now, 2)]
+                    yield [Event(net.now, R_OUT)]
                 fire(net, ev['y_made'])
                 yield [ev['sent_dy'], credit]
                 net.spawn(reduce_x(net, part, y_made, rx_scratch, ev['y_reduced'], rs_pool.again()))
@@ -1032,7 +1036,7 @@
                 fire(net, ev['acts'])
 
             def layer0_hidden(step):
-                yield [dy_here[step], ev['acts'], ev['back_down0'], ev['d_up1'], Event(0.0, 2)]
+                yield [dy_here[step], ev['acts'], ev['back_down0'], ev['d_up1'], Event(0.0, R_PRE)]
                 pre_back_rows(net, net.at('x', step), u, down0, a0, ds)
                 backs[0] -= 1
                 if backs[0] == 0:
@@ -1040,14 +1044,14 @@
 
             def layer0():
                 for h in range(2):
-                    yield [ev['da0'], ev['got_u0'], Event(0.0, 3)]
+                    yield [ev['da0'], ev['got_u0'], Event(0.0, R_GUP)]
                     grad_tiles(net, g.at[:, :, columns(h)], ds, stage, d_up0.at[columns(h)])
                 fire(net, ev['d_up0'])
                 for h in range(2):
-                    yield [ev['got_dy'], ev['acts'], Event(0.0, 3)]
+                    yield [ev['got_dy'], ev['acts'], Event(0.0, R_GDOWN)]
                     grad_tiles(net, s0, u.at[:, :, columns(h)], stage, d_down0.at[:, columns(h)])
                 fire(net, ev['d_down0'])
-                yield [ev['y_reduced'], ev['back_up0'], ev['back_up0_rest'], Event(0.0, 2)]
+                yield [ev['y_reduced'], ev['back_up0'], ev['back_up0_rest'], Event(0.0, R_DX)]
                 net.drain(ev['y_reduced'].copies + ev['got_down1'].copies)
                 x0 = down1.at[pl.ds(0, x_halves.shape[0])]
                 yield [net.grant(9, 'xp'), net.load(x_halves, x0)]
@@ -1055,7 +1059,7 @@
                 for k, step in enumerate(STEPS):
                     input_back_rows(net, net.at('x', step), ds, up0, part.at[k])
                     fire(net, du_made[k])
-                    yield [Event(net.now, 2)]
+                    yield [Event(net.now, R_DX)]
                 yield [ev['du_reduced'], ev['x_saved']]
                 for q in range(x_halves.shape[0]):
                     rows_q = pl.ds(q * dr, dr)
@@ -1074,12 +1078,14 @@
                 pool.again()
                 fire(net, event)
 
-            def sum_job(n, place, ref, ready, name, credits=()):
+            def sum_job(job, place, ref, ready, name, credits=()):
                 passed = [Event(), Event()]
                 for k in range(2):
                     start = Event()
-                    net.spawn(gate(start, ready + ([credits[k]] if credits else []), job_pools[n][k]))
-                    net.spawn(jobs[n][k].run(place(ref, k), start, ev['sum_%s%d' % (name, k)], frees[k], passed[k], job_pools[n][k]))
+                    n = job % 2
+                    net.spawn(gate(start, ready[k] + ([credits[k]] if credits else []), job_pools[n][k]))
+                    sums = Sums(net, AXES[job][k], job_scratch[n][k], stages[k])
+                    net.spawn(sums.run(place(ref, k), start, ev['sum_%s%d' % (name, k)], frees[k], passed[k], job_pools[n][k], WINDOWS[2 * job + k], LEAD[min(job, 2)]))
                 return passed
 
             def out_down(layer, dw_down, credit):
@@ -1099,7 +1105,7 @@
                 totals = [ev['sum_up%d%d' % (layer, k)] for k in range(2)]
                 yield totals
                 net.drain(totals[0].copies + totals[1].copies)
-                spare = jobs[n][0].scratch[0].at[0]
+                spare = job_scratch[n][0][0].at[0]
                 for k, done in enumerate(totals):
                     for q in range(2):
                         copy_rows(net, done.total.at[pl.ds(q * spare.shape[1], spare.shape[1])], spare.at[2 * k + q])
@@ -1111,10 +1117,10 @@
                         yield [net.grant(credit + k, 'yz')]
                         fire(net, freed[credit + k])
 
-            passed = sum_job(0, down_place, d_down1, [ev['d_down1']], 'down1')
-            passed = sum_job(1, up_place, d_up1, [ev['d_up1']] + passed, 'up1')
-            passed = sum_job(0, up_place, d_up0, [ev['d_up0']] + passed, 'up0', [freed[10], freed[11]])
-            sum_job(1, down_place, d_down0, [ev['d_down0']] + passed, 'down0', [freed[12], freed[13]])
+            passed = sum_job(0, down_place, d_down1, [[ev['d_down1_0'], ev['weights_in']], [ev['d_down1'], ev['weights_in']]], 'down1')
+            passed = sum_job(1, up_place, d_up1, [[ev['d_up1']] + passed] * 2, 'up1')
+            passed = sum_job(2, up_place, d_up0, [[ev['d_up0']] + passed] * 2, 'up0', [freed[10], freed[11]])
+            sum_job(3, down_place, d_down0, [[ev['d_down0']] + passed] * 2, 'down0', [freed[12], freed[13]])
             out_down(1, dw_down1, 10)
             net.spawn(out_up(1, 1, dw_up1, 12))
             net.spawn(out_up(0, 0, dw_up0, None))
@@ -1123,17 +1129,28 @@
                 net.spawn(layer1(k, STEPS[k]))
             for step in (0, -1, 1, 2):
                 net.spawn(layer0_hidden(step))
-            for flow in (up_first(), second(), hidden_flow(), down_flow(), next_layer(), back_flow(), again(), grads1(), act(), layer1_out(),
+            for flow in (up_first(), second(), hidden_flow(), down_flow(), next_layer(), back_flow(), again(), weights(), grads1(), act(), layer1_out(),
                          bring_back(), bring_acts(), layer0()):
                 net.spawn(flow)
             net.run()
 
-        def finish(up1_ref, up0_ref, down1_ref, down0_ref, x_ref, dx_ref, x_out, dx_out, up_out, down_out):
-            for l, (up_ref, down_ref) in enumerate(((up0_ref, down0_ref), (up1_ref, down1_ref))):
-                join_columns(up_ref, up_out.at[l])
-                rows_loop(dr, 16, lambda at: down_out.at[l].__setitem__((at, slice(None)), down_ref[at, :]))
-            rows_loop(rows, 16, lambda at: x_out.__setitem__((at, slice(None)), x_ref[at, :]))
-            rows_loop(rows, 16, lambda at: dx_out.__setitem__((at, slice(None)), dx_ref[at, :]))
+        def finish(*refs):
+            sources, targets, held, ups, sems = refs[:6], refs[6:10], refs[10:16], refs[16:18], refs[18]
+            x_out, dx_out, up_out, down_out = targets
+            loads = [pltpu.make_async_copy(src, dst, sems.at[k]) for k, (src, dst) in enumerate(zip(sources, held))]
+            stores = [(ups[1], up_out.at[1]), (ups[0], up_out.at[0]), (held[2], down_out.at[1]), (held[3], down_out.at[0]), (held[4], x_out), (held[5], dx_out)]
+            stores = [pltpu.make_async_copy(src, dst, sems.at[6 + k]) for k, (src, dst) in enumerate(stores)]
+            for load in loads:
+                load.start()
+            for k in (2, 3, 4, 5):
+                loads[k].wait()
+                stores[k].start()
+            for k in (0, 1):
+                loads[k].wait()
+                join_columns(held[k], ups[1 - k])
+                stores[k].start()
+            for store in stores:
+                store.wait()
 
         d_up_own, d_down_own = shape((nd, ur, hidden), F32), shape((dr, width), F32)
 
@@ -1145,9 +1162,11 @@
             + [pltpu.VMEM((2, hidden // 4, width // 2), F32)] + rx + sums, TR, TS, TL, 0,
             tokens, tokens.reshape(rows // dr, dr, width), grad_out, w_up, w_down)
         up1_own, down1_own, up0_own, down0_own = grads
+        held = [d_up_own, d_up_own, d_down_own, d_down_own, own, own]
         return pl.pallas_call(
             finish, out_shape=[own, own, shape(w_up.shape, F32), shape(w_down.shape, F32)], name='finish',
-            in_specs=[pl.BlockSpec(memory_space=pltpu.VMEM)] * 6, out_specs=[pl.BlockSpec(memory_space=pltpu.VMEM)] * 4,
+            in_specs=[pl.BlockSpec(memory_space=pl.ANY)] * 6, out_specs=[pl.BlockSpec(memory_space=pl.ANY)] * 4,
+            scratch_shapes=[vmem(like) for like in held] + [pltpu.VMEM(w_up.shape[1:], F32)] * 2 + [pltpu.SemaphoreType.DMA((12,))],
         )(up1_own, up0_own, down1_own, down0_own, x_out, dx)
 
     return jax.shard_map(device_fn, mesh=mesh, in_specs=(tok_spec, tok_spec, w_spec, w_spec), out_specs=(tok_spec, tok_spec, w_spec, w_spec), check_vma=False)

time: 318 us -> 314 us (0.987)
  Pallas kernels: 316 us -> 312 us
    pallas_call x1, Pallas kernels: 312 us -> 309 us  [call(): pl.pallas_call(kernel, out_shape=out_shape, in_specs=[spaces[s] for s in...]
where the time goes in v10:
time: 314 us; the launch traced here: 313 us
  Pallas kernels  312 us (99%)
    pallas_call x1, Pallas kernels, call(): pl.pallas_call(kernel, out_shape=out_shape, in_specs=[spaces[s] for s in...  309 us

profile of v10, /device:TPU:1, one launch (start us, length us, event | category | flops | bytes accessed | tf_op | source)
XLA Modules:
  0.0 313.0 jit_solution(17200642512644541415)
XLA Ops:
  0.6 309.1 %step.1 = (bf16[128,2048]{1,0:T(8,128)(2,1)}, bf16[128,2048]{1,0:T(8,128)(2,1)}, bf16[2,128,1024]{2,1,0:T(8,128)(2,1)}, bf16[8,128,2048]{2,1,0:T(8,128)(2,1)}, b...) custom-call(bf16[128,2048]{1,0:T(8,128)(2,1)} %refs_0_.1, ...), custom_call_target="tpu_custom_call" | custom-call | flops 100000000 | bytes 10000000 | tf_op jit(solution)/shard_map/step/pallas_call | solution.py:662
  309.7 3.1 %finish.1 = (bf16[128,2048]{1,0:T(8,128)(2,1)}, bf16[128,2048]{1,0:T(8,128)(2,1)}, f32[2,16,8192]{2,1,0:T(8,128)}, f32[2,64,2048]{2,1,0:T(8,128)}) custom-call(f32[8,16,1024]{2,1,0:T(8,128)} %get-tuple-element.10.refs_0_, f32[8,16,1024]{2,1,0:T(8,128)} %get-tuple-element.11.refs_1_, f32[64,2048]{1,0:T(8,128)} %get-tuple-element.12.refs_2_, ...), custom_call_target="tpu_custom_call" | custom-call | tf_op jit(solution)/shard_map/finish/pallas_call | solution.py:1166

commit v11 on v10

--- a/solution.py
+++ b/solution.py
@@ -270,20 +270,20 @@
         print('   %7.1f %s' % (net.now, event.name))
 
 
-def exchange(net, source, dst, done):
+def exchange(net, source, dst, done, pool):
     rows = dst.shape[0] // (2 * RING)
 
     def mine():
         return dst.at[pl.ds(pl.multiple_of(net.data * rows, rows), rows)]
 
     own = net.load(source(net.data), mine())
-    copies = [net.send(source(net.hops[k]), mine(), 'd', k) for k in (4, 5, 2, 3, 6, 7, 1)]
+    copies = [net.send(source(net.hops[k]), mine(), 'd', k, pool) for k in (4, 5, 2, 3, 6, 7, 1)]
     yield [own] + copies
     net.drain(copies)
     fire(net, done)
 
 
-def exchange_back(net, src, dst, done):
+def exchange_back(net, src, dst, done, pool):
     rows = dst.shape[1]
     per = src.shape[1] // rows
 
@@ -291,7 +291,7 @@
         return src.at[lax.div(k, per), pl.ds(pl.multiple_of(lax.rem(k, per) * rows, rows), rows)]
 
     own = net.load(block(net.data), dst.at[net.data])
-    copies = [net.send(block(net.hops[k]), dst.at[net.data], 'd', k) for k in (4, 5, 2, 3, 6, 7, 1)]
+    copies = [net.send(block(net.hops[k]), dst.at[net.data], 'd', k, pool) for k in (4, 5, 2, 3, 6, 7, 1)]
     yield [own] + copies
     net.drain(copies)
     fire(net, done)
@@ -457,13 +457,14 @@
     for k in range(RING):
         net.spawn(pair(k))
     sent = {}
-    started = Event()
+    started, relayed = Event(), Event()
 
     def part_flow(k):
-        yield [ready[k]]
+        yield [ready[k]] + ([relayed] if k else [])
         if k == 0:
             sent['first_f'] = net.send(acc(0, lo), relay_f, 'x', 1, pool=pool)
             sent['first_b'] = net.send(acc(0, hi), relay_b, 'x', -1, pool=pool)
+            fire(net, relayed)
         elif k == 1:
             sent['direct_f'] = net.send(acc(1, hi), last_f.at[hi], 'x', 1, pool=pool)
         else:
@@ -675,13 +676,14 @@
 WIDE = 512
 EARLY = 3
 SLACK = 0.1
-R_HIDDEN, R_DOWN, R_BACK, R_TURN, R_DU, R_DDOWN, R_DDOWN2, R_DUP, R_OUT, R_PRE, R_GUP, R_GDOWN, R_DX = 2, 1, 3, 1, 3, 2, 2, 4, 2, 2, 3, 3, 2
+R_HIDDEN, R_DOWN, R_BACK, R_TURN, R_DDOWN, R_DDOWN2, R_DUP, R_OUT, R_PRE, R_GUP, R_GDOWN, R_DX = 2, 1, 3, 1, 2, 2, 4, 2, 2, 3, 3, 2
+R_DU, HOLD = (3, 3.1, 3.2, 3.3), (0, 1, 2)
 WINDOWS = (2, 2, 2, 2, 2, 2, 2, 2)
 AXES = ('yz', 'yz', 'yz', 'yz')
 TOP = 6
 NEAR = 'z'
 LEAD = (3, 3, 3)
-TR, TS, TL = 278, 64, 19
+TR, TS, TL = 264, 64, 9
 
 
 def wide_loop(total, body):
@@ -863,7 +865,7 @@
             half_up = nd * ur // 2
             act_pool, rs_pool = Pool(), Pool()
             job_pools = [[Pool(), Pool()], [Pool(), Pool()]]
-            pools = {'up0': [Pool(), Pool()], 'down0': [Pool(), Pool()], 'up1': job_pools[0], 'down1': job_pools[1]}
+            pools = {'up0': [Pool(), Pool()], 'down0': [Pool(), Pool()], 'up1': job_pools[0], 'down1': job_pools[1], 'blocks': [Pool(), Pool()]}
             stages = (scratch[21:24], scratch[24:27])
             job_scratch = [[scratch[5 + 8 * n + 4 * k:9 + 8 * n + 4 * k] for k in range(2)] for n in range(2)]
             frees = [[Event(0.0) for _ in range(3)] for _ in range(2)]
@@ -873,7 +875,7 @@
                 return pl.ds(h * wide, wide)
 
             inputs = [net.load(x_in, x)]
-            inputs += [net.load(w_up_in.at[l, :, pl.ds(k * hidden, hidden)], ds.at[k, pl.ds(l * ur, ur)]) for l in range(num_layers) for k in range(nd)]
+            inputs += [net.load(w_up_in.at[:, pl.ds(k * hidden, hidden)], ds.at[k, pl.ds(0, num_layers * ur)]) for k in range(nd)]
 
             def gather(name, own, full, split):
                 size = own.shape[0] // 2
@@ -890,14 +892,12 @@
                 net.spawn(join('got_', got))
                 net.spawn(join('sent_', sent))
 
+            net.take(inputs)
+            split_columns(ds, s, num_layers * ur)
+            norm_rows(x, u.at[net.data])
             net.enter()
             gather('down0', w_down_in.at[0], down0, False)
-            net.take(inputs)
-            split_columns(ds, s, num_layers * ur)
-            net.spend(0.5)
-            net.spawn(exchange(net, lambda k: s.at[k, pl.ds(0, ur)], block_out.at[0], ev['blocks']))
-            norm_rows(x, u.at[net.data])
-            net.spend(0.7)
+            net.spawn(exchange(net, lambda k: s.at[k, pl.ds(0, ur)], block_out.at[0], ev['blocks'], pools['blocks'][0]))
             own_grads = net.load(g_in, g.at[net.data])
 
             def up_first():
@@ -905,7 +905,7 @@
                 gather('up0', block_out.at[0], up0, True)
                 net.spawn(gather_x(net, u, ev['got_u'], ev['sent_u'], pool=act_pool))
                 yield [ev['sent_u']]
-                net.spawn(exchange(net, lambda k: s.at[k, pl.ds(ur, ur)], block_out.at[1], ev['blocks1']))
+                net.spawn(exchange(net, lambda k: s.at[k, pl.ds(ur, ur)], block_out.at[1], ev['blocks1'], pools['blocks'][1]))
                 yield [own_grads]
                 net.spawn(gather_x(net, g, ev['got_g']))
 
@@ -971,13 +971,18 @@
 
             left = [RING, RING]
 
+            turned = [Event() for _ in STEPS]
+
             def layer1(k, step):
                 yield [here[step], ev['ds_made'], ev['got_up1'], Event(0.0, R_TURN)]
                 hidden_turn_rows(net, net.at('x', step), u, up1, s, ds)
+                fire(net, turned[k])
                 left[0] -= 1
                 if left[0] == 0:
                     fire(net, ev['hidden'])
-                yield [Event(net.now, R_DU)]
+
+            def layer1_back(k, step):
+                yield [turned[k], Event(0.0, R_DU[k])] + ([ev['hidden']] if k in HOLD else [])
                 input_back_rows(net, net.at('x', step), ds, up1, part.at[k])
                 fire(net, made1[k])
                 left[1] -= 1
@@ -1110,7 +1115,7 @@
                     for q in range(2):
                         copy_rows(net, done.total.at[pl.ds(q * spare.shape[1], spare.shape[1])], spare.at[2 * k + q])
                 done = ev['out_up%d' % layer]
-                net.spawn(exchange_back(net, spare, dw_up, done))
+                net.spawn(exchange_back(net, spare, dw_up, done, pools['blocks'][layer].again()))
                 if credit is not None:
                     yield [done]
                     for k in range(2):
@@ -1127,6 +1132,8 @@
             out_down(0, dw_down0, None)
             for k in (3, 2, 1, 0):
                 net.spawn(layer1(k, STEPS[k]))
+            for k in range(RING):
+                net.spawn(layer1_back(k, STEPS[k]))
             for step in (0, -1, 1, 2):
                 net.spawn(layer0_hidden(step))
             for flow in (up_first(), second(), hidden_flow(), down_flow(), next_layer(), back_flow(), again(), weights(), grads1(), act(), layer1_out(),
@@ -1160,7 +1167,7 @@
             + [d_up_own, d_down_own] * 2, 'h' * 14, 'hhhhh',
             [vmem(own)] + [vmem(act_full)] * 2 + [vmem(up_full)] * 2 + [vmem(down_full)] * 2 + [vmem(hid_full)] * 2
             + [pltpu.VMEM((2, hidden // 4, width // 2), F32)] + rx + sums, TR, TS, TL, 0,
-            tokens, tokens.reshape(rows // dr, dr, width), grad_out, w_up, w_down)
+            tokens, tokens.reshape(rows // dr, dr, width), grad_out, w_up.reshape(num_layers * ur, ffn), w_down)
         up1_own, down1_own, up0_own, down0_own = grads
         held = [d_up_own, d_up_own, d_down_own, d_down_own, own, own]
         return pl.pallas_call(

time: 314 us -> 312 us (level)
  no operation moved by 1% of the time
where the time goes in v11:
time: 312 us; the launch traced here: 311 us
  Pallas kernels  310 us (99%)
    pallas_call x1, Pallas kernels, call(): pl.pallas_call(kernel, out_shape=out_shape, in_specs=[spaces[s] for s in...  307 us

profile of v11, /device:TPU:1, one launch (start us, length us, event | category | flops | bytes accessed | tf_op | source)
XLA Modules:
  0.0 311.2 jit_solution(17964267487837955388)
XLA Ops:
  0.6 307.3 %step.1 = (bf16[128,2048]{1,0:T(8,128)(2,1)}, bf16[128,2048]{1,0:T(8,128)(2,1)}, bf16[2,128,1024]{2,1,0:T(8,128)(2,1)}, bf16[8,128,2048]{2,1,0:T(8,128)(2,1)}, b...) custom-call(bf16[128,2048]{1,0:T(8,128)(2,1)} %refs_0_.1, ...), custom_call_target="tpu_custom_call" | custom-call | flops 100000000 | bytes 10000000 | tf_op jit(solution)/shard_map/step/pallas_call | solution.py:663
  307.9 3.1 %finish.1 = (bf16[128,2048]{1,0:T(8,128)(2,1)}, bf16[128,2048]{1,0:T(8,128)(2,1)}, f32[2,16,8192]{2,1,0:T(8,128)}, f32[2,64,2048]{2,1,0:T(8,128)}) custom-call(f32[8,16,1024]{2,1,0:T(8,128)} %get-tuple-element.10.refs_0_, f32[8,16,1024]{2,1,0:T(8,128)} %get-tuple-element.11.refs_1_, f32[64,2048]{1,0:T(8,128)} %get-tuple-element.12.refs_2_, ...), custom_call_target="tpu_custom_call" | custom-call | tf_op jit(solution)/shard_map/finish/pallas_call | solution.py:1173

commit v12 on v11

--- a/solution.py
+++ b/solution.py
@@ -147,9 +147,10 @@
         if pool is not None:
             pool.next += 1
         if not self.free_sends:
-            if PRINT:
+            over = [copy for copy in self.sent if copy.time + 1.0 < self.now]
+            if PRINT and not over:
                 print('EXHAUSTED', round(self.now, 1))
-            self.drain([min(self.sent, key=lambda copy: copy.time)])
+            self.drain(over or [min(self.sent, key=lambda copy: copy.time)])
         send_slot = self.free_sends.pop()
         desc = pltpu.make_async_remote_copy(
             src_ref=src, dst_ref=dst, send_sem=self.send_sems.at[send_slot], recv_sem=self.recv_sems.at[k],
@@ -675,6 +676,7 @@
 
 WIDE = 512
 EARLY = 3
+GRAD_TIME = 3.4
 SLACK = 0.1
 R_HIDDEN, R_DOWN, R_BACK, R_TURN, R_DDOWN, R_DDOWN2, R_DUP, R_OUT, R_PRE, R_GUP, R_GDOWN, R_DX = 2, 1, 3, 1, 2, 2, 4, 2, 2, 3, 3, 2
 R_DU, HOLD = (3, 3.1, 3.2, 3.3), (0, 1, 2)
@@ -683,7 +685,7 @@
 TOP = 6
 NEAR = 'z'
 LEAD = (3, 3, 3)
-TR, TS, TL = 264, 64, 9
+TR, TS, TL = 264, 56, 9
 
 
 def wide_loop(total, body):
@@ -812,13 +814,20 @@
 
 
 def grad_tiles(net, lhs, rhs, stage, out):
-    wide = stage.shape[1]
+    _, high, wide = stage.shape
+    across = rhs.shape[2] // wide
+
+    def columns(t):
+        return pl.ds(pl.multiple_of(lax.rem(t, across) * wide, wide), wide)
+
+    def rows(t):
+        return pl.ds(pl.multiple_of(lax.div(t, across) * high, high), high)
 
     def compute(t, slot):
-        slot[...] = dot_tokens(lhs[:, :, pl.ds(pl.multiple_of(t * wide, wide), wide)], rhs[...])
-
-    stored_tiles(net, lhs.shape[2] // wide, compute, stage, lambda t: out.at[pl.ds(pl.multiple_of(t * wide, wide), wide)])
-    net.spend(4.35 * lhs.shape[2] / 1024)
+        slot[...] = dot_tokens(lhs[:, :, rows(t)], rhs[:, :, columns(t)])
+
+    stored_tiles(net, lhs.shape[2] // high * across, compute, stage, lambda t: out.at[rows(t), columns(t)])
+    net.spend(GRAD_TIME * lhs.shape[2] / 1024)
 
 
 def solution(mesh):
@@ -1166,7 +1175,7 @@
             step, [own, own, shape((num_layers, nd * ur, hidden), BF16), act_full, hid_full, hid_full] + [d_up_full, d_down_full] * 2
             + [d_up_own, d_down_own] * 2, 'h' * 14, 'hhhhh',
             [vmem(own)] + [vmem(act_full)] * 2 + [vmem(up_full)] * 2 + [vmem(down_full)] * 2 + [vmem(hid_full)] * 2
-            + [pltpu.VMEM((2, hidden // 4, width // 2), F32)] + rx + sums, TR, TS, TL, 0,
+            + [pltpu.VMEM((2, hidden // 2, width // 4), F32)] + rx + sums, TR, TS, TL, 0,
             tokens, tokens.reshape(rows // dr, dr, width), grad_out, w_up.reshape(num_layers * ur, ffn), w_down)
         up1_own, down1_own, up0_own, down0_own = grads
         held = [d_up_own, d_up_own, d_down_own, d_down_own, own, own]

time: 312 us -> 312 us (level)
  no operation moved by 1% of the time
where the time goes in v12:
time: 312 us; the launch traced here: 311 us
  Pallas kernels  310 us (99%)
    pallas_call x1, Pallas kernels, call(): pl.pallas_call(kernel, out_shape=out_shape, in_specs=[spaces[s] for s in...  307 us

profile of v12, /device:TPU:1, one launch (start us, length us, event | category | flops | bytes accessed | tf_op | source)
XLA Modules:
  0.0 311.1 jit_solution(3550398981135385650)
XLA Ops:
  0.6 307.2 %step.1 = (bf16[128,2048]{1,0:T(8,128)(2,1)}, bf16[128,2048]{1,0:T(8,128)(2,1)}, bf16[2,128,1024]{2,1,0:T(8,128)(2,1)}, bf16[8,128,2048]{2,1,0:T(8,128)(2,1)}, b...) custom-call(bf16[128,2048]{1,0:T(8,128)(2,1)} %refs_0_.1, ...), custom_call_target="tpu_custom_call" | custom-call | flops 100000000 | bytes 10000000 | tf_op jit(solution)/shard_map/step/pallas_call | solution.py:664
  307.8 3.1 %finish.1 = (bf16[128,2048]{1,0:T(8,128)(2,1)}, bf16[128,2048]{1,0:T(8,128)(2,1)}, f32[2,16,8192]{2,1,0:T(8,128)}, f32[2,64,2048]{2,1,0:T(8,128)}) custom-call(f32[8,16,1024]{2,1,0:T(8,128)} %get-tuple-element.10.refs_0_, f32[8,16,1024]{2,1,0:T(8,128)} %get-tuple-element.11.refs_1_, f32[64,2048]{1,0:T(8,128)} %get-tuple-element.12.refs_2_, ...), custom_call_target="tpu_custom_call" | custom-call | tf_op jit(solution)/shard_map/finish/pallas_call | solution.py:1182

commit v13 on v12

--- a/solution.py
+++ b/solution.py
@@ -1,5 +1,3 @@
-import contextlib
-
 import jax
 import jax.numpy as jnp
 from jax import lax
@@ -20,17 +18,13 @@
 LOCAL_RATE = 3000e3
 HOP = 2.4
 PAIR_HOP = 1.0
-ENTRY = 4.0
+ENTRY = 4.2
 GELU_C = 0.7978845608028654
 
 
-def scope(label):
-    return jax.named_scope(label) if SCOPES else contextlib.nullcontext()
-
-
 class Event:
-    def __init__(self, time=None, rank=0, name=''):
-        self.time, self.rank, self.name = time, rank, name
+    def __init__(self, time=None, rank=0):
+        self.time, self.rank = time, rank
 
 
 class Copy:
@@ -71,7 +65,6 @@
         self.free = {}
         self.sent = []
         self.flows = []
-        self.labels = {}
         here, there = lax.axis_index('local'), lax.axis_index('data')
         pos = {'z': here // RING, 'y': lax.rem(here, RING), 'x': there // 2}
         self.data, self.core = there, lax.rem(there, 2)
@@ -148,8 +141,6 @@
             pool.next += 1
         if not self.free_sends:
             over = [copy for copy in self.sent if copy.time + 1.0 < self.now]
-            if PRINT and not over:
-                print('EXHAUSTED', round(self.now, 1))
             self.drain(over or [min(self.sent, key=lambda copy: copy.time)])
         send_slot = self.free_sends.pop()
         desc = pltpu.make_async_remote_copy(
@@ -161,7 +152,7 @@
             size *= n
         size *= dst.dtype.itemsize
         rate = PAIR_RATE if axis == 'p' else LINK_RATE
-        extra = 2.0 if axis == 'd' else 0.0
+        extra = 4.4 if axis == 'd' else 0.0
         if axis == 'd':
             axis, step, size = ('p', 1, size) if step == 1 else ('x', 1 if step < RING + 2 else -1, size)
         key = (axis, step)
@@ -188,11 +179,6 @@
         copy.slot = k
         return copy
 
-    def save(self, src, dst):
-        copy = self.load(src, dst)
-        copy.time += 4.0
-        return copy
-
     def spend(self, microseconds):
         self.now += microseconds
 
@@ -201,9 +187,6 @@
 
     def step(self, flow):
         try:
-            if flow not in self.labels:
-                self.labels[flow] = [flow.__name__, len(self.labels), 0]
-            self.labels[flow][2] += 1
             self.flows.append((flow, next(flow)))
         except StopIteration:
             pass
@@ -222,20 +205,14 @@
             _, k, time = best
             flow, items = self.flows.pop(k)
             self.idle(time - self.now)
-            label = '%s_%d_%d' % tuple(self.labels[flow])
-            with scope('w_' + label):
-                for item in items:
-                    if not isinstance(item, Event) and not item.waited:
-                        item.wait()
-                        item.waited = True
-                        if isinstance(item, Copy) and not item.remote:
-                            self.free_locals.append(item.slot)
-            before = self.now
+            for item in items:
+                if not isinstance(item, Event) and not item.waited:
+                    item.wait()
+                    item.waited = True
+                    if isinstance(item, Copy) and not item.remote:
+                        self.free_locals.append(item.slot)
             self.now = max(self.now, time)
-            if PRINT:
-                print('STEP', label, round(before, 2), round(self.now, 2))
-            with scope('s_' + label):
-                self.step(flow)
+            self.step(flow)
 
     def finish(self):
         for copy in self.sent:
@@ -267,8 +244,6 @@
 
 def fire(net, event):
     event.time = net.now
-    if PRINT and event.name:
-        print('   %7.1f %s' % (net.now, event.name))
 
 
 def exchange(net, source, dst, done, pool):
@@ -431,13 +406,10 @@
     return net.places[one % RING][two % RING] if first == 'z' else net.places[two % RING][one % RING]
 
 
-FAR = [(2, 0), (2, 1), (2, -1), (2, 2), (0, 2), (1, 2), (-1, 2)]
-
-
 STEPS = (2, 1, -1, 0)
 
 
-def reduce_x(net, part, made, scratch, done, pool=None):
+def reduce_x(net, part, made, scratch, done, pool=None, relayed=None):
     other, relay_f, relay_b, last_f, last_b = scratch
     half = part.shape[2] // 2
     lo, hi = pl.ds(0, half), pl.ds(half, half)
@@ -458,7 +430,7 @@
     for k in range(RING):
         net.spawn(pair(k))
     sent = {}
-    started, relayed = Event(), Event()
+    started, relayed = Event(), relayed or Event()
 
     def part_flow(k):
         yield [ready[k]] + ([relayed] if k else [])
@@ -491,15 +463,6 @@
 def reduce_x_scratch(rows, cols):
     return [pltpu.VMEM((RING, rows, cols), F32), pltpu.VMEM((rows // 2, cols), F32), pltpu.VMEM((rows // 2, cols), F32),
             pltpu.VMEM((rows, cols), F32), pltpu.VMEM((rows, cols), F32)]
-
-
-def load_parts(net, src, part, made):
-    for k, step in enumerate(STEPS):
-        def bring(k=k, step=step):
-            yield [net.load(src.at[pl.ds(net.at('x', step) * 2, 2)], part.at[k])]
-            fire(net, made[k])
-
-        net.spawn(bring())
 
 
 class Sums:
@@ -658,8 +621,6 @@
         body(net, *refs[:-5])
         net.finish()
         assert net.n_remote <= remote and net.n_local <= local, (body.__name__, net.n_remote, net.n_local)
-        if PRINT:
-            print(body.__name__, net.n_remote, net.n_local, round(net.now, 1))
 
     return pl.pallas_call(
         kernel, out_shape=out_shape, in_specs=[spaces[s] for s in in_spaces], out_specs=[spaces[s] for s in out_spaces],
@@ -670,14 +631,10 @@
         name=body.__name__)(*args)
 
 
-PRINT = False
-SCOPES = False
-
-
 WIDE = 512
 EARLY = 3
-GRAD_TIME = 3.4
-SLACK = 0.1
+GRAD_TIME = 4.25
+SLACK = 0.3
 R_HIDDEN, R_DOWN, R_BACK, R_TURN, R_DDOWN, R_DDOWN2, R_DUP, R_OUT, R_PRE, R_GUP, R_GDOWN, R_DX = 2, 1, 3, 1, 2, 2, 4, 2, 2, 3, 3, 2
 R_DU, HOLD = (3, 3.1, 3.2, 3.3), (0, 1, 2)
 WINDOWS = (2, 2, 2, 2, 2, 2, 2, 2)
@@ -861,15 +818,14 @@
             names = ('blocks', 'blocks1', 'sent_u', 'got_u', 'got_g', 'sent_up0', 'sent_down0', 'sent_up1', 'sent_down1', 'got_up0', 'got_down0',
                      'got_up1', 'got_down1', 'saved', 'free0', 'reduced0', 'ds_made', 'got_u1', 'hidden', 'all_du', 'reduced1', 'sent_dy', 'got_dy',
                      'back_up0', 'back_up0_rest', 'back_down0', 'd_down1', 'd_up1', 'y_reduced', 'acts', 'd_down0', 'da0', 'd_up0', 'du_reduced',
-                     'out_up1', 'out_up0', 'got_u0', 'y_made', 'x_saved', 'weights_in', 'd_down1_0')
-            ev = {name: Event(name=name) for name in names}
+                     'out_up1', 'out_up0', 'got_u0', 'y_made', 'x_saved', 'weights_in', 'd_down1_0', 'relayed0')
+            ev = {name: Event() for name in names}
             for kind in ('up', 'down'):
                 for layer in range(2):
                     for k in range(2):
-                        ev['sum_%s%d%d' % (kind, layer, k)] = Event(name='sum_%s%d%d' % (kind, layer, k))
+                        ev['sum_%s%d%d' % (kind, layer, k)] = Event()
             ev['got_up0'].rank = R_HIDDEN
-            hidden_made, made0, made1, y_made, du_made = ([Event(name='%s%d' % (name, k)) for k in range(RING)]
-                                                          for name in ('hidden_', 'made0_', 'made1_', 'y_made_', 'du_made_'))
+            hidden_made, made0, made1, y_made, du_made = ([Event() for _ in STEPS] for _ in range(5))
             wide = width // 2
             half_up = nd * ur // 2
             act_pool, rs_pool = Pool(), Pool()
@@ -929,19 +885,19 @@
                 for k, step in enumerate(STEPS):
                     hidden_rows(net, net.at('x', step), u, up0, ds, s)
                     fire(net, hidden_made[k])
-                    yield [Event(net.now, R_HIDDEN)]
+                    yield [Event(net.now, R_HIDDEN)] + ([ev['relayed0']] if k == 1 else [])
                 yield [net.load(ds, a_out), net.load(s, s_out), net.load(u, u_out)]
                 fire(net, ev['saved'])
 
             def down_flow():
                 for k, step in enumerate(STEPS):
-                    yield [hidden_made[k], ev['got_down0'], Event(0.0, R_DOWN)]
+                    yield [hidden_made[k], ev['got_down0'], Event(0.0, R_DOWN)] + ([ev['relayed0']] if k == 1 else [])
                     down_rows(net, net.at('x', step), s, down0, part.at[k])
                     fire(net, made0[k])
                 fire(net, ev['free0'])
 
-            net.spawn(reduce_x(net, part, made0, rx_scratch, ev['reduced0'], rs_pool))
-            here = {step: Event(name='u%d' % step) for step in STEPS}
+            net.spawn(reduce_x(net, part, made0, rx_scratch, ev['reduced0'], rs_pool, ev['relayed0']))
+            here = {step: Event() for step in STEPS}
             dy_here = {step: Event() for step in STEPS}
 
             def next_layer():

time: 312 us -> 313 us (level)
  no operation moved by 1% of the time
where the time goes in v13:
time: 313 us; the launch traced here: 312 us
  Pallas kernels  311 us (99%)
    pallas_call x1, Pallas kernels, call(): pl.pallas_call(kernel, out_shape=out_shape, in_specs=[spaces[s] for s in...  308 us

profile of v13, /device:TPU:1, one launch (start us, length us, event | category | flops | bytes accessed | tf_op | source)
XLA Modules:
  0.0 311.9 jit_solution(255570659904543222)
XLA Ops:
  0.6 307.9 %step.1 = (bf16[128,2048]{1,0:T(8,128)(2,1)}, bf16[128,2048]{1,0:T(8,128)(2,1)}, bf16[2,128,1024]{2,1,0:T(8,128)(2,1)}, bf16[8,128,2048]{2,1,0:T(8,128)(2,1)}, b...) custom-call(bf16[128,2048]{1,0:T(8,128)(2,1)} %refs_0_.1, ...), custom_call_target="tpu_custom_call" | custom-call | flops 100000000 | bytes 10000000 | tf_op jit(solution)/shard_map/step/pallas_call | solution.py:625
  308.6 3.1 %finish.1 = (bf16[128,2048]{1,0:T(8,128)(2,1)}, bf16[128,2048]{1,0:T(8,128)(2,1)}, f32[2,16,8192]{2,1,0:T(8,128)}, f32[2,64,2048]{2,1,0:T(8,128)}) custom-call(f32[8,16,1024]{2,1,0:T(8,128)} %get-tuple-element.10.refs_0_, f32[8,16,1024]{2,1,0:T(8,128)} %get-tuple-element.11.refs_1_, f32[64,2048]{1,0:T(8,128)} %get-tuple-element.12.refs_2_, ...), custom_call_target="tpu_custom_call" | custom-call | tf_op jit(solution)/shard_map/finish/pallas_call | solution.py:1138

commit v14 on v13

--- a/solution.py
+++ b/solution.py
@@ -281,9 +281,10 @@
     net.spend(0.2)
 
 
-def gather_x(net, full, done, issued=None, chips=None, pool=None):
-    half = full.shape[1] // 2
-    lo, hi = pl.ds(0, half), pl.ds(half, half)
+def gather_x(net, full, done, issued=None, chips=None, pool=None, strip=(0, 1)):
+    size = full.shape[1] // strip[1]
+    base, half = strip[0] * size, size // 2
+    lo, hi, both = pl.ds(base, half), pl.ds(base + half, half), pl.ds(base, size)
     chips = chips or {step: Event() for step in STEPS}
     left = [2]
     done.copies = []
@@ -293,7 +294,7 @@
         return done.copies[-1]
 
     def block(step):
-        return full.at[net.block(step)]
+        return full.at[net.block(step), both]
 
     def part(step, rows):
         return full.at[net.block(step), rows]
@@ -409,54 +410,67 @@
 STEPS = (2, 1, -1, 0)
 
 
-def reduce_x(net, part, made, scratch, done, pool=None, relayed=None):
+def reduce_x(net, part, made, scratch, done, pool=None, relayed=None, strips=None):
     other, relay_f, relay_b, last_f, last_b = scratch
-    half = part.shape[2] // 2
-    lo, hi = pl.ds(0, half), pl.ds(half, half)
+    strips = strips or [Event()]
+    size = part.shape[2] // len(strips)
+    done.copies = []
 
     def acc(k, rows=None):
         return part.at[k, net.core] if rows is None else part.at[k, net.core, rows]
 
-    pairs = [None] * RING
+    def send(*args):
+        done.copies.append(net.send(*args, pool=pool))
+        return done.copies[-1]
+
     ready = [Event() for _ in STEPS]
 
     def pair(k):
         yield [made[k]]
-        pairs[k] = net.send(part.at[k, net.other], other.at[k], 'p', pool=pool)
-        yield [pairs[k]]
+        yield [send(part.at[k, net.other], other.at[k], 'p')]
         add_into(net, acc(k), other.at[k])
         fire(net, ready[k])
 
     for k in range(RING):
         net.spawn(pair(k))
-    sent = {}
-    started, relayed = Event(), relayed or Event()
-
-    def part_flow(k):
-        yield [ready[k]] + ([relayed] if k else [])
-        if k == 0:
-            sent['first_f'] = net.send(acc(0, lo), relay_f, 'x', 1, pool=pool)
-            sent['first_b'] = net.send(acc(0, hi), relay_b, 'x', -1, pool=pool)
-            fire(net, relayed)
-        elif k == 1:
-            sent['direct_f'] = net.send(acc(1, hi), last_f.at[hi], 'x', 1, pool=pool)
-        else:
-            sent['direct_b'] = net.send(acc(2, lo), last_b.at[lo], 'x', -1, pool=pool)
-        if len(sent) == 4:
-            fire(net, started)
-
-    for k in range(3):
-        net.spawn(part_flow(k))
-    yield [started]
-    yield [sent['first_f']]
-    add_into(net, acc(1, lo), relay_f)
-    summed_f = net.send(acc(1, lo), last_f.at[lo], 'x', 1, pool=pool)
-    yield [sent['first_b']]
-    add_into(net, acc(2, hi), relay_b)
-    summed_b = net.send(acc(2, hi), last_b.at[hi], 'x', -1, pool=pool)
-    yield [ready[3], sent['direct_f'], sent['direct_b'], summed_f, summed_b]
-    add_into(net, acc(3), last_f, last_b)
-    done.copies = pairs + list(sent.values()) + [summed_f, summed_b]
+
+    def strip(n, end):
+        half = size // 2
+        lo, hi, both, relay_rows = pl.ds(n * size, half), pl.ds(n * size + half, half), pl.ds(n * size, size), pl.ds(n * half, half)
+        sent = {}
+        started, relay_sent = Event(), Event()
+
+        def part_flow(k):
+            yield [ready[k]] + ([relay_sent] if k else [])
+            if k == 0:
+                sent['first_f'] = send(acc(0, lo), relay_f.at[relay_rows], 'x', 1)
+                sent['first_b'] = send(acc(0, hi), relay_b.at[relay_rows], 'x', -1)
+                fire(net, relay_sent)
+                if n == len(strips) - 1 and relayed is not None:
+                    fire(net, relayed)
+            elif k == 1:
+                sent['direct_f'] = send(acc(1, hi), last_f.at[hi], 'x', 1)
+            else:
+                sent['direct_b'] = send(acc(2, lo), last_b.at[lo], 'x', -1)
+            if len(sent) == 4:
+                fire(net, started)
+
+        for k in range(3):
+            net.spawn(part_flow(k))
+        yield [started]
+        yield [sent['first_f']]
+        add_into(net, acc(1, lo), relay_f.at[relay_rows])
+        summed_f = send(acc(1, lo), last_f.at[lo], 'x', 1)
+        yield [sent['first_b']]
+        add_into(net, acc(2, hi), relay_b.at[relay_rows])
+        summed_b = send(acc(2, hi), last_b.at[hi], 'x', -1)
+        yield [ready[3], sent['direct_f'], sent['direct_b'], summed_f, summed_b]
+        add_into(net, acc(3, both), last_f.at[both], last_b.at[both])
+        fire(net, end)
+
+    for n, end in enumerate(strips):
+        net.spawn(strip(n, end))
+    yield strips
     fire(net, done)
 
 
@@ -633,16 +647,17 @@
 
 WIDE = 512
 EARLY = 3
+STRIPS = 2
 GRAD_TIME = 4.25
-SLACK = 0.3
-R_HIDDEN, R_DOWN, R_BACK, R_TURN, R_DDOWN, R_DDOWN2, R_DUP, R_OUT, R_PRE, R_GUP, R_GDOWN, R_DX = 2, 1, 3, 1, 2, 2, 4, 2, 2, 3, 3, 2
-R_DU, HOLD = (3, 3.1, 3.2, 3.3), (0, 1, 2)
-WINDOWS = (2, 2, 2, 2, 2, 2, 2, 2)
+SLACK = 0.4
+R_HIDDEN, R_DOWN, R_BACK, R_TURN, R_DDOWN, R_DDOWN2, R_DUP, R_OUT, R_PRE, R_GUP, R_GDOWN, R_DX = 2, 1, 3, 1, 2, 2, 4, 2, 2, 1, 3, 2
+R_DU, HOLD = (3, 3.1, 3, 3.3), (0, 1, 2, 3)
+WINDOWS = (2, 2, 3, 2, 1, 2, 3, 4)
 AXES = ('yz', 'yz', 'yz', 'yz')
 TOP = 6
 NEAR = 'z'
 LEAD = (3, 3, 3)
-TR, TS, TL = 264, 56, 9
+TR, TS, TL = 281, 64, 9
 
 
 def wide_loop(total, body):
@@ -896,22 +911,43 @@
                     fire(net, made0[k])
                 fire(net, ev['free0'])
 
-            net.spawn(reduce_x(net, part, made0, rx_scratch, ev['reduced0'], rs_pool, ev['relayed0']))
             here = {step: Event() for step in STEPS}
             dy_here = {step: Event() for step in STEPS}
+
+            strips0 = [Event() for _ in range(STRIPS)]
+            net.spawn(reduce_x(net, part, made0, rx_scratch, ev['reduced0'], rs_pool, ev['relayed0'], strips0))
 
             def next_layer():
                 yield [ev['saved'], ev['got_g']]
                 net.drain(ev['got_u'].copies + ev['got_g'].copies)
                 credit = net.grant(3, 'xp')
-                yield [ev['reduced0'], credit]
-                add_rows(x, part.at[3, net.core], x)
-                norm_rows(x, u.at[net.data])
-                net.spend(1.0)
-                net.spawn(gather_x(net, u, ev['got_u1'], chips=here, pool=act_pool.again()))
+                act_pool.again()
+                got = [Event() for _ in strips0]
+                chips = [{step: Event() for step in STEPS} for _ in strips0]
+
+                def strip(n):
+                    at = pl.ds(n * (rows // STRIPS), rows // STRIPS)
+                    yield [strips0[n], credit]
+                    add_rows(x.at[at], part.at[3, net.core, at], x.at[at])
+                    norm_rows(x.at[at], u.at[net.data, at])
+                    net.spend(1.0 / STRIPS)
+                    net.spawn(gather_x(net, u, got[n], chips=chips[n], pool=act_pool, strip=(n, STRIPS)))
+
+                def chip(step):
+                    yield [arrived[step] for arrived in chips]
+                    fire(net, here[step])
+
+                for n in range(STRIPS):
+                    net.spawn(strip(n))
+                for step in STEPS:
+                    net.spawn(chip(step))
+                yield [ev['reduced0']]
                 net.drain(ev['reduced0'].copies)
                 yield [net.grant(4, 'xp')]
                 net.spawn(reduce_x(net, part, made1, rx_scratch, ev['reduced1'], rs_pool.again()))
+                yield got
+                ev['got_u1'].copies = sum((event.copies for event in got), [])
+                fire(net, ev['got_u1'])
 
             def back_flow():
                 for k, step in enumerate(STEPS):

time: 313 us -> 311 us (level)
  no operation moved by 1% of the time
where the time goes in v14:
time: 311 us; the launch traced here: 310 us
  Pallas kernels  309 us (99%)
    pallas_call x1, Pallas kernels, call(): pl.pallas_call(kernel, out_shape=out_shape, in_specs=[spaces[s] for s in...  306 us

profile of v14, /device:TPU:1, one launch (start us, length us, event | category | flops | bytes accessed | tf_op | source)
XLA Modules:
  0.0 310.1 jit_solution(4342427468034399923)
XLA Ops:
  0.6 306.1 %step.1 = (bf16[128,2048]{1,0:T(8,128)(2,1)}, bf16[128,2048]{1,0:T(8,128)(2,1)}, bf16[2,128,1024]{2,1,0:T(8,128)(2,1)}, bf16[8,128,2048]{2,1,0:T(8,128)(2,1)}, b...) custom-call(bf16[128,2048]{1,0:T(8,128)(2,1)} %refs_0_.1, ...), custom_call_target="tpu_custom_call" | custom-call | flops 100000000 | bytes 10000000 | tf_op jit(solution)/shard_map/step/pallas_call | solution.py:639
  306.8 3.1 %finish.1 = (bf16[128,2048]{1,0:T(8,128)(2,1)}, bf16[128,2048]{1,0:T(8,128)(2,1)}, f32[2,16,8192]{2,1,0:T(8,128)}, f32[2,64,2048]{2,1,0:T(8,128)}) custom-call(f32[8,16,1024]{2,1,0:T(8,128)} %get-tuple-element.10.refs_0_, f32[8,16,1024]{2,1,0:T(8,128)} %get-tuple-element.11.refs_1_, f32[64,2048]{1,0:T(8,128)} %get-tuple-element.12.refs_2_, ...), custom_call_target="tpu_custom_call" | custom-call | tf_op jit(solution)/shard_map/finish/pallas_call | solution.py:1174

commit v15 on v14

--- a/solution.py
+++ b/solution.py
@@ -18,7 +18,7 @@
 LOCAL_RATE = 3000e3
 HOP = 2.4
 PAIR_HOP = 1.0
-ENTRY = 4.2
+ENTRY = 3.2
 GELU_C = 0.7978845608028654
 
 
@@ -44,6 +44,17 @@
 
     def wait(self):
         pl.semaphore_wait(self.semaphore, self.count)
+
+
+class Both:
+    def __init__(self, net, dst, one, two):
+        self.desc = pltpu.make_async_remote_copy(
+            src_ref=dst, dst_ref=dst, send_sem=net.send_sems.at[one.slot], recv_sem=net.recv_sems.at[one.receive],
+            device_id=net.device('p', 1), device_id_type=MESH)
+        self.time, self.rank, self.waited = max(one.time, two.time), 0, False
+
+    def wait(self):
+        self.desc.wait_recv()
 
 
 class Pool:
@@ -129,15 +140,17 @@
         over = [copy for copy in self.sent if copy.time + 1.5 < self.now]
         self.drain(over[:int(gap / 0.05)])
 
-    def send(self, src, dst, axis, step=1, pool=None):
-        if pool is not None and pool.next < len(pool.slots):
+    def send(self, src, dst, axis, step=1, pool=None, partner=None):
+        if partner is not None:
+            k = partner.receive
+        elif pool is not None and pool.next < len(pool.slots):
             k = pool.slots[pool.next]
         else:
             k = self.n_remote
             self.n_remote += 1
             if pool is not None:
                 pool.slots.append(k)
-        if pool is not None:
+        if pool is not None and partner is None:
             pool.next += 1
         if not self.free_sends:
             over = [copy for copy in self.sent if copy.time + 1.0 < self.now]
@@ -159,7 +172,7 @@
         done = max(self.free.get(key, 0.0), self.now) + size / rate
         self.free[key] = done
         copy = Copy(desc, done + extra + (PAIR_HOP if axis == 'p' else HOP), True)
-        copy.slot = send_slot
+        copy.slot, copy.receive = send_slot, k
         self.sent.append(copy)
         return copy
 
@@ -492,8 +505,8 @@
         lo, hi, all_rows = pl.ds(0, half), pl.ds(half, half), pl.ds(0, 2 * half)
         done.copies = []
 
-        def send(*args):
-            done.copies.append(net.send(*args, pool=pool))
+        def send(*args, partner=None):
+            done.copies.append(net.send(*args, pool=pool, partner=partner))
             return done.copies[-1]
 
         def term(one, two, rows=all_rows):
@@ -525,13 +538,13 @@
             yield [first_f, got[0][k]]
             add_into(net, relay1.at[0, k], ahead)
             fire(net, chain[0][k + 1])
-            summed_f = send(relay1.at[0, k], last1.at[0, k, lo], first, 1)
+            summed_f = send(relay1.at[0, k], last1.at[0, k, lo], first, 1, partner=direct_f)
             yield [first_b, got[1][k]]
             add_into(net, relay1.at[1, k], behind)
             fire(net, chain[1][k + 1])
-            summed_b = send(relay1.at[1, k], last1.at[1, k, hi], first, -1)
+            summed_b = send(relay1.at[1, k], last1.at[1, k, hi], first, -1, partner=direct_b)
             fire(net, passed[k])
-            yield [direct_f, direct_b, summed_f, summed_b, got[2][k]]
+            yield [Both(net, last1.at[0, k], direct_f, summed_f), Both(net, last1.at[1, k], direct_b, summed_b), got[2][k]]
             add_into(net, last1.at[0, k], last1.at[1, k], mine)
             fire(net, chain[2][k + 1])
             fire(net, ends[k])
@@ -551,11 +564,11 @@
         direct_b = send(sums(2, lo), last2.at[1, lo], second, -1)
         yield [first_f]
         add_into(net, sums(1, lo), relay2.at[0])
-        summed_f = send(sums(1, lo), last2.at[0, lo], second, 1)
+        summed_f = send(sums(1, lo), last2.at[0, lo], second, 1, partner=direct_f)
         yield [first_b]
         add_into(net, sums(2, hi), relay2.at[1])
-        summed_b = send(sums(2, hi), last2.at[1, hi], second, -1)
-        yield [ends[3], direct_f, direct_b, summed_f, summed_b]
+        summed_b = send(sums(2, hi), last2.at[1, hi], second, -1, partner=direct_b)
+        yield [ends[3], Both(net, last2.at[0], direct_f, summed_f), Both(net, last2.at[1], direct_b, summed_b)]
         add_into(net, sums(3), last2.at[0], last2.at[1])
         done.total = sums(3)
         fire(net, done)
@@ -657,7 +670,7 @@
 TOP = 6
 NEAR = 'z'
 LEAD = (3, 3, 3)
-TR, TS, TL = 281, 64, 9
+TR, TS, TL = 260, 64, 11
 
 
 def wide_loop(total, body):
@@ -872,12 +885,14 @@
                 net.spawn(join('got_', got))
                 net.spawn(join('sent_', sent))
 
+            net.enter()
+            gather('down0', w_down_in.at[0], down0, False)
             net.take(inputs)
             split_columns(ds, s, num_layers * ur)
+            net.spend(0.6)
+            net.spawn(exchange(net, lambda k: s.at[k, pl.ds(0, ur)], block_out.at[0], ev['blocks'], pools['blocks'][0]))
             norm_rows(x, u.at[net.data])
-            net.enter()
-            gather('down0', w_down_in.at[0], down0, False)
-            net.spawn(exchange(net, lambda k: s.at[k, pl.ds(0, ur)], block_out.at[0], ev['blocks'], pools['blocks'][0]))
+            net.spend(0.7)
             own_grads = net.load(g_in, g.at[net.data])
 
             def up_first():

time: 311 us -> 313 us (level)
  no operation moved by 1% of the time
where the time goes in v15:
time: 313 us; the launch traced here: 312 us
  Pallas kernels  311 us (99%)
    pallas_call x1, Pallas kernels, call(): pl.pallas_call(kernel, out_shape=out_shape, in_specs=[spaces[s] for s in...  308 us

profile of v15, /device:TPU:1, one launch (start us, length us, event | category | flops | bytes accessed | tf_op | source)
XLA Modules:
  0.0 312.1 jit_solution(5311980174871537349)
XLA Ops:
  0.6 308.1 %step.1 = (bf16[128,2048]{1,0:T(8,128)(2,1)}, bf16[128,2048]{1,0:T(8,128)(2,1)}, bf16[2,128,1024]{2,1,0:T(8,128)(2,1)}, bf16[8,128,2048]{2,1,0:T(8,128)(2,1)}, b...) custom-call(bf16[128,2048]{1,0:T(8,128)(2,1)} %refs_0_.1, ...), custom_call_target="tpu_custom_call" | custom-call | flops 100000000 | bytes 10000000 | tf_op jit(solution)/shard_map/step/pallas_call | solution.py:652
  308.8 3.1 %finish.1 = (bf16[128,2048]{1,0:T(8,128)(2,1)}, bf16[128,2048]{1,0:T(8,128)(2,1)}, f32[2,16,8192]{2,1,0:T(8,128)}, f32[2,64,2048]{2,1,0:T(8,128)}) custom-call(f32[8,16,1024]{2,1,0:T(8,128)} %get-tuple-element.10.refs_0_, f32[8,16,1024]{2,1,0:T(8,128)} %get-tuple-element.11.refs_1_, f32[64,2048]{1,0:T(8,128)} %get-tuple-element.12.refs_2_, ...), custom_call_target="tpu_custom_call" | custom-call | tf_op jit(solution)/shard_map/finish/pallas_call | solution.py:1189

commit v16 on v15

--- a/solution.py
+++ b/solution.py
@@ -18,7 +18,7 @@
 LOCAL_RATE = 3000e3
 HOP = 2.4
 PAIR_HOP = 1.0
-ENTRY = 3.2
+ENTRY = 4.2
 GELU_C = 0.7978845608028654
 
 
@@ -670,7 +670,7 @@
 TOP = 6
 NEAR = 'z'
 LEAD = (3, 3, 3)
-TR, TS, TL = 260, 64, 11
+TR, TS, TL = 260, 64, 9
 
 
 def wide_loop(total, body):
@@ -885,12 +885,11 @@
                 net.spawn(join('got_', got))
                 net.spawn(join('sent_', sent))
 
-            net.enter()
-            gather('down0', w_down_in.at[0], down0, False)
             net.take(inputs)
             split_columns(ds, s, num_layers * ur)
-            net.spend(0.6)
+            net.enter()
             net.spawn(exchange(net, lambda k: s.at[k, pl.ds(0, ur)], block_out.at[0], ev['blocks'], pools['blocks'][0]))
+            gather('down0', w_down_in.at[0], down0, False)
             norm_rows(x, u.at[net.data])
             net.spend(0.7)
             own_grads = net.load(g_in, g.at[net.data])

time: 313 us -> 311 us (level)
  no operation moved by 1% of the time
where the time goes in v16:
time: 311 us; the launch traced here: 310 us
  Pallas kernels  309 us (99%)
    pallas_call x1, Pallas kernels, call(): pl.pallas_call(kernel, out_shape=out_shape, in_specs=[spaces[s] for s in...  306 us

profile of v16, /device:TPU:1, one launch (start us, length us, event | category | flops | bytes accessed | tf_op | source)
XLA Modules:
  0.0 309.8 jit_solution(6392517373553048949)
XLA Ops:
  0.6 305.9 %step.1 = (bf16[128,2048]{1,0:T(8,128)(2,1)}, bf16[128,2048]{1,0:T(8,128)(2,1)}, bf16[2,128,1024]{2,1,0:T(8,128)(2,1)}, bf16[8,128,2048]{2,1,0:T(8,128)(2,1)}, b...) custom-call(bf16[128,2048]{1,0:T(8,128)(2,1)} %refs_0_.1, ...), custom_call_target="tpu_custom_call" | custom-call | flops 100000000 | bytes 10000000 | tf_op jit(solution)/shard_map/step/pallas_call | solution.py:652
  306.5 3.1 %finish.1 = (bf16[128,2048]{1,0:T(8,128)(2,1)}, bf16[128,2048]{1,0:T(8,128)(2,1)}, f32[2,16,8192]{2,1,0:T(8,128)}, f32[2,64,2048]{2,1,0:T(8,128)}) custom-call(f32[8,16,1024]{2,1,0:T(8,128)} %get-tuple-element.10.refs_0_, f32[8,16,1024]{2,1,0:T(8,128)} %get-tuple-element.11.refs_1_, f32[64,2048]{1,0:T(8,128)} %get-tuple-element.12.refs_2_, ...), custom_call_target="tpu_custom_call" | custom-call | tf_op jit(solution)/shard_map/finish/pallas_call | solution.py:1188

commit v17 on v16

--- a/solution.py
+++ b/solution.py
@@ -662,10 +662,10 @@
 EARLY = 3
 STRIPS = 2
 GRAD_TIME = 4.25
-SLACK = 0.4
-R_HIDDEN, R_DOWN, R_BACK, R_TURN, R_DDOWN, R_DDOWN2, R_DUP, R_OUT, R_PRE, R_GUP, R_GDOWN, R_DX = 2, 1, 3, 1, 2, 2, 4, 2, 2, 1, 3, 2
+SLACK = 0.3
+R_HIDDEN, R_DOWN, R_BACK, R_TURN, R_DDOWN, R_DDOWN2, R_DUP, R_OUT, R_PRE, R_GUP, R_GDOWN, R_DX = 2, 1, 3, 1, 2, 2, 4, 2, 2, 3, 3, 2
 R_DU, HOLD = (3, 3.1, 3, 3.3), (0, 1, 2, 3)
-WINDOWS = (2, 2, 3, 2, 1, 2, 3, 4)
+WINDOWS = (2, 2, 2, 2, 2, 2, 2, 4)
 AXES = ('yz', 'yz', 'yz', 'yz')
 TOP = 6
 NEAR = 'z'

time: 311 us -> 310 us (level)
  no operation moved by 1% of the time
where the time goes in v17:
time: 310 us
  Pallas kernels  309 us (100%)
    pallas_call x1, Pallas kernels, call(): pl.pallas_call(kernel, out_shape=out_shape, in_specs=[spaces[s] for s in...  306 us

profile of v17, /device:TPU:1, one launch (start us, length us, event | category | flops | bytes accessed | tf_op | source)
XLA Modules:
  0.0 309.5 jit_solution(3889211988827571195)
XLA Ops:
  0.6 305.6 %step.1 = (bf16[128,2048]{1,0:T(8,128)(2,1)}, bf16[128,2048]{1,0:T(8,128)(2,1)}, bf16[2,128,1024]{2,1,0:T(8,128)(2,1)}, bf16[8,128,2048]{2,1,0:T(8,128)(2,1)}, b...) custom-call(bf16[128,2048]{1,0:T(8,128)(2,1)} %refs_0_.1, ...), custom_call_target="tpu_custom_call" | custom-call | flops 100000000 | bytes 10000000 | tf_op jit(solution)/shard_map/step/pallas_call | solution.py:652
  306.2 3.1 %finish.1 = (bf16[128,2048]{1,0:T(8,128)(2,1)}, bf16[128,2048]{1,0:T(8,128)(2,1)}, f32[2,16,8192]{2,1,0:T(8,128)}, f32[2,64,2048]{2,1,0:T(8,128)}) custom-call(f32[8,16,1024]{2,1,0:T(8,128)} %get-tuple-element.10.refs_0_, f32[8,16,1024]{2,1,0:T(8,128)} %get-tuple-element.11.refs_1_, f32[64,2048]{1,0:T(8,128)} %get-tuple-element.12.refs_2_, ...), custom_call_target="tpu_custom_call" | custom-call | tf_op jit(solution)/shard_map/finish/pallas_call | solution.py:1188

commit v18 on v17

--- a/solution.py
+++ b/solution.py
@@ -662,10 +662,10 @@
 EARLY = 3
 STRIPS = 2
 GRAD_TIME = 4.25
-SLACK = 0.3
+SLACK = 0.2
 R_HIDDEN, R_DOWN, R_BACK, R_TURN, R_DDOWN, R_DDOWN2, R_DUP, R_OUT, R_PRE, R_GUP, R_GDOWN, R_DX = 2, 1, 3, 1, 2, 2, 4, 2, 2, 3, 3, 2
 R_DU, HOLD = (3, 3.1, 3, 3.3), (0, 1, 2, 3)
-WINDOWS = (2, 2, 2, 2, 2, 2, 2, 4)
+WINDOWS = (2, 2, 2, 2, 2, 2, 2, 2)
 AXES = ('yz', 'yz', 'yz', 'yz')
 TOP = 6
 NEAR = 'z'

time: 310 us -> 312 us (level)
  no operation moved by 1% of the time
where the time goes in v18:
time: 312 us; the launch traced here: 311 us
  Pallas kernels  310 us (99%)
    pallas_call x1, Pallas kernels, call(): pl.pallas_call(kernel, out_shape=out_shape, in_specs=[spaces[s] for s in...  307 us

profile of v18, /device:TPU:1, one launch (start us, length us, event | category | flops | bytes accessed | tf_op | source)
XLA Modules:
  0.0 310.9 jit_solution(6030205157334224967)
XLA Ops:
  0.6 306.9 %step.1 = (bf16[128,2048]{1,0:T(8,128)(2,1)}, bf16[128,2048]{1,0:T(8,128)(2,1)}, bf16[2,128,1024]{2,1,0:T(8,128)(2,1)}, bf16[8,128,2048]{2,1,0:T(8,128)(2,1)}, b...) custom-call(bf16[128,2048]{1,0:T(8,128)(2,1)} %refs_0_.1, ...), custom_call_target="tpu_custom_call" | custom-call | flops 100000000 | bytes 10000000 | tf_op jit(solution)/shard_map/step/pallas_call | solution.py:652
  307.6 3.1 %finish.1 = (bf16[128,2048]{1,0:T(8,128)(2,1)}, bf16[128,2048]{1,0:T(8,128)(2,1)}, f32[2,16,8192]{2,1,0:T(8,128)}, f32[2,64,2048]{2,1,0:T(8,128)}) custom-call(f32[8,16,1024]{2,1,0:T(8,128)} %get-tuple-element.10.refs_0_, f32[8,16,1024]{2,1,0:T(8,128)} %get-tuple-element.11.refs_1_, f32[64,2048]{1,0:T(8,128)} %get-tuple-element.12.refs_2_, ...), custom_call_target="tpu_custom_call" | custom-call | tf_op jit(solution)/shard_map/finish/pallas_call | solution.py:1188
